TPU v7x, 32 devices: a whole 2x2x4 slice. The times are simulated.
32 devices in a mesh: rep: 8 (over y, x, core), shard: 4 (over z).
Axes of the slice: x: 2, y: 2, z: 4, core: 2. Of those that a mesh axis runs over, the one named last changes fastest.
Arguments:
- tokens: bfloat16 [4096, 2048], P(('rep', 'shard')), may hold values from -6 to 6
- segments: int32 [32, 128], P(('rep', 'shard')), may hold values from 0 to 7, never falling along the last dimension, each value on 1 to 64 neighbouring positions
- routes: int32 [4096, 8], P(('rep', 'shard')), may hold values from 0 to 31, all different within a row; in each aligned block of 128 rows (0 to 127, 128 to 255, ...) at most 64 rows name the same one
- attn_gain: bfloat16 [2048], P('shard'), may hold values from 0.5 to 1.5
- w_query: bfloat16 [2048, 4096], P('shard'), may hold values from -0.125 to 0.125
- key_weight: bfloat16 [2048, 512], P('shard'), may hold values from -0.125 to 0.125
- value_weight: bfloat16 [2048, 512], P('shard'), may hold values from -0.125 to 0.125
- w_out: bfloat16 [4096, 2048], P('shard'), may hold values from -0.75 to 0.75
- query_gain: bfloat16 [128], P('shard'), may hold values from 0.099609375 to 1.8984375
- key_gain: bfloat16 [128], P('shard'), may hold values from 0.099609375 to 1.8984375
- ffn_gain: bfloat16 [2048], P('shard'), may hold values from 0.5 to 1.5
- w_router: bfloat16 [2048, 32], P('shard'), may hold values from -0.125 to 0.125
- w_gate: bfloat16 [32, 2048, 768], P(('rep', 'shard')), may hold values from -0.125 to 0.125
- w_up: bfloat16 [32, 2048, 768], P(('rep', 'shard')), may hold values from -0.125 to 0.125
- w_down: bfloat16 [32, 768, 2048], P(('rep', 'shard')), may hold values from -0.875 to 0.875
- cotangent: bfloat16 [4096, 2048], P(('rep', 'shard')), may hold values from -6 to 6
Outputs:
- output: bfloat16 [4096, 2048], P(('rep', 'shard'))
- grad_tokens: float32 [4096, 2048], P(('rep', 'shard'))
- grad_attn_gain: float32 [2048], P('shard')
- grad_w_query: float32 [2048, 4096], P('shard')
- grad_w_key: float32 [2048, 512], P('shard')
- grad_w_value: float32 [2048, 512], P('shard')
- grad_w_out: float32 [4096, 2048], P('shard')
- grad_query_gain: float32 [128], P('shard')
- grad_key_gain: float32 [128], P('shard')
- grad_ffn_gain: float32 [2048], P('shard')
- grad_w_router: float32 [2048, 32], P('shard')
- grad_w_gate: float32 [32, 2048, 768], P(('rep', 'shard'))
- grad_w_up: float32 [32, 2048, 768], P(('rep', 'shard'))
- grad_w_down: float32 [32, 768, 2048], P(('rep', 'shard'))
Inputs may be any that keep to these rules, and one draw needn't show every extreme that they name: `segments`: each device's row never falls, and each sequence has 1 to 64 tokens. `routes`: each token names 8 different experts; among the tokens of one device no expert is named by more than 64 of them.
All inputs are finite; a program needn't handle non-finite values.
Results may differ from a plain program's by a relative error of at most 0.02.
Values may be sent and summed in bfloat16 or wider, within the bound.
A program may use at most 384 MiB of HBM per device.

v0:
```python
import jax
import jax.numpy as jnp
from jax import lax
from jax.sharding import PartitionSpec as P

epsilon = 1e-06
rope_base = 1000000.0
masked_score = -1e30


def inverse_rms(values):
    return lax.rsqrt(jnp.mean(values * values, axis=-1, keepdims=True) + epsilon)


def rotate(values):
    half = values.shape[-1] // 2
    return jnp.concatenate([-values[..., half:], values[..., :half]], axis=-1)


def rope_tables(segment_row, width):
    length = segment_row.shape[0]
    places = jnp.arange(length, dtype=jnp.int32)
    same = segment_row[:, None] == segment_row[None, :]
    first = jnp.min(jnp.where(same, places[None, :], length), axis=1)
    offset = (places - first).astype(jnp.float32)
    half = width // 2
    frequency = rope_base ** (-2.0 * jnp.arange(half, dtype=jnp.float32) / width)
    angle = offset[:, None] * frequency[None, :]
    cosine = jnp.concatenate([jnp.cos(angle), jnp.cos(angle)], axis=1)[:, None, :]
    sine = jnp.concatenate([jnp.sin(angle), jnp.sin(angle)], axis=1)[:, None, :]
    allowed = same & (places[None, :] <= places[:, None])
    return (cosine, sine, allowed)


def norm_back(grad_scaled, unit, inverse, gain):
    gained = grad_scaled * gain
    return inverse * (gained - unit * jnp.mean(gained * unit, axis=-1, keepdims=True))


def score_block(query_rot, key_rot, allowed, kv_heads, group):
    length, heads, head_dim = query_rot.shape
    grouped = query_rot.reshape(length, kv_heads, group, head_dim)
    scores = jnp.einsum(
        "tkgh,skh->kgts", grouped, key_rot, preferred_element_type=jnp.float32
    ) * head_dim ** (-0.5)
    return jnp.where(allowed[None, None], scores, masked_score)


def local(
    tokens,
    segments,
    routes,
    attn_gain,
    w_query,
    key_weight,
    value_weight,
    w_out,
    query_gain,
    key_gain,
    ffn_gain,
    w_router,
    w_gate,
    w_up,
    w_down,
    cotangent,
):
    device_count = lax.axis_size(("rep", "shard"))
    gathered = (
        lax.all_gather(attn_gain, "shard", axis=0, tiled=True),
        lax.all_gather(w_query, "shard", axis=0, tiled=True),
        lax.all_gather(key_weight, "shard", axis=0, tiled=True),
        lax.all_gather(value_weight, "shard", axis=0, tiled=True),
        lax.all_gather(w_out, "shard", axis=0, tiled=True),
        lax.all_gather(query_gain, "shard", axis=0, tiled=True),
        lax.all_gather(key_gain, "shard", axis=0, tiled=True),
        lax.all_gather(ffn_gain, "shard", axis=0, tiled=True),
        lax.all_gather(w_router, "shard", axis=0, tiled=True),
    )
    (
        gain_one,
        query_full,
        key_full,
        value_full,
        out_full,
        qgain_full,
        kgain_full,
        gain_two,
        router_full,
    ) = gathered
    length, width = tokens.shape
    head_dim = qgain_full.shape[0]
    heads = query_full.shape[1] // head_dim
    kv_heads = key_full.shape[1] // head_dim
    group = heads // kv_heads
    experts = router_full.shape[1]
    top = routes.shape[1]
    local_experts = w_gate.shape[0]
    capacity = 2 * length * top // experts
    wide_tokens = tokens.astype(jnp.float32)
    inverse_one = inverse_rms(wide_tokens)
    normed_one = wide_tokens * inverse_one
    hidden_in = (normed_one * gain_one.astype(jnp.float32)).astype(jnp.bfloat16)
    query_raw = jnp.dot(hidden_in, query_full, preferred_element_type=jnp.float32).reshape(
        length, heads, head_dim
    )
    key_raw = jnp.dot(hidden_in, key_full, preferred_element_type=jnp.float32).reshape(
        length, kv_heads, head_dim
    )
    values = jnp.dot(hidden_in, value_full, preferred_element_type=jnp.float32).astype(jnp.bfloat16)
    values = values.reshape(length, kv_heads, head_dim)
    inverse_query = inverse_rms(query_raw)
    query_unit = query_raw * inverse_query
    inverse_key = inverse_rms(key_raw)
    key_unit = key_raw * inverse_key
    cosine, sine, allowed = rope_tables(segments[0], head_dim)
    query_scaled = query_unit * qgain_full.astype(jnp.float32)
    key_scaled = key_unit * kgain_full.astype(jnp.float32)
    query_rot = (query_scaled * cosine + rotate(query_scaled) * sine).astype(jnp.bfloat16)
    key_rot = (key_scaled * cosine + rotate(key_scaled) * sine).astype(jnp.bfloat16)
    scores = score_block(query_rot, key_rot, allowed, kv_heads, group)
    highest = jnp.max(scores, axis=-1, keepdims=True)
    log_total = highest + jnp.log(jnp.sum(jnp.exp(scores - highest), axis=-1, keepdims=True))
    probs_low = jnp.exp(scores - log_total).astype(jnp.bfloat16)
    mixed = jnp.einsum("kgts,skh->tkgh", probs_low, values, preferred_element_type=jnp.float32)
    attn_out = mixed.reshape(length, heads * head_dim).astype(jnp.bfloat16)
    resid = wide_tokens + jnp.dot(attn_out, out_full, preferred_element_type=jnp.float32)
    inverse_two = inverse_rms(resid)
    normed_two = resid * inverse_two
    hidden_two = (normed_two * gain_two.astype(jnp.float32)).astype(jnp.bfloat16)
    logits = jnp.dot(hidden_two, router_full, preferred_element_type=jnp.float32)
    gate_probs = jax.nn.softmax(logits, axis=-1)
    chosen = routes[:, :, None] == jnp.arange(experts, dtype=jnp.int32)[None, None, :]
    picked = jnp.sum(jnp.where(chosen, gate_probs[:, None, :], 0.0), axis=-1)
    picked_total = jnp.sum(picked, axis=-1, keepdims=True)
    mix_weights = picked / picked_total
    onehot = chosen.reshape(length * top, experts).astype(jnp.int32)
    before = jnp.cumsum(onehot, axis=0) - onehot
    slot = jnp.sum(before * onehot, axis=1)
    target = routes.reshape(-1) * capacity + slot
    source_row = jnp.arange(length * top, dtype=jnp.int32) // top
    outgoing = (
        jnp.zeros((experts * capacity, width), jnp.bfloat16).at[target].set(hidden_two[source_row])
    )
    outgoing = outgoing.reshape(experts, capacity, width)
    arrived = lax.all_to_all(outgoing, ("rep", "shard"), split_axis=0, concat_axis=0, tiled=True)
    count = arrived.shape[1]
    rows = arrived.reshape(device_count, local_experts, count, width)
    gate = jnp.einsum("sxcd,xdf->sxcf", rows, w_gate, preferred_element_type=jnp.float32)
    up = jnp.einsum("sxcd,xdf->sxcf", rows, w_up, preferred_element_type=jnp.float32)
    activated = (gate * jax.nn.sigmoid(gate) * up).astype(jnp.bfloat16)
    produced = jnp.einsum(
        "sxcf,xfd->sxcd", activated, w_down, preferred_element_type=jnp.float32
    ).astype(jnp.bfloat16)
    returned = lax.all_to_all(
        produced.reshape(device_count * local_experts, count, width),
        ("rep", "shard"),
        split_axis=0,
        concat_axis=0,
        tiled=True,
    )
    results = (
        returned,
        arrived,
        gate.reshape(device_count * local_experts, count, -1),
        up.reshape(device_count * local_experts, count, -1),
    )
    returned = results[0]
    expert_rows = results[1].reshape(device_count, local_experts, capacity, width)
    gate = results[2].reshape(device_count, local_experts, capacity, -1)
    up = results[3].reshape(device_count, local_experts, capacity, -1)
    per_pair = (
        returned.reshape(experts * capacity, width)[target]
        .reshape(length, top, width)
        .astype(jnp.float32)
    )
    output = (resid + jnp.sum(mix_weights[:, :, None] * per_pair, axis=1)).astype(jnp.bfloat16)
    grad_out = cotangent.astype(jnp.float32)
    grad_mix = jnp.sum(grad_out[:, None, :] * per_pair, axis=-1)
    grad_pair = (mix_weights[:, :, None] * grad_out[:, None, :]).astype(jnp.bfloat16)
    send_grads = (
        jnp.zeros((experts * capacity, width), jnp.bfloat16)
        .at[target]
        .set(grad_pair.reshape(length * top, width))
    )
    grad_arrived = lax.all_to_all(
        send_grads.reshape(experts, capacity, width),
        ("rep", "shard"),
        split_axis=0,
        concat_axis=0,
        tiled=True,
    )
    grad_arrived = grad_arrived.reshape(device_count, local_experts, capacity, width)
    sigmoid_gate = jax.nn.sigmoid(gate)
    activated = (gate * sigmoid_gate * up).astype(jnp.bfloat16)
    grad_act = jnp.einsum(
        "sxcd,xfd->sxcf", grad_arrived, w_down, preferred_element_type=jnp.float32
    )
    grad_w_down = jnp.einsum(
        "sxcf,sxcd->xfd", activated, grad_arrived, preferred_element_type=jnp.float32
    )
    grad_gate = (grad_act * up * sigmoid_gate * (1.0 + gate * (1.0 - sigmoid_gate))).astype(
        jnp.bfloat16
    )
    grad_up = (grad_act * gate * sigmoid_gate).astype(jnp.bfloat16)
    grad_w_gate = jnp.einsum(
        "sxcd,sxcf->xdf", expert_rows, grad_gate, preferred_element_type=jnp.float32
    )
    grad_w_up = jnp.einsum(
        "sxcd,sxcf->xdf", expert_rows, grad_up, preferred_element_type=jnp.float32
    )
    grad_in = (
        jnp.einsum("sxcf,xdf->sxcd", grad_gate, w_gate, preferred_element_type=jnp.float32)
        + jnp.einsum("sxcf,xdf->sxcd", grad_up, w_up, preferred_element_type=jnp.float32)
    ).astype(jnp.bfloat16)
    grad_back = lax.all_to_all(
        grad_in.reshape(experts, capacity, width),
        ("rep", "shard"),
        split_axis=0,
        concat_axis=0,
        tiled=True,
    )
    grad_hidden_two = jnp.sum(
        grad_back.reshape(experts * capacity, width)[target]
        .reshape(length, top, width)
        .astype(jnp.float32),
        axis=1,
    )
    grad_picked = (
        grad_mix - jnp.sum(grad_mix * mix_weights, axis=-1, keepdims=True)
    ) / picked_total
    grad_probs = jnp.sum(jnp.where(chosen, grad_picked[:, :, None], 0.0), axis=1)
    grad_logits = (
        gate_probs * (grad_probs - jnp.sum(grad_picked * picked, axis=-1, keepdims=True))
    ).astype(jnp.bfloat16)
    grad_hidden_two = grad_hidden_two + jnp.dot(
        grad_logits, router_full.T, preferred_element_type=jnp.float32
    )
    grad_ffn_gain = jnp.sum(grad_hidden_two * normed_two, axis=0)
    grad_resid = grad_out + norm_back(
        grad_hidden_two, normed_two, inverse_two, gain_two.astype(jnp.float32)
    )
    grad_attn = grad_resid.astype(jnp.bfloat16)
    grad_mixed = jnp.dot(grad_attn, out_full.T, preferred_element_type=jnp.float32).astype(
        jnp.bfloat16
    )
    grad_mixed = grad_mixed.reshape(length, kv_heads, group, head_dim)
    probs = jnp.exp(score_block(query_rot, key_rot, allowed, kv_heads, group) - log_total)
    grad_weights = jnp.einsum(
        "tkgh,skh->kgts", grad_mixed, values, preferred_element_type=jnp.float32
    )
    centre = jnp.sum(probs * grad_weights, axis=-1, keepdims=True)
    grad_scores = (probs * (grad_weights - centre) * head_dim ** (-0.5)).astype(jnp.bfloat16)
    grad_values = jnp.einsum(
        "kgts,tkgh->skh", probs.astype(jnp.bfloat16), grad_mixed, preferred_element_type=jnp.float32
    )
    grad_query_rot = jnp.einsum(
        "kgts,skh->tkgh", grad_scores, key_rot, preferred_element_type=jnp.float32
    )
    grad_query_rot = grad_query_rot.reshape(length, heads, head_dim)
    grad_key_rot = jnp.einsum(
        "kgts,tkgh->skh",
        grad_scores,
        query_rot.reshape(length, kv_heads, group, head_dim),
        preferred_element_type=jnp.float32,
    )
    grad_query_scaled = grad_query_rot * cosine - rotate(grad_query_rot * sine)
    grad_key_scaled = grad_key_rot * cosine - rotate(grad_key_rot * sine)
    grad_query_gain = jnp.sum(grad_query_scaled * query_unit, axis=(0, 1))
    grad_key_gain = jnp.sum(grad_key_scaled * key_unit, axis=(0, 1))
    grad_query = norm_back(
        grad_query_scaled, query_unit, inverse_query, qgain_full.astype(jnp.float32)
    )
    grad_query = grad_query.reshape(length, heads * head_dim).astype(jnp.bfloat16)
    grad_key = norm_back(grad_key_scaled, key_unit, inverse_key, kgain_full.astype(jnp.float32))
    grad_key = grad_key.reshape(length, kv_heads * head_dim).astype(jnp.bfloat16)
    grad_value = grad_values.reshape(length, kv_heads * head_dim).astype(jnp.bfloat16)
    grad_hidden_in = (
        jnp.dot(grad_query, query_full.T, preferred_element_type=jnp.float32)
        + jnp.dot(grad_key, key_full.T, preferred_element_type=jnp.float32)
        + jnp.dot(grad_value, value_full.T, preferred_element_type=jnp.float32)
    )
    grad_attn_gain = jnp.sum(grad_hidden_in * normed_one, axis=0)
    grad_tokens = grad_resid + norm_back(
        grad_hidden_in, normed_one, inverse_one, gain_one.astype(jnp.float32)
    )
    grad_w_router = jnp.dot(hidden_two.T, grad_logits, preferred_element_type=jnp.float32)
    grad_w_out = jnp.dot(attn_out.T, grad_attn, preferred_element_type=jnp.float32)
    hidden_cols = hidden_in.T
    grad_w_query = jnp.dot(hidden_cols, grad_query, preferred_element_type=jnp.float32)
    grad_w_key = jnp.dot(hidden_cols, grad_key, preferred_element_type=jnp.float32)
    grad_w_value = jnp.dot(hidden_cols, grad_value, preferred_element_type=jnp.float32)
    pieces = (
        lax.psum_scatter(
            grad_attn_gain.astype(jnp.bfloat16), "shard", scatter_dimension=0, tiled=True
        ).astype(jnp.float32),
        lax.psum_scatter(
            grad_w_query.astype(jnp.bfloat16), "shard", scatter_dimension=0, tiled=True
        ).astype(jnp.float32),
        lax.psum_scatter(
            grad_w_key.astype(jnp.bfloat16), "shard", scatter_dimension=0, tiled=True
        ).astype(jnp.float32),
        lax.psum_scatter(
            grad_w_value.astype(jnp.bfloat16), "shard", scatter_dimension=0, tiled=True
        ).astype(jnp.float32),
        lax.psum_scatter(
            grad_w_out.astype(jnp.bfloat16), "shard", scatter_dimension=0, tiled=True
        ).astype(jnp.float32),
        lax.psum_scatter(
            grad_query_gain.astype(jnp.bfloat16), "shard", scatter_dimension=0, tiled=True
        ).astype(jnp.float32),
        lax.psum_scatter(
            grad_key_gain.astype(jnp.bfloat16), "shard", scatter_dimension=0, tiled=True
        ).astype(jnp.float32),
        lax.psum_scatter(
            grad_ffn_gain.astype(jnp.bfloat16), "shard", scatter_dimension=0, tiled=True
        ).astype(jnp.float32),
        lax.psum_scatter(
            grad_w_router.astype(jnp.bfloat16), "shard", scatter_dimension=0, tiled=True
        ).astype(jnp.float32),
    )
    owned = (
        lax.psum(pieces[0].astype(jnp.bfloat16), "rep").astype(jnp.float32),
        lax.psum(pieces[1].astype(jnp.bfloat16), "rep").astype(jnp.float32),
        lax.psum(pieces[2].astype(jnp.bfloat16), "rep").astype(jnp.float32),
        lax.psum(pieces[3].astype(jnp.bfloat16), "rep").astype(jnp.float32),
        lax.psum(pieces[4].astype(jnp.bfloat16), "rep").astype(jnp.float32),
        lax.psum(pieces[5].astype(jnp.bfloat16), "rep").astype(jnp.float32),
        lax.psum(pieces[6].astype(jnp.bfloat16), "rep").astype(jnp.float32),
        lax.psum(pieces[7].astype(jnp.bfloat16), "rep").astype(jnp.float32),
        lax.psum(pieces[8].astype(jnp.bfloat16), "rep").astype(jnp.float32),
    )
    return (
        output,
        grad_tokens,
        owned[0],
        owned[1],
        owned[2],
        owned[3],
        owned[4],
        owned[5],
        owned[6],
        owned[7],
        owned[8],
        grad_w_gate,
        grad_w_up,
        grad_w_down,
    )


def solution(mesh):
    return jax.shard_map(
        local,
        mesh=mesh,
        in_specs=(
            P(("rep", "shard"), None),
            P(("rep", "shard"), None),
            P(("rep", "shard"), None),
            P("shard"),
            P("shard", None),
            P("shard", None),
            P("shard", None),
            P("shard", None),
            P("shard"),
            P("shard"),
            P("shard"),
            P("shard", None),
            P(("rep", "shard"), None, None),
            P(("rep", "shard"), None, None),
            P(("rep", "shard"), None, None),
            P(("rep", "shard"), None),
        ),
        out_specs=(
            P(("rep", "shard"), None),
            P(("rep", "shard"), None),
            P("shard"),
            P("shard", None),
            P("shard", None),
            P("shard", None),
            P("shard", None),
            P("shard"),
            P("shard"),
            P("shard"),
            P("shard", None),
            P(("rep", "shard"), None, None),
            P(("rep", "shard"), None, None),
            P(("rep", "shard"), None, None),
        ),
        check_vma=False,
    )
```

profile of v0, /device:TPU:17, one launch (start us, length us, event | category | flops | bytes accessed | tf_op | source)
XLA Modules:
  0.0 2405.2 jit_solution(17318051869919746952)
XLA Ops:
  12.7 7.0 all-reduce.9
  20.8 12.5 all-gather.1
  33.4 9.1 all-gather
  43.3 9.0 reduce-window.6
  59.8 2.3 convolution_convert_fusion.8
  62.7 38.6 %all-gather.9.cloned.1.call-done = bf16[2048,512]{1,0:T(8,128)(2,1)} async-done(((bf16[512,512]{1,0:T(8,128)(2,1)}), bf16[2048,512]{1,0:T(8,128)(2,1)}) %all-gather.9.cloned.1.call-update) | async-done | bytes 2097168 | tf_op jit(solution)/shard_map/all_gather | solution.py:71
  101.3 2.3 fusion.97
  111.8 276.1 %all-gather.11.cloned.1.call-done = bf16[2048,4096]{1,0:T(8,128)(2,1)} async-done(((bf16[512,4096]{1,0:T(8,128)(2,1)}), bf16[2048,4096]{1,0:T(8,128)(2,1)}) %all-gather.11.cloned.1.call-update) | async-done | bytes 16777232 | tf_op jit(solution)/shard_map/all_gather | solution.py:70
  387.9 9.8 fusion.95
  397.7 3.2 copy.248
  400.9 2.3 multiply_reduce_fusion.2
  409.8 264.4 %all-gather.13.cloned.1.call-done = bf16[4096,2048]{1,0:T(8,128)(2,1)} async-done(((bf16[1024,2048]{1,0:T(8,128)(2,1)}), bf16[4096,2048]{1,0:T(8,128)(2,1)}) %all-gather.13.cloned.1.call-update) | async-done | bytes 16777232 | tf_op jit(solution)/shard_map/all_gather | solution.py:73
  674.3 8.6 multiply_reduce_fusion.5
  684.8 25.7 %scatter_custom_fusion = bf16[2048,2048]{1,0:T(8,128)(2,1)} fusion(s32[1024]{0:T(1024)S(1)} %bitcast.322, bf16[128,2048]{1,0:T(8,128)(2,1)} %multiply_convert_fusion, s32[1024]{0:T(1024)} %broadcast_clamp_fusion.1, bf16[]{:T(256)} %constant.61.clone.1), kind=kCustom, calls=%fused_computation.35 | custom fusion | bytes 8389120 | tf_op jit(solution)/shard_map/scatter | solution.py:142
  710.5 6.3 all-to-all-start
  716.8 2.1 convert_element_type.234
  718.9 186.4 %all_gather.35 = bf16[2048,32]{0,1:T(8,128)(2,1)S(1)} all-gather(bf16[512,32]{0,1:T(8,128)(2,1)S(1)} %copy-done.50), channel_id=1, replica_groups=mesh['rep'=8,'shard'=4] {'shard'}, dimensions={0}, use_global_device_ids=true | all-gather | bytes 163840 | tf_op jit(solution)/shard_map/all_gather | solution.py:77
  907.0 12.2 scatter_custom_fusion.1
  919.3 9.7 all-to-all-start.2
  929.0 11.8 fusion.33
  940.8 10.7 fusion.36
  951.5 162.6 %all-to-all-done.2 = bf16[32,64,2048]{2,1,0:T(8,128)(2,1)} async-done(((bf16[32,64,2048]{2,1,0:T(8,128)(2,1)}), bf16[32,64,2048]{2,1,0:T(8,128)(2,1)}, u32[]{:S(2)}, u32[]{:S(2)}) %all-to-all-start.2) | async-done | bytes 8388640 | tf_op jit(solution)/shard_map/all_to_all | solution.py:185
  1114.1 15.9 fusion.8
  1131.6 8.9 convolution_convert_fusion.2
  1140.5 4.9 all-to-all-start.1
  1145.5 12.2 fusion.25
  1157.7 12.4 add_convert_fusion
  1170.1 160.5 %all-to-all-done.1 = bf16[32,64,2048]{2,1,0:T(8,128)(2,1)} async-done(((bf16[32,64,2048]{2,1,0:T(8,128)(2,1)}), bf16[32,64,2048]{2,1,0:T(8,128)(2,1)}, u32[]{:S(2)}, u32[]{:S(2)}) %all-to-all-start.1) | async-done | bytes 8388640 | tf_op jit(solution)/shard_map/all_to_all | solution.py:154
  1330.6 4.5 all-to-all-start.3
  1335.2 13.4 gather_fusion
  1348.6 4.9 fusion.2
  1353.6 166.9 %all-to-all-done.3 = bf16[32,64,2048]{2,1,0:T(8,128)(2,1)} async-done(((bf16[32,64,2048]{2,1,0:T(8,128)(2,1)}), bf16[32,64,2048]{2,1,0:T(8,128)(2,1)}, u32[]{:S(2)}, u32[]{:S(2)}) %all-to-all-start.3) | async-done | bytes 8388640 | tf_op jit(solution)/shard_map/all_to_all | solution.py:215
  1520.5 13.7 gather_fusion.1
  1534.3 5.1 convert_reduce_fusion
  1541.2 11.8 fusion.55
  1555.3 5.7 broadcast_multiply_fusion.1
  1563.4 2.1 convolution_convert_fusion.5
  1567.3 2.0 fusion.57
  1569.3 2.2 convolution_convert_fusion.4
  1571.6 8.4 convolution_convert_fusion
  1582.7 4.6 fusion.50
  1587.3 2.0 copy.251
  1589.3 2.0 copy.227
  1593.2 2.8 slice_negate_fusion
  1596.0 3.8 copy.229
  1599.7 3.6 copy.230
  1603.4 3.2 multiply_reduce_fusion
  1606.7 3.0 pad_maximum_fusion
  1612.0 5.0 fusion.40
  1617.0 9.7 convolution_convert_fusion.1
  1628.1 12.0 convolution_bitcast_fusion
  1641.0 11.9 convolution_bitcast_fusion.1
  1652.9 283.4 %reduce-scatter.12.cloned.1.call-done = bf16[1024,2048]{1,0:T(8,128)(2,1)} async-done(((bf16[4096,2048]{1,0:T(8,128)(2,1)}), bf16[1024,2048]{1,0:T(8,128)(2,1)}) %reduce-scatter.12.cloned.1.call-update) | async-done | bytes 4194320 | tf_op jit(solution)/shard_map/reduce_scatter | solution.py:305
  1936.2 283.5 %reduce-scatter.6.cloned.1.call-done = bf16[512,4096]{1,0:T(8,128)(2,1)} async-done(((bf16[2048,4096]{1,0:T(8,128)(2,1)}), bf16[512,4096]{1,0:T(8,128)(2,1)}) %reduce-scatter.6.cloned.1.call-update) | async-done | bytes 4194320 | tf_op jit(solution)/shard_map/reduce_scatter | solution.py:296
  2219.7 11.9 convolution_bitcast_fusion.2
  2231.6 11.4 fusion.103
  2243.0 2.6 convolution_add_fusion.1
  2246.6 6.5 all-reduce.8
  2254.8 25.8 %all-reduce.6 = (bf16[512]{0:T(512)(128)(2,1)S(1)}, bf16[32]{0:T(256)(128)(2,1)S(1)}, bf16[32]{0:T(256)(128)(2,1)S(1)}, bf16[512]{0:T(512)(128)(2,1)S(1)}, bf16[512,32]{0,1:T(8,128)(2,1)S(1)}) all-reduce(bf16[512]{0:T(512)(128)(2,1)S(1)} %dynamic-slice.3, ...), channel_id=1, replica_groups=mesh['rep'=8,'shard'=4] {'rep'}, use_global_device_ids=true, to_apply=%region_29.30 | all-reduce | flops 17472 | bytes 69888 | tf_op jit(solution)/shard_map/psum | solution.py:322
  2283.4 99.0 %all-reduce.12.cloned.1.call-done = (bf16[512,4096]{1,0:T(8,128)(2,1)}, bf16[512,512]{1,0:T(8,128)(2,1)}, bf16[512,512]{1,0:T(8,128)(2,1)}, bf16[1024,2048]{1,0:T(8,128)(2,1)}) async-done(((bf16[512,4096]{1,0:T(8,128)(2,1)}, bf16[512,512]{1,0:T(8,128)(2,1)}, bf16[512,512]{1,0:T(8,128)(2,1)}, bf16[1024,2048]{1,0:T(8,128)(2,1)}), (bf16[512,4096]{1,0:T(8,128)(2,1)}, bf16[512,512]{1,0:T(8,128)(2,1)}, ...) | async-done | bytes 9437200 | tf_op jit(solution)/shard_map/psum | solution.py:323
  2382.4 2.1 convert_element_type.256
  2384.6 2.1 convert_element_type.258
  2386.7 6.8 convert_element_type.254
  2393.5 4.4 convert_element_type.260
  (259 shorter events, 56.3 us)
Async XLA Ops:
  7.2 1106.9 %copy-start = (bf16[1,768,2048]{2,1,0:T(8,128)(2,1)S(1)}, bf16[1,768,2048]{2,1,0:T(8,128)(2,1)}, u32[]{:S(2)}) copy-start(bf16[1,768,2048]{2,1,0:T(8,128)(2,1)} %param.30) | copy-start | bytes 9437188
  7.2 52.6 %all-gather.7.cloned.1.call-start = ((), (), s32[]{:S(2)}) async-start(), calls=%async_computation.9 | async-start | bytes 2621440 | tf_op jit(solution)/shard_map/all_gather | solution.py:72
  7.9 93.4 %all-gather.9.cloned.1.call-start = ((), (), s32[]{:S(2)}) async-start(), calls=%async_computation.10 | async-start | bytes 2621440 | tf_op jit(solution)/shard_map/all_gather | solution.py:71
  8.7 379.2 %all-gather.11.cloned.1.call-start = ((), (), s32[]{:S(2)}) async-start(), calls=%async_computation.11 | async-start | bytes 20971520 | tf_op jit(solution)/shard_map/all_gather | solution.py:70
  9.4 2.8 copy-start.62
  9.4 3.0 copy-start.63
  9.5 11.3 copy-start.57
  9.5 11.3 copy-start.58
  9.5 43.8 %copy-start.55 = (s32[1,128]{1,0:T(1,128)S(1)}, s32[1,128]{1,0:T(1,128)}, u32[]{:S(2)}) copy-start(s32[1,128]{1,0:T(1,128)} %param.17) | copy-start | bytes 1540
  9.5 664.8 %all-gather.13.cloned.1.call-start = ((), (), s32[]{:S(2)}) async-start(), calls=%async_computation.12 | async-start | bytes 20971520 | tf_op jit(solution)/shard_map/all_gather | solution.py:73
  42.4 345.4 %copy-start.29 = (f32[4,1,512]{2,1,0:T(1,128)}, f32[4,1,512]{2,1,0:T(1,128)S(1)}, u32[]{:S(2)}) copy-start(f32[4,1,512]{2,1,0:T(1,128)S(1)} %convert_element_type.271) | copy-start | bytes 24580
  53.6 350.7 %copy-start.25 = (f32[128,128]{0,1:T(8,128)}, f32[128,128]{0,1:T(8,128)S(1)}, u32[]{:S(2)}) copy-start(f32[128,128]{0,1:T(8,128)S(1)} %get-tuple-element.73) | copy-start | bytes 196612
  53.6 350.7 %copy-start.33 = (f32[128,128]{0,1:T(8,128)}, f32[128,128]{0,1:T(8,128)S(1)}, u32[]{:S(2)}) copy-start(f32[128,128]{0,1:T(8,128)S(1)} %get-tuple-element.74) | copy-start | bytes 196612
  56.5 6.3 copy-start.48
  105.5 292.2 %copy-start.19 = (f32[128,4,128]{0,2,1:T(8,128)}, f32[128,4,128]{0,2,1:T(8,128)S(1)}, u32[]{:S(2)}) copy-start(f32[128,4,128]{0,2,1:T(8,128)S(1)} %copy.205) | copy-start | bytes 786436
  397.7 5.5 copy-start.53
  400.9 2.8 copy-start.2
  405.2 2.2 copy-start.24
  405.7 2.7 copy-start.31
  674.3 10.5 copy-start.51
  710.5 8.4 copy-start.50
  710.5 196.2 %copy-start.45 = (s32[128,8]{0,1:T(8,128)S(1)}, s32[128,8]{0,1:T(8,128)}, u32[]{:S(2)}) copy-start(s32[128,8]{0,1:T(8,128)} %param.18) | copy-start | bytes 12292
  710.5 208.7 %all-to-all-start = ((bf16[32,64,2048]{2,1,0:T(8,128)(2,1)}), bf16[32,64,2048]{2,1,0:T(8,128)(2,1)}, u32[]{:S(2)}, u32[]{:S(2)}) async-start(bf16[32,64,2048]{2,1,0:T(8,128)(2,1)} %bitcast.286), calls=%async_computation | async-start | bytes 16777216 | tf_op jit(solution)/shard_map/all_to_all | solution.py:145
  919.3 194.8 %all-to-all-start.2 = ((bf16[32,64,2048]{2,1,0:T(8,128)(2,1)}), bf16[32,64,2048]{2,1,0:T(8,128)(2,1)}, u32[]{:S(2)}, u32[]{:S(2)}) async-start(bf16[32,64,2048]{2,1,0:T(8,128)(2,1)} %bitcast.287), calls=%async_computation.2 | async-start | bytes 16777216 | tf_op jit(solution)/shard_map/all_to_all | solution.py:185
  928.9 11.8 copy-start.59
  1140.5 4.9 copy-start.60
  1140.5 190.1 %all-to-all-start.1 = ((bf16[32,64,2048]{2,1,0:T(8,128)(2,1)}), bf16[32,64,2048]{2,1,0:T(8,128)(2,1)}, u32[]{:S(2)}, u32[]{:S(2)}) async-start(bf16[32,64,2048]{2,1,0:T(8,128)(2,1)} %convolution_convert_fusion.2), calls=%async_computation.1 | async-start | bytes 16777216 | tf_op jit(solution)/shard_map/all_to_all | solution.py:154
  1145.5 12.2 copy-start.61
  1145.5 12.2 copy-start.65
  1330.6 189.9 %all-to-all-start.3 = ((bf16[32,64,2048]{2,1,0:T(8,128)(2,1)}), bf16[32,64,2048]{2,1,0:T(8,128)(2,1)}, u32[]{:S(2)}, u32[]{:S(2)}) async-start(bf16[32,64,2048]{2,1,0:T(8,128)(2,1)} %add_convert_fusion), calls=%async_computation.3 | async-start | bytes 16777216 | tf_op jit(solution)/shard_map/all_to_all | solution.py:215
  1335.1 317.7 %reduce-scatter.8.cloned.1.call-start = ((), (), s32[]{:S(2)}) async-start(), calls=%async_computation.14 | async-start | bytes 2621440 | tf_op jit(solution)/shard_map/reduce_scatter | solution.py:299
  1335.2 13.4 copy-start.13
  1534.2 5.2 copy-start.9
  1534.3 5.7 copy-start.27
  1541.2 30.4 %copy-start.10 = (f32[128,2048]{1,0:T(8,128)}, f32[128,2048]{1,0:T(8,128)S(1)}, u32[]{:S(2)}) copy-start(f32[128,2048]{1,0:T(8,128)S(1)} %get-tuple-element.51) | copy-start | bytes 3145732
  1541.2 12.1 copy-start.32
  1553.0 2.2 copy-start.34
  1553.0 2.2 copy-start.42
  1553.3 7.7 copy-start.23
  1555.2 6.8 copy-start.20
  1555.2 6.8 copy-start.26
  1555.2 6.8 copy-start.47
  1555.2 6.8 copy-start.52
  1555.2 8.1 copy-start.4
  1555.2 8.1 copy-start.30
  1555.3 8.1 copy-start.49
  1562.0 3.6 copy-start.15
  1565.6 87.3 %reduce-scatter.10.cloned.1.call-start = ((), (), s32[]{:S(2)}) async-start(), calls=%async_computation.15 | async-start | bytes 2621440 | tf_op jit(solution)/shard_map/reduce_scatter | solution.py:302
  1569.3 2.3 copy-start.12
  1571.5 364.7 %reduce-scatter.12.cloned.1.call-start = ((), (), s32[]{:S(2)}) async-start(), calls=%async_computation.16 | async-start | bytes 20971520 | tf_op jit(solution)/shard_map/reduce_scatter | solution.py:305
  1580.0 639.7 %reduce-scatter.6.cloned.1.call-start = ((), (), s32[]{:S(2)}) async-start(), calls=%async_computation.13 | async-start | bytes 20971520 | tf_op jit(solution)/shard_map/reduce_scatter | solution.py:296
  1587.3 4.0 copy-start.5
  1596.0 7.4 copy-start.3
  1596.0 7.4 copy-start.38
  1606.7 3.8 copy-start.18
  1609.8 2.2 copy-start.17
  1626.7 628.1 %reduce-scatter.14.cloned.1.call-start = ((), (), s32[]{:S(2)}) async-start(), calls=%async_computation.17 | async-start | bytes 163840 | tf_op jit(solution)/shard_map/reduce_scatter | solution.py:317
  1628.1 12.0 copy-start.21
  1640.9 741.5 %all-reduce.12.cloned.1.call-start = ((), (), s32[]{:S(2)}) async-start(), calls=%async_computation.18 | async-start | bytes 18874368 | tf_op jit(solution)/shard_map/psum | solution.py:323
  2219.7 11.9 copy-start.16
  2243.0 2.6 copy-start.28
  2245.6 7.9 copy-start.11
  2386.7 6.8 copy-start.22
  2393.5 4.5 copy-start.1
  (16 other events, 17.5 us)
Sparse Core Ops, SparseCore 0:
  9.6 45.6 all-gather.6
  56.8 44.4 all-gather.8
  102.9 284.9 all-gather.10
  389.3 284.9 all-gather.12
  1565.7 42.1 reduce-scatter.7
  1610.0 42.7 reduce-scatter.9
  1655.2 281.0 reduce-scatter.11
  1938.6 281.0 reduce-scatter.5
  2222.5 15.2 reduce-scatter.13
  2241.7 140.7 all-reduce.11
where the time goes:
time: 2420 us; the launch traced here: 2410 us
  waiting for transfers between devices  1740 us (72%)
  blocking collectives  247 us (10%)
  matrix products  199 us (8%)
  other arithmetic  90.2 us (4%)
  local copies, waits for them, and re-layouts  88.1 us (4%)
  starting transfers between devices  25.8 us (1%)
    reduce_scatter x1, waiting for transfers between devices, local(): lax.psum_scatter(grad_w_query.astype(jnp.bfloat16), 'shard', scatter_dime...  283 us
    reduce_scatter x1, waiting for transfers between devices, local(): lax.psum_scatter(grad_w_out.astype(jnp.bfloat16), 'shard', scatter_dimens...  283 us
    all_gather x1, waiting for transfers between devices, local(): lax.all_gather(w_query, 'shard', axis=0, tiled=True)  276 us
    all_gather x1, waiting for transfers between devices, local(): lax.all_gather(w_out, 'shard', axis=0, tiled=True)  264 us
    all_gather x1, blocking collectives, local(): lax.all_gather(w_router, 'shard', axis=0, tiled=True)  186 us
    all_to_all x1, waiting for transfers between devices, local(): lax.all_to_all(grad_in.reshape(experts, capacity, width), ('rep', 'shard'...  167 us
    all_to_all x1, waiting for transfers between devices, local(): lax.all_to_all(send_grads.reshape(experts, capacity, width), ('rep', 'sha...  163 us
    all_to_all x1, waiting for transfers between devices, local(): lax.all_to_all(produced.reshape(device_count * local_experts, count, widt...  161 us
  transfers between devices with their start and end apart: 14, of which 9 were waited for; matrix products, arithmetic and copies ran while one was open for 10% of the time, Pallas kernels for 0%

commit v1 on v0

v1 whole, which is shorter than its diff:
```python
import functools
import jax
import jax.numpy as jnp
from jax import lax
from jax.experimental import pallas as pl
from jax.experimental.pallas import tpu as pltpu
from jax.sharding import PartitionSpec as P

bf16 = jnp.bfloat16
f32 = jnp.float32
vmem_cap = 62 * 1024 * 1024
epsilon = 1e-06
rope_base = 1000000.0
masked_score = -1e30


class Grid:
    def __init__(self, reps, shards):
        self.reps, self.shards = reps, shards
        self.devices = reps * shards
        self.places = reps // 2
        self.los = self.places // 2

    def here(self):
        self.r = lax.axis_index("rep")
        self.z = lax.axis_index("shard")
        self.core = self.r % 2
        place = self.r // 2
        self.hi = place // self.los
        self.lo = place % self.los
        return self

    def rep_of(self, hi, lo, core):
        return (hi * self.los + lo) * 2 + core

    def device(self, rep, shard):
        return {"rep": rep, "shard": shard}

    def other_lo(self, step):
        return (self.lo + step) % self.los

    def nearest(self):
        n = self.shards
        rows = [sorted(range(n), key=lambda p: (abs(p - z), p)) for z in range(n)]
        return [pick(self.z, [rows[z][turn] for z in range(n)]) for turn in range(n)]


def pick(index, values):
    out = jnp.int32(values[0])
    for i in range(1, len(values)):
        out = jnp.where(index == i, jnp.int32(values[i]), out)
    return out


class Sends:
    def __init__(self, sems):
        self.sems, self.used, self.open = sems, 0, []

    def start(self, src, dst, recv, device, when=None):
        copy = pltpu.make_async_remote_copy(
            src_ref=src,
            dst_ref=dst,
            send_sem=self.sems.at[self.used],
            recv_sem=recv,
            device_id=device,
            device_id_type=pl.DeviceIdType.MESH,
        )
        self.used += 1
        self.open.append((copy, when))
        if when is None:
            copy.start()
        else:
            pl.when(when)(copy.start)

    def arrived(self, dst, recv, device, when=None):
        copy = pltpu.make_async_remote_copy(
            src_ref=dst,
            dst_ref=dst,
            send_sem=self.sems.at[0],
            recv_sem=recv,
            device_id=device,
            device_id_type=pl.DeviceIdType.MESH,
        )
        if when is None:
            copy.wait_recv()
        else:
            pl.when(when)(copy.wait_recv)

    def drain(self):
        for copy, when in self.open:
            if when is None:
                copy.wait_send()
            else:
                pl.when(when)(copy.wait_send)
        self.open = []


def greet_line(g):
    barrier = pltpu.get_barrier_semaphore()
    for step in range(1, g.shards):
        pl.semaphore_signal(
            barrier,
            inc=1,
            device_id=g.device(g.r, (g.z + step) % g.shards),
            device_id_type=pl.DeviceIdType.MESH,
        )
    pl.semaphore_wait(barrier, g.shards - 1)


def greet_all(g):
    barrier = pltpu.get_barrier_semaphore()
    me = g.r * g.shards + g.z

    def one(step, carry):
        peer = (me + step) % g.devices
        pl.semaphore_signal(
            barrier,
            inc=1,
            device_id=g.device(peer // g.shards, peer % g.shards),
            device_id_type=pl.DeviceIdType.MESH,
        )
        return carry

    lax.fori_loop(1, g.devices, one, 0)
    pl.semaphore_wait(barrier, g.devices - 1)


def push_rows(g, src, dst, send_sems, recv_sems):
    me = g.r * g.shards + g.z

    def one(step, carry):
        peer = (me + step) % g.devices
        pltpu.make_async_remote_copy(
            src_ref=src.at[peer],
            dst_ref=dst.at[me],
            send_sem=send_sems.at[step],
            recv_sem=recv_sems.at[step],
            device_id=g.device(peer // g.shards, peer % g.shards),
            device_id_type=pl.DeviceIdType.MESH,
        ).start()
        return carry

    lax.fori_loop(1, g.devices, one, 0)


def push_wait(g, src, dst, send_sems, recv_sems):
    me = g.r * g.shards + g.z

    def one(step, carry):
        peer = (me + g.devices - step) % g.devices
        copy = pltpu.make_async_remote_copy(
            src_ref=src.at[peer],
            dst_ref=dst.at[peer],
            send_sem=send_sems.at[step],
            recv_sem=recv_sems.at[step],
            device_id=g.device(peer // g.shards, peer % g.shards),
            device_id_type=pl.DeviceIdType.MESH,
        )
        copy.wait_send()
        copy.wait_recv()
        return carry

    lax.fori_loop(1, g.devices, one, 0)


def gather_all_kernel(reps, shards, x_ref, slab_ref, out_ref, slabs_ref, sems, zr, lr, hr, dr, cr, ps, pr, ls):
    g = Grid(reps, shards).here()
    s = Sends(sems)
    rows = x_ref.shape[0]
    half = rows // 2
    n = g.shards
    parts = (pl.ds(0, half), pl.ds(half, half))
    order = g.nearest()

    def block(hi, lo, core, zp):
        return out_ref.at[g.rep_of(hi, lo, core) * n + zp]

    partner = g.device(g.rep_of(g.hi, g.lo, 1 - g.core), g.z)
    far = 1 - g.hi

    def at(hi, lo):
        return g.device(g.rep_of(hi, lo, g.core), g.z)

    keep = pltpu.make_async_copy(x_ref, block(g.hi, g.lo, g.core, g.z), ls.at[0])
    keep.start()
    greet_all(g)
    push_rows(g, slab_ref, slabs_ref, ps, pr)
    me = g.r * n + g.z
    keep_slab = pltpu.make_async_copy(slab_ref.at[me], slabs_ref.at[me], ls.at[1])
    keep_slab.start()

    def own_line(turn):
        zp = order[turn]
        dst = block(g.hi, g.lo, g.core, zp)
        if turn == 0:
            src = x_ref
        else:
            src = dst
            s.arrived(dst, zr.at[zp], g.device(g.r, zp))
        s.start(src, dst, zr.at[zp], g.device(g.r, jnp.minimum(g.z + 1, n - 1)), (zp <= g.z) & (g.z + 1 < n))
        s.start(src, dst, zr.at[zp], g.device(g.r, jnp.maximum(g.z - 1, 0)), (zp >= g.z) & (g.z > 0))
        for part in (0, 1):
            for step in range(1, g.los):
                s.start(src.at[parts[part]], dst.at[parts[part]], lr.at[zp, part, step - 1], at(g.hi, g.other_lo(step)))
            s.start(src.at[parts[1 - part]], dst.at[parts[1 - part]], hr.at[zp, 1 - part], at(far, g.lo))
        s.start(src, dst, cr.at[zp, 0], partner)

    def first(turn):
        zp = order[turn]
        for step in range(1, g.los):
            frm = (g.lo + g.los - step) % g.los
            dst = block(g.hi, frm, g.core, zp)
            s.arrived(dst.at[parts[0]], lr.at[zp, 0, step - 1], at(g.hi, frm))
            s.start(dst.at[parts[0]], dst.at[parts[0]], dr.at[zp, 0, step - 1], at(far, g.lo))
            s.start(dst.at[parts[0]], dst.at[parts[0]], cr.at[zp, 5 * step], partner)
        dst = block(far, g.lo, g.core, zp)
        s.arrived(dst.at[parts[1]], hr.at[zp, 1], at(far, g.lo))
        for step in range(1, g.los):
            s.start(dst.at[parts[1]], dst.at[parts[1]], dr.at[zp, 1, step - 1], at(g.hi, g.other_lo(step)))
        s.start(dst.at[parts[1]], dst.at[parts[1]], cr.at[zp, 1], partner)
        for step in range(1, g.los):
            frm = (g.lo + g.los - step) % g.los
            dst = block(g.hi, frm, g.core, zp)
            s.arrived(dst.at[parts[1]], lr.at[zp, 1, step - 1], at(g.hi, frm))
            s.start(dst.at[parts[1]], dst.at[parts[1]], cr.at[zp, 5 * step + 1], partner)
        dst = block(far, g.lo, g.core, zp)
        s.arrived(dst.at[parts[0]], hr.at[zp, 0], at(far, g.lo))
        s.start(dst.at[parts[0]], dst.at[parts[0]], cr.at[zp, 2], partner)

    def second(turn):
        zp = order[turn]
        for step in range(1, g.los):
            frm = (g.lo + g.los - step) % g.los
            dst = block(far, frm, g.core, zp)
            s.arrived(dst.at[parts[0]], dr.at[zp, 0, step - 1], at(far, g.lo))
            s.start(dst.at[parts[0]], dst.at[parts[0]], cr.at[zp, 5 * step + 2], partner)
            s.arrived(dst.at[parts[1]], dr.at[zp, 1, step - 1], at(g.hi, frm))
            s.start(dst.at[parts[1]], dst.at[parts[1]], cr.at[zp, 5 * step + 3], partner)

    def from_partner(turn):
        zp = order[turn]
        other = 1 - g.core
        s.arrived(block(g.hi, g.lo, other, zp), cr.at[zp, 0], partner)
        dst = block(far, g.lo, other, zp)
        s.arrived(dst.at[parts[1]], cr.at[zp, 1], partner)
        s.arrived(dst.at[parts[0]], cr.at[zp, 2], partner)
        for step in range(1, g.los):
            frm = (g.lo + g.los - step) % g.los
            dst = block(g.hi, frm, other, zp)
            s.arrived(dst.at[parts[0]], cr.at[zp, 5 * step], partner)
            s.arrived(dst.at[parts[1]], cr.at[zp, 5 * step + 1], partner)
            dst = block(far, frm, other, zp)
            s.arrived(dst.at[parts[0]], cr.at[zp, 5 * step + 2], partner)
            s.arrived(dst.at[parts[1]], cr.at[zp, 5 * step + 3], partner)

    for turn in range(n + 2):
        if turn < n:
            own_line(turn)
        if 0 <= turn - 1 < n:
            first(turn - 1)
        if 0 <= turn - 2 < n:
            second(turn - 2)
    for turn in range(n):
        from_partner(turn)
    keep.wait()
    keep_slab.wait()
    push_wait(g, slab_ref, slabs_ref, ps, pr)
    s.drain()


def gather_all(reps, shards, x, slab, ident):
    g = Grid(reps, shards)
    n, los = shards, g.los
    per_turn = 2 + 2 * los + 1 + (3 * (los - 1)) + los + 1 + 1 + 2 * (los - 1) + los
    dma = pltpu.SemaphoreType.DMA
    return pl.pallas_call(
        functools.partial(gather_all_kernel, reps, shards),
        out_shape=(
            jax.ShapeDtypeStruct((g.devices,) + x.shape, x.dtype),
            jax.ShapeDtypeStruct(slab.shape, slab.dtype),
        ),
        in_specs=[pl.BlockSpec(memory_space=pltpu.VMEM)] * 2,
        out_specs=(pl.BlockSpec(memory_space=pl.ANY), pl.BlockSpec(memory_space=pltpu.VMEM)),
        scratch_shapes=[
            dma((n * (per_turn + 4),)),
            dma((n,)),
            dma((n, 2, max(1, los - 1))),
            dma((n, 2)),
            dma((n, 2, max(1, los - 1))),
            dma((n, 5 * los)),
            dma((g.devices,)),
            dma((g.devices,)),
            dma((2,)),
        ],
        compiler_params=pltpu.CompilerParams(collective_id=ident, has_side_effects=True, vmem_limit_bytes=vmem_cap),
        name="gather_all",
    )(x, slab)


def add_rows(dst, *srcs, rows):
    def one(i, carry):
        at = pl.ds(pl.multiple_of(i * 16, 16), 16)
        total = srcs[0][at, :].astype(f32)
        for src in srcs[1:]:
            total = total + src[at, :].astype(f32)
        dst[at, :] = total.astype(dst.dtype)
        return carry

    lax.fori_loop(0, rows // 16, one, 0)


def scatter_all_kernel(reps, shards, slabbed, *refs):
    if slabbed:
        p_ref, slab_ref, out_ref, slabs_ref, *rest = refs
    else:
        p_ref, out_ref, *rest = refs
    own, ra, rb0, rb1, rc0, rc1, rl, rr, sems, sa, sb0, sb1, sc0, sc1, sl, sr, ps, pr, ls = rest
    g = Grid(reps, shards).here()
    s = Sends(sems)
    n, los = g.shards, g.los
    rows = out_ref.shape[0]
    half = rows // 2
    top, bottom = pl.ds(0, half), pl.ds(half, half)
    order = g.nearest()[::-1]
    partner = g.device(g.rep_of(g.hi, g.lo, 1 - g.core), g.z)
    far = 1 - g.hi

    def at(hi, lo):
        return g.device(g.rep_of(hi, lo, g.core), g.z)

    loads = []
    for turn in range(n):
        load = pltpu.make_async_copy(p_ref.at[:, g.core, order[turn]], own.at[turn], ls.at[turn])
        load.start()
        loads.append(load)
    greet_all(g)
    if slabbed:
        push_rows(g, slab_ref, slabs_ref, ps, pr)
        me = g.r * n + g.z
        keep_slab = pltpu.make_async_copy(slab_ref.at[me], slabs_ref.at[me], ls.at[n])
        keep_slab.start()
    for turn in range(n):
        s.start(p_ref.at[:, 1 - g.core, order[turn]], ra.at[turn], sa.at[turn], partner)

    def stage_a(turn):
        loads[turn].wait()
        s.arrived(ra.at[turn], sa.at[turn], partner)

        def one(i, carry):
            a = pl.ds(pl.multiple_of(i * 16, 16), 16)
            for q in range(g.places):
                own[turn, q, a, :] = (own[turn, q, a, :].astype(f32) + ra[turn, q, a, :].astype(f32)).astype(own.dtype)
            return carry

        lax.fori_loop(0, rows // 16, one, 0)
        s.start(own.at[turn, pl.ds(far * los, los), top], rb0.at[turn], sb0.at[turn], at(far, g.lo))
        for step in range(1, los):
            to = g.other_lo(step)
            for hi in range(2):
                s.start(own.at[turn, hi * los + to, bottom], rb1.at[turn, step - 1, hi], sb1.at[turn, step - 1, hi], at(g.hi, to))

    def stage_b(turn):
        s.arrived(rb0.at[turn], sb0.at[turn], at(far, g.lo))
        for lo in range(los):
            line = own.at[turn, g.hi * los + lo, top]
            add_rows(line, line, rb0.at[turn, lo], rows=half)
        for step in range(1, los):
            frm = (g.lo + los - step) % los
            for hi in range(2):
                s.arrived(rb1.at[turn, step - 1, hi], sb1.at[turn, step - 1, hi], at(g.hi, frm))
        for hi in range(2):
            line = own.at[turn, hi * los + g.lo, bottom]
            add_rows(line, line, *[rb1.at[turn, step, hi] for step in range(los - 1)], rows=half)
        for step in range(1, los):
            to = g.other_lo(step)
            s.start(own.at[turn, g.hi * los + to, top], rc0.at[turn, step - 1], sc0.at[turn, step - 1], at(g.hi, to))
        s.start(own.at[turn, far * los + g.lo, bottom], rc1.at[turn], sc1.at[turn], at(far, g.lo))

    def stage_c(turn):
        mine = g.hi * los + g.lo
        for step in range(1, los):
            s.arrived(rc0.at[turn, step - 1], sc0.at[turn, step - 1], at(g.hi, (g.lo + los - step) % los))
        line = own.at[turn, mine, top]
        add_rows(line, line, *[rc0.at[turn, step] for step in range(los - 1)], rows=half)
        s.arrived(rc1.at[turn], sc1.at[turn], at(far, g.lo))
        line = own.at[turn, mine, bottom]
        add_rows(line, line, rc1.at[turn], rows=half)
        send_line(g, s, order[turn], own.at[turn, mine], out_ref, rl, rr, sl, sr, last=turn == n - 1)

    for turn in range(n + 2):
        if turn < n:
            stage_a(turn)
        if 0 <= turn - 1 < n:
            stage_b(turn - 1)
        if 0 <= turn - 2 < n:
            stage_c(turn - 2)
    if slabbed:
        keep_slab.wait()
        push_wait(g, slab_ref, slabs_ref, ps, pr)
    s.drain()


def send_line(g, s, zp, line, out_ref, rl, rr, sl, sr, last):
    n, rows = g.shards, line.shape[0]
    left, right = g.device(g.r, jnp.maximum(g.z - 1, 0)), g.device(g.r, jnp.minimum(g.z + 1, n - 1))
    has_left, has_right = g.z > 0, g.z + 1 < n
    if last:
        s.arrived(rl.at[g.z], sl.at[g.z], left, has_left)
        s.arrived(rr.at[g.z], sr.at[g.z], right, has_right)

        @pl.when(has_left & has_right)
        def _():
            add_rows(out_ref, line, rl.at[g.z], rr.at[g.z], rows=rows)

        @pl.when(has_left & jnp.logical_not(has_right))
        def _():
            add_rows(out_ref, line, rl.at[g.z], rows=rows)

        @pl.when(has_right & jnp.logical_not(has_left))
        def _():
            add_rows(out_ref, line, rr.at[g.z], rows=rows)
    else:
        onward_right, onward_left = zp > g.z, zp < g.z

        @pl.when(onward_right & has_left)
        def _():
            s.arrived(rl.at[zp], sl.at[zp], left)
            add_rows(line, line, rl.at[zp], rows=rows)

        @pl.when(onward_left & has_right)
        def _():
            s.arrived(rr.at[zp], sr.at[zp], right)
            add_rows(line, line, rr.at[zp], rows=rows)

        s.start(line, rl.at[zp], sl.at[zp], right, onward_right)
        s.start(line, rr.at[zp], sr.at[zp], left, onward_left)


def scatter_all(reps, shards, p, slab, ident):
    g = Grid(reps, shards)
    n, los, places = shards, g.los, g.places
    _, rows, width = p.shape
    half = rows // 2
    lo_others = max(1, los - 1)
    dma = pltpu.SemaphoreType.DMA
    v = pltpu.VMEM
    slabbed = slab is not None
    out_shape = (jax.ShapeDtypeStruct((rows, width), f32),)
    if slabbed:
        out_shape += (jax.ShapeDtypeStruct(slab.shape, slab.dtype),)
    vmem = pl.BlockSpec(memory_space=pltpu.VMEM)
    done = pl.pallas_call(
        functools.partial(scatter_all_kernel, reps, shards, slabbed),
        out_shape=out_shape,
        in_specs=[pl.BlockSpec(memory_space=pl.ANY)] + [vmem] * slabbed,
        out_specs=(vmem,) * len(out_shape),
        scratch_shapes=[
            v((n, places, rows, width), p.dtype),
            v((n, places, rows, width), p.dtype),
            v((n, los, half, width), p.dtype),
            v((n, lo_others, 2, half, width), p.dtype),
            v((n, lo_others, half, width), p.dtype),
            v((n, half, width), p.dtype),
            v((n, rows, width), p.dtype),
            v((n, rows, width), p.dtype),
            dma((n * (6 + 3 * los),)),
            dma((n,)),
            dma((n,)),
            dma((n, lo_others, 2)),
            dma((n, lo_others)),
            dma((n,)),
            dma((n,)),
            dma((n,)),
            dma((g.devices,)),
            dma((g.devices,)),
            dma((n + 1,)),
        ],
        compiler_params=pltpu.CompilerParams(collective_id=ident, has_side_effects=True, vmem_limit_bytes=vmem_cap),
        name="scatter_all",
    )(p.reshape(places, 2, n, rows, width), *([slab] if slabbed else []))
    return done if slabbed else done[0]


def scatter_wide(reps, shards, p, slab, ident, chunks):
    if chunks == 1:
        return scatter_all(reps, shards, p, slab, ident)
    step = p.shape[2] // chunks
    parts = [
        scatter_all(reps, shards, p[:, :, i * step : (i + 1) * step], slab if i == 0 else None, ident + i)
        for i in range(chunks)
    ]
    if slab is None:
        return jnp.concatenate(parts, axis=1)
    first, slabs = parts[0]
    return jnp.concatenate([first] + parts[1:], axis=1), slabs


def gather_line_kernel(reps, shards, x_ref, out_ref, sems, zr, ls):
    g = Grid(reps, shards).here()
    s = Sends(sems)
    n = g.shards
    order = g.nearest()
    keep = pltpu.make_async_copy(x_ref, out_ref.at[g.z], ls.at[0])
    keep.start()
    greet_line(g)
    for turn in range(n):
        zp = order[turn]
        dst = out_ref.at[zp]
        src = x_ref if turn == 0 else dst
        if turn:
            s.arrived(dst, zr.at[zp], g.device(g.r, zp))
        s.start(src, dst, zr.at[zp], g.device(g.r, jnp.minimum(g.z + 1, n - 1)), (zp <= g.z) & (g.z + 1 < n))
        s.start(src, dst, zr.at[zp], g.device(g.r, jnp.maximum(g.z - 1, 0)), (zp >= g.z) & (g.z > 0))
    keep.wait()
    s.drain()


def gather_line(reps, shards, x, ident):
    dma = pltpu.SemaphoreType.DMA
    return pl.pallas_call(
        functools.partial(gather_line_kernel, reps, shards),
        out_shape=jax.ShapeDtypeStruct((shards,) + x.shape, x.dtype),
        in_specs=[pl.BlockSpec(memory_space=pltpu.VMEM)],
        out_specs=pl.BlockSpec(memory_space=pltpu.VMEM),
        scratch_shapes=[dma((2 * shards,)), dma((shards,)), dma((1,))],
        compiler_params=pltpu.CompilerParams(collective_id=ident, has_side_effects=True),
        name="gather_line",
    )(x)


def scatter_line_kernel(reps, shards, p_ref, out_ref, own, rl, rr, sems, sl, sr, ls):
    g = Grid(reps, shards).here()
    s = Sends(sems)
    n = g.shards
    order = g.nearest()[::-1]
    loads = []
    for turn in range(n):
        load = pltpu.make_async_copy(p_ref.at[order[turn]], own.at[turn], ls.at[turn])
        load.start()
        loads.append(load)
    greet_line(g)
    for turn in range(n):
        loads[turn].wait()
        send_line(g, s, order[turn], own.at[turn], out_ref, rl, rr, sl, sr, last=turn == n - 1)
    s.drain()


def scatter_line(reps, shards, p, ident):
    dma = pltpu.SemaphoreType.DMA
    _, rows, width = p.shape
    return pl.pallas_call(
        functools.partial(scatter_line_kernel, reps, shards),
        out_shape=jax.ShapeDtypeStruct((rows, width), f32),
        in_specs=[pl.BlockSpec(memory_space=pl.ANY)],
        out_specs=pl.BlockSpec(memory_space=pltpu.VMEM),
        scratch_shapes=[
            pltpu.VMEM((shards, rows, width), p.dtype),
            pltpu.VMEM((shards, rows, width), p.dtype),
            pltpu.VMEM((shards, rows, width), p.dtype),
            dma((2 * shards,)),
            dma((shards,)),
            dma((shards,)),
            dma((shards,)),
        ],
        compiler_params=pltpu.CompilerParams(collective_id=ident, has_side_effects=True),
        name="scatter_line",
    )(p)


def inverse_rms(values):
    return lax.rsqrt(jnp.mean(values * values, axis=-1, keepdims=True) + epsilon)


def rotate(values):
    half = values.shape[-1] // 2
    return jnp.concatenate([-values[..., half:], values[..., :half]], axis=-1)


def rope_tables(segment_rows, width):
    length = segment_rows.shape[1]
    places = jnp.arange(length, dtype=jnp.int32)
    same = segment_rows[:, :, None] == segment_rows[:, None, :]
    first = jnp.min(jnp.where(same, places[None, None, :], length), axis=2)
    offset = (places[None] - first).astype(f32)
    half = width // 2
    frequency = rope_base ** (-2.0 * jnp.arange(half, dtype=f32) / width)
    angle = offset[..., None] * frequency[None, None, :]
    cosine, sine = jnp.cos(angle), jnp.sin(angle)
    cosine = jnp.concatenate([cosine, cosine], axis=-1)
    sine = jnp.concatenate([sine, sine], axis=-1)
    allowed = same & (places[None, None, :] <= places[None, :, None])
    return cosine, sine, allowed


def norm_back(grad_scaled, unit, inverse, gain):
    gained = grad_scaled * gain
    return inverse * (gained - unit * jnp.mean(gained * unit, axis=-1, keepdims=True))


def matmul(a, b, dims=((1,), (0,))):
    return lax.dot_general(a, b, (dims, ((), ())), preferred_element_type=f32)


def local(
    tokens,
    segments,
    routes,
    attn_gain,
    w_query,
    key_weight,
    value_weight,
    w_out,
    query_gain,
    key_gain,
    ffn_gain,
    w_router,
    w_gate,
    w_up,
    w_down,
    cotangent,
):
    reps, shards = lax.axis_size("rep"), lax.axis_size("shard")
    devices = reps * shards
    r, z = lax.axis_index("rep"), lax.axis_index("shard")
    length, width = tokens.shape
    deep = w_query.shape[0]
    head_dim = query_gain.shape[0] * shards
    heads = w_query.shape[1] // head_dim
    kv_heads = key_weight.shape[1] // head_dim
    experts = w_router.shape[1]
    top = routes.shape[1]
    capacity = 2 * length * top // experts
    my_heads = heads // shards
    my_kv = max(1, kv_heads // shards)
    shared_by = max(1, shards // kv_heads)
    group = my_heads // my_kv
    q_cols, kv_cols = my_heads * head_dim, my_kv * head_dim
    cols = q_cols + 2 * kv_cols
    piece = deep // reps
    chunks = max(1, devices // 32)
    part = head_dim // shards

    def column(values, rows=deep):
        return jnp.pad(values.reshape(-1, 1), ((0, rows - values.size), (0, 0)))

    small = jnp.concatenate(
        [
            w_router,
            column(attn_gain),
            column(ffn_gain),
            column(query_gain),
            column(key_gain),
            column(segments[0].astype(bf16)),
        ],
        axis=1,
    )
    small_cols = -(-small.shape[1] // 128) * 128
    small = jnp.pad(small, ((0, 0), (0, small_cols - small.shape[1])))
    small_all = gather_line(reps, shards, small, 1)
    router_full = small_all[:, :, :experts].reshape(width, experts)
    gain_one = small_all[:, :, experts].reshape(1, width).astype(f32)
    gain_two = small_all[:, :, experts + 1].reshape(1, width).astype(f32)
    qgain = small_all[:, :part, experts + 2].reshape(head_dim).astype(f32)
    kgain = small_all[:, :part, experts + 3].reshape(head_dim).astype(f32)
    segment_rows = small_all[:, :length, experts + 4].astype(jnp.int32)

    def by_shard(weight, count):
        mine = lax.dynamic_slice_in_dim(weight, r * piece, piece, 0)
        mine = mine.reshape(piece, -1, count)
        if mine.shape[1] < shards:
            mine = jnp.repeat(mine, shards // mine.shape[1], axis=1)
        return mine.transpose(1, 0, 2)

    packed = jnp.concatenate(
        [by_shard(w_query, q_cols), by_shard(key_weight, kv_cols), by_shard(value_weight, kv_cols)], axis=2
    )
    packed = lax.all_to_all(packed, "shard", split_axis=0, concat_axis=0, tiled=True)
    packed = lax.all_gather(packed, "rep", axis=0)
    w_in = packed.transpose(1, 0, 2, 3).reshape(width, cols)

    cotangents = lax.all_gather(cotangent, ("rep", "shard"), axis=0)
    block_tokens = gather_line(reps, shards, tokens, 2).reshape(shards * length, width)

    wide = block_tokens.astype(f32)
    inverse_one = inverse_rms(wide)
    normed_one = wide * inverse_one
    hidden_in = (normed_one * gain_one).astype(bf16)
    qkv = matmul(hidden_in, w_in)
    query_raw = qkv[:, :q_cols].reshape(shards, length, my_heads, head_dim)
    key_raw = qkv[:, q_cols : q_cols + kv_cols].reshape(shards, length, my_kv, head_dim)
    values = qkv[:, q_cols + kv_cols :].astype(bf16).reshape(shards, length, my_kv, head_dim)
    inverse_query = inverse_rms(query_raw)
    query_unit = query_raw * inverse_query
    inverse_key = inverse_rms(key_raw)
    key_unit = key_raw * inverse_key
    cosine, sine, allowed = rope_tables(segment_rows, head_dim)
    cosine, sine = cosine[:, :, None, :], sine[:, :, None, :]
    query_scaled = query_unit * qgain
    key_scaled = key_unit * kgain
    query_rot = (query_scaled * cosine + rotate(query_scaled) * sine).astype(bf16)
    key_rot = (key_scaled * cosine + rotate(key_scaled) * sine).astype(bf16)
    grouped = query_rot.reshape(shards, length, my_kv, group, head_dim)
    scores = jnp.einsum("btkgh,bskh->bkgts", grouped, key_rot, preferred_element_type=f32) * head_dim ** (-0.5)
    scores = jnp.where(allowed[:, None, None], scores, masked_score)
    highest = jnp.max(scores, axis=-1, keepdims=True)
    raised = jnp.exp(scores - highest)
    probs = raised / jnp.sum(raised, axis=-1, keepdims=True)
    probs_low = probs.astype(bf16)
    mixed = jnp.einsum("bkgts,bskh->btkgh", probs_low, values, preferred_element_type=f32)
    attn_out = mixed.reshape(shards * length, q_cols).astype(bf16)
    projected = matmul(attn_out, w_out).astype(bf16)
    own_tokens = tokens.astype(f32)
    resid = own_tokens + scatter_line(reps, shards, projected.reshape(shards, length, width), 3)

    inverse_two = inverse_rms(resid)
    normed_two = resid * inverse_two
    hidden_two = (normed_two * gain_two).astype(bf16)
    logits = matmul(hidden_two, router_full)
    gate_probs = jax.nn.softmax(logits, axis=-1)
    chosen = jnp.any(routes[:, :, None] == jnp.arange(experts, dtype=jnp.int32)[None, None, :], axis=1)
    picked = jnp.where(chosen, gate_probs, 0.0)
    picked_total = jnp.sum(picked, axis=-1, keepdims=True)
    mix = picked / picked_total
    slab = jnp.where(chosen, mix, -1.0).T.reshape(experts, 1, length)
    slab = jnp.broadcast_to(slab, (experts, 8, length))
    hiddens, slabs = gather_all(reps, shards, hidden_two, slab, 4)

    share = slabs[:, 0, :]
    member = share >= 0.0
    earlier = jnp.arange(length)[:, None] < jnp.arange(length)[None, :]
    slot = matmul(member.astype(bf16), earlier.astype(bf16))
    place = (jnp.arange(capacity, dtype=f32)[None, :, None] == slot[:, None, :]) & member[:, None, :]
    row_weight = jnp.sum(jnp.where(place, share[:, None, :], 0.0), axis=2, keepdims=True)
    onehot = place.astype(bf16)

    def dispatch(blocks):
        taken = jnp.einsum("bst,btd->bsd", onehot, blocks, preferred_element_type=f32)
        return taken.astype(bf16).reshape(devices * capacity, width)

    rows = dispatch(hiddens)
    row_grads = dispatch(cotangents)
    row_weight = row_weight.reshape(devices * capacity, 1)
    gate = matmul(rows, w_gate[0])
    up = matmul(rows, w_up[0])
    sigmoid_gate = jax.nn.sigmoid(gate)
    activated = (gate * sigmoid_gate * up).astype(bf16)
    produced = matmul(activated, w_down[0]).astype(bf16).astype(f32)
    row_grads = row_grads.astype(f32)
    weighted = (row_weight * produced).astype(bf16)
    row_mix = jnp.sum(row_grads * produced, axis=1).reshape(devices, capacity, 1)
    back_mix = jnp.sum(jnp.where(place, row_mix, 0.0), axis=1).reshape(devices, 1, length)
    back_mix = jnp.broadcast_to(back_mix, (devices, 8, length))
    grad_pair = (row_weight * row_grads).astype(bf16)
    grad_act = matmul(grad_pair, w_down[0], ((1,), (1,)))
    grad_gate = (grad_act * up * sigmoid_gate * (1.0 + gate * (1.0 - sigmoid_gate))).astype(bf16)
    grad_up = (grad_act * gate * sigmoid_gate).astype(bf16)
    grad_in = matmul(grad_gate, w_gate[0], ((1,), (1,))) + matmul(grad_up, w_up[0], ((1,), (1,)))
    grad_w_down = matmul(activated, grad_pair, ((0,), (0,)))
    grad_w_gate = matmul(rows, grad_gate, ((0,), (0,)))
    grad_w_up = matmul(rows, grad_up, ((0,), (0,)))

    def combine(values):
        values = values.reshape(devices, capacity, width)
        return jnp.einsum("bst,bsd->btd", onehot, values, preferred_element_type=f32).astype(bf16)

    grad_hidden, mixes = scatter_wide(reps, shards, combine(grad_in.astype(bf16)), back_mix, 8, chunks)
    output = (resid + scatter_wide(reps, shards, combine(weighted), None, 16, chunks)).astype(bf16)

    grad_out = cotangent.astype(f32)
    grad_mix = mixes[:, 0, :].T
    grad_picked = jnp.where(chosen, grad_mix - jnp.sum(grad_mix * mix, axis=-1, keepdims=True), 0.0) / picked_total
    grad_logits = (gate_probs * (grad_picked - jnp.sum(grad_picked * picked, axis=-1, keepdims=True))).astype(bf16)
    grad_hidden = grad_hidden + matmul(grad_logits, router_full, ((1,), (1,)))
    grad_ffn_gain = jnp.sum(grad_hidden * normed_two, axis=0)
    grad_resid = grad_out + norm_back(grad_hidden, normed_two, inverse_two, gain_two)
    grad_w_router = matmul(hidden_two, grad_logits, ((0,), (0,)))
    grad_attn = gather_line(reps, shards, grad_resid.astype(bf16), 5).reshape(shards * length, width)

    grad_w_out = matmul(attn_out, grad_attn, ((0,), (0,)))
    grad_mixed = matmul(grad_attn, w_out, ((1,), (1,))).astype(bf16)
    grad_mixed = grad_mixed.reshape(shards, length, my_kv, group, head_dim)
    grad_weights = jnp.einsum("btkgh,bskh->bkgts", grad_mixed, values, preferred_element_type=f32)
    centre = jnp.sum(probs * grad_weights, axis=-1, keepdims=True)
    grad_scores = (probs * (grad_weights - centre) * head_dim ** (-0.5)).astype(bf16)
    grad_values = jnp.einsum("bkgts,btkgh->bskh", probs_low, grad_mixed, preferred_element_type=f32)
    grad_query_rot = jnp.einsum("bkgts,bskh->btkgh", grad_scores, key_rot, preferred_element_type=f32)
    grad_query_rot = grad_query_rot.reshape(shards, length, my_heads, head_dim)
    grad_key_rot = jnp.einsum("bkgts,btkgh->bskh", grad_scores, grouped, preferred_element_type=f32)
    grad_query_scaled = grad_query_rot * cosine - rotate(grad_query_rot * sine)
    grad_key_scaled = grad_key_rot * cosine - rotate(grad_key_rot * sine)
    grad_query_gain = jnp.sum(grad_query_scaled * query_unit, axis=(0, 1, 2))
    grad_key_gain = jnp.sum(grad_key_scaled * key_unit, axis=(0, 1, 2))
    grad_query = norm_back(grad_query_scaled, query_unit, inverse_query, qgain)
    grad_key = norm_back(grad_key_scaled, key_unit, inverse_key, kgain)
    grad_qkv = jnp.concatenate(
        [
            grad_query.reshape(shards * length, q_cols).astype(bf16),
            grad_key.reshape(shards * length, kv_cols).astype(bf16),
            grad_values.reshape(shards * length, kv_cols).astype(bf16),
        ],
        axis=1,
    )
    grad_part = matmul(grad_qkv, w_in, ((1,), (1,)))
    grad_attn_gain = jnp.sum(grad_part * normed_one, axis=0)
    grad_hidden_in = scatter_line(reps, shards, grad_part.astype(bf16).reshape(shards, length, width), 6)
    own_inverse = inverse_rms(own_tokens)
    own_normed = own_tokens * own_inverse
    grad_tokens = grad_resid + norm_back(grad_hidden_in, own_normed, own_inverse, gain_one)

    grad_w_in = matmul(hidden_in, grad_qkv, ((0,), (0,)))

    def spread(values):
        return jnp.pad(values.reshape(shards, part), ((0, 0), (0, deep - part))).reshape(width, 1)

    small_grads = jnp.concatenate(
        [
            grad_w_router,
            grad_attn_gain.reshape(width, 1),
            grad_ffn_gain.reshape(width, 1),
            spread(grad_query_gain),
            spread(grad_key_gain),
        ],
        axis=1,
    )
    small_grads = jnp.pad(small_grads, ((0, 0), (0, small_cols - small_grads.shape[1])))
    sent = jnp.concatenate([grad_w_in, small_grads], axis=1).astype(bf16)
    sent = sent.reshape(shards, reps, piece, cols + small_cols).transpose(1, 0, 2, 3)
    sent = lax.psum_scatter(sent, "rep", scatter_dimension=0, tiled=True)[0]
    sent = lax.all_to_all(sent, "shard", split_axis=0, concat_axis=0, tiled=True)
    sent = lax.all_gather(sent, "rep", axis=1, tiled=True)
    owned_out = lax.psum(grad_w_out.astype(bf16), "rep").astype(f32)

    def joined(values):
        if shared_by > 1:
            values = values.astype(f32).reshape(-1, shared_by, deep, values.shape[-1]).sum(axis=1)
        return values.transpose(1, 0, 2).reshape(deep, -1).astype(f32)

    owned_small = jnp.sum(sent[:, :, cols:].astype(f32), axis=0)
    return (
        output,
        grad_tokens,
        owned_small[:, experts],
        sent[:, :, :q_cols].transpose(1, 0, 2).reshape(deep, -1).astype(f32),
        joined(sent[:, :, q_cols : q_cols + kv_cols]),
        joined(sent[:, :, q_cols + kv_cols : cols]),
        owned_out,
        owned_small[:part, experts + 2],
        owned_small[:part, experts + 3],
        owned_small[:, experts + 1],
        owned_small[:, :experts],
        grad_w_gate[None],
        grad_w_up[None],
        grad_w_down[None],
    )


def solution(mesh):
    split = P(("rep", "shard"))
    row = P("shard")
    return jax.shard_map(
        local,
        mesh=mesh,
        in_specs=(split,) * 3 + (row,) * 9 + (split,) * 4,
        out_specs=(split,) * 2 + (row,) * 9 + (split,) * 3,
        check_vma=False,
    )
```

time: 2420 us -> 1020 us (0.42)
  waiting for transfers between devices: 1740 us -> 146 us
  Pallas kernels: 0 us -> 472 us
  blocking collectives: 247 us -> 39.6 us
  starting transfers between devices: 25.8 us -> 0.16 us
    all_gather x4 -> x3, waiting for transfers between devices: 579 us -> 0.01 us  [the longest x1 0.01 us: local(): packed = lax.all_gather(packed, 'rep', axis=0)]
    reduce_scatter x5 -> x0, waiting for transfers between devices: 567 us -> none  [the longest x1 283 us: local(): lax.psum_scatter(grad_w_query.astype(jnp.bfloat16), 'shard', scatter_dime...]
    all_to_all x4 -> x0, waiting for transfers between devices: 490 us -> none  [the longest x1 167 us: local(): lax.all_to_all(grad_in.reshape(experts, capacity, width), ('rep', 'shard'...]
    pallas_call x0 -> x8, Pallas kernels: none -> 472 us  [the longest x2 178 us: scatter_all(): pl.pallas_call(functools.partial(scatter_all_kernel, reps, shards, slabbe...]
    all_gather x3 -> x0, blocking collectives: 208 us -> none  [the longest x1 186 us: local(): lax.all_gather(w_router, 'shard', axis=0, tiled=True)]
    unnamed x10 -> x5, waiting for transfers between devices: 2.68 us -> 146 us
    psum x1 -> x0, waiting for transfers between devices: 99 us -> none  [local(): lax.psum(pieces[1].astype(jnp.bfloat16), 'rep').astype(jnp.float32)]
    all_to_all x0 -> x2, blocking collectives: none -> 39.6 us  [the longest x1 20.6 us: local(): lax.all_to_all(sent, 'shard', split_axis=0, concat_axis=0, tiled=True)]
  transfers between devices with their start and end apart: 14 -> 4, of which waited for: 9 -> 1; matrix products, arithmetic and copies ran while one was open for 10% -> 14% of each run, Pallas kernels for 0% -> 35%
where the time goes in v1:
time: 1020 us; the launch traced here: 1010 us
  Pallas kernels  472 us (46%)
  matrix products  184 us (18%)
  waiting for transfers between devices  146 us (14%)
  local copies, waits for them, and re-layouts  77.3 us (8%)
  other arithmetic  72.8 us (7%)
  blocking collectives  39.6 us (4%)
  between operations  15.8 us (2%)
    pallas_call x2, Pallas kernels, scatter_all(): pl.pallas_call(functools.partial(scatter_all_kernel, reps, shards, slabbe...  178 us
    unnamed x5, waiting for transfers between devices  146 us
    dot_general x19, matrix products, matmul(): return lax.dot_general(a, b, (dims, ((), ())), preferred_element_type=f32)  134 us
    pallas_call x2, Pallas kernels, scatter_line(): pl.pallas_call(functools.partial(scatter_line_kernel, reps, shards), out_...  119 us
    pallas_call x1, Pallas kernels, gather_all(): pl.pallas_call(functools.partial(gather_all_kernel, reps, shards), out_sh...  87.4 us
    pallas_call x3, Pallas kernels, gather_line(): pl.pallas_call(functools.partial(gather_line_kernel, reps, shards), out_s...  87 us
    unnamed x198, local copies, waits for them, and re-layouts  35.7 us
    dot_general x2, matrix products, combine(): jnp.einsum('bst,bsd->btd', onehot, values, preferred_element_type=f32)  28.1 us
  transfers between devices with their start and end apart: 4, of which 1 were waited for; matrix products, arithmetic and copies ran while one was open for 14% of the time, Pallas kernels for 35%

profile of v1, /device:TPU:17, one launch (start us, length us, event | category | flops | bytes accessed | tf_op | source)
XLA Modules:
  0.0 1006.8 jit_solution(18205868231735797465)
XLA Ops:
  10.1 18.9 %all_to_all.10 = bf16[4,64,1280]{2,1,0:T(8,128)(2,1)} all-to-all(bf16[4,64,1280]{2,1,0:T(8,128)(2,1)S(1)} %copy.294), channel_id=1, replica_groups=mesh['rep'=8,'shard'=4] {'shard'}, dimensions={0} | all-to-all | bytes 1310720 | tf_op jit(solution)/shard_map/all_to_all | solution.py:677
  30.9 13.1 %gather_line.4 = bf16[4,512,128]{2,1,0:T(8,128)(2,1)} custom-call(bf16[512,128]{1,0:T(8,128)(2,1)} %pad.32.x_ref), custom_call_target="tpu_custom_call" | custom-call | tf_op jit(solution)/shard_map/gather_line/pallas_call | solution.py:520
  44.0 1.9 convert_reduce_fusion
  45.9 37.9 %gather_line.3 = bf16[4,128,2048]{2,1,0:T(8,128)(2,1)} custom-call(bf16[128,2048]{1,0:T(8,128)(2,1)} %x_ref.1), custom_call_target="tpu_custom_call" | custom-call | tf_op jit(solution)/shard_map/gather_line/pallas_call | solution.py:520
  87.0 2.1 multiply_reduce_fusion.1
  91.6 1.9 multiply_convert_fusion.4
  93.5 3.0 copy.295
  96.7 2.9 fusion.82
  103.6 1.9 copy.299
  105.7 1.3 pad_maximum_fusion.5
  113.3 1.5 copy.315
  117.2 5.9 convolution_convert_fusion.7
  123.1 83.0 %scatter_line.2 = f32[128,2048]{1,0:T(8,128)} custom-call(bf16[4,128,2048]{2,1,0:T(8,128)(2,1)} %bitcast.348), custom_call_target="tpu_custom_call" | custom-call | tf_op jit(solution)/shard_map/scatter_line/pallas_call | solution.py:551
  206.0 2.0 multiply_reduce_fusion.7
  209.8 87.4 %gather_all.1 = (bf16[32,128,2048]{2,1,0:T(8,128)(2,1)}, f32[32,8,128]{2,1,0:T(8,128)}) custom-call(bf16[128,2048]{1,0:T(8,128)(2,1)} %copy-done.20, f32[32,8,128]{2,1,0:T(8,128)} %broadcast_in_dim.79.slab_ref), custom_call_target="tpu_custom_call" | custom-call | tf_op jit(solution)/shard_map/gather_all/pallas_call | solution.py:276
  298.3 8.1 convolution_convert_fusion.5
  306.4 11.2 %fusion.12 = f32[2048,768]{1,0:T(8,128)S(1)} fusion(bf16[2048,2048]{1,0:T(8,128)(2,1)S(1)} %bitcast.316, bf16[1,2048,768]{2,1,0:T(8,128)(2,1)} %param.28), kind=kOutput, calls=%fused_computation.37 | convolution fusion | flops 6442450944 | bytes 17825792 | tf_op jit(solution)/shard_map/dot_general | solution.py:601
  317.7 2.7 copy-done.84
  320.4 9.9 multiply_convert_fusion.2
  330.3 8.1 convolution_convert_fusion.4
  338.4 14.5 %fusion.1 = (f32[2048]{0:T(1024)S(1)}, bf16[2048,2048]{1,0:T(8,128)(2,1)}) fusion(bf16[32,64,2048]{2,1,0:T(8,128)(2,1)S(1)} %convolution_convert_fusion.4, bf16[2048,768]{1,0:T(8,128)(2,1)} %get-tuple-element.190, bf16[1,768,2048]{2,1,0:T(8,128)(2,1)} %param.30), kind=kOutput, calls=%fused_computation.3 | convolution fusion | flops 6463420416 | bytes 23076864 | tf_op jit(solution)/shard_map/dot_general | solution.py:601
  353.7 8.2 fusion.2
  362.0 15.3 %multiply_convert_fusion = (bf16[2048,768]{1,0:T(8,128)(2,1)}, bf16[2048,768]{1,0:T(8,128)(2,1)S(1)}) fusion(f32[2048,768]{1,0:T(8,128)} %copy-done.84, f32[2048,768]{1,0:T(8,128)} %get-tuple-element.191, bf16[2048,2048]{1,0:T(8,128)(2,1)} %bitcast.327, bf16[1,768,2048]{2,1,0:T(8,128)(2,1)S(1)} %copy-done.74), kind=kOutput, calls=%fused_computation.12 | convolution fusion | flops 6462898176 | bytes 30408704 | tf_op jit(solution)/shard_map/dot_general | solution.py:601
  377.4 9.7 fusion.10
  387.1 12.4 %add_convert_fusion = bf16[2048,2048]{1,0:T(8,128)(2,1)} fusion(f32[2048,2048]{1,0:T(8,128)} %fusion.10, bf16[2048,768]{1,0:T(8,128)(2,1)S(1)} %copy-done.82, bf16[1,2048,768]{2,1,0:T(8,128)(2,1)S(1)} %copy-done.77), kind=kOutput, calls=%fused_computation.8 | convolution fusion | flops 6450839552 | bytes 31457280 | tf_op jit(solution)/shard_map/dot_general | solution.py:601
  399.4 13.7 %convolution_convert_fusion = bf16[32,128,2048]{2,1,0:T(8,128)(2,1)} fusion(bf16[32,64,2048]{2,1,0:T(8,128)(2,1)} %bitcast.315, f32[32,128]{1,0:T(8,128)S(1)} %fusion.65, pred[32,128]{1,0:T(8,128)(4,1)S(1)} %compare_bitcast_fusion), kind=kOutput, calls=%fused_computation.9 | convolution fusion | flops 1082654720 | bytes 25186304 | tf_op jit(solution)/shard_map/bst,bsd->btd/dot_general | solution.py:764
  413.8 86.6 %scatter_all.3 = (f32[128,2048]{1,0:T(8,128)}, f32[32,8,128]{2,1,0:T(8,128)}) custom-call(bf16[4,2,4,128,2048]{4,3,2,1,0:T(8,128)(2,1)} %bitcast.310, f32[32,8,128]{2,1,0:T(8,128)} %broadcast_in_dim.132.refs_1_), custom_call_target="tpu_custom_call" | custom-call | tf_op jit(solution)/shard_map/scatter_all/pallas_call | solution.py:452
  501.4 2.0 multiply_reduce_fusion.5
  505.6 36.0 %gather_line.5 = bf16[4,128,2048]{2,1,0:T(8,128)(2,1)} custom-call(bf16[128,2048]{1,0:T(8,128)(2,1)} %fusion.78.x_ref), custom_call_target="tpu_custom_call" | custom-call | tf_op jit(solution)/shard_map/gather_line/pallas_call | solution.py:520
  541.6 5.3 fusion.27
  550.4 1.2 bitcast_multiply_fusion.8
  552.1 4.5 convolution_convert_fusion.6
  556.8 1.3 copy-done.2
  558.1 2.1 multiply_reduce_fusion.2
  560.3 2.9 copy.311
  563.2 3.4 copy.309
  566.7 1.1 multiply_reduce_fusion.8
  568.1 1.7 fusion.32
  572.9 2.9 fusion.16
  575.9 4.4 multiply_reduce_fusion
  580.3 3.9 copy.316
  584.2 6.8 convolution_convert_fusion.3
  591.8 5.6 maximum_bitcast_fusion
  598.6 144.9 %all-reduce.11.cloned.1.call-done = (bf16[8,4,64,1408]{3,2,0,1:T(8,128)(2,1)}, bf16[1024,2048]{1,0:T(8,128)(2,1)}) async-done(((bf16[8,4,64,1408]{3,2,0,1:T(8,128)(2,1)}, bf16[1024,2048]{1,0:T(8,128)(2,1)}), (bf16[8,4,64,1408]{3,2,0,1:T(8,128)(2,1)}, bf16[1024,2048]{1,0:T(8,128)(2,1)})) %all-reduce.11.cloned.1.call-update) | async-done | bytes 9961488
  743.5 1.8 dynamic-slice_bitcast_fusion
  745.3 20.6 %all_to_all.11 = bf16[4,64,1408]{2,1,0:T(8,128)(2,1)S(1)} all-to-all(bf16[4,64,1408]{2,1,0:T(8,128)(2,1)S(1)} %dynamic-slice_bitcast_fusion), channel_id=1, replica_groups=mesh['rep'=8,'shard'=4] {'shard'}, dimensions={0} | all-to-all | bytes 1441792 | tf_op jit(solution)/shard_map/all_to_all | solution.py:829
  766.0 1.4 copy.318
  767.5 14.2 %fusion.3 = (bf16[2048,2048]{1,0:T(8,128)(2,1)}, bf16[2048,2048]{1,0:T(8,128)(2,1)}) fusion(bf16[32,64,2048]{2,1,0:T(8,128)(2,1)} %copy-done, f32[2048]{0:T(1024)S(1)} %mul.469, bf16[2048,2048]{1,0:T(8,128)(2,1)} %get-tuple-element.193), kind=kLoop, calls=%fused_computation.7 | loop fusion | flops 25165824 | bytes 33562624 | tf_op jit(solution)/shard_map/convert_element_type | solution.py:753
  781.7 14.4 %convolution_convert_fusion.1 = bf16[32,128,2048]{2,1,0:T(8,128)(2,1)} fusion(bf16[32,64,2048]{2,1,0:T(8,128)(2,1)} %bitcast.312, f32[32,128]{1,0:T(8,128)S(1)} %fusion.65, pred[32,128]{1,0:T(8,128)(4,1)S(1)} %compare_bitcast_fusion), kind=kOutput, calls=%fused_computation.10 | convolution fusion | flops 1082654720 | bytes 25186304 | tf_op jit(solution)/shard_map/bst,bsd->btd/dot_general | solution.py:764
  796.1 91.6 %scatter_all.2 = f32[128,2048]{1,0:T(8,128)} custom-call(bf16[4,2,4,128,2048]{4,3,2,1,0:T(8,128)(2,1)} %bitcast.311), custom_call_target="tpu_custom_call" | custom-call | tf_op jit(solution)/shard_map/scatter_all/pallas_call | solution.py:452
  887.7 36.3 %scatter_line.3 = f32[128,2048]{1,0:T(8,128)} custom-call(bf16[4,128,2048]{2,1,0:T(8,128)(2,1)} %bitcast.347), custom_call_target="tpu_custom_call" | custom-call | tf_op jit(solution)/shard_map/scatter_line/pallas_call | solution.py:551
  924.0 1.7 fusion.33
  925.7 4.1 fusion.36
  929.8 10.8 %convolution_bitcast_fusion = f32[1,768,2048]{2,1,0:T(8,128)} fusion(bf16[2048,768]{1,0:T(8,128)(2,1)} %get-tuple-element.190, bf16[2048,2048]{1,0:T(8,128)(2,1)S(1)} %copy-done.15), kind=kOutput, calls=%fused_computation.25 | convolution fusion | flops 6442450944 | bytes 17825792 | tf_op jit(solution)/shard_map/dot_general | solution.py:601
  940.6 9.0 convolution_bitcast_fusion.1
  949.6 9.2 convolution_bitcast_fusion.2
  958.8 4.5 convert_element_type.341
  963.3 1.9 fusion.79
  966.9 5.6 slice.127
  972.5 7.5 copy.345
  980.0 6.7 convert_element_type.352
  986.7 8.9 copy.323
  996.0 1.3 copy.324
  997.8 1.3 copy.325
  (299 shorter events, 43.3 us)
Async XLA Ops:
  7.2 86.3 %all-gather.8.cloned.1.call-start = ((), (), s32[]{:S(2)}) async-start(), calls=%async_computation.3 | async-start | bytes 5898240 | tf_op jit(solution)/shard_map/all_gather | solution.py:678
  9.3 20.6 %copy-start.78 = (s32[1,128]{1,0:T(1,128)S(1)}, s32[1,128]{1,0:T(1,128)}, u32[]{:S(2)}) copy-start(s32[1,128]{1,0:T(1,128)} %param.17) | copy-start | bytes 1540
  9.3 20.6 %copy-start.72 = (bf16[32]{0:T(256)(128)(2,1)S(1)}, bf16[32]{0:T(256)(128)(2,1)}, u32[]{:S(2)}) copy-start(bf16[32]{0:T(256)(128)(2,1)} %param.24) | copy-start | bytes 196
  9.3 20.6 %copy-start.73 = (bf16[32]{0:T(256)(128)(2,1)S(1)}, bf16[32]{0:T(256)(128)(2,1)}, u32[]{:S(2)}) copy-start(bf16[32]{0:T(256)(128)(2,1)} %param.25) | copy-start | bytes 196
  9.3 20.6 %copy-start.69 = (bf16[512]{0:T(512)(128)(2,1)S(1)}, bf16[512]{0:T(512)(128)(2,1)}, u32[]{:S(2)}) copy-start(bf16[512]{0:T(512)(128)(2,1)} %param.19) | copy-start | bytes 3076
  9.3 20.7 %copy-start.70 = (bf16[512]{0:T(512)(128)(2,1)S(1)}, bf16[512]{0:T(512)(128)(2,1)}, u32[]{:S(2)}) copy-start(bf16[512]{0:T(512)(128)(2,1)} %param.26) | copy-start | bytes 3076
  9.3 20.7 %copy-start.60 = (bf16[512,32]{0,1:T(8,128)(2,1)S(1)}, bf16[512,32]{0,1:T(8,128)(2,1)}, u32[]{:S(2)}) copy-start(bf16[512,32]{0,1:T(8,128)(2,1)} %param.27) | copy-start | bytes 98308
  29.0 56.7 %copy-start.67 = (s32[128,8]{0,1:T(8,128)S(1)}, s32[128,8]{0,1:T(8,128)}, u32[]{:S(2)}) copy-start(s32[128,8]{0,1:T(8,128)} %param.18) | copy-start | bytes 12292
  29.1 301.2 %all-gather.10.cloned.1.call-start = ((), (), s32[]{:S(2)}) async-start(), calls=%async_computation.4 | async-start | bytes 17301504 | tf_op jit(solution)/shard_map/all_gather | solution.py:681
  29.8 713.7 %all-reduce.11.cloned.1.call-start = ((), (), s32[]{:S(2)}) async-start(), calls=%async_computation.5 | async-start | bytes 19922944
  45.9 47.6 %copy-start.56 = (f32[1,4,4,128]{3,1,2,0:T(4,128)}, f32[1,4,4,128]{3,1,2,0:T(4,128)S(1)}, u32[]{:S(2)}) copy-start(f32[1,4,4,128]{3,1,2,0:T(4,128)S(1)} %copy.353) | copy-start | bytes 24580
  83.8 7.8 copy-start.6
  85.7 24.5 %copy-start.62 = (f32[128]{0:T(128)}, f32[128]{0:T(128)S(1)}, u32[]{:S(2)}) copy-start(f32[128]{0:T(128)S(1)} %reshape.523) | copy-start | bytes 1540
  91.6 14.1 %copy-start.39 = (f32[4,128,64]{1,2,0:T(8,128)}, f32[4,128,64]{1,2,0:T(8,128)S(1)}, u32[]{:S(2)}) copy-start(f32[4,128,64]{1,2,0:T(8,128)S(1)} %get-tuple-element.182) | copy-start | bytes 393220
  91.6 14.1 %copy-start.41 = (f32[4,128,64]{1,2,0:T(8,128)}, f32[4,128,64]{1,2,0:T(8,128)S(1)}, u32[]{:S(2)}) copy-start(f32[4,128,64]{1,2,0:T(8,128)S(1)} %get-tuple-element.183) | copy-start | bytes 393220
  93.5 3.2 copy-start.36
  96.5 3.0 copy-start.24
  99.6 15.2 %copy-start.47 = (bf16[512,128]{1,0:T(8,128)(2,1)}, bf16[512,128]{1,0:T(8,128)(2,1)S(1)}, u32[]{:S(2)}) copy-start(bf16[512,128]{1,0:T(8,128)(2,1)S(1)} %slice.159) | copy-start | bytes 393220
  100.6 4.9 copy-start.31
  102.2 3.3 copy-start.66
  102.2 3.3 copy-start.64
  105.5 4.7 copy-start.1
  107.0 3.2 copy-start.27
  107.1 3.2 copy-start.33
  107.1 3.8 copy-start.37
  111.5 3.2 copy-start.51
  123.1 83.0 %copy-start.18 = (bf16[128,2048]{1,0:T(8,128)(2,1)S(1)}, bf16[128,2048]{1,0:T(8,128)(2,1)}, u32[]{:S(2)}) copy-start(bf16[128,2048]{1,0:T(8,128)(2,1)} %x_ref.1) | copy-start | bytes 1572868
  123.1 85.2 %copy-start.10 = (bf16[4,512,128]{2,1,0:T(8,128)(2,1)S(1)}, bf16[4,512,128]{2,1,0:T(8,128)(2,1)}, u32[]{:S(2)}) copy-start(bf16[4,512,128]{2,1,0:T(8,128)(2,1)} %gather_line.4) | copy-start | bytes 1572868
  306.4 11.3 %copy-start.5 = (bf16[32,64,2048]{2,1,0:T(8,128)(2,1)}, bf16[32,64,2048]{2,1,0:T(8,128)(2,1)S(1)}, u32[]{:S(2)}) copy-start(bf16[32,64,2048]{2,1,0:T(8,128)(2,1)S(1)} %convolution_convert_fusion.5) | copy-start | bytes 25165828
  306.4 14.0 %copy-start.76 = (bf16[1,2048,768]{2,1,0:T(8,128)(2,1)S(1)}, bf16[1,2048,768]{2,1,0:T(8,128)(2,1)}, u32[]{:S(2)}) copy-start(bf16[1,2048,768]{2,1,0:T(8,128)(2,1)} %param.29) | copy-start | bytes 9437188
  338.4 14.5 %copy-start = (bf16[32,64,2048]{2,1,0:T(8,128)(2,1)}, bf16[32,64,2048]{2,1,0:T(8,128)(2,1)S(1)}, u32[]{:S(2)}) copy-start(bf16[32,64,2048]{2,1,0:T(8,128)(2,1)S(1)} %convolution_convert_fusion.4) | copy-start | bytes 25165828
  353.7 8.2 copy-start.74
  362.0 15.4 %copy-start.75 = (bf16[1,2048,768]{2,1,0:T(8,128)(2,1)S(1)}, bf16[1,2048,768]{2,1,0:T(8,128)(2,1)}, u32[]{:S(2)}) copy-start(bf16[1,2048,768]{2,1,0:T(8,128)(2,1)} %param.28) | copy-start | bytes 9437188
  377.3 9.7 copy-start.80
  377.3 9.7 copy-start.77
  377.3 9.7 copy-start.82
  500.4 4.1 copy-start.25
  541.6 5.7 copy-start.4
  541.6 5.7 copy-start.48
  541.6 5.7 copy-start.52
  541.6 5.7 copy-start.55
  550.4 6.4 copy-start.8
  563.2 3.4 copy-start.32
  563.2 3.4 copy-start.40
  563.2 3.5 copy-start.59
  563.2 3.5 copy-start.65
  563.2 4.9 copy-start.29
  566.7 3.8 copy-start.43
  568.1 3.2 copy-start.61
  569.9 3.0 copy-start.23
  569.9 5.9 slice-start.2
  572.9 2.9 slice-start.3
  572.9 2.9 copy-start.57
  572.9 2.9 copy-start.68
  597.4 170.0 %copy-start.71 = (f32[128]{0:T(128)S(1)}, f32[128]{0:T(128)}, u32[]{:S(2)}) copy-start(f32[128]{0:T(128)} %get-tuple-element.172) | copy-start | bytes 1540
  597.4 365.9 %all-gather.6.cloned.1.call-start = ((), (), s32[]{:S(2)}) async-start(), calls=%async_computation.2 | async-start | bytes 6488064 | tf_op jit(solution)/shard_map/all_gather | solution.py:830
  887.7 36.3 %copy-start.19 = (bf16[128,2048]{1,0:T(8,128)(2,1)S(1)}, bf16[128,2048]{1,0:T(8,128)(2,1)}, u32[]{:S(2)}) copy-start(bf16[128,2048]{1,0:T(8,128)(2,1)} %x_ref.1) | copy-start | bytes 1572868
  887.7 38.0 %copy-start.12 = (f32[128,2048]{1,0:T(8,128)S(1)}, f32[128,2048]{1,0:T(8,128)}, u32[]{:S(2)}) copy-start(f32[128,2048]{1,0:T(8,128)} %copy-done.11) | copy-start | bytes 3145732
  924.0 5.8 copy-start.15
  925.7 14.9 %slice-start = ((s8[8388608]{0:T(1024)(128)(4,1)}), s8[4194304]{0:T(1024)(128)(4,1)S(1)}, s32[]{:S(2)}) async-start(s8[8388608]{0:T(1024)(128)(4,1)} %bitcast.318), calls=%async_computation.6 | async-start | bytes 8388608
  929.8 10.8 %slice-start.1 = ((s8[8388608]{0:T(1024)(128)(4,1)}), s8[4194304]{0:T(1024)(128)(4,1)S(1)}, s32[]{:S(2)}) async-start(s8[8388608]{0:T(1024)(128)(4,1)} %bitcast.318), calls=%async_computation.7 | async-start | bytes 8388608
  929.8 10.8 %copy-start.83 = (bf16[2048,768]{1,0:T(8,128)(2,1)S(1)}, bf16[2048,768]{1,0:T(8,128)(2,1)}, u32[]{:S(2)}) copy-start(bf16[2048,768]{1,0:T(8,128)(2,1)} %get-tuple-element.155) | copy-start | bytes 9437188
  940.6 9.0 copy-start.81
  949.6 9.2 copy-start.26
  (29 other events, 46.9 us)
Sparse Core Ops, SparseCore 0:
  29.2 43.4 all-gather.7
  75.7 137.7 all-gather.9
  597.5 145.9 all-reduce.10
  767.5 47.2 all-gather.5

commit v2 on v1

--- a/solution.py
+++ b/solution.py
@@ -163,245 +163,213 @@
     lax.fori_loop(1, g.devices, one, 0)
 
 
-def gather_all_kernel(reps, shards, x_ref, slab_ref, out_ref, slabs_ref, sems, zr, lr, hr, dr, cr, ps, pr, ls):
-    g = Grid(reps, shards).here()
-    s = Sends(sems)
-    rows = x_ref.shape[0]
-    half = rows // 2
-    n = g.shards
-    parts = (pl.ds(0, half), pl.ds(half, half))
-    order = g.nearest()
-
-    def block(hi, lo, core, zp):
-        return out_ref.at[g.rep_of(hi, lo, core) * n + zp]
-
-    partner = g.device(g.rep_of(g.hi, g.lo, 1 - g.core), g.z)
-    far = 1 - g.hi
-
-    def at(hi, lo):
-        return g.device(g.rep_of(hi, lo, g.core), g.z)
-
-    keep = pltpu.make_async_copy(x_ref, block(g.hi, g.lo, g.core, g.z), ls.at[0])
-    keep.start()
-    greet_all(g)
-    push_rows(g, slab_ref, slabs_ref, ps, pr)
-    me = g.r * n + g.z
-    keep_slab = pltpu.make_async_copy(slab_ref.at[me], slabs_ref.at[me], ls.at[1])
-    keep_slab.start()
-
-    def own_line(turn):
-        zp = order[turn]
-        dst = block(g.hi, g.lo, g.core, zp)
-        if turn == 0:
-            src = x_ref
-        else:
-            src = dst
-            s.arrived(dst, zr.at[zp], g.device(g.r, zp))
-        s.start(src, dst, zr.at[zp], g.device(g.r, jnp.minimum(g.z + 1, n - 1)), (zp <= g.z) & (g.z + 1 < n))
-        s.start(src, dst, zr.at[zp], g.device(g.r, jnp.maximum(g.z - 1, 0)), (zp >= g.z) & (g.z > 0))
+class PlaneGather:
+    def __init__(self, g, s, view, lr, hr, dr, cr):
+        self.g, self.s, self.view = g, s, view
+        self.lr, self.hr, self.dr, self.cr = lr, hr, dr, cr
+
+    @staticmethod
+    def scratch(g, units):
+        dma, others = pltpu.SemaphoreType.DMA, max(1, g.los - 1)
+        return [dma((units, 2, others)), dma((units, 2)), dma((units, 2, others)), dma((units, 5 * g.los))]
+
+    @staticmethod
+    def sends(g, units):
+        return 9 * g.los * units
+
+    def at(self, hi, lo):
+        return self.g.device(self.g.rep_of(hi, lo, self.g.core), self.g.z)
+
+    def partner(self):
+        g = self.g
+        return g.device(g.rep_of(g.hi, g.lo, 1 - g.core), g.z)
+
+    def own(self, u, src=None):
+        g, s = self.g, self.s
+
+        def dst(part):
+            return self.view(u, g.hi, g.lo, g.core, part)
+
+        src = src or dst
         for part in (0, 1):
             for step in range(1, g.los):
-                s.start(src.at[parts[part]], dst.at[parts[part]], lr.at[zp, part, step - 1], at(g.hi, g.other_lo(step)))
-            s.start(src.at[parts[1 - part]], dst.at[parts[1 - part]], hr.at[zp, 1 - part], at(far, g.lo))
-        s.start(src, dst, cr.at[zp, 0], partner)
-
-    def first(turn):
-        zp = order[turn]
+                s.start(src(part), dst(part), self.lr.at[u, part, step - 1], self.at(g.hi, g.other_lo(step)))
+            s.start(src(1 - part), dst(1 - part), self.hr.at[u, 1 - part], self.at(1 - g.hi, g.lo))
+        s.start(src(None), dst(None), self.cr.at[u, 0], self.partner())
+
+    def take(self, u, hi, lo, part, recv, frm, partner_slot, onward=()):
+        ref = self.view(u, hi, lo, self.g.core, part)
+        self.s.arrived(ref, recv, frm)
+        for sem, device in onward:
+            self.s.start(ref, ref, sem, device)
+        self.s.start(ref, ref, self.cr.at[u, partner_slot], self.partner())
+
+    def first(self, u):
+        g = self.g
+        far = 1 - g.hi
         for step in range(1, g.los):
             frm = (g.lo + g.los - step) % g.los
-            dst = block(g.hi, frm, g.core, zp)
-            s.arrived(dst.at[parts[0]], lr.at[zp, 0, step - 1], at(g.hi, frm))
-            s.start(dst.at[parts[0]], dst.at[parts[0]], dr.at[zp, 0, step - 1], at(far, g.lo))
-            s.start(dst.at[parts[0]], dst.at[parts[0]], cr.at[zp, 5 * step], partner)
-        dst = block(far, g.lo, g.core, zp)
-        s.arrived(dst.at[parts[1]], hr.at[zp, 1], at(far, g.lo))
-        for step in range(1, g.los):
-            s.start(dst.at[parts[1]], dst.at[parts[1]], dr.at[zp, 1, step - 1], at(g.hi, g.other_lo(step)))
-        s.start(dst.at[parts[1]], dst.at[parts[1]], cr.at[zp, 1], partner)
+            onward = [(self.dr.at[u, 0, step - 1], self.at(far, g.lo))]
+            self.take(u, g.hi, frm, 0, self.lr.at[u, 0, step - 1], self.at(g.hi, frm), 5 * step, onward)
+        onward = [(self.dr.at[u, 1, step - 1], self.at(g.hi, g.other_lo(step))) for step in range(1, g.los)]
+        self.take(u, far, g.lo, 1, self.hr.at[u, 1], self.at(far, g.lo), 1, onward)
         for step in range(1, g.los):
             frm = (g.lo + g.los - step) % g.los
-            dst = block(g.hi, frm, g.core, zp)
-            s.arrived(dst.at[parts[1]], lr.at[zp, 1, step - 1], at(g.hi, frm))
-            s.start(dst.at[parts[1]], dst.at[parts[1]], cr.at[zp, 5 * step + 1], partner)
-        dst = block(far, g.lo, g.core, zp)
-        s.arrived(dst.at[parts[0]], hr.at[zp, 0], at(far, g.lo))
-        s.start(dst.at[parts[0]], dst.at[parts[0]], cr.at[zp, 2], partner)
-
-    def second(turn):
-        zp = order[turn]
+            self.take(u, g.hi, frm, 1, self.lr.at[u, 1, step - 1], self.at(g.hi, frm), 5 * step + 1)
+        self.take(u, far, g.lo, 0, self.hr.at[u, 0], self.at(far, g.lo), 2)
+
+    def second(self, u):
+        g = self.g
+        far = 1 - g.hi
         for step in range(1, g.los):
             frm = (g.lo + g.los - step) % g.los
-            dst = block(far, frm, g.core, zp)
-            s.arrived(dst.at[parts[0]], dr.at[zp, 0, step - 1], at(far, g.lo))
-            s.start(dst.at[parts[0]], dst.at[parts[0]], cr.at[zp, 5 * step + 2], partner)
-            s.arrived(dst.at[parts[1]], dr.at[zp, 1, step - 1], at(g.hi, frm))
-            s.start(dst.at[parts[1]], dst.at[parts[1]], cr.at[zp, 5 * step + 3], partner)
-
-    def from_partner(turn):
-        zp = order[turn]
-        other = 1 - g.core
-        s.arrived(block(g.hi, g.lo, other, zp), cr.at[zp, 0], partner)
-        dst = block(far, g.lo, other, zp)
-        s.arrived(dst.at[parts[1]], cr.at[zp, 1], partner)
-        s.arrived(dst.at[parts[0]], cr.at[zp, 2], partner)
+            self.take(u, far, frm, 0, self.dr.at[u, 0, step - 1], self.at(far, g.lo), 5 * step + 2)
+            self.take(u, far, frm, 1, self.dr.at[u, 1, step - 1], self.at(g.hi, frm), 5 * step + 3)
+
+    def from_partner(self, u):
+        g = self.g
+        far, other = 1 - g.hi, 1 - g.core
+
+        def got(hi, lo, part, slot):
+            self.s.arrived(self.view(u, hi, lo, other, part), self.cr.at[u, slot], self.partner())
+
+        got(g.hi, g.lo, None, 0)
+        got(far, g.lo, 1, 1)
+        got(far, g.lo, 0, 2)
         for step in range(1, g.los):
             frm = (g.lo + g.los - step) % g.los
-            dst = block(g.hi, frm, other, zp)
-            s.arrived(dst.at[parts[0]], cr.at[zp, 5 * step], partner)
-            s.arrived(dst.at[parts[1]], cr.at[zp, 5 * step + 1], partner)
-            dst = block(far, frm, other, zp)
-            s.arrived(dst.at[parts[0]], cr.at[zp, 5 * step + 2], partner)
-            s.arrived(dst.at[parts[1]], cr.at[zp, 5 * step + 3], partner)
-
-    for turn in range(n + 2):
-        if turn < n:
-            own_line(turn)
-        if 0 <= turn - 1 < n:
-            first(turn - 1)
-        if 0 <= turn - 2 < n:
-            second(turn - 2)
-    for turn in range(n):
-        from_partner(turn)
-    keep.wait()
-    keep_slab.wait()
-    push_wait(g, slab_ref, slabs_ref, ps, pr)
-    s.drain()
-
-
-def gather_all(reps, shards, x, slab, ident):
-    g = Grid(reps, shards)
-    n, los = shards, g.los
-    per_turn = 2 + 2 * los + 1 + (3 * (los - 1)) + los + 1 + 1 + 2 * (los - 1) + los
-    dma = pltpu.SemaphoreType.DMA
-    return pl.pallas_call(
-        functools.partial(gather_all_kernel, reps, shards),
-        out_shape=(
-            jax.ShapeDtypeStruct((g.devices,) + x.shape, x.dtype),
-            jax.ShapeDtypeStruct(slab.shape, slab.dtype),
-        ),
-        in_specs=[pl.BlockSpec(memory_space=pltpu.VMEM)] * 2,
-        out_specs=(pl.BlockSpec(memory_space=pl.ANY), pl.BlockSpec(memory_space=pltpu.VMEM)),
-        scratch_shapes=[
-            dma((n * (per_turn + 4),)),
-            dma((n,)),
-            dma((n, 2, max(1, los - 1))),
-            dma((n, 2)),
-            dma((n, 2, max(1, los - 1))),
-            dma((n, 5 * los)),
-            dma((g.devices,)),
-            dma((g.devices,)),
-            dma((2,)),
-        ],
-        compiler_params=pltpu.CompilerParams(collective_id=ident, has_side_effects=True, vmem_limit_bytes=vmem_cap),
-        name="gather_all",
-    )(x, slab)
-
-
-def add_rows(dst, *srcs, rows):
+            got(g.hi, frm, 0, 5 * step)
+            got(g.hi, frm, 1, 5 * step + 1)
+            got(far, frm, 0, 5 * step + 2)
+            got(far, frm, 1, 5 * step + 3)
+
+
+def add_rows(dst, *srcs, step=16):
     def one(i, carry):
-        at = pl.ds(pl.multiple_of(i * 16, 16), 16)
+        at = pl.ds(pl.multiple_of(i * step, step), step)
         total = srcs[0][at, :].astype(f32)
         for src in srcs[1:]:
             total = total + src[at, :].astype(f32)
         dst[at, :] = total.astype(dst.dtype)
         return carry
 
-    lax.fori_loop(0, rows // 16, one, 0)
-
-
-def scatter_all_kernel(reps, shards, slabbed, *refs):
-    if slabbed:
-        p_ref, slab_ref, out_ref, slabs_ref, *rest = refs
-    else:
-        p_ref, out_ref, *rest = refs
-    own, ra, rb0, rb1, rc0, rc1, rl, rr, sems, sa, sb0, sb1, sc0, sc1, sl, sr, ps, pr, ls = rest
-    g = Grid(reps, shards).here()
-    s = Sends(sems)
-    n, los = g.shards, g.los
-    rows = out_ref.shape[0]
-    half = rows // 2
-    top, bottom = pl.ds(0, half), pl.ds(half, half)
-    order = g.nearest()[::-1]
-    partner = g.device(g.rep_of(g.hi, g.lo, 1 - g.core), g.z)
-    far = 1 - g.hi
-
-    def at(hi, lo):
-        return g.device(g.rep_of(hi, lo, g.core), g.z)
-
-    loads = []
-    for turn in range(n):
-        load = pltpu.make_async_copy(p_ref.at[:, g.core, order[turn]], own.at[turn], ls.at[turn])
-        load.start()
-        loads.append(load)
-    greet_all(g)
-    if slabbed:
-        push_rows(g, slab_ref, slabs_ref, ps, pr)
-        me = g.r * n + g.z
-        keep_slab = pltpu.make_async_copy(slab_ref.at[me], slabs_ref.at[me], ls.at[n])
-        keep_slab.start()
-    for turn in range(n):
-        s.start(p_ref.at[:, 1 - g.core, order[turn]], ra.at[turn], sa.at[turn], partner)
-
-    def stage_a(turn):
-        loads[turn].wait()
-        s.arrived(ra.at[turn], sa.at[turn], partner)
-
-        def one(i, carry):
-            a = pl.ds(pl.multiple_of(i * 16, 16), 16)
-            for q in range(g.places):
-                own[turn, q, a, :] = (own[turn, q, a, :].astype(f32) + ra[turn, q, a, :].astype(f32)).astype(own.dtype)
+    lax.fori_loop(0, dst.shape[0] // step, one, 0)
+
+
+class PlaneScatter:
+    def __init__(self, g, s, p, cut, own, ra, rb0, rb1, rc0, rc1, sa, sb0, sb1, sc0, sc1, ls):
+        self.g, self.s, self.p, self.cut, self.owned = g, s, p, cut, own
+        self.ra, self.rb0, self.rb1, self.rc0, self.rc1 = ra, rb0, rb1, rc0, rc1
+        self.sa, self.sb0, self.sb1, self.sc0, self.sc1, self.ls = sa, sb0, sb1, sc0, sc1, ls
+
+    @staticmethod
+    def scratch(g, units, block, halves, dtype):
+        dma, others, v = pltpu.SemaphoreType.DMA, max(1, g.los - 1), pltpu.VMEM
+        first, second = halves
+        return [
+            v((units, g.places) + block, dtype),
+            v((units, g.places) + block, dtype),
+            v((units, g.los) + first, dtype),
+            v((units, others, 2) + second, dtype),
+            v((units, others) + first, dtype),
+            v((units,) + second, dtype),
+            dma((units,)),
+            dma((units,)),
+            dma((units, others, 2)),
+            dma((units, others)),
+            dma((units,)),
+            dma((units,)),
+        ]
+
+    @staticmethod
+    def sends(g, units):
+        return units * (3 * g.los + 2)
+
+    def at(self, hi, lo):
+        return self.g.device(self.g.rep_of(hi, lo, self.g.core), self.g.z)
+
+    def partner(self):
+        g = self.g
+        return g.device(g.rep_of(g.hi, g.lo, 1 - g.core), g.z)
+
+    def load(self, units):
+        self.loads = []
+        for turn in range(units):
+            load = pltpu.make_async_copy(self.p(turn, self.g.core), self.owned.at[turn], self.ls.at[turn])
+            load.start()
+            self.loads.append(load)
+
+    def to_partner(self, turn):
+        self.s.start(self.p(turn, 1 - self.g.core), self.ra.at[turn], self.sa.at[turn], self.partner())
+
+    def half(self, turn, place, part):
+        return self.owned.at[(turn, place) + self.cut(part)]
+
+    def mine(self, turn):
+        return self.owned.at[turn, self.g.hi * self.g.los + self.g.lo]
+
+    def a(self, turn):
+        g, s = self.g, self.s
+        far = 1 - g.hi
+        self.loads[turn].wait()
+        s.arrived(self.ra.at[turn], self.sa.at[turn], self.partner())
+
+        def one(q, carry):
+            line = self.owned.at[turn, q]
+            add_rows(line, line, self.ra.at[turn, q])
             return carry
 
-        lax.fori_loop(0, rows // 16, one, 0)
-        s.start(own.at[turn, pl.ds(far * los, los), top], rb0.at[turn], sb0.at[turn], at(far, g.lo))
-        for step in range(1, los):
+        lax.fori_loop(0, g.places, one, 0)
+        block = self.owned.at[(turn, pl.ds(far * g.los, g.los)) + self.cut(0)]
+        s.start(block, self.rb0.at[turn], self.sb0.at[turn], self.at(far, g.lo))
+        for step in range(1, g.los):
             to = g.other_lo(step)
             for hi in range(2):
-                s.start(own.at[turn, hi * los + to, bottom], rb1.at[turn, step - 1, hi], sb1.at[turn, step - 1, hi], at(g.hi, to))
-
-    def stage_b(turn):
-        s.arrived(rb0.at[turn], sb0.at[turn], at(far, g.lo))
-        for lo in range(los):
-            line = own.at[turn, g.hi * los + lo, top]
-            add_rows(line, line, rb0.at[turn, lo], rows=half)
-        for step in range(1, los):
-            frm = (g.lo + los - step) % los
+                sem = self.sb1.at[turn, step - 1, hi]
+                s.start(self.half(turn, hi * g.los + to, 1), self.rb1.at[turn, step - 1, hi], sem, self.at(g.hi, to))
+
+    def b(self, turn):
+        g, s = self.g, self.s
+        far = 1 - g.hi
+        s.arrived(self.rb0.at[turn], self.sb0.at[turn], self.at(far, g.lo))
+        for lo in range(g.los):
+            line = self.half(turn, g.hi * g.los + lo, 0)
+            add_rows(line, line, self.rb0.at[turn, lo])
+        for step in range(1, g.los):
+            to = g.other_lo(step)
+            sem = self.sc0.at[turn, step - 1]
+            s.start(self.half(turn, g.hi * g.los + to, 0), self.rc0.at[turn, step - 1], sem, self.at(g.hi, to))
+        for step in range(1, g.los):
+            frm = (g.lo + g.los - step) % g.los
             for hi in range(2):
-                s.arrived(rb1.at[turn, step - 1, hi], sb1.at[turn, step - 1, hi], at(g.hi, frm))
+                s.arrived(self.rb1.at[turn, step - 1, hi], self.sb1.at[turn, step - 1, hi], self.at(g.hi, frm))
         for hi in range(2):
-            line = own.at[turn, hi * los + g.lo, bottom]
-            add_rows(line, line, *[rb1.at[turn, step, hi] for step in range(los - 1)], rows=half)
-        for step in range(1, los):
-            to = g.other_lo(step)
-            s.start(own.at[turn, g.hi * los + to, top], rc0.at[turn, step - 1], sc0.at[turn, step - 1], at(g.hi, to))
-        s.start(own.at[turn, far * los + g.lo, bottom], rc1.at[turn], sc1.at[turn], at(far, g.lo))
-
-    def stage_c(turn):
-        mine = g.hi * los + g.lo
-        for step in range(1, los):
-            s.arrived(rc0.at[turn, step - 1], sc0.at[turn, step - 1], at(g.hi, (g.lo + los - step) % los))
-        line = own.at[turn, mine, top]
-        add_rows(line, line, *[rc0.at[turn, step] for step in range(los - 1)], rows=half)
-        s.arrived(rc1.at[turn], sc1.at[turn], at(far, g.lo))
-        line = own.at[turn, mine, bottom]
-        add_rows(line, line, rc1.at[turn], rows=half)
-        send_line(g, s, order[turn], own.at[turn, mine], out_ref, rl, rr, sl, sr, last=turn == n - 1)
-
-    for turn in range(n + 2):
-        if turn < n:
-            stage_a(turn)
-        if 0 <= turn - 1 < n:
-            stage_b(turn - 1)
-        if 0 <= turn - 2 < n:
-            stage_c(turn - 2)
-    if slabbed:
-        keep_slab.wait()
-        push_wait(g, slab_ref, slabs_ref, ps, pr)
-    s.drain()
+            line = self.half(turn, hi * g.los + g.lo, 1)
+            add_rows(line, line, *[self.rb1.at[turn, step, hi] for step in range(g.los - 1)])
+        s.start(self.half(turn, far * g.los + g.lo, 1), self.rc1.at[turn], self.sc1.at[turn], self.at(far, g.lo))
+
+    def c(self, turn):
+        g, s = self.g, self.s
+        place = g.hi * g.los + g.lo
+        for step in range(1, g.los):
+            frm = (g.lo + g.los - step) % g.los
+            s.arrived(self.rc0.at[turn, step - 1], self.sc0.at[turn, step - 1], self.at(g.hi, frm))
+        line = self.half(turn, place, 0)
+        add_rows(line, line, *[self.rc0.at[turn, step] for step in range(g.los - 1)])
+        s.arrived(self.rc1.at[turn], self.sc1.at[turn], self.at(1 - g.hi, g.lo))
+        line = self.half(turn, place, 1)
+        add_rows(line, line, self.rc1.at[turn])
+
+
+def pass_along(g, s, zp, src, dst, zr):
+    n = g.shards
+    right, left = g.device(g.r, jnp.minimum(g.z + 1, n - 1)), g.device(g.r, jnp.maximum(g.z - 1, 0))
+    s.start(src, dst, zr.at[zp], right, (zp <= g.z) & (g.z + 1 < n))
+    s.start(src, dst, zr.at[zp], left, (zp >= g.z) & (g.z > 0))
 
 
 def send_line(g, s, zp, line, out_ref, rl, rr, sl, sr, last):
-    n, rows = g.shards, line.shape[0]
+    n = g.shards
     left, right = g.device(g.r, jnp.maximum(g.z - 1, 0)), g.device(g.r, jnp.minimum(g.z + 1, n - 1))
     has_left, has_right = g.z > 0, g.z + 1 < n
     if last:
@@ -410,107 +378,56 @@
 
         @pl.when(has_left & has_right)
         def _():
-            add_rows(out_ref, line, rl.at[g.z], rr.at[g.z], rows=rows)
+            add_rows(out_ref, line, rl.at[g.z], rr.at[g.z])
 
         @pl.when(has_left & jnp.logical_not(has_right))
         def _():
-            add_rows(out_ref, line, rl.at[g.z], rows=rows)
+            add_rows(out_ref, line, rl.at[g.z])
 
         @pl.when(has_right & jnp.logical_not(has_left))
         def _():
-            add_rows(out_ref, line, rr.at[g.z], rows=rows)
+            add_rows(out_ref, line, rr.at[g.z])
     else:
         onward_right, onward_left = zp > g.z, zp < g.z
 
         @pl.when(onward_right & has_left)
         def _():
             s.arrived(rl.at[zp], sl.at[zp], left)
-            add_rows(line, line, rl.at[zp], rows=rows)
+            add_rows(line, line, rl.at[zp])
 
         @pl.when(onward_left & has_right)
         def _():
             s.arrived(rr.at[zp], sr.at[zp], right)
-            add_rows(line, line, rr.at[zp], rows=rows)
+            add_rows(line, line, rr.at[zp])
 
         s.start(line, rl.at[zp], sl.at[zp], right, onward_right)
         s.start(line, rr.at[zp], sr.at[zp], left, onward_left)
 
 
-def scatter_all(reps, shards, p, slab, ident):
-    g = Grid(reps, shards)
-    n, los, places = shards, g.los, g.places
-    _, rows, width = p.shape
-    half = rows // 2
-    lo_others = max(1, los - 1)
-    dma = pltpu.SemaphoreType.DMA
-    v = pltpu.VMEM
-    slabbed = slab is not None
-    out_shape = (jax.ShapeDtypeStruct((rows, width), f32),)
-    if slabbed:
-        out_shape += (jax.ShapeDtypeStruct(slab.shape, slab.dtype),)
-    vmem = pl.BlockSpec(memory_space=pltpu.VMEM)
-    done = pl.pallas_call(
-        functools.partial(scatter_all_kernel, reps, shards, slabbed),
-        out_shape=out_shape,
-        in_specs=[pl.BlockSpec(memory_space=pl.ANY)] + [vmem] * slabbed,
-        out_specs=(vmem,) * len(out_shape),
-        scratch_shapes=[
-            v((n, places, rows, width), p.dtype),
-            v((n, places, rows, width), p.dtype),
-            v((n, los, half, width), p.dtype),
-            v((n, lo_others, 2, half, width), p.dtype),
-            v((n, lo_others, half, width), p.dtype),
-            v((n, half, width), p.dtype),
-            v((n, rows, width), p.dtype),
-            v((n, rows, width), p.dtype),
-            dma((n * (6 + 3 * los),)),
-            dma((n,)),
-            dma((n,)),
-            dma((n, lo_others, 2)),
-            dma((n, lo_others)),
-            dma((n,)),
-            dma((n,)),
-            dma((n,)),
-            dma((g.devices,)),
-            dma((g.devices,)),
-            dma((n + 1,)),
-        ],
-        compiler_params=pltpu.CompilerParams(collective_id=ident, has_side_effects=True, vmem_limit_bytes=vmem_cap),
-        name="scatter_all",
-    )(p.reshape(places, 2, n, rows, width), *([slab] if slabbed else []))
-    return done if slabbed else done[0]
-
-
-def scatter_wide(reps, shards, p, slab, ident, chunks):
-    if chunks == 1:
-        return scatter_all(reps, shards, p, slab, ident)
-    step = p.shape[2] // chunks
-    parts = [
-        scatter_all(reps, shards, p[:, :, i * step : (i + 1) * step], slab if i == 0 else None, ident + i)
-        for i in range(chunks)
-    ]
-    if slab is None:
-        return jnp.concatenate(parts, axis=1)
-    first, slabs = parts[0]
-    return jnp.concatenate([first] + parts[1:], axis=1), slabs
+def line_scratch(shards, block, dtype):
+    v, dma = pltpu.VMEM, pltpu.SemaphoreType.DMA
+    return [v((shards,) + block, dtype), v((shards,) + block, dtype), dma((shards,)), dma((shards,))]
+
+
+hbm = pl.BlockSpec(memory_space=pl.ANY)
+vmem = pl.BlockSpec(memory_space=pltpu.VMEM)
+
+
+def params(ident):
+    return pltpu.CompilerParams(collective_id=ident, has_side_effects=True, vmem_limit_bytes=vmem_cap)
 
 
 def gather_line_kernel(reps, shards, x_ref, out_ref, sems, zr, ls):
     g = Grid(reps, shards).here()
     s = Sends(sems)
-    n = g.shards
-    order = g.nearest()
     keep = pltpu.make_async_copy(x_ref, out_ref.at[g.z], ls.at[0])
     keep.start()
     greet_line(g)
-    for turn in range(n):
-        zp = order[turn]
+    for turn, zp in enumerate(g.nearest()):
         dst = out_ref.at[zp]
-        src = x_ref if turn == 0 else dst
         if turn:
             s.arrived(dst, zr.at[zp], g.device(g.r, zp))
-        s.start(src, dst, zr.at[zp], g.device(g.r, jnp.minimum(g.z + 1, n - 1)), (zp <= g.z) & (g.z + 1 < n))
-        s.start(src, dst, zr.at[zp], g.device(g.r, jnp.maximum(g.z - 1, 0)), (zp >= g.z) & (g.z > 0))
+        pass_along(g, s, zp, dst if turn else x_ref, dst, zr)
     keep.wait()
     s.drain()
 
@@ -520,15 +437,15 @@
     return pl.pallas_call(
         functools.partial(gather_line_kernel, reps, shards),
         out_shape=jax.ShapeDtypeStruct((shards,) + x.shape, x.dtype),
-        in_specs=[pl.BlockSpec(memory_space=pltpu.VMEM)],
-        out_specs=pl.BlockSpec(memory_space=pltpu.VMEM),
+        in_specs=[vmem],
+        out_specs=vmem,
         scratch_shapes=[dma((2 * shards,)), dma((shards,)), dma((1,))],
-        compiler_params=pltpu.CompilerParams(collective_id=ident, has_side_effects=True),
+        compiler_params=params(ident),
         name="gather_line",
     )(x)
 
 
-def scatter_line_kernel(reps, shards, p_ref, out_ref, own, rl, rr, sems, sl, sr, ls):
+def scatter_line_kernel(reps, shards, p_ref, out_ref, own, rl, rr, sl, sr, sems, ls):
     g = Grid(reps, shards).here()
     s = Sends(sems)
     n = g.shards
@@ -551,20 +468,362 @@
     return pl.pallas_call(
         functools.partial(scatter_line_kernel, reps, shards),
         out_shape=jax.ShapeDtypeStruct((rows, width), f32),
-        in_specs=[pl.BlockSpec(memory_space=pl.ANY)],
-        out_specs=pl.BlockSpec(memory_space=pltpu.VMEM),
-        scratch_shapes=[
-            pltpu.VMEM((shards, rows, width), p.dtype),
-            pltpu.VMEM((shards, rows, width), p.dtype),
-            pltpu.VMEM((shards, rows, width), p.dtype),
-            dma((2 * shards,)),
-            dma((shards,)),
-            dma((shards,)),
-            dma((shards,)),
-        ],
-        compiler_params=pltpu.CompilerParams(collective_id=ident, has_side_effects=True),
+        in_specs=[hbm],
+        out_specs=vmem,
+        scratch_shapes=[pltpu.VMEM(p.shape, p.dtype)]
+        + line_scratch(shards, (rows, width), p.dtype)
+        + [dma((2 * shards,)), dma((shards,))],
+        compiler_params=params(ident),
         name="scatter_line",
     )(p)
+
+
+def collect_kernel(reps, shards, layout, x_ref, small_ref, wq_ref, wk_ref, wv_ref, xs_ref, smalls_ref, w_ref, sems, xr, mr, wr, lr, hr, dr, cr, ls):
+    g = Grid(reps, shards).here()
+    s = Sends(sems)
+    n = g.shards
+    q_cols, kv_cols, kv_heads, head_dim = layout
+    deep = wq_ref.shape[0]
+    piece = deep // g.reps
+    cols = q_cols + 2 * kv_cols
+    first = cols // 2 // 128 * 128
+    spans = {0: pl.ds(0, first), 1: pl.ds(first, cols - first), None: pl.ds(0, cols)}
+    mine = pl.ds(pl.multiple_of(g.r * piece, piece), piece)
+
+    def view(u, hi, lo, core, part):
+        row = pl.multiple_of(u * deep + g.rep_of(hi, lo, core) * piece, piece)
+        return w_ref.at[pl.ds(row, piece), spans[part]]
+
+    def pieces(zp, u):
+        row = pl.ds(pl.multiple_of(u * deep + g.r * piece, piece), piece)
+        at_q = pl.ds(pl.multiple_of(zp * q_cols, 128), q_cols)
+        at_kv = pl.ds(pl.multiple_of(zp * kv_heads // n * head_dim, 128), kv_cols)
+        return (
+            (wq_ref.at[mine, at_q], w_ref.at[row, pl.ds(0, q_cols)]),
+            (wk_ref.at[mine, at_kv], w_ref.at[row, pl.ds(q_cols, kv_cols)]),
+            (wv_ref.at[mine, at_kv], w_ref.at[row, pl.ds(q_cols + kv_cols, kv_cols)]),
+        )
+
+    keeps = [
+        pltpu.make_async_copy(x_ref, xs_ref.at[g.z], ls.at[0]),
+        pltpu.make_async_copy(small_ref, smalls_ref.at[g.z], ls.at[1]),
+    ]
+    locals_ = [pltpu.make_async_copy(src, dst, ls.at[2 + i]) for i, (src, dst) in enumerate(pieces(g.z, g.z))]
+    for copy in locals_ + keeps:
+        copy.start()
+    barrier = pltpu.get_barrier_semaphore()
+    peers = [g.device(g.r, (g.z + step) % n) for step in range(1, n)]
+    peers += [g.device(g.rep_of(g.hi, g.other_lo(step), g.core), g.z) for step in range(1, g.los)]
+    peers += [g.device(g.rep_of(1 - g.hi, g.lo, g.core), g.z), g.device(g.rep_of(g.hi, g.lo, 1 - g.core), g.z)]
+    for peer in peers:
+        pl.semaphore_signal(barrier, inc=1, device_id=peer, device_id_type=pl.DeviceIdType.MESH)
+    pl.semaphore_wait(barrier, len(peers))
+
+    plane = PlaneGather(g, s, view, lr, hr, dr, cr)
+    for step in range(1, n):
+        zp = (g.z + step) % n
+        for i, (src, dst) in enumerate(pieces(zp, g.z)):
+            s.start(src, dst, wr.at[step, i], g.device(g.r, zp))
+    order = g.nearest()
+
+    def line(turn):
+        zp = order[turn]
+        if turn:
+            s.arrived(smalls_ref.at[zp], mr.at[zp], g.device(g.r, zp))
+        pass_along(g, s, zp, smalls_ref.at[zp] if turn else small_ref, smalls_ref.at[zp], mr)
+        if turn:
+            s.arrived(xs_ref.at[zp], xr.at[zp], g.device(g.r, zp))
+        pass_along(g, s, zp, xs_ref.at[zp] if turn else x_ref, xs_ref.at[zp], xr)
+
+    line(0)
+    for copy in locals_:
+        copy.wait()
+    plane.own(g.z)
+
+    def unit(step):
+        return (g.z + n - step) % n
+
+    for step in range(1, n):
+        u = unit(step)
+        for i, (_, dst) in enumerate(pieces(g.z, u)):
+            s.arrived(dst, wr.at[step, i], g.device(g.r, u))
+        plane.own(u)
+    line(1)
+    for step in range(n):
+        plane.first(unit(step))
+        if step:
+            plane.second(unit(step - 1))
+        if 2 + step < n:
+            line(2 + step)
+    plane.second(unit(n - 1))
+    for step in range(n):
+        plane.from_partner(unit(step))
+    for copy in keeps:
+        copy.wait()
+    s.drain()
+
+
+def collect(reps, shards, x, small, wq, wk, wv, layout, ident):
+    g = Grid(reps, shards)
+    dma = pltpu.SemaphoreType.DMA
+    n = shards
+    cols = layout[0] + 2 * layout[1]
+    return pl.pallas_call(
+        functools.partial(collect_kernel, reps, shards, layout),
+        out_shape=(
+            jax.ShapeDtypeStruct((n,) + x.shape, x.dtype),
+            jax.ShapeDtypeStruct((n,) + small.shape, small.dtype),
+            jax.ShapeDtypeStruct((n * wq.shape[0], cols), wq.dtype),
+        ),
+        in_specs=[vmem, vmem, hbm, hbm, hbm],
+        out_specs=(vmem, vmem, vmem),
+        scratch_shapes=[dma((PlaneGather.sends(g, n) + 7 * n,)), dma((n,)), dma((n,)), dma((n, 3))]
+        + PlaneGather.scratch(g, n)
+        + [dma((5,))],
+        compiler_params=params(ident),
+        name="collect",
+    )(x, small, wq, wk, wv)
+
+
+def gather_all_kernel(reps, shards, x_ref, slab_ref, out_ref, slabs_ref, sems, zr, ps, pr, ls, lr, hr, dr, cr):
+    g = Grid(reps, shards).here()
+    s = Sends(sems)
+    half = x_ref.shape[0] // 2
+    n = g.shards
+    spans = {0: pl.ds(0, half), 1: pl.ds(half, half), None: pl.ds(0, 2 * half)}
+    order = g.nearest()
+
+    def view(u, hi, lo, core, part):
+        return out_ref.at[g.rep_of(hi, lo, core) * n + u, spans[part]]
+
+    plane = PlaneGather(g, s, view, lr, hr, dr, cr)
+    keep = pltpu.make_async_copy(x_ref, view(g.z, g.hi, g.lo, g.core, None), ls.at[0])
+    keep.start()
+    greet_all(g)
+    push_rows(g, slab_ref, slabs_ref, ps, pr)
+    me = g.r * n + g.z
+    keep_slab = pltpu.make_async_copy(slab_ref.at[me], slabs_ref.at[me], ls.at[1])
+    keep_slab.start()
+    for turn in range(n + 2):
+        if turn < n:
+            zp = order[turn]
+            dst = view(zp, g.hi, g.lo, g.core, None)
+            if turn:
+                s.arrived(dst, zr.at[zp], g.device(g.r, zp))
+            pass_along(g, s, zp, dst if turn else x_ref, dst, zr)
+            plane.own(zp, None if turn else lambda part: x_ref.at[spans[part]])
+        if 0 <= turn - 1 < n:
+            plane.first(order[turn - 1])
+        if 0 <= turn - 2 < n:
+            plane.second(order[turn - 2])
+    for turn in range(n):
+        plane.from_partner(order[turn])
+    keep.wait()
+    keep_slab.wait()
+    push_wait(g, slab_ref, slabs_ref, ps, pr)
+    s.drain()
+
+
+def gather_all(reps, shards, x, slab, ident):
+    g = Grid(reps, shards)
+    dma = pltpu.SemaphoreType.DMA
+    n = shards
+    return pl.pallas_call(
+        functools.partial(gather_all_kernel, reps, shards),
+        out_shape=(
+            jax.ShapeDtypeStruct((g.devices,) + x.shape, x.dtype),
+            jax.ShapeDtypeStruct(slab.shape, slab.dtype),
+        ),
+        in_specs=[vmem, vmem],
+        out_specs=(hbm, vmem),
+        scratch_shapes=[
+            dma((PlaneGather.sends(g, n) + 2 * n,)),
+            dma((n,)),
+            dma((g.devices,)),
+            dma((g.devices,)),
+            dma((2,)),
+        ]
+        + PlaneGather.scratch(g, n),
+        compiler_params=params(ident),
+        name="gather_all",
+    )(x, slab)
+
+
+def scatter_all_kernel(reps, shards, slabbed, *refs):
+    if slabbed:
+        p_ref, slab_ref, out_ref, slabs_ref, *rest = refs
+    else:
+        p_ref, out_ref, *rest = refs
+    rl, rr, sl, sr, sems, ps, pr, slab_sem, *rest = rest
+    g = Grid(reps, shards).here()
+    s = Sends(sems)
+    n = g.shards
+    half = out_ref.shape[0] // 2
+    order = g.nearest()[::-1]
+    plane = PlaneScatter(
+        g, s, lambda turn, core: p_ref.at[:, core, order[turn]], lambda part: (pl.ds(part * half, half),), *rest
+    )
+    plane.load(n)
+    greet_all(g)
+    for turn in range(n):
+        plane.to_partner(turn)
+    if slabbed:
+        push_rows(g, slab_ref, slabs_ref, ps, pr)
+        me = g.r * n + g.z
+        keep_slab = pltpu.make_async_copy(slab_ref.at[me], slabs_ref.at[me], slab_sem.at[0])
+        keep_slab.start()
+    for turn in range(n + 2):
+        if turn < n:
+            plane.a(turn)
+        if 0 <= turn - 1 < n:
+            plane.b(turn - 1)
+        if 0 <= turn - 2 < n:
+            plane.c(turn - 2)
+            send_line(g, s, order[turn - 2], plane.mine(turn - 2), out_ref, rl, rr, sl, sr, last=turn - 2 == n - 1)
+    if slabbed:
+        keep_slab.wait()
+        push_wait(g, slab_ref, slabs_ref, ps, pr)
+    s.drain()
+
+
+def scatter_all(reps, shards, p, slab, ident):
+    g = Grid(reps, shards)
+    n = shards
+    _, rows, width = p.shape
+    half = rows // 2
+    dma = pltpu.SemaphoreType.DMA
+    slabbed = slab is not None
+    out_shape = (jax.ShapeDtypeStruct((rows, width), f32),)
+    if slabbed:
+        out_shape += (jax.ShapeDtypeStruct(slab.shape, slab.dtype),)
+    done = pl.pallas_call(
+        functools.partial(scatter_all_kernel, reps, shards, slabbed),
+        out_shape=out_shape,
+        in_specs=[hbm] + [vmem] * slabbed,
+        out_specs=(vmem,) * len(out_shape),
+        scratch_shapes=line_scratch(n, (rows, width), p.dtype)
+        + [dma((PlaneScatter.sends(g, n) + 2 * n,)), dma((g.devices,)), dma((g.devices,)), dma((1,))]
+        + PlaneScatter.scratch(g, n, (rows, width), ((half, width), (half, width)), p.dtype),
+        compiler_params=params(ident),
+        name="scatter_all",
+    )(p.reshape(g.places, 2, n, rows, width), *([slab] if slabbed else []))
+    return done if slabbed else done[0]
+
+
+def scatter_wide(reps, shards, p, slab, ident, chunks):
+    if chunks == 1:
+        return scatter_all(reps, shards, p, slab, ident)
+    step = p.shape[2] // chunks
+    parts = [
+        scatter_all(reps, shards, p[:, :, i * step : (i + 1) * step], slab if i == 0 else None, ident + i)
+        for i in range(chunks)
+    ]
+    if slab is None:
+        return jnp.concatenate(parts, axis=1)
+    first, slabs = parts[0]
+    return jnp.concatenate([first] + parts[1:], axis=1), slabs
+
+
+def deliver_kernel(reps, shards, p_ref, w_ref, out_ref, ws_ref, line_own, rl, rr, sl, sr, sems, line_loads, wr, keep_sem, *rest):
+    g = Grid(reps, shards).here()
+    s = Sends(sems)
+    n = g.shards
+    gather_refs, scatter_refs = rest[:4], rest[4:]
+    cols = w_ref.shape[-1]
+    first = cols // 2 // 128 * 128
+    spans = {0: pl.ds(0, first), 1: pl.ds(first, cols - first), None: pl.ds(0, cols)}
+    order = g.nearest()[::-1]
+    scatter = PlaneScatter(
+        g, s, lambda turn, core: w_ref.at[turn, :, core], lambda part: (slice(None), spans[part]), *scatter_refs
+    )
+    gather = PlaneGather(
+        g, s, lambda u, hi, lo, core, part: ws_ref.at[u, g.rep_of(hi, lo, core), :, spans[part]], *gather_refs
+    )
+    scatter.load(n)
+    loads = []
+    for turn in range(n):
+        load = pltpu.make_async_copy(p_ref.at[order[turn]], line_own.at[turn], line_loads.at[turn])
+        load.start()
+        loads.append(load)
+    barrier = pltpu.get_barrier_semaphore()
+    peers = [g.device(g.r, (g.z + step) % n) for step in range(1, n)]
+    peers += [g.device(g.rep_of(g.hi, g.other_lo(step), g.core), g.z) for step in range(1, g.los)]
+    peers += [g.device(g.rep_of(1 - g.hi, g.lo, g.core), g.z), g.device(g.rep_of(g.hi, g.lo, 1 - g.core), g.z)]
+    for peer in peers:
+        pl.semaphore_signal(barrier, inc=1, device_id=peer, device_id_type=pl.DeviceIdType.MESH)
+    pl.semaphore_wait(barrier, len(peers))
+
+    for turn in range(n):
+        scatter.to_partner(turn)
+
+    def line(turn):
+        loads[turn].wait()
+        send_line(g, s, order[turn], line_own.at[turn], out_ref, rl, rr, sl, sr, last=turn == n - 1)
+
+    def owner(turn):
+        scatter.c(turn)
+        dst = ws_ref.at[g.z, g.r]
+        keep = pltpu.make_async_copy(scatter.mine(turn), dst, keep_sem.at[0])
+        pl.when(g.z == turn)(keep.start)
+        s.start(scatter.mine(turn), dst, wr.at[g.z], g.device(g.r, turn), g.z != turn)
+        pl.when(g.z == turn)(keep.wait)
+
+    line(0)
+    for turn in range(n + 2):
+        if turn < n:
+            scatter.a(turn)
+        if 0 <= turn - 1 < n:
+            scatter.b(turn - 1)
+        if 1 <= turn < n - 1:
+            line(turn)
+        if 0 <= turn - 2 < n:
+            owner(turn - 2)
+    gather.own(g.z)
+
+    def unit(step):
+        return (g.z + n - step) % n
+
+    for step in range(1, n):
+        u = unit(step)
+        s.arrived(ws_ref.at[u, g.r], wr.at[u], g.device(g.r, u))
+        gather.own(u)
+        gather.first(unit(step - 1))
+        if step > 1:
+            gather.second(unit(step - 2))
+    gather.first(unit(n - 1))
+    gather.second(unit(n - 2))
+    gather.second(unit(n - 1))
+    line(n - 1)
+    for step in range(n):
+        gather.from_partner(unit(step))
+    s.drain()
+
+
+def deliver(reps, shards, p, w, ident):
+    g = Grid(reps, shards)
+    n = shards
+    dma = pltpu.SemaphoreType.DMA
+    _, rows, width = p.shape
+    _, _, piece, cols = w.shape
+    first = cols // 2 // 128 * 128
+    return pl.pallas_call(
+        functools.partial(deliver_kernel, reps, shards),
+        out_shape=(jax.ShapeDtypeStruct((rows, width), f32), jax.ShapeDtypeStruct(w.shape, w.dtype)),
+        in_specs=[hbm, hbm],
+        out_specs=(vmem, vmem),
+        scratch_shapes=[pltpu.VMEM(p.shape, p.dtype)]
+        + line_scratch(n, (rows, width), p.dtype)
+        + [
+            dma((PlaneGather.sends(g, n) + PlaneScatter.sends(g, n) + 3 * n,)),
+            dma((n,)),
+            dma((n,)),
+            dma((1,)),
+        ]
+        + PlaneGather.scratch(g, n)
+        + PlaneScatter.scratch(g, n, (piece, cols), ((piece, first), (piece, cols - first)), w.dtype),
+        compiler_params=params(ident),
+        name="deliver",
+    )(p, w.reshape(n, g.places, 2, piece, cols))
 
 
 def inverse_rms(values):
@@ -656,7 +915,11 @@
     )
     small_cols = -(-small.shape[1] // 128) * 128
     small = jnp.pad(small, ((0, 0), (0, small_cols - small.shape[1])))
-    small_all = gather_line(reps, shards, small, 1)
+    layout = (q_cols, kv_cols, kv_heads, head_dim)
+    block_tokens, small_all, w_in = collect(
+        reps, shards, tokens, small, w_query, key_weight, value_weight, layout, 1
+    )
+    block_tokens = block_tokens.reshape(shards * length, width)
     router_full = small_all[:, :, :experts].reshape(width, experts)
     gain_one = small_all[:, :, experts].reshape(1, width).astype(f32)
     gain_two = small_all[:, :, experts + 1].reshape(1, width).astype(f32)
@@ -664,22 +927,7 @@
     kgain = small_all[:, :part, experts + 3].reshape(head_dim).astype(f32)
     segment_rows = small_all[:, :length, experts + 4].astype(jnp.int32)
 
-    def by_shard(weight, count):
-        mine = lax.dynamic_slice_in_dim(weight, r * piece, piece, 0)
-        mine = mine.reshape(piece, -1, count)
-        if mine.shape[1] < shards:
-            mine = jnp.repeat(mine, shards // mine.shape[1], axis=1)
-        return mine.transpose(1, 0, 2)
-
-    packed = jnp.concatenate(
-        [by_shard(w_query, q_cols), by_shard(key_weight, kv_cols), by_shard(value_weight, kv_cols)], axis=2
-    )
-    packed = lax.all_to_all(packed, "shard", split_axis=0, concat_axis=0, tiled=True)
-    packed = lax.all_gather(packed, "rep", axis=0)
-    w_in = packed.transpose(1, 0, 2, 3).reshape(width, cols)
-
     cotangents = lax.all_gather(cotangent, ("rep", "shard"), axis=0)
-    block_tokens = gather_line(reps, shards, tokens, 2).reshape(shards * length, width)
 
     wide = block_tokens.astype(f32)
     inverse_one = inverse_rms(wide)
@@ -777,6 +1025,7 @@
     grad_attn = gather_line(reps, shards, grad_resid.astype(bf16), 5).reshape(shards * length, width)
 
     grad_w_out = matmul(attn_out, grad_attn, ((0,), (0,)))
+    owned_out = lax.psum(grad_w_out.astype(bf16), "rep").astype(f32)
     grad_mixed = matmul(grad_attn, w_out, ((1,), (1,))).astype(bf16)
     grad_mixed = grad_mixed.reshape(shards, length, my_kv, group, head_dim)
     grad_weights = jnp.einsum("btkgh,bskh->bkgts", grad_mixed, values, preferred_element_type=f32)
@@ -802,11 +1051,6 @@
     )
     grad_part = matmul(grad_qkv, w_in, ((1,), (1,)))
     grad_attn_gain = jnp.sum(grad_part * normed_one, axis=0)
-    grad_hidden_in = scatter_line(reps, shards, grad_part.astype(bf16).reshape(shards, length, width), 6)
-    own_inverse = inverse_rms(own_tokens)
-    own_normed = own_tokens * own_inverse
-    grad_tokens = grad_resid + norm_back(grad_hidden_in, own_normed, own_inverse, gain_one)
-
     grad_w_in = matmul(hidden_in, grad_qkv, ((0,), (0,)))
 
     def spread(values):
@@ -824,11 +1068,13 @@
     )
     small_grads = jnp.pad(small_grads, ((0, 0), (0, small_cols - small_grads.shape[1])))
     sent = jnp.concatenate([grad_w_in, small_grads], axis=1).astype(bf16)
-    sent = sent.reshape(shards, reps, piece, cols + small_cols).transpose(1, 0, 2, 3)
-    sent = lax.psum_scatter(sent, "rep", scatter_dimension=0, tiled=True)[0]
-    sent = lax.all_to_all(sent, "shard", split_axis=0, concat_axis=0, tiled=True)
-    sent = lax.all_gather(sent, "rep", axis=1, tiled=True)
-    owned_out = lax.psum(grad_w_out.astype(bf16), "rep").astype(f32)
+    sent = sent.reshape(shards, reps, piece, cols + small_cols)
+    grad_part = grad_part.astype(bf16).reshape(shards, length, width)
+    grad_hidden_in, sent = deliver(reps, shards, grad_part, sent, 6)
+    sent = sent.reshape(shards, deep, cols + small_cols)
+    own_inverse = inverse_rms(own_tokens)
+    own_normed = own_tokens * own_inverse
+    grad_tokens = grad_resid + norm_back(grad_hidden_in, own_normed, own_inverse, gain_one)
 
     def joined(values):
         if shared_by > 1:

time: 1020 us -> 938 us (0.920)
  waiting for transfers between devices: 146 us -> 48.5 us
  Pallas kernels: 472 us -> 545 us
  blocking collectives: 39.6 us -> 0 us
  local copies, waits for them, and re-layouts: 77.3 us -> 50.5 us
    pallas_call x0 -> x2, Pallas kernels: none -> 199 us  [the longest x1 119 us: collect(): pl.pallas_call(functools.partial(collect_kernel, reps, shards, layout), o...]
    unnamed x5 -> x2, waiting for transfers between devices: 146 us -> 0.7 us
    pallas_call x2 -> x1, Pallas kernels: 119 us -> 53.4 us  [scatter_line(): pl.pallas_call(functools.partial(scatter_line_kernel, reps, shards), out_...]
    pallas_call x3 -> x1, Pallas kernels: 87 us -> 35.9 us  [gather_line(): pl.pallas_call(functools.partial(gather_line_kernel, reps, shards), out_s...]
    psum x0 -> x1, waiting for transfers between devices: none -> 47.8 us  [local(): owned_out = lax.psum(grad_w_out.astype(bf16), 'rep').astype(f32)]
    all_to_all x2 -> x0, blocking collectives: 39.6 us -> none  [the longest x1 20.6 us: local(): lax.all_to_all(sent, 'shard', split_axis=0, concat_axis=0, tiled=True)]
    unnamed x198 -> x239, local copies, waits for them, and re-layouts: 35.7 us -> 14.2 us
  transfers between devices with their start and end apart: 4 -> 2, of which waited for: 1 -> 1; matrix products, arithmetic and copies ran while one was open for 14% -> 12% of each run, Pallas kernels for 35% -> 28%
where the time goes in v2:
time: 938 us; the launch traced here: 926 us
  Pallas kernels  545 us (58%)
  matrix products  190 us (20%)
  other arithmetic  75.1 us (8%)
  local copies, waits for them, and re-layouts  50.5 us (5%)
  waiting for transfers between devices  48.5 us (5%)
  between operations  16.1 us (2%)
    pallas_call x2, Pallas kernels, scatter_all(): pl.pallas_call(functools.partial(scatter_all_kernel, reps, shards, slabbe...  172 us
    dot_general x19, matrix products, matmul(): return lax.dot_general(a, b, (dims, ((), ())), preferred_element_type=f32)  140 us
    pallas_call x1, Pallas kernels, collect(): pl.pallas_call(functools.partial(collect_kernel, reps, shards, layout), o...  119 us
    pallas_call x1, Pallas kernels, gather_all(): pl.pallas_call(functools.partial(gather_all_kernel, reps, shards), out_sh...  85 us
    pallas_call x1, Pallas kernels, deliver(): pl.pallas_call(functools.partial(deliver_kernel, reps, shards), out_shape...  80.7 us
    pallas_call x1, Pallas kernels, scatter_line(): pl.pallas_call(functools.partial(scatter_line_kernel, reps, shards), out_...  53.4 us
    psum x1, waiting for transfers between devices, local(): owned_out = lax.psum(grad_w_out.astype(bf16), 'rep').astype(f32)  47.8 us
    pallas_call x1, Pallas kernels, gather_line(): pl.pallas_call(functools.partial(gather_line_kernel, reps, shards), out_s...  35.9 us
  transfers between devices with their start and end apart: 2, of which 1 were waited for; matrix products, arithmetic and copies ran while one was open for 12% of the time, Pallas kernels for 28%

profile of v2, /device:TPU:17, one launch (start us, length us, event | category | flops | bytes accessed | tf_op | source)
XLA Modules:
  0.0 926.0 jit_solution(5998400436579937131)
XLA Ops:
  12.9 118.7 %collect.1 = (bf16[4,128,2048]{2,1,0:T(8,128)(2,1)}, bf16[4,512,128]{2,1,0:T(8,128)(2,1)}, bf16[2048,1280]{1,0:T(8,128)(2,1)}) custom-call(bf16[128,2048]{1,0:T(8,128)(2,1)} %x_ref.1, bf16[512,128]{1,0:T(8,128)(2,1)} %pad.32.small_ref, bf16[512,4096]{1,0:T(8,128)(2,1)} %wq_ref.1, bf16[512,512]{1,0:T(8,128)(2,1)} %wk_ref.1, bf16[512,512]{1,0:T(8,128)(2,1)} %wv_ref.1), custom_call_target="tpu_custom_call" | custom-call | tf_op jit(solution)/shard_map/collect/pallas_call | solution.py:571
  131.6 2.1 convert_reduce_fusion
  133.7 2.2 multiply_reduce_fusion.1
  137.1 2.9 fusion.80
  141.1 1.6 convert_reduce_fusion.4
  143.2 1.8 copy.251
  145.0 1.9 copy.204
  147.1 2.9 multiply_reduce_fusion.4
  150.0 1.1 convert_reduce_fusion.3
  158.3 1.5 copy.220
  160.3 1.2 copy.209
  161.5 6.2 convolution_convert_fusion.7
  167.7 53.4 %scatter_line.1 = f32[128,2048]{1,0:T(8,128)} custom-call(bf16[4,128,2048]{2,1,0:T(8,128)(2,1)} %bitcast.333), custom_call_target="tpu_custom_call" | custom-call | tf_op jit(solution)/shard_map/scatter_line/pallas_call | solution.py:468
  221.1 1.6 multiply_reduce_fusion.7
  225.1 85.0 %gather_all.1 = (bf16[32,128,2048]{2,1,0:T(8,128)(2,1)}, f32[32,8,128]{2,1,0:T(8,128)}) custom-call(bf16[128,2048]{1,0:T(8,128)(2,1)} %copy-done.20, f32[32,8,128]{2,1,0:T(8,128)} %broadcast_in_dim.79.slab_ref), custom_call_target="tpu_custom_call" | custom-call | tf_op jit(solution)/shard_map/gather_all/pallas_call | solution.py:631
  311.0 3.9 copy.221
  315.7 8.1 convolution_convert_fusion.5
  323.8 11.2 %fusion.12 = f32[2048,768]{1,0:T(8,128)S(1)} fusion(bf16[2048,2048]{1,0:T(8,128)(2,1)S(1)} %bitcast.306, bf16[1,2048,768]{2,1,0:T(8,128)(2,1)} %param.28), kind=kOutput, calls=%fused_computation.37 | convolution fusion | flops 6442450944 | bytes 17825792 | tf_op jit(solution)/shard_map/dot_general | solution.py:860
  335.1 2.7 copy-done.108
  337.8 9.7 %multiply_convert_fusion.2 = (bf16[2048,768]{1,0:T(8,128)(2,1)}, f32[2048,768]{1,0:T(8,128)}) fusion(f32[2048,768]{1,0:T(8,128)S(1)} %fusion.12, bf16[2048,2048]{1,0:T(8,128)(2,1)S(1)} %bitcast.307, bf16[1,2048,768]{2,1,0:T(8,128)(2,1)S(1)} %copy-done.103), kind=kOutput, calls=%fused_computation.15 | convolution fusion | flops 6451888128 | bytes 27262976 | tf_op jit(solution)/shard_map/dot_general | solution.py:860
  347.4 8.1 convolution_convert_fusion.4
  355.6 14.5 %fusion.1 = (f32[2048]{0:T(1024)S(1)}, bf16[2048,2048]{1,0:T(8,128)(2,1)}) fusion(bf16[32,64,2048]{2,1,0:T(8,128)(2,1)S(1)} %convolution_convert_fusion.4, bf16[2048,768]{1,0:T(8,128)(2,1)} %get-tuple-element.152, bf16[1,768,2048]{2,1,0:T(8,128)(2,1)} %param.30), kind=kOutput, calls=%fused_computation.3 | convolution fusion | flops 6463420416 | bytes 23076864 | tf_op jit(solution)/shard_map/dot_general | solution.py:860
  370.9 8.2 fusion.2
  379.1 15.4 %multiply_convert_fusion = (bf16[2048,768]{1,0:T(8,128)(2,1)}, bf16[2048,768]{1,0:T(8,128)(2,1)S(1)}) fusion(f32[2048,768]{1,0:T(8,128)} %copy-done.108, f32[2048,768]{1,0:T(8,128)} %get-tuple-element.153, bf16[2048,2048]{1,0:T(8,128)(2,1)} %bitcast.315, bf16[1,768,2048]{2,1,0:T(8,128)(2,1)S(1)} %copy-done.101), kind=kOutput, calls=%fused_computation.13 | convolution fusion | flops 6462898176 | bytes 30408704 | tf_op jit(solution)/shard_map/dot_general | solution.py:860
  394.5 9.7 %fusion.10 = f32[2048,2048]{1,0:T(8,128)} fusion(bf16[2048,768]{1,0:T(8,128)(2,1)S(1)} %get-tuple-element.122, bf16[1,2048,768]{2,1,0:T(8,128)(2,1)S(1)} %copy-done.102), kind=kOutput, calls=%fused_computation.35 | convolution fusion | flops 6442450944 | bytes 23068672 | tf_op jit(solution)/shard_map/dot_general | solution.py:860
  404.2 12.6 %add_convert_fusion = bf16[2048,2048]{1,0:T(8,128)(2,1)} fusion(f32[2048,2048]{1,0:T(8,128)} %fusion.10, bf16[2048,768]{1,0:T(8,128)(2,1)S(1)} %copy-done.106, bf16[1,2048,768]{2,1,0:T(8,128)(2,1)S(1)} %copy-done.104), kind=kOutput, calls=%fused_computation.8 | convolution fusion | flops 6450839552 | bytes 31457280 | tf_op jit(solution)/shard_map/dot_general | solution.py:860
  416.9 13.7 %convolution_convert_fusion = bf16[32,128,2048]{2,1,0:T(8,128)(2,1)} fusion(bf16[32,64,2048]{2,1,0:T(8,128)(2,1)} %bitcast.305, f32[32,128]{1,0:T(8,128)S(1)} %fusion.65, pred[32,128]{1,0:T(8,128)(4,1)S(1)} %compare_bitcast_fusion), kind=kOutput, calls=%fused_computation.9 | convolution fusion | flops 1082654720 | bytes 25186304 | tf_op jit(solution)/shard_map/bst,bsd->btd/dot_general | solution.py:1012
  431.2 86.5 %scatter_all.3 = (f32[128,2048]{1,0:T(8,128)}, f32[32,8,128]{2,1,0:T(8,128)}) custom-call(bf16[4,2,4,128,2048]{4,3,2,1,0:T(8,128)(2,1)} %bitcast.299, f32[32,8,128]{2,1,0:T(8,128)} %broadcast_in_dim.132.refs_1_), custom_call_target="tpu_custom_call" | custom-call | tf_op jit(solution)/shard_map/scatter_all/pallas_call | solution.py:699
  518.8 2.4 multiply_reduce_fusion.5
  522.2 1.1 fusion.77.x_ref
  523.3 35.9 %gather_line.1 = bf16[4,128,2048]{2,1,0:T(8,128)(2,1)} custom-call(bf16[128,2048]{1,0:T(8,128)(2,1)} %fusion.77.x_ref), custom_call_target="tpu_custom_call" | custom-call | tf_op jit(solution)/shard_map/gather_line/pallas_call | solution.py:437
  559.2 5.3 fusion.27
  567.1 1.1 bitcast_multiply_fusion.8
  568.3 2.4 bitcast_multiply_fusion.6
  572.4 1.9 multiply_reduce_fusion.8
  574.3 1.1 multiply_convert_fusion.5
  576.2 1.8 slice_negate_fusion
  578.4 2.6 multiply_reduce_fusion.2
  581.8 2.9 copy.216
  584.7 2.0 copy.214
  586.7 2.1 fusion.32
  588.8 1.7 mul.492
  591.9 2.9 fusion.16
  595.0 4.2 multiply_reduce_fusion
  600.5 1.1 pad.35.clone
  601.7 4.5 convolution_convert_fusion.3
  606.2 3.1 pad_maximum_fusion.w_ref
  609.3 80.7 %deliver.1 = (f32[128,2048]{1,0:T(8,128)}, bf16[4,8,64,1408]{3,2,1,0:T(8,128)(2,1)}) custom-call(bf16[4,128,2048]{2,1,0:T(8,128)(2,1)} %bitcast.336, bf16[4,4,2,64,1408]{4,3,2,1,0:T(8,128)(2,1)} %pad_maximum_fusion.w_ref), custom_call_target="tpu_custom_call" | custom-call | tf_op jit(solution)/shard_map/deliver/pallas_call | solution.py:809
  690.0 1.1 convert_reduce_fusion.2
  691.1 6.5 convert_bitcast_fusion
  697.6 2.8 convert_bitcast_fusion.1
  700.4 4.4 convolution_convert_fusion.6
  704.8 12.2 %convolution_bitcast_fusion.2 = f32[1,2048,768]{2,1,0:T(8,128)} fusion(bf16[2048,2048]{1,0:T(8,128)(2,1)} %bitcast.308, bf16[2048,768]{1,0:T(8,128)(2,1)} %copy-done.105), kind=kOutput, calls=%fused_computation.27 | convolution fusion | flops 6442450944 | bytes 17825792 | tf_op jit(solution)/shard_map/dot_general | solution.py:860
  717.4 14.0 %fusion.3 = (bf16[2048,2048]{1,0:T(8,128)(2,1)}, bf16[2048,2048]{1,0:T(8,128)(2,1)}) fusion(bf16[32,64,2048]{2,1,0:T(8,128)(2,1)} %copy-done, f32[2048]{0:T(1024)S(1)} %copy-done.74, bf16[2048,2048]{1,0:T(8,128)(2,1)} %get-tuple-element.155), kind=kLoop, calls=%fused_computation.7 | loop fusion | flops 25165824 | bytes 33562624 | tf_op jit(solution)/shard_map/convert_element_type | solution.py:1001
  731.4 13.7 %convolution_convert_fusion.1 = bf16[32,128,2048]{2,1,0:T(8,128)(2,1)} fusion(bf16[32,64,2048]{2,1,0:T(8,128)(2,1)} %bitcast.301, f32[32,128]{1,0:T(8,128)S(1)} %fusion.65, pred[32,128]{1,0:T(8,128)(4,1)S(1)} %copy-done.51), kind=kOutput, calls=%fused_computation.10 | convolution fusion | flops 1082654720 | bytes 25186304 | tf_op jit(solution)/shard_map/bst,bsd->btd/dot_general | solution.py:1012
  745.1 85.2 %scatter_all.2 = f32[128,2048]{1,0:T(8,128)} custom-call(bf16[4,2,4,128,2048]{4,3,2,1,0:T(8,128)(2,1)} %bitcast.300), custom_call_target="tpu_custom_call" | custom-call | tf_op jit(solution)/shard_map/scatter_all/pallas_call | solution.py:699
  831.4 12.2 %convolution_bitcast_fusion = f32[1,768,2048]{2,1,0:T(8,128)} fusion(bf16[2048,768]{1,0:T(8,128)(2,1)} %get-tuple-element.152, bf16[2048,2048]{1,0:T(8,128)(2,1)} %get-tuple-element.144), kind=kOutput, calls=%fused_computation.25 | convolution fusion | flops 6442450944 | bytes 17825792 | tf_op jit(solution)/shard_map/dot_general | solution.py:860
  843.6 1.7 fusion.36
  846.0 4.3 copy.247
  850.3 1.1 copy.282
  851.4 1.1 copy.281
  853.3 11.0 %convolution_bitcast_fusion.1 = f32[1,2048,768]{2,1,0:T(8,128)} fusion(bf16[2048,2048]{1,0:T(8,128)(2,1)} %bitcast.309, bf16[2048,768]{1,0:T(8,128)(2,1)S(1)} %copy-done.107), kind=kOutput, calls=%fused_computation.26 | convolution fusion | flops 6442450944 | bytes 17825792 | tf_op jit(solution)/shard_map/dot_general | solution.py:860
  864.2 47.8 %all-reduce.9.cloned.1.call-done = bf16[1024,2048]{1,0:T(8,128)(2,1)} async-done(((bf16[1024,2048]{1,0:T(8,128)(2,1)}), bf16[1024,2048]{1,0:T(8,128)(2,1)}) %all-reduce.9.cloned.1.call-update) | async-done | bytes 4194320 | tf_op jit(solution)/shard_map/psum | solution.py:1028
  912.1 6.7 convert_element_type.333
  (320 shorter events, 35.0 us)
Async XLA Ops:
  7.2 340.3 %all-gather.3.cloned.1.call-start = ((), (), s32[]{:S(2)}) async-start(), calls=%async_computation.1 | async-start | bytes 17301504 | tf_op jit(solution)/shard_map/all_gather | solution.py:930
  7.9 904.1 %all-reduce.9.cloned.1.call-start = ((), (), s32[]{:S(2)}) async-start(), calls=%async_computation | async-start | bytes 8388608 | tf_op jit(solution)/shard_map/psum | solution.py:1028
  131.6 4.4 copy-start.17
  140.0 5.0 copy-start.22
  140.1 19.7 %copy-start.52 = (bf16[512,128]{1,0:T(8,128)(2,1)}, bf16[512,128]{1,0:T(8,128)(2,1)S(1)}, u32[]{:S(2)}) copy-start(bf16[512,128]{1,0:T(8,128)(2,1)S(1)} %slice.163) | copy-start | bytes 393220
  141.1 10.8 %copy-start.34 = (f32[4,128,1,128]{1,3,0,2:T(8,128)}, f32[4,128,1,128]{1,3,0,2:T(8,128)S(1)}, u32[]{:S(2)}) copy-start(f32[4,128,1,128]{1,3,0,2:T(8,128)S(1)} %copy.202) | copy-start | bytes 786436
  142.8 9.3 copy-start.85
  145.0 6.3 copy-start.90
  147.0 8.4 copy-start.1
  147.1 167.9 %copy-start.83 = (f32[128]{0:T(128)}, f32[128]{0:T(128)S(1)}, u32[]{:S(2)}) copy-start(f32[128]{0:T(128)S(1)} %reshape.500) | copy-start | bytes 1540
  161.5 6.2 copy-start.48
  167.7 55.8 %copy-start.8 = (bf16[4,512,128]{2,1,0:T(8,128)(2,1)S(1)}, bf16[4,512,128]{2,1,0:T(8,128)(2,1)}, u32[]{:S(2)}) copy-start(bf16[4,512,128]{2,1,0:T(8,128)(2,1)} %get-tuple-element.24) | copy-start | bytes 1572868
  221.1 300.1 %copy-start.59 = (f32[1,4,4,128]{3,1,2,0:T(4,128)}, f32[1,4,4,128]{3,1,2,0:T(4,128)S(1)}, u32[]{:S(2)}) copy-start(f32[1,4,4,128]{3,1,2,0:T(4,128)S(1)} %copy.253) | copy-start | bytes 24580
  223.3 297.9 %copy-start.81 = (f32[128]{0:T(128)}, f32[128]{0:T(128)S(1)}, u32[]{:S(2)}) copy-start(f32[128]{0:T(128)S(1)} %get-tuple-element.165) | copy-start | bytes 1540
  224.3 294.5 %copy-start.72 = (f32[128]{0:T(128)}, f32[128]{0:T(128)S(1)}, u32[]{:S(2)}) copy-start(f32[128]{0:T(128)S(1)} %get-tuple-element.150) | copy-start | bytes 1540
  224.3 294.5 %copy-start.75 = (f32[128]{0:T(128)}, f32[128]{0:T(128)S(1)}, u32[]{:S(2)}) copy-start(f32[128]{0:T(128)S(1)} %fusion.70) | copy-start | bytes 1540
  224.3 294.5 %copy-start.61 = (pred[128,32]{0,1:T(8,128)(4,1)}, pred[128,32]{0,1:T(8,128)(4,1)S(1)}, u32[]{:S(2)}) copy-start(pred[128,32]{0,1:T(8,128)(4,1)S(1)} %fusion.64) | copy-start | bytes 12292
  224.4 294.4 %copy-start.77 = (f32[128]{0:T(128)}, f32[128]{0:T(128)S(1)}, u32[]{:S(2)}) copy-start(f32[128]{0:T(128)S(1)} %fusion.71) | copy-start | bytes 1540
  315.6 101.3 %copy-start.50 = (pred[32,128]{1,0:T(8,128)(4,1)}, pred[32,128]{1,0:T(8,128)(4,1)S(1)}, u32[]{:S(2)}) copy-start(pred[32,128]{1,0:T(8,128)(4,1)S(1)} %compare_bitcast_fusion) | copy-start | bytes 12292
  323.8 11.3 %copy-start.5 = (bf16[32,64,2048]{2,1,0:T(8,128)(2,1)}, bf16[32,64,2048]{2,1,0:T(8,128)(2,1)S(1)}, u32[]{:S(2)}) copy-start(bf16[32,64,2048]{2,1,0:T(8,128)(2,1)S(1)} %convolution_convert_fusion.5) | copy-start | bytes 25165828
  323.8 14.0 %copy-start.103 = (bf16[1,2048,768]{2,1,0:T(8,128)(2,1)S(1)}, bf16[1,2048,768]{2,1,0:T(8,128)(2,1)}, u32[]{:S(2)}) copy-start(bf16[1,2048,768]{2,1,0:T(8,128)(2,1)} %param.29) | copy-start | bytes 9437188
  355.5 14.5 %copy-start = (bf16[32,64,2048]{2,1,0:T(8,128)(2,1)}, bf16[32,64,2048]{2,1,0:T(8,128)(2,1)S(1)}, u32[]{:S(2)}) copy-start(bf16[32,64,2048]{2,1,0:T(8,128)(2,1)S(1)} %convolution_convert_fusion.4) | copy-start | bytes 25165828
  370.9 8.2 copy-start.65
  370.9 8.2 copy-start.101
  379.1 15.4 %copy-start.102 = (bf16[1,2048,768]{2,1,0:T(8,128)(2,1)S(1)}, bf16[1,2048,768]{2,1,0:T(8,128)(2,1)}, u32[]{:S(2)}) copy-start(bf16[1,2048,768]{2,1,0:T(8,128)(2,1)} %param.28) | copy-start | bytes 9437188
  394.5 9.7 %copy-start.105 = (bf16[2048,768]{1,0:T(8,128)(2,1)}, bf16[2048,768]{1,0:T(8,128)(2,1)S(1)}, u32[]{:S(2)}) copy-start(bf16[2048,768]{1,0:T(8,128)(2,1)S(1)} %get-tuple-element.122) | copy-start | bytes 9437188
  394.5 9.7 %copy-start.104 = (bf16[1,2048,768]{2,1,0:T(8,128)(2,1)S(1)}, bf16[1,2048,768]{2,1,0:T(8,128)(2,1)}, u32[]{:S(2)}) copy-start(bf16[1,2048,768]{2,1,0:T(8,128)(2,1)} %param.29) | copy-start | bytes 9437188
  394.5 9.7 %copy-start.106 = (bf16[2048,768]{1,0:T(8,128)(2,1)S(1)}, bf16[2048,768]{1,0:T(8,128)(2,1)}, u32[]{:S(2)}) copy-start(bf16[2048,768]{1,0:T(8,128)(2,1)} %get-tuple-element.121) | copy-start | bytes 9437188
  431.2 87.6 %copy-start.9 = (bf16[4,512,128]{2,1,0:T(8,128)(2,1)S(1)}, bf16[4,512,128]{2,1,0:T(8,128)(2,1)}, u32[]{:S(2)}) copy-start(bf16[4,512,128]{2,1,0:T(8,128)(2,1)} %get-tuple-element.24) | copy-start | bytes 1572868
  517.7 4.5 copy-start.24
  518.7 4.6 copy-start.86
  518.8 4.6 copy-start.92
  521.2 38.0 %copy-start.96 = (f32[128]{0:T(128)}, f32[128]{0:T(128)S(1)}, u32[]{:S(2)}) copy-start(f32[128]{0:T(128)S(1)} %broadcast_multiply_fusion.3) | copy-start | bytes 1540
  559.2 5.7 copy-start.4
  559.2 5.7 copy-start.53
  559.2 5.7 copy-start.58
  559.2 5.7 copy-start.64
  572.3 5.7 copy-start.2
  572.3 5.7 copy-start.32
  588.8 6.1 copy-start.69
  588.8 6.0 slice-start.2
  594.8 4.3 copy-start.45
  594.9 4.2 copy-start.80
  594.9 4.2 copy-start.99
  594.9 4.3 copy-start.98
  594.9 4.5 copy-start.54
  594.9 6.7 copy-start.38
  704.8 12.2 %copy-start.16 = (bf16[128,2048]{1,0:T(8,128)(2,1)S(1)}, bf16[128,2048]{1,0:T(8,128)(2,1)}, u32[]{:S(2)}) copy-start(bf16[128,2048]{1,0:T(8,128)(2,1)} %x_ref.1) | copy-start | bytes 1572868
  704.8 12.2 %copy-start.29 = (f32[128,2048]{1,0:T(8,128)S(1)}, f32[128,2048]{1,0:T(8,128)}, u32[]{:S(2)}) copy-start(f32[128,2048]{1,0:T(8,128)} %get-tuple-element.30) | copy-start | bytes 3145732
  704.8 12.2 %copy-start.68 = (f32[1,4,4,128]{3,1,2,0:T(4,128)S(1)}, f32[1,4,4,128]{3,1,2,0:T(4,128)}, u32[]{:S(2)}) copy-start(f32[1,4,4,128]{3,1,2,0:T(4,128)} %copy-done.67) | copy-start | bytes 24580
  704.8 12.2 %copy-start.94 = (f32[128]{0:T(128)S(1)}, f32[128]{0:T(128)}, u32[]{:S(2)}) copy-start(f32[128]{0:T(128)} %get-tuple-element.164) | copy-start | bytes 1540
  704.8 12.6 %copy-start.74 = (f32[2048]{0:T(1024)S(1)}, f32[2048]{0:T(1024)}, u32[]{:S(2)}) copy-start(f32[2048]{0:T(1024)} %mul.453) | copy-start | bytes 24580
  717.4 14.1 %copy-start.51 = (pred[32,128]{1,0:T(8,128)(4,1)S(1)}, pred[32,128]{1,0:T(8,128)(4,1)}, u32[]{:S(2)}) copy-start(pred[32,128]{1,0:T(8,128)(4,1)} %copy-done.50) | copy-start | bytes 12292
  831.3 14.7 %slice-start = ((s8[8388608]{0:T(1024)(128)(4,1)}), s8[4194304]{0:T(1024)(128)(4,1)S(1)}, s32[]{:S(2)}) async-start(s8[8388608]{0:T(1024)(128)(4,1)} %bitcast.303), calls=%async_computation.2 | async-start | bytes 8388608
  831.3 12.3 %copy-start.11 = (f32[128,2048]{1,0:T(8,128)S(1)}, f32[128,2048]{1,0:T(8,128)}, u32[]{:S(2)}) copy-start(f32[128,2048]{1,0:T(8,128)} %copy-done.10) | copy-start | bytes 3145732
  831.3 12.3 %copy-start.25 = (bf16[128,2048]{1,0:T(8,128)(2,1)S(1)}, bf16[128,2048]{1,0:T(8,128)(2,1)}, u32[]{:S(2)}) copy-start(bf16[128,2048]{1,0:T(8,128)(2,1)} %param.31) | copy-start | bytes 1572868
  831.3 12.3 %copy-start.26 = (f32[128,2048]{1,0:T(8,128)S(1)}, f32[128,2048]{1,0:T(8,128)}, u32[]{:S(2)}) copy-start(f32[128,2048]{1,0:T(8,128)} %scatter_all.2) | copy-start | bytes 3145732
  831.3 12.3 %copy-start.30 = (f32[128,2048]{1,0:T(8,128)S(1)}, f32[128,2048]{1,0:T(8,128)}, u32[]{:S(2)}) copy-start(f32[128,2048]{1,0:T(8,128)} %get-tuple-element.30) | copy-start | bytes 3145732
  831.3 12.3 %copy-start.60 = (f32[1,4,4,128]{3,1,2,0:T(4,128)S(1)}, f32[1,4,4,128]{3,1,2,0:T(4,128)}, u32[]{:S(2)}) copy-start(f32[1,4,4,128]{3,1,2,0:T(4,128)} %copy-done.59) | copy-start | bytes 24580
  831.3 12.3 %copy-start.82 = (f32[128]{0:T(128)S(1)}, f32[128]{0:T(128)}, u32[]{:S(2)}) copy-start(f32[128]{0:T(128)} %copy-done.81) | copy-start | bytes 1540
  831.3 12.3 %copy-start.97 = (f32[128]{0:T(128)S(1)}, f32[128]{0:T(128)}, u32[]{:S(2)}) copy-start(f32[128]{0:T(128)} %copy-done.96) | copy-start | bytes 1540
  831.3 14.7 %slice-start.1 = ((s8[8388608]{0:T(1024)(128)(4,1)}), s8[4194304]{0:T(1024)(128)(4,1)S(1)}, s32[]{:S(2)}) async-start(s8[8388608]{0:T(1024)(128)(4,1)} %bitcast.303), calls=%async_computation.3 | async-start | bytes 8388608
  846.0 4.3 copy-start.28
  846.0 5.4 copy-start.27
  (51 other events, 130.0 us)
Sparse Core Ops, SparseCore 0:
  11.0 139.2 all-gather.2
  831.4 80.6 all-reduce.8

commit v3 on v2

--- a/solution.py
+++ b/solution.py
@@ -415,67 +415,6 @@
 
 def params(ident):
     return pltpu.CompilerParams(collective_id=ident, has_side_effects=True, vmem_limit_bytes=vmem_cap)
-
-
-def gather_line_kernel(reps, shards, x_ref, out_ref, sems, zr, ls):
-    g = Grid(reps, shards).here()
-    s = Sends(sems)
-    keep = pltpu.make_async_copy(x_ref, out_ref.at[g.z], ls.at[0])
-    keep.start()
-    greet_line(g)
-    for turn, zp in enumerate(g.nearest()):
-        dst = out_ref.at[zp]
-        if turn:
-            s.arrived(dst, zr.at[zp], g.device(g.r, zp))
-        pass_along(g, s, zp, dst if turn else x_ref, dst, zr)
-    keep.wait()
-    s.drain()
-
-
-def gather_line(reps, shards, x, ident):
-    dma = pltpu.SemaphoreType.DMA
-    return pl.pallas_call(
-        functools.partial(gather_line_kernel, reps, shards),
-        out_shape=jax.ShapeDtypeStruct((shards,) + x.shape, x.dtype),
-        in_specs=[vmem],
-        out_specs=vmem,
-        scratch_shapes=[dma((2 * shards,)), dma((shards,)), dma((1,))],
-        compiler_params=params(ident),
-        name="gather_line",
-    )(x)
-
-
-def scatter_line_kernel(reps, shards, p_ref, out_ref, own, rl, rr, sl, sr, sems, ls):
-    g = Grid(reps, shards).here()
-    s = Sends(sems)
-    n = g.shards
-    order = g.nearest()[::-1]
-    loads = []
-    for turn in range(n):
-        load = pltpu.make_async_copy(p_ref.at[order[turn]], own.at[turn], ls.at[turn])
-        load.start()
-        loads.append(load)
-    greet_line(g)
-    for turn in range(n):
-        loads[turn].wait()
-        send_line(g, s, order[turn], own.at[turn], out_ref, rl, rr, sl, sr, last=turn == n - 1)
-    s.drain()
-
-
-def scatter_line(reps, shards, p, ident):
-    dma = pltpu.SemaphoreType.DMA
-    _, rows, width = p.shape
-    return pl.pallas_call(
-        functools.partial(scatter_line_kernel, reps, shards),
-        out_shape=jax.ShapeDtypeStruct((rows, width), f32),
-        in_specs=[hbm],
-        out_specs=vmem,
-        scratch_shapes=[pltpu.VMEM(p.shape, p.dtype)]
-        + line_scratch(shards, (rows, width), p.dtype)
-        + [dma((2 * shards,)), dma((shards,))],
-        compiler_params=params(ident),
-        name="scatter_line",
-    )(p)
 
 
 def collect_kernel(reps, shards, layout, x_ref, small_ref, wq_ref, wk_ref, wv_ref, xs_ref, smalls_ref, w_ref, sems, xr, mr, wr, lr, hr, dr, cr, ls):
@@ -826,13 +765,310 @@
     )(p, w.reshape(n, g.places, 2, piece, cols))
 
 
+def turned(x, cosine, sine):
+    return x * cosine + pltpu.roll(x, x.shape[-1] // 2, 1) * sine
+
+
+def mean_last(x):
+    return jnp.sum(x, axis=-1, keepdims=True) * (1.0 / x.shape[-1])
+
+
+def unit_of(x):
+    inverse = lax.rsqrt(mean_last(x * x) + epsilon)
+    return inverse, x * inverse
+
+
+def dot_t(a, b):
+    return lax.dot_general(a, b, (((1,), (1,)), ((), ())), preferred_element_type=f32)
+
+
+def t_dot(a, b):
+    return lax.dot_general(a, b, (((0,), (0,)), ((), ())), preferred_element_type=f32)
+
+
+def softmax_rows(q_rot, k_rot, bias, head_dim):
+    scores = dot_t(q_rot, k_rot) * head_dim ** (-0.5) + bias
+    raised = jnp.exp(scores - jnp.max(scores, axis=-1, keepdims=True))
+    return raised * (1.0 / jnp.sum(raised, axis=-1, keepdims=True))
+
+
+def back_unit(grad_scaled, unit, inverse, gain):
+    gained = grad_scaled * gain
+    return inverse * (gained - unit * mean_last(gained * unit))
+
+
+def attend_block(b, heads, x_ref, w_ref, wo_ref, gain_ref, qg_ref, kg_ref, cos_ref, sin_ref, bias_ref, hid_ref, qkv_ref, att_ref, line):
+    my_heads, my_kv, head_dim = heads
+    x = x_ref[b].astype(f32)
+    _, unit = unit_of(x)
+    hid_ref[b] = (unit * gain_ref[...]).astype(bf16)
+    qkv_ref[b] = jnp.dot(hid_ref[b], w_ref[...], preferred_element_type=f32)
+    cosine, sine, bias = cos_ref[b], sin_ref[b], bias_ref[b]
+    group = my_heads // my_kv
+    for n in range(my_kv):
+        at_k = (my_heads + n) * head_dim
+        at_v = (my_heads + my_kv + n) * head_dim
+        _, k_unit = unit_of(qkv_ref[b, :, at_k : at_k + head_dim])
+        k_rot = turned(k_unit * kg_ref[...], cosine, sine).astype(bf16)
+        values = qkv_ref[b, :, at_v : at_v + head_dim].astype(bf16)
+        for h in range(n * group, (n + 1) * group):
+            span = slice(h * head_dim, (h + 1) * head_dim)
+            _, q_unit = unit_of(qkv_ref[b, :, span])
+            q_rot = turned(q_unit * qg_ref[...], cosine, sine).astype(bf16)
+            probs = softmax_rows(q_rot, k_rot, bias, head_dim)
+            mixed = jnp.dot(probs.astype(bf16), values, preferred_element_type=f32)
+            att_ref[b, :, span] = mixed.astype(bf16)
+    line[...] = jnp.dot(att_ref[b], wo_ref[...], preferred_element_type=f32).astype(bf16)
+
+
+def attend_back_block(b, heads, ga_ref, qkv_ref, wo_ref, qg_ref, kg_ref, cos_ref, sin_ref, bias_ref, gm_ref, gqkv_ref, qsum_ref, ksum_ref):
+    my_heads, my_kv, head_dim = heads
+    gm_ref[...] = dot_t(ga_ref[b], wo_ref[...]).astype(bf16)
+    cosine, sine, bias = cos_ref[b], sin_ref[b], bias_ref[b]
+    group = my_heads // my_kv
+    qg, kg = qg_ref[...], kg_ref[...]
+    for n in range(my_kv):
+        at_k = (my_heads + n) * head_dim
+        at_v = (my_heads + my_kv + n) * head_dim
+        k_inverse, k_unit = unit_of(qkv_ref[b, :, at_k : at_k + head_dim])
+        k_rot = turned(k_unit * kg, cosine, sine).astype(bf16)
+        values = qkv_ref[b, :, at_v : at_v + head_dim].astype(bf16)
+        grad_k = jnp.zeros(k_unit.shape, f32)
+        grad_v = jnp.zeros(k_unit.shape, f32)
+        for h in range(n * group, (n + 1) * group):
+            span = slice(h * head_dim, (h + 1) * head_dim)
+            q_inverse, q_unit = unit_of(qkv_ref[b, :, span])
+            q_rot = turned(q_unit * qg, cosine, sine).astype(bf16)
+            probs = softmax_rows(q_rot, k_rot, bias, head_dim)
+            grad_mixed = gm_ref[:, span]
+            grad_weights = dot_t(grad_mixed, values)
+            centre = jnp.sum(probs * grad_weights, axis=-1, keepdims=True)
+            grad_scores = (probs * (grad_weights - centre) * head_dim ** (-0.5)).astype(bf16)
+            grad_v = grad_v + t_dot(probs.astype(bf16), grad_mixed)
+            grad_k = grad_k + t_dot(grad_scores, q_rot)
+            grad_q = jnp.dot(grad_scores, k_rot, preferred_element_type=f32)
+            grad_q = turned(grad_q, cosine, -sine)
+            qsum_ref[...] += jnp.sum(grad_q * q_unit, axis=0, keepdims=True)
+            gqkv_ref[b, :, span] = back_unit(grad_q, q_unit, q_inverse, qg).astype(bf16)
+        grad_k = turned(grad_k, cosine, -sine)
+        ksum_ref[...] += jnp.sum(grad_k * k_unit, axis=0, keepdims=True)
+        gqkv_ref[b, :, at_k : at_k + head_dim] = back_unit(grad_k, k_unit, k_inverse, kg).astype(bf16)
+        gqkv_ref[b, :, at_v : at_v + head_dim] = grad_v.astype(bf16)
+
+
+class GatherAll:
+    def __init__(self, g, s, x_ref, out_ref, zr, plane_sems):
+        self.g, self.s, self.x_ref, self.out_ref, self.zr = g, s, x_ref, out_ref, zr
+        half = x_ref.shape[0] // 2
+        self.spans = {0: pl.ds(0, half), 1: pl.ds(half, half), None: pl.ds(0, 2 * half)}
+        self.order = g.nearest()
+        self.plane = PlaneGather(g, s, self.view, *plane_sems)
+
+    @staticmethod
+    def scratch(g):
+        dma = pltpu.SemaphoreType.DMA
+        return [dma((g.shards,))] + PlaneGather.scratch(g, g.shards)
+
+    @staticmethod
+    def sends(g):
+        return PlaneGather.sends(g, g.shards) + 2 * g.shards
+
+    def view(self, u, hi, lo, core, part):
+        return self.out_ref.at[self.g.rep_of(hi, lo, core) * self.g.shards + u, self.spans[part]]
+
+    def own(self):
+        g = self.g
+        return self.view(g.z, g.hi, g.lo, g.core, None)
+
+    def line(self, turn):
+        g, zp = self.g, self.order[turn]
+        dst = self.view(zp, g.hi, g.lo, g.core, None)
+        if turn:
+            self.s.arrived(dst, self.zr.at[zp], g.device(g.r, zp))
+        pass_along(g, self.s, zp, dst if turn else self.x_ref, dst, self.zr)
+        self.plane.own(zp, None if turn else lambda part: self.x_ref.at[self.spans[part]])
+
+    def first(self, turn):
+        self.plane.first(self.order[turn])
+
+    def second(self, turn):
+        self.plane.second(self.order[turn])
+
+    def finish(self):
+        for turn in range(self.g.shards):
+            self.plane.from_partner(self.order[turn])
+
+
+class ScatterAll:
+    def __init__(self, g, s, p_ref, out_ref, rl, rr, sl, sr, *plane_refs):
+        self.g, self.s, self.out_ref = g, s, out_ref
+        self.lines = (rl, rr, sl, sr)
+        half = out_ref.shape[0] // 2
+        self.order = g.nearest()[::-1]
+        self.plane = PlaneScatter(
+            g,
+            s,
+            lambda turn, core: p_ref.at[:, core, self.order[turn]],
+            lambda part: (pl.ds(part * half, half),),
+            *plane_refs,
+        )
+
+    @staticmethod
+    def scratch(g, block, dtype):
+        rows, width = block
+        half = (rows // 2, width)
+        return line_scratch(g.shards, block, dtype) + PlaneScatter.scratch(g, g.shards, block, (half, half), dtype)
+
+    @staticmethod
+    def sends(g):
+        return PlaneScatter.sends(g, g.shards) + 2 * g.shards
+
+    def load(self):
+        self.plane.load(self.g.shards)
+
+    def to_partner(self):
+        for turn in range(self.g.shards):
+            self.plane.to_partner(turn)
+
+    def step(self, turn):
+        n = self.g.shards
+        if turn < n:
+            self.plane.a(turn)
+        if 0 <= turn - 1 < n:
+            self.plane.b(turn - 1)
+        if 0 <= turn - 2 < n:
+            t = turn - 2
+            self.plane.c(t)
+            send_line(self.g, self.s, self.order[t], self.plane.mine(t), self.out_ref, *self.lines, last=t == n - 1)
+
+
+def attend_kernel(reps, shards, heads, *refs):
+    (
+        x_ref, w_ref, wo_ref, gain_ref, qg_ref, kg_ref, cos_ref, sin_ref, bias_ref, cot_ref,
+        hid_ref, qkv_ref, att_ref, out_ref, cots_ref,
+        own, rl, rr, sl, sr, sems, keep_sem, *gather_sems,
+    ) = refs
+    g = Grid(reps, shards).here()
+    s = Sends(sems)
+    n = g.shards
+    gather = GatherAll(g, s, cot_ref, cots_ref, gather_sems[0], gather_sems[1:])
+    keep = pltpu.make_async_copy(cot_ref, gather.own(), keep_sem.at[0])
+    keep.start()
+    greet_all(g)
+    gather.line(0)
+    order = g.nearest()[::-1]
+    for turn in range(n):
+        zp = order[turn]
+        attend_block(
+            zp, heads, x_ref, w_ref, wo_ref, gain_ref, qg_ref, kg_ref, cos_ref, sin_ref, bias_ref,
+            hid_ref, qkv_ref, att_ref, own.at[turn],
+        )
+        send_line(g, s, zp, own.at[turn], out_ref, rl, rr, sl, sr, last=turn == n - 1)
+        if turn + 1 < n:
+            gather.line(turn + 1)
+            gather.first(turn)
+        if turn > 0:
+            gather.second(turn - 1)
+    gather.first(n - 1)
+    gather.second(n - 1)
+    gather.finish()
+    keep.wait()
+    s.drain()
+
+
+def attend(reps, shards, heads, x, w, wo, gain, qg, kg, cosine, sine, bias, cot, ident):
+    g = Grid(reps, shards)
+    dma, v = pltpu.SemaphoreType.DMA, pltpu.VMEM
+    n, rows, width = x.shape
+    cols = w.shape[1]
+    return pl.pallas_call(
+        functools.partial(attend_kernel, reps, shards, heads),
+        out_shape=(
+            jax.ShapeDtypeStruct(x.shape, bf16),
+            jax.ShapeDtypeStruct((n, rows, cols), f32),
+            jax.ShapeDtypeStruct((n, rows, wo.shape[0]), bf16),
+            jax.ShapeDtypeStruct((rows, width), f32),
+            jax.ShapeDtypeStruct((g.devices, rows, width), bf16),
+        ),
+        in_specs=[vmem] * 10,
+        out_specs=(vmem, vmem, vmem, vmem, hbm),
+        scratch_shapes=[v((n, rows, width), bf16)]
+        + line_scratch(n, (rows, width), bf16)
+        + [dma((GatherAll.sends(g) + 2 * n,)), dma((1,))]
+        + GatherAll.scratch(g),
+        compiler_params=params(ident),
+        name="attend",
+    )(x, w, wo, gain, qg, kg, cosine, sine, bias, cot)
+
+
+def attend_back_kernel(reps, shards, heads, *refs):
+    (
+        ga_ref, qkv_ref, wo_ref, qg_ref, kg_ref, cos_ref, sin_ref, bias_ref, p_ref,
+        gas_ref, gqkv_ref, qsum_ref, ksum_ref, out_ref,
+        gm, zr, sems, keep_sem, *scatter_refs,
+    ) = refs
+    g = Grid(reps, shards).here()
+    s = Sends(sems)
+    n = g.shards
+    scatter = ScatterAll(g, s, p_ref, out_ref, *scatter_refs)
+    scatter.load()
+    keep = pltpu.make_async_copy(ga_ref, gas_ref.at[g.z], keep_sem.at[0])
+    keep.start()
+    qsum_ref[...] = jnp.zeros(qsum_ref.shape, f32)
+    ksum_ref[...] = jnp.zeros(ksum_ref.shape, f32)
+    greet_all(g)
+    order = g.nearest()
+
+    def line(turn):
+        zp = order[turn]
+        dst = gas_ref.at[zp]
+        if turn:
+            s.arrived(dst, zr.at[zp], g.device(g.r, zp))
+        pass_along(g, s, zp, dst if turn else ga_ref, dst, zr)
+
+    line(0)
+    scatter.to_partner()
+    keep.wait()
+    for turn in range(n):
+        scatter.step(turn)
+        if turn + 1 < n:
+            line(turn + 1)
+        attend_back_block(
+            order[turn], heads, gas_ref, qkv_ref, wo_ref, qg_ref, kg_ref, cos_ref, sin_ref, bias_ref,
+            gm, gqkv_ref, qsum_ref, ksum_ref,
+        )
+    scatter.step(n)
+    scatter.step(n + 1)
+    s.drain()
+
+
+def attend_back(reps, shards, heads, ga, qkv, wo, qg, kg, cosine, sine, bias, p, ident):
+    g = Grid(reps, shards)
+    dma, v = pltpu.SemaphoreType.DMA, pltpu.VMEM
+    n = shards
+    rows, width = ga.shape
+    out_width = p.shape[2]
+    row = jax.ShapeDtypeStruct(qg.shape, f32)
+    return pl.pallas_call(
+        functools.partial(attend_back_kernel, reps, shards, heads),
+        out_shape=(
+            jax.ShapeDtypeStruct((n, rows, width), bf16),
+            jax.ShapeDtypeStruct(qkv.shape, bf16),
+            row,
+            row,
+            jax.ShapeDtypeStruct((rows, out_width), f32),
+        ),
+        in_specs=[vmem] * 8 + [hbm],
+        out_specs=(vmem,) * 5,
+        scratch_shapes=[v((rows, wo.shape[0]), bf16), dma((n,)), dma((ScatterAll.sends(g) + 2 * n,)), dma((1,))]
+        + ScatterAll.scratch(g, (rows, out_width), p.dtype),
+        compiler_params=params(ident),
+        name="attend_back",
+    )(ga, qkv, wo, qg, kg, cosine, sine, bias, p.reshape(g.places, 2, n, rows, out_width))
+
+
 def inverse_rms(values):
     return lax.rsqrt(jnp.mean(values * values, axis=-1, keepdims=True) + epsilon)
-
-
-def rotate(values):
-    half = values.shape[-1] // 2
-    return jnp.concatenate([-values[..., half:], values[..., :half]], axis=-1)
 
 
 def rope_tables(segment_rows, width):
@@ -846,7 +1082,7 @@
     angle = offset[..., None] * frequency[None, None, :]
     cosine, sine = jnp.cos(angle), jnp.sin(angle)
     cosine = jnp.concatenate([cosine, cosine], axis=-1)
-    sine = jnp.concatenate([sine, sine], axis=-1)
+    sine = jnp.concatenate([-sine, sine], axis=-1)
     allowed = same & (places[None, None, :] <= places[None, :, None])
     return cosine, sine, allowed
 
@@ -892,7 +1128,6 @@
     my_heads = heads // shards
     my_kv = max(1, kv_heads // shards)
     shared_by = max(1, shards // kv_heads)
-    group = my_heads // my_kv
     q_cols, kv_cols = my_heads * head_dim, my_kv * head_dim
     cols = q_cols + 2 * kv_cols
     piece = deep // reps
@@ -919,46 +1154,21 @@
     block_tokens, small_all, w_in = collect(
         reps, shards, tokens, small, w_query, key_weight, value_weight, layout, 1
     )
-    block_tokens = block_tokens.reshape(shards * length, width)
     router_full = small_all[:, :, :experts].reshape(width, experts)
     gain_one = small_all[:, :, experts].reshape(1, width).astype(f32)
     gain_two = small_all[:, :, experts + 1].reshape(1, width).astype(f32)
-    qgain = small_all[:, :part, experts + 2].reshape(head_dim).astype(f32)
-    kgain = small_all[:, :part, experts + 3].reshape(head_dim).astype(f32)
+    qgain = small_all[:, :part, experts + 2].reshape(1, head_dim).astype(f32)
+    kgain = small_all[:, :part, experts + 3].reshape(1, head_dim).astype(f32)
     segment_rows = small_all[:, :length, experts + 4].astype(jnp.int32)
 
-    cotangents = lax.all_gather(cotangent, ("rep", "shard"), axis=0)
-
-    wide = block_tokens.astype(f32)
-    inverse_one = inverse_rms(wide)
-    normed_one = wide * inverse_one
-    hidden_in = (normed_one * gain_one).astype(bf16)
-    qkv = matmul(hidden_in, w_in)
-    query_raw = qkv[:, :q_cols].reshape(shards, length, my_heads, head_dim)
-    key_raw = qkv[:, q_cols : q_cols + kv_cols].reshape(shards, length, my_kv, head_dim)
-    values = qkv[:, q_cols + kv_cols :].astype(bf16).reshape(shards, length, my_kv, head_dim)
-    inverse_query = inverse_rms(query_raw)
-    query_unit = query_raw * inverse_query
-    inverse_key = inverse_rms(key_raw)
-    key_unit = key_raw * inverse_key
+    head_sizes = (my_heads, my_kv, head_dim)
     cosine, sine, allowed = rope_tables(segment_rows, head_dim)
-    cosine, sine = cosine[:, :, None, :], sine[:, :, None, :]
-    query_scaled = query_unit * qgain
-    key_scaled = key_unit * kgain
-    query_rot = (query_scaled * cosine + rotate(query_scaled) * sine).astype(bf16)
-    key_rot = (key_scaled * cosine + rotate(key_scaled) * sine).astype(bf16)
-    grouped = query_rot.reshape(shards, length, my_kv, group, head_dim)
-    scores = jnp.einsum("btkgh,bskh->bkgts", grouped, key_rot, preferred_element_type=f32) * head_dim ** (-0.5)
-    scores = jnp.where(allowed[:, None, None], scores, masked_score)
-    highest = jnp.max(scores, axis=-1, keepdims=True)
-    raised = jnp.exp(scores - highest)
-    probs = raised / jnp.sum(raised, axis=-1, keepdims=True)
-    probs_low = probs.astype(bf16)
-    mixed = jnp.einsum("bkgts,bskh->btkgh", probs_low, values, preferred_element_type=f32)
-    attn_out = mixed.reshape(shards * length, q_cols).astype(bf16)
-    projected = matmul(attn_out, w_out).astype(bf16)
+    bias = jnp.where(allowed, 0.0, masked_score)
+    hidden_in, qkv, attn_out, mixed, cotangents = attend(
+        reps, shards, head_sizes, block_tokens, w_in, w_out, gain_one, qgain, kgain, cosine, sine, bias, cotangent, 2
+    )
     own_tokens = tokens.astype(f32)
-    resid = own_tokens + scatter_line(reps, shards, projected.reshape(shards, length, width), 3)
+    resid = own_tokens + mixed
 
     inverse_two = inverse_rms(resid)
     normed_two = resid * inverse_two
@@ -1012,7 +1222,7 @@
         return jnp.einsum("bst,bsd->btd", onehot, values, preferred_element_type=f32).astype(bf16)
 
     grad_hidden, mixes = scatter_wide(reps, shards, combine(grad_in.astype(bf16)), back_mix, 8, chunks)
-    output = (resid + scatter_wide(reps, shards, combine(weighted), None, 16, chunks)).astype(bf16)
+    sums = combine(weighted)
 
     grad_out = cotangent.astype(f32)
     grad_mix = mixes[:, 0, :].T
@@ -1022,33 +1232,22 @@
     grad_ffn_gain = jnp.sum(grad_hidden * normed_two, axis=0)
     grad_resid = grad_out + norm_back(grad_hidden, normed_two, inverse_two, gain_two)
     grad_w_router = matmul(hidden_two, grad_logits, ((0,), (0,)))
-    grad_attn = gather_line(reps, shards, grad_resid.astype(bf16), 5).reshape(shards * length, width)
-
-    grad_w_out = matmul(attn_out, grad_attn, ((0,), (0,)))
+
+    fused = width // chunks
+    grad_attn, grad_qkv, grad_query_gain, grad_key_gain, moe = attend_back(
+        reps, shards, head_sizes, grad_resid.astype(bf16), qkv, w_out, qgain, kgain, cosine, sine, bias,
+        sums[:, :, :fused], 5,
+    )
+    if chunks > 1:
+        rest = scatter_wide(reps, shards, sums[:, :, fused:], None, 16, chunks - 1)
+        moe = jnp.concatenate([moe, rest], axis=1)
+    output = (resid + moe).astype(bf16)
+    grad_attn = grad_attn.reshape(shards * length, width)
+    grad_qkv = grad_qkv.reshape(shards * length, cols)
+    grad_w_out = matmul(attn_out.reshape(shards * length, q_cols), grad_attn, ((0,), (0,)))
     owned_out = lax.psum(grad_w_out.astype(bf16), "rep").astype(f32)
-    grad_mixed = matmul(grad_attn, w_out, ((1,), (1,))).astype(bf16)
-    grad_mixed = grad_mixed.reshape(shards, length, my_kv, group, head_dim)
-    grad_weights = jnp.einsum("btkgh,bskh->bkgts", grad_mixed, values, preferred_element_type=f32)
-    centre = jnp.sum(probs * grad_weights, axis=-1, keepdims=True)
-    grad_scores = (probs * (grad_weights - centre) * head_dim ** (-0.5)).astype(bf16)
-    grad_values = jnp.einsum("bkgts,btkgh->bskh", probs_low, grad_mixed, preferred_element_type=f32)
-    grad_query_rot = jnp.einsum("bkgts,bskh->btkgh", grad_scores, key_rot, preferred_element_type=f32)
-    grad_query_rot = grad_query_rot.reshape(shards, length, my_heads, head_dim)
-    grad_key_rot = jnp.einsum("bkgts,btkgh->bskh", grad_scores, grouped, preferred_element_type=f32)
-    grad_query_scaled = grad_query_rot * cosine - rotate(grad_query_rot * sine)
-    grad_key_scaled = grad_key_rot * cosine - rotate(grad_key_rot * sine)
-    grad_query_gain = jnp.sum(grad_query_scaled * query_unit, axis=(0, 1, 2))
-    grad_key_gain = jnp.sum(grad_key_scaled * key_unit, axis=(0, 1, 2))
-    grad_query = norm_back(grad_query_scaled, query_unit, inverse_query, qgain)
-    grad_key = norm_back(grad_key_scaled, key_unit, inverse_key, kgain)
-    grad_qkv = jnp.concatenate(
-        [
-            grad_query.reshape(shards * length, q_cols).astype(bf16),
-            grad_key.reshape(shards * length, kv_cols).astype(bf16),
-            grad_values.reshape(shards * length, kv_cols).astype(bf16),
-        ],
-        axis=1,
-    )
+    hidden_in = hidden_in.reshape(shards * length, width)
+    _, normed_one = unit_of(block_tokens.reshape(shards * length, width).astype(f32))
     grad_part = matmul(grad_qkv, w_in, ((1,), (1,)))
     grad_attn_gain = jnp.sum(grad_part * normed_one, axis=0)
     grad_w_in = matmul(hidden_in, grad_qkv, ((0,), (0,)))

time: 938 us -> 829 us (0.88)
  waiting for transfers between devices: 48.5 us -> 0.02 us
  local copies, waits for them, and re-layouts: 50.5 us -> 19.9 us
  other arithmetic: 75.1 us -> 55.5 us
  matrix products: 190 us -> 176 us
    pallas_call x2, Pallas kernels: 89.2 us -> 206 us  [the longest x1 107 us: attend(): pl.pallas_call(functools.partial(attend_kernel, reps, shards, heads), out...]
    pallas_call x2 -> x1, Pallas kernels: 172 us -> 86.1 us  [scatter_all(): pl.pallas_call(functools.partial(scatter_all_kernel, reps, shards, slabbe...]
    pallas_call x1, Pallas kernels: 119 us -> 61.1 us  [collect(): pl.pallas_call(functools.partial(collect_kernel, reps, shards, layout), o...]
    psum x1, waiting for transfers between devices: 47.8 us -> 0.01 us  [local(): owned_out = lax.psum(grad_w_out.astype(bf16), 'rep').astype(f32)]
    pallas_call x1, Pallas kernels: 80.7 us -> 105 us  [deliver(): pl.pallas_call(functools.partial(deliver_kernel, reps, shards), out_shape...]
    unnamed x239 -> x65, local copies, waits for them, and re-layouts: 14.2 us -> 2.61 us
    pallas_call x1, Pallas kernels: 85 us -> 96 us  [gather_all(): pl.pallas_call(functools.partial(gather_all_kernel, reps, shards), out_sh...]
    dot_general x19 -> x16, matrix products: 140 us -> 129 us  [matmul(): return lax.dot_general(a, b, (dims, ((), ())), preferred_element_type=f32)]
  transfers between devices with their start and end apart: 2 -> 1, of which waited for: 1 -> 0; matrix products, arithmetic and copies ran while one was open for 12% -> 8% of each run, Pallas kernels for 28% -> 13%
where the time goes in v3:
time: 829 us; the launch traced here: 821 us
  Pallas kernels  554 us (67%)
  matrix products  176 us (21%)
  other arithmetic  55.5 us (7%)
  local copies, waits for them, and re-layouts  19.9 us (2%)
  between operations  15 us (2%)
    dot_general x16, matrix products, matmul(): return lax.dot_general(a, b, (dims, ((), ())), preferred_element_type=f32)  129 us
    pallas_call x1, Pallas kernels, attend(): pl.pallas_call(functools.partial(attend_kernel, reps, shards, heads), out...  107 us
    pallas_call x1, Pallas kernels, deliver(): pl.pallas_call(functools.partial(deliver_kernel, reps, shards), out_shape...  105 us
    pallas_call x1, Pallas kernels, attend_back(): pl.pallas_call(functools.partial(attend_back_kernel, reps, shards, heads)...  98.7 us
    pallas_call x1, Pallas kernels, gather_all(): pl.pallas_call(functools.partial(gather_all_kernel, reps, shards), out_sh...  96 us
    pallas_call x1, Pallas kernels, scatter_all(): pl.pallas_call(functools.partial(scatter_all_kernel, reps, shards, slabbe...  86.1 us
    pallas_call x1, Pallas kernels, collect(): pl.pallas_call(functools.partial(collect_kernel, reps, shards, layout), o...  61.1 us
    dot_general x2, matrix products, combine(): jnp.einsum('bst,bsd->btd', onehot, values, preferred_element_type=f32)  27.3 us
  transfers between devices with their start and end apart: 1, of which 0 were waited for; matrix products, arithmetic and copies ran while one was open for 8% of the time, Pallas kernels for 13%

profile of v3, /device:TPU:17, one launch (start us, length us, event | category | flops | bytes accessed | tf_op | source)
XLA Modules:
  0.0 820.9 jit_solution(13646985732177224020)
XLA Ops:
  7.2 0.7 reshape.272
  7.9 0.7 reshape.273
  8.6 0.7 pad.29
  9.3 0.7 pad.30
  9.9 0.7 convert_bitcast_fusion.3
  10.6 0.8 concatenate.22
  11.5 0.7 pad.32.small_ref
  12.2 61.1 %collect.1 = (bf16[4,128,2048]{2,1,0:T(8,128)(2,1)}, bf16[4,512,128]{2,1,0:T(8,128)(2,1)}, bf16[2048,1280]{1,0:T(8,128)(2,1)}) custom-call(bf16[128,2048]{1,0:T(8,128)(2,1)} %x_ref.1, bf16[512,128]{1,0:T(8,128)(2,1)} %pad.32.small_ref, bf16[512,4096]{1,0:T(8,128)(2,1)} %wq_ref.1, bf16[512,512]{1,0:T(8,128)(2,1)} %wk_ref.1, bf16[512,512]{1,0:T(8,128)(2,1)} %wv_ref.1), custom_call_target="tpu_custom_call" | custom-call | tf_op jit(solution)/shard_map/collect/pallas_call | solution.py:510
  73.4 1.9 convert_reduce_fusion
  75.3 1.0 convert_reduce_fusion.4
  76.4 1.1 convert_reduce_fusion.3
  77.5 0.6 copy.91
  78.1 0.6 reshape.292.refs_4_.refs_3_
  78.7 0.6 reshape.293.refs_5_.refs_4_
  79.6 0.8 fusion.37.refs_8_.refs_7_
  80.4 1.0 fusion.39
  81.4 1.0 pad_maximum_fusion.1
  82.4 107.0 %attend.1 = (bf16[4,128,2048]{2,1,0:T(8,128)(2,1)}, f32[4,128,1280]{2,1,0:T(8,128)}, bf16[4,128,1024]{2,1,0:T(8,128)(2,1)}, f32[128,2048]{1,0:T(8,128)}, bf16[32,128,2048]{2,1,0:T(8,128)(2,1)}) custom-call(bf16[4,128,2048]{2,1,0:T(8,128)(2,1)} %get-tuple-element.33.refs_0_, bf16[2048,1280]{1,0:T(8,128)(2,1)} %get-tuple-element.34.refs_1_, ...), custom_call_target="tpu_custom_call" | custom-call | tf_op jit(solution)/shard_map/attend/pallas_call | solution.py:984
  189.4 2.2 multiply_reduce_fusion.3
  191.8 0.8 copy-done.5
  192.6 1.4 fusion.50
  194.0 0.7 broadcast_in_dim.105.slab_ref
  194.7 96.0 %gather_all.1 = (bf16[32,128,2048]{2,1,0:T(8,128)(2,1)}, f32[32,8,128]{2,1,0:T(8,128)}) custom-call(bf16[128,2048]{1,0:T(8,128)(2,1)} %copy-done.5, f32[32,8,128]{2,1,0:T(8,128)} %broadcast_in_dim.105.slab_ref), custom_call_target="tpu_custom_call" | custom-call | tf_op jit(solution)/shard_map/gather_all/pallas_call | solution.py:570
  290.7 0.9 copy.77
  291.8 11.5 %convolution_convert_fusion.3 = bf16[32,64,2048]{2,1,0:T(8,128)(2,1)} fusion(bf16[32,128,2048]{2,1,0:T(8,128)(2,1)} %get-tuple-element.39, f32[32,128]{1,0:T(8,128)S(1)} %fusion.40, pred[32,128]{1,0:T(8,128)(4,1)S(1)} %compare_bitcast_fusion), kind=kOutput, calls=%fused_computation.20 | convolution fusion | flops 1078460416 | bytes 25186304 | tf_op jit(solution)/shard_map/bst,btd->bsd/dot_general | solution.py:1195
  303.3 8.1 convolution_convert_fusion.4
  311.4 14.7 %fusion.8 = f32[2048,768]{1,0:T(8,128)} fusion(bf16[2048,2048]{1,0:T(8,128)(2,1)} %bitcast.143, bf16[1,2048,768]{2,1,0:T(8,128)(2,1)} %param.28), kind=kOutput, calls=%fused_computation.31 | convolution fusion | flops 6442450944 | bytes 17825792 | tf_op jit(solution)/shard_map/dot_general | solution.py:1096
  326.1 11.6 %multiply_convert_fusion = (bf16[2048,768]{1,0:T(8,128)(2,1)}, f32[2048,768]{1,0:T(8,128)}) fusion(f32[2048,768]{1,0:T(8,128)} %fusion.8, bf16[2048,2048]{1,0:T(8,128)(2,1)S(1)} %bitcast.146, bf16[1,2048,768]{2,1,0:T(8,128)(2,1)S(1)} %copy-done.18), kind=kOutput, calls=%fused_computation.15 | convolution fusion | flops 6451888128 | bytes 27262976 | tf_op jit(solution)/shard_map/dot_general | solution.py:1096
  337.7 11.6 %fusion = (f32[2048]{0:T(1024)S(1)}, bf16[2048,2048]{1,0:T(8,128)(2,1)}) fusion(bf16[32,64,2048]{2,1,0:T(8,128)(2,1)S(1)} %convolution_convert_fusion.4, bf16[2048,768]{1,0:T(8,128)(2,1)} %get-tuple-element.124, bf16[1,768,2048]{2,1,0:T(8,128)(2,1)S(1)} %copy-done.16), kind=kOutput, calls=%fused_computation.2 | convolution fusion | flops 6463420416 | bytes 23076864 | tf_op jit(solution)/shard_map/dot_general | solution.py:1096
  349.4 0.8 select_reduce_fusion
  350.2 8.0 fusion.2
  358.2 14.3 %multiply_convert_fusion.1 = (bf16[2048,768]{1,0:T(8,128)(2,1)S(1)}, bf16[2048,768]{1,0:T(8,128)(2,1)S(1)}) fusion(f32[2048,768]{1,0:T(8,128)} %fusion.8, f32[2048,768]{1,0:T(8,128)} %get-tuple-element.125, bf16[2048,2048]{1,0:T(8,128)(2,1)} %bitcast.151, bf16[1,768,2048]{2,1,0:T(8,128)(2,1)} %param.30), kind=kOutput, calls=%fused_computation.16 | convolution fusion | flops 6462898176 | bytes 30408704 | tf_op jit(solution)/shard_map/dot_general | solution.py:1096
  372.6 9.6 %fusion.6 = f32[2048,2048]{1,0:T(8,128)} fusion(bf16[2048,768]{1,0:T(8,128)(2,1)S(1)} %get-tuple-element.109, bf16[1,2048,768]{2,1,0:T(8,128)(2,1)S(1)} %copy-done.17), kind=kOutput, calls=%fused_computation.29 | convolution fusion | flops 6442450944 | bytes 23068672 | tf_op jit(solution)/shard_map/dot_general | solution.py:1096
  382.2 12.6 %add_convert_fusion = bf16[2048,2048]{1,0:T(8,128)(2,1)} fusion(f32[2048,2048]{1,0:T(8,128)} %fusion.6, bf16[2048,768]{1,0:T(8,128)(2,1)S(1)} %get-tuple-element.108, bf16[1,2048,768]{2,1,0:T(8,128)(2,1)S(1)} %copy-done.19), kind=kOutput, calls=%fused_computation.8 | convolution fusion | flops 6450839552 | bytes 31457280 | tf_op jit(solution)/shard_map/dot_general | solution.py:1096
  394.9 13.6 %convolution_convert_fusion.1 = bf16[32,128,2048]{2,1,0:T(8,128)(2,1)} fusion(bf16[32,64,2048]{2,1,0:T(8,128)(2,1)} %bitcast.142, f32[32,128]{1,0:T(8,128)S(1)} %fusion.40, pred[32,128]{1,0:T(8,128)(4,1)S(1)} %compare_bitcast_fusion), kind=kOutput, calls=%fused_computation.10 | convolution fusion | flops 1082654720 | bytes 25186304 | tf_op jit(solution)/shard_map/bst,bsd->btd/dot_general | solution.py:1222
  408.5 0.7 broadcast_in_dim.110.refs_1_
  409.2 86.1 %scatter_all.1 = (f32[128,2048]{1,0:T(8,128)}, f32[32,8,128]{2,1,0:T(8,128)}) custom-call(bf16[4,2,4,128,2048]{4,3,2,1,0:T(8,128)(2,1)} %bitcast.140, f32[32,8,128]{2,1,0:T(8,128)} %broadcast_in_dim.110.refs_1_), custom_call_target="tpu_custom_call" | custom-call | tf_op jit(solution)/shard_map/scatter_all/pallas_call | solution.py:638
  495.3 0.9 slice.58
  496.3 2.0 multiply_reduce_fusion.1
  498.3 14.4 %fusion.3 = (bf16[2048,2048]{1,0:T(8,128)(2,1)}, bf16[2048,2048]{1,0:T(8,128)(2,1)}) fusion(bf16[32,64,2048]{2,1,0:T(8,128)(2,1)} %copy-done, f32[2048]{0:T(1024)S(1)} %mul.208, bf16[2048,2048]{1,0:T(8,128)(2,1)} %get-tuple-element.127), kind=kLoop, calls=%fused_computation.7 | loop fusion | flops 25165824 | bytes 33562624 | tf_op jit(solution)/shard_map/convert_element_type | solution.py:1211
  512.7 13.7 %convolution_convert_fusion = bf16[32,128,2048]{2,1,0:T(8,128)(2,1)} fusion(bf16[32,64,2048]{2,1,0:T(8,128)(2,1)} %bitcast.141, f32[32,128]{1,0:T(8,128)S(1)} %fusion.40, pred[32,128]{1,0:T(8,128)(4,1)S(1)} %compare_bitcast_fusion), kind=kOutput, calls=%fused_computation.9 | convolution fusion | flops 1082654720 | bytes 25186304 | tf_op jit(solution)/shard_map/bst,bsd->btd/dot_general | solution.py:1222
  526.4 1.1 fusion.49.refs_0_
  527.5 98.7 %attend_back.1 = (bf16[4,128,2048]{2,1,0:T(8,128)(2,1)}, bf16[4,128,1280]{2,1,0:T(8,128)(2,1)}, f32[1,128]{1,0:T(1,128)}, f32[1,128]{1,0:T(1,128)}, f32[128,2048]{1,0:T(8,128)}) custom-call(bf16[128,2048]{1,0:T(8,128)(2,1)} %fusion.49.refs_0_, f32[4,128,1280]{2,1,0:T(8,128)} %get-tuple-element.42.refs_1_, bf16[1024,2048]{1,0:T(8,128)(2,1)} %refs_2_.3, ...), custom_call_target="tpu_custom_call" | custom-call | tf_op jit(solution)/shard_map/attend_back/pallas_call | solution.py:1052
  626.2 6.4 bitcast_convert_fusion.1
  632.6 2.1 multiply_reduce_fusion
  634.9 7.8 fusion.5
  643.5 4.9 bitcast_convert_fusion
  648.4 3.1 pad_maximum_fusion.w_ref
  651.5 105.2 %deliver.1 = (f32[128,2048]{1,0:T(8,128)}, bf16[4,8,64,1408]{3,2,1,0:T(8,128)(2,1)}) custom-call(bf16[4,128,2048]{2,1,0:T(8,128)(2,1)} %bitcast.159, bf16[4,4,2,64,1408]{4,3,2,1,0:T(8,128)(2,1)} %pad_maximum_fusion.w_ref), custom_call_target="tpu_custom_call" | custom-call | tf_op jit(solution)/shard_map/deliver/pallas_call | solution.py:748
  756.8 1.1 convert_reduce_fusion.2
  757.9 3.4 convert_bitcast_fusion
  761.3 2.5 convert_bitcast_fusion.1
  763.8 11.1 %convolution_bitcast_fusion.2 = f32[1,2048,768]{2,1,0:T(8,128)} fusion(bf16[2048,2048]{1,0:T(8,128)(2,1)} %bitcast.144, bf16[2048,768]{1,0:T(8,128)(2,1)S(1)} %copy-done.24), kind=kOutput, calls=%fused_computation.28 | convolution fusion | flops 6442450944 | bytes 17825792 | tf_op jit(solution)/shard_map/dot_general | solution.py:1096
  775.0 0.3 fusion.18
  775.3 1.0 slice_reduce_fusion
  776.3 8.8 %convolution_bitcast_fusion = f32[1,768,2048]{2,1,0:T(8,128)} fusion(bf16[2048,768]{1,0:T(8,128)(2,1)S(1)} %copy-done.22, bf16[2048,2048]{1,0:T(8,128)(2,1)S(1)} %bitcast.150), kind=kOutput, calls=%fused_computation.26 | convolution fusion | flops 6442450944 | bytes 17825792 | tf_op jit(solution)/shard_map/dot_general | solution.py:1096
  785.2 1.7 fusion.21
  786.8 0.7 slice_reduce_fusion.2
  787.5 4.2 copy.88
  791.8 1.1 copy.99
  792.9 1.1 copy.98
  794.0 0.7 copy.84
  794.7 12.1 %convolution_bitcast_fusion.1 = f32[1,2048,768]{2,1,0:T(8,128)} fusion(bf16[2048,2048]{1,0:T(8,128)(2,1)} %bitcast.145, bf16[2048,768]{1,0:T(8,128)(2,1)} %copy-done.25), kind=kOutput, calls=%fused_computation.27 | convolution fusion | flops 6442450944 | bytes 17825792 | tf_op jit(solution)/shard_map/dot_general | solution.py:1096
  806.9 6.7 convert_element_type.240
  (98 shorter events, 2.2 us)
Async XLA Ops:
  7.2 799.7 %all-reduce.9.cloned.1.call-start = ((), (), s32[]{:S(2)}) async-start(), calls=%async_computation | async-start | bytes 8388608 | tf_op jit(solution)/shard_map/psum | solution.py:1248
  75.3 2.2 copy-start.12
  82.4 109.2 %copy-start.14 = (s32[128,8]{0,1:T(8,128)S(1)}, s32[128,8]{0,1:T(8,128)}, u32[]{:S(2)}) copy-start(s32[128,8]{0,1:T(8,128)} %param.18) | copy-start | bytes 12292
  191.8 0.8 copy-start.5
  311.3 26.3 %copy-start = (bf16[32,64,2048]{2,1,0:T(8,128)(2,1)}, bf16[32,64,2048]{2,1,0:T(8,128)(2,1)S(1)}, u32[]{:S(2)}) copy-start(bf16[32,64,2048]{2,1,0:T(8,128)(2,1)S(1)} %convolution_convert_fusion.4) | copy-start | bytes 25165828
  311.4 14.7 %copy-start.1 = (bf16[32,64,2048]{2,1,0:T(8,128)(2,1)S(1)}, bf16[32,64,2048]{2,1,0:T(8,128)(2,1)}, u32[]{:S(2)}) copy-start(bf16[32,64,2048]{2,1,0:T(8,128)(2,1)} %convolution_convert_fusion.3) | copy-start | bytes 25165828
  311.4 14.7 %copy-start.18 = (bf16[1,2048,768]{2,1,0:T(8,128)(2,1)S(1)}, bf16[1,2048,768]{2,1,0:T(8,128)(2,1)}, u32[]{:S(2)}) copy-start(bf16[1,2048,768]{2,1,0:T(8,128)(2,1)} %param.29) | copy-start | bytes 9437188
  326.1 11.6 %copy-start.16 = (bf16[1,768,2048]{2,1,0:T(8,128)(2,1)S(1)}, bf16[1,768,2048]{2,1,0:T(8,128)(2,1)}, u32[]{:S(2)}) copy-start(bf16[1,768,2048]{2,1,0:T(8,128)(2,1)} %param.30) | copy-start | bytes 9437188
  358.2 14.4 %copy-start.17 = (bf16[1,2048,768]{2,1,0:T(8,128)(2,1)S(1)}, bf16[1,2048,768]{2,1,0:T(8,128)(2,1)}, u32[]{:S(2)}) copy-start(bf16[1,2048,768]{2,1,0:T(8,128)(2,1)} %param.28) | copy-start | bytes 9437188
  372.6 9.6 %copy-start.23 = (bf16[2048,768]{1,0:T(8,128)(2,1)}, bf16[2048,768]{1,0:T(8,128)(2,1)S(1)}, u32[]{:S(2)}) copy-start(bf16[2048,768]{1,0:T(8,128)(2,1)S(1)} %get-tuple-element.109) | copy-start | bytes 9437188
  372.6 9.6 %copy-start.25 = (bf16[2048,768]{1,0:T(8,128)(2,1)}, bf16[2048,768]{1,0:T(8,128)(2,1)S(1)}, u32[]{:S(2)}) copy-start(bf16[2048,768]{1,0:T(8,128)(2,1)S(1)} %get-tuple-element.108) | copy-start | bytes 9437188
  372.6 9.6 %copy-start.19 = (bf16[1,2048,768]{2,1,0:T(8,128)(2,1)S(1)}, bf16[1,2048,768]{2,1,0:T(8,128)(2,1)}, u32[]{:S(2)}) copy-start(bf16[1,2048,768]{2,1,0:T(8,128)(2,1)} %param.29) | copy-start | bytes 9437188
  498.3 28.1 %copy-start.2 = (f32[128,2048]{1,0:T(8,128)}, f32[128,2048]{1,0:T(8,128)S(1)}, u32[]{:S(2)}) copy-start(f32[128,2048]{1,0:T(8,128)S(1)} %get-tuple-element.128) | copy-start | bytes 3145732
  512.7 13.7 %copy-start.7 = (bf16[128,2048]{1,0:T(8,128)(2,1)S(1)}, bf16[128,2048]{1,0:T(8,128)(2,1)}, u32[]{:S(2)}) copy-start(bf16[128,2048]{1,0:T(8,128)(2,1)} %refs_9_.1) | copy-start | bytes 1572868
  626.2 8.5 %copy-start.6 = (bf16[128,2048]{1,0:T(8,128)(2,1)S(1)}, bf16[128,2048]{1,0:T(8,128)(2,1)}, u32[]{:S(2)}) copy-start(bf16[128,2048]{1,0:T(8,128)(2,1)} %copy-done.5) | copy-start | bytes 1572868
  634.9 7.8 copy-start.21
  634.9 7.9 copy-start.20
  757.9 5.9 copy-start.24
  761.3 15.0 %slice-start = ((s8[8388608]{0:T(1024)(128)(4,1)}), s8[4194304]{0:T(1024)(128)(4,1)S(1)}, s32[]{:S(2)}) async-start(s8[8388608]{0:T(1024)(128)(4,1)} %bitcast.149), calls=%async_computation.1 | async-start | bytes 8388608
  763.8 11.2 %copy-start.13 = (f32[4,512]{1,0:T(4,128)S(1)}, f32[4,512]{1,0:T(4,128)}, u32[]{:S(2)}) copy-start(f32[4,512]{1,0:T(4,128)} %copy-done.12) | copy-start | bytes 24580
  763.8 11.2 %copy-start.15 = (f32[128]{0:T(128)S(1)}, f32[128]{0:T(128)}, u32[]{:S(2)}) copy-start(f32[128]{0:T(128)} %get-tuple-element.116) | copy-start | bytes 1540
  763.8 11.2 %copy-start.4 = (bf16[128,2048]{1,0:T(8,128)(2,1)S(1)}, bf16[128,2048]{1,0:T(8,128)(2,1)}, u32[]{:S(2)}) copy-start(bf16[128,2048]{1,0:T(8,128)(2,1)} %x_ref.1) | copy-start | bytes 1572868
  763.8 11.2 %copy-start.10 = (f32[128,2048]{1,0:T(8,128)S(1)}, f32[128,2048]{1,0:T(8,128)}, u32[]{:S(2)}) copy-start(f32[128,2048]{1,0:T(8,128)} %get-tuple-element.48) | copy-start | bytes 3145732
  763.8 12.5 %slice-start.1 = ((s8[8388608]{0:T(1024)(128)(4,1)}), s8[4194304]{0:T(1024)(128)(4,1)S(1)}, s32[]{:S(2)}) async-start(s8[8388608]{0:T(1024)(128)(4,1)} %bitcast.149), calls=%async_computation.2 | async-start | bytes 8388608
  763.8 12.5 %copy-start.22 = (bf16[2048,768]{1,0:T(8,128)(2,1)S(1)}, bf16[2048,768]{1,0:T(8,128)(2,1)}, u32[]{:S(2)}) copy-start(bf16[2048,768]{1,0:T(8,128)(2,1)} %get-tuple-element.124) | copy-start | bytes 9437188
  776.3 8.9 %copy-start.3 = (f32[128,2048]{1,0:T(8,128)S(1)}, f32[128,2048]{1,0:T(8,128)}, u32[]{:S(2)}) copy-start(f32[128,2048]{1,0:T(8,128)} %copy-done.2) | copy-start | bytes 3145732
  776.3 8.9 %copy-start.8 = (bf16[128,2048]{1,0:T(8,128)(2,1)S(1)}, bf16[128,2048]{1,0:T(8,128)(2,1)}, u32[]{:S(2)}) copy-start(bf16[128,2048]{1,0:T(8,128)(2,1)} %refs_9_.1) | copy-start | bytes 1572868
  776.3 8.8 %copy-start.11 = (f32[128,2048]{1,0:T(8,128)S(1)}, f32[128,2048]{1,0:T(8,128)}, u32[]{:S(2)}) copy-start(f32[128,2048]{1,0:T(8,128)} %get-tuple-element.43) | copy-start | bytes 3145732
  787.5 4.2 copy-start.9
Sparse Core Ops, SparseCore 0:
  632.7 112.9 all-reduce.8

commit v4 on v3

--- a/solution.py
+++ b/solution.py
@@ -54,57 +54,47 @@
 
 class Sends:
     def __init__(self, sems):
-        self.sems, self.used, self.open = sems, 0, []
-
-    def start(self, src, dst, recv, device, when=None):
-        copy = pltpu.make_async_remote_copy(
+        self.sems, self.used, self.open, self.samples = sems, 0, [], []
+
+    def copy(self, src, dst, sem, recv, device):
+        return pltpu.make_async_remote_copy(
             src_ref=src,
             dst_ref=dst,
-            send_sem=self.sems.at[self.used],
+            send_sem=self.sems.at[sem],
             recv_sem=recv,
             device_id=device,
             device_id_type=pl.DeviceIdType.MESH,
         )
+
+    def start(self, src, dst, recv, device, when=None):
+        copy = self.copy(src, dst, self.used, recv, device)
+        sample = src
+        for other in self.samples:
+            if other.shape == src.shape:
+                sample = other
+        self.open.append((self.used, sample, when))
         self.used += 1
-        self.open.append((copy, when))
         if when is None:
             copy.start()
         else:
-            pl.when(when)(copy.start)
+            pl.when(when())(copy.start)
 
     def arrived(self, dst, recv, device, when=None):
-        copy = pltpu.make_async_remote_copy(
-            src_ref=dst,
-            dst_ref=dst,
-            send_sem=self.sems.at[0],
-            recv_sem=recv,
-            device_id=device,
-            device_id_type=pl.DeviceIdType.MESH,
-        )
+        copy = self.copy(dst, dst, 0, recv, device)
         if when is None:
             copy.wait_recv()
         else:
-            pl.when(when)(copy.wait_recv)
+            pl.when(when())(copy.wait_recv)
 
     def drain(self):
-        for copy, when in self.open:
+        here = {"rep": lax.axis_index("rep"), "shard": lax.axis_index("shard")}
+        for sem, sample, when in self.open:
+            copy = self.copy(sample, sample, sem, self.sems.at[sem], here)
             if when is None:
                 copy.wait_send()
             else:
-                pl.when(when)(copy.wait_send)
+                pl.when(when())(copy.wait_send)
         self.open = []
-
-
-def greet_line(g):
-    barrier = pltpu.get_barrier_semaphore()
-    for step in range(1, g.shards):
-        pl.semaphore_signal(
-            barrier,
-            inc=1,
-            device_id=g.device(g.r, (g.z + step) % g.shards),
-            device_id_type=pl.DeviceIdType.MESH,
-        )
-    pl.semaphore_wait(barrier, g.shards - 1)
 
 
 def greet_all(g):
@@ -364,8 +354,8 @@
 def pass_along(g, s, zp, src, dst, zr):
     n = g.shards
     right, left = g.device(g.r, jnp.minimum(g.z + 1, n - 1)), g.device(g.r, jnp.maximum(g.z - 1, 0))
-    s.start(src, dst, zr.at[zp], right, (zp <= g.z) & (g.z + 1 < n))
-    s.start(src, dst, zr.at[zp], left, (zp >= g.z) & (g.z > 0))
+    s.start(src, dst, zr.at[zp], right, lambda: (zp <= g.z) & (g.z + 1 < n))
+    s.start(src, dst, zr.at[zp], left, lambda: (zp >= g.z) & (g.z > 0))
 
 
 def send_line(g, s, zp, line, out_ref, rl, rr, sl, sr, last):
@@ -373,8 +363,8 @@
     left, right = g.device(g.r, jnp.maximum(g.z - 1, 0)), g.device(g.r, jnp.minimum(g.z + 1, n - 1))
     has_left, has_right = g.z > 0, g.z + 1 < n
     if last:
-        s.arrived(rl.at[g.z], sl.at[g.z], left, has_left)
-        s.arrived(rr.at[g.z], sr.at[g.z], right, has_right)
+        s.arrived(rl.at[g.z], sl.at[g.z], left, lambda: g.z > 0)
+        s.arrived(rr.at[g.z], sr.at[g.z], right, lambda: g.z + 1 < n)
 
         @pl.when(has_left & has_right)
         def _():
@@ -400,13 +390,18 @@
             s.arrived(rr.at[zp], sr.at[zp], right)
             add_rows(line, line, rr.at[zp])
 
-        s.start(line, rl.at[zp], sl.at[zp], right, onward_right)
-        s.start(line, rr.at[zp], sr.at[zp], left, onward_left)
+        s.start(line, rl.at[zp], sl.at[zp], right, lambda: zp > g.z)
+        s.start(line, rr.at[zp], sr.at[zp], left, lambda: zp < g.z)
 
 
 def line_scratch(shards, block, dtype):
     v, dma = pltpu.VMEM, pltpu.SemaphoreType.DMA
     return [v((shards,) + block, dtype), v((shards,) + block, dtype), dma((shards,)), dma((shards,))]
+
+
+def wait_for(copies, k):
+    for copy in copies(k):
+        copy.wait()
 
 
 hbm = pl.BlockSpec(memory_space=pl.ANY)
@@ -524,143 +519,137 @@
     )(x, small, wq, wk, wv)
 
 
-def gather_all_kernel(reps, shards, x_ref, slab_ref, out_ref, slabs_ref, sems, zr, ps, pr, ls, lr, hr, dr, cr):
+def scatter_all_kernel(reps, shards, slabbed, *refs):
+    if slabbed:
+        (
+            p_ref, slab_ref, x_ref, c_ref, gg_ref, gu_ref, act_ref, out_ref, slabs_ref, wg_ref, wu_ref, wd_ref,
+            xt, ct, og, ou, od, tile_sems, out_sems, *rest,
+        ) = refs
+    else:
+        p_ref, out_ref, *rest = refs
+    sems, ps, pr, slab_sem, *rest = rest
     g = Grid(reps, shards).here()
     s = Sends(sems)
-    half = x_ref.shape[0] // 2
     n = g.shards
-    spans = {0: pl.ds(0, half), 1: pl.ds(half, half), None: pl.ds(0, 2 * half)}
-    order = g.nearest()
-
-    def view(u, hi, lo, core, part):
-        return out_ref.at[g.rep_of(hi, lo, core) * n + u, spans[part]]
-
-    plane = PlaneGather(g, s, view, lr, hr, dr, cr)
-    keep = pltpu.make_async_copy(x_ref, view(g.z, g.hi, g.lo, g.core, None), ls.at[0])
-    keep.start()
+    scatter = ScatterAll(g, s, p_ref, out_ref, *rest)
+    half = pl.ds(0, out_ref.shape[0] // 2)
+    own = scatter.plane.owned
+    s.samples = [own.at[0, 0], own.at[0, 0, half], own.at[0, pl.ds(0, g.los), half]]
+    scatter.load()
+    if not slabbed:
+        greet_all(g)
+        scatter.to_partner()
+        for turn in range(n + 2):
+            scatter.step(turn)
+        s.drain()
+        return
+
+    tile = xt.shape[2]
+    tiles = x_ref.shape[1] // tile
+
+    def tile_in(j, slot):
+        span = pl.ds(pl.multiple_of(j * tile, tile), tile)
+        return [
+            pltpu.make_async_copy(x_ref.at[:, span], xt.at[slot], tile_sems.at[slot, 0]),
+            pltpu.make_async_copy(c_ref.at[:, span], ct.at[slot], tile_sems.at[slot, 1]),
+        ]
+
+    def tile_out(j):
+        span = pl.ds(pl.multiple_of(j * tile, tile), tile)
+        return [
+            pltpu.make_async_copy(og, wg_ref.at[span, :], out_sems.at[0]),
+            pltpu.make_async_copy(ou, wu_ref.at[span, :], out_sems.at[1]),
+            pltpu.make_async_copy(od, wd_ref.at[:, span], out_sems.at[2]),
+        ]
+
+    for copy in tile_in(0, 0):
+        copy.start()
     greet_all(g)
+    scatter.to_partner()
     push_rows(g, slab_ref, slabs_ref, ps, pr)
     me = g.r * n + g.z
-    keep_slab = pltpu.make_async_copy(slab_ref.at[me], slabs_ref.at[me], ls.at[1])
+    keep_slab = pltpu.make_async_copy(slab_ref.at[me], slabs_ref.at[me], slab_sem.at[0])
     keep_slab.start()
-    for turn in range(n + 2):
-        if turn < n:
-            zp = order[turn]
-            dst = view(zp, g.hi, g.lo, g.core, None)
-            if turn:
-                s.arrived(dst, zr.at[zp], g.device(g.r, zp))
-            pass_along(g, s, zp, dst if turn else x_ref, dst, zr)
-            plane.own(zp, None if turn else lambda part: x_ref.at[spans[part]])
-        if 0 <= turn - 1 < n:
-            plane.first(order[turn - 1])
-        if 0 <= turn - 2 < n:
-            plane.second(order[turn - 2])
-    for turn in range(n):
-        plane.from_partner(order[turn])
-    keep.wait()
+
+    def next_tiles(j):
+        for copy in tile_in(j + 1, (j + 1) % 2):
+            copy.start()
+
+    def weight_grads(j, carry):
+        for turn in range(n):
+            pl.when(j == turn * tiles // n)(functools.partial(scatter.step, turn))
+        pl.when(j + 1 < tiles)(functools.partial(next_tiles, j))
+        slot = j % 2
+        for copy in tile_in(j, slot):
+            copy.wait()
+        pl.when(j > 0)(functools.partial(wait_for, tile_out, j))
+        og[...] = t_dot(xt[slot], gg_ref[...])
+        ou[...] = t_dot(xt[slot], gu_ref[...])
+        od[...] = t_dot(act_ref[...], ct[slot])
+        for copy in tile_out(j):
+            copy.start()
+        return carry
+
+    lax.fori_loop(0, tiles, weight_grads, 0)
+    scatter.step(n)
+    scatter.step(n + 1)
+    wait_for(tile_out, 0)
     keep_slab.wait()
     push_wait(g, slab_ref, slabs_ref, ps, pr)
     s.drain()
 
 
-def gather_all(reps, shards, x, slab, ident):
-    g = Grid(reps, shards)
-    dma = pltpu.SemaphoreType.DMA
-    n = shards
-    return pl.pallas_call(
-        functools.partial(gather_all_kernel, reps, shards),
-        out_shape=(
-            jax.ShapeDtypeStruct((g.devices,) + x.shape, x.dtype),
-            jax.ShapeDtypeStruct(slab.shape, slab.dtype),
-        ),
-        in_specs=[vmem, vmem],
-        out_specs=(hbm, vmem),
-        scratch_shapes=[
-            dma((PlaneGather.sends(g, n) + 2 * n,)),
-            dma((n,)),
-            dma((g.devices,)),
-            dma((g.devices,)),
-            dma((2,)),
-        ]
-        + PlaneGather.scratch(g, n),
-        compiler_params=params(ident),
-        name="gather_all",
-    )(x, slab)
-
-
-def scatter_all_kernel(reps, shards, slabbed, *refs):
-    if slabbed:
-        p_ref, slab_ref, out_ref, slabs_ref, *rest = refs
-    else:
-        p_ref, out_ref, *rest = refs
-    rl, rr, sl, sr, sems, ps, pr, slab_sem, *rest = rest
-    g = Grid(reps, shards).here()
-    s = Sends(sems)
-    n = g.shards
-    half = out_ref.shape[0] // 2
-    order = g.nearest()[::-1]
-    plane = PlaneScatter(
-        g, s, lambda turn, core: p_ref.at[:, core, order[turn]], lambda part: (pl.ds(part * half, half),), *rest
-    )
-    plane.load(n)
-    greet_all(g)
-    for turn in range(n):
-        plane.to_partner(turn)
-    if slabbed:
-        push_rows(g, slab_ref, slabs_ref, ps, pr)
-        me = g.r * n + g.z
-        keep_slab = pltpu.make_async_copy(slab_ref.at[me], slabs_ref.at[me], slab_sem.at[0])
-        keep_slab.start()
-    for turn in range(n + 2):
-        if turn < n:
-            plane.a(turn)
-        if 0 <= turn - 1 < n:
-            plane.b(turn - 1)
-        if 0 <= turn - 2 < n:
-            plane.c(turn - 2)
-            send_line(g, s, order[turn - 2], plane.mine(turn - 2), out_ref, rl, rr, sl, sr, last=turn - 2 == n - 1)
-    if slabbed:
-        keep_slab.wait()
-        push_wait(g, slab_ref, slabs_ref, ps, pr)
-    s.drain()
-
-
-def scatter_all(reps, shards, p, slab, ident):
+def scatter_all(reps, shards, p, slab, fill, ident):
     g = Grid(reps, shards)
     n = shards
     _, rows, width = p.shape
-    half = rows // 2
-    dma = pltpu.SemaphoreType.DMA
+    dma, v = pltpu.SemaphoreType.DMA, pltpu.VMEM
     slabbed = slab is not None
     out_shape = (jax.ShapeDtypeStruct((rows, width), f32),)
+    out_specs, in_specs, extra, scratch = (vmem,), [hbm], [], []
     if slabbed:
-        out_shape += (jax.ShapeDtypeStruct(slab.shape, slab.dtype),)
+        x, c, gg, gu, act = fill
+        count, wide = x.shape
+        inner = gg.shape[1]
+        tile = 256
+        narrow = jax.ShapeDtypeStruct((wide, inner), f32)
+        out_shape += (
+            jax.ShapeDtypeStruct(slab.shape, slab.dtype), narrow, narrow, jax.ShapeDtypeStruct((inner, wide), f32)
+        )
+        out_specs += (vmem, hbm, hbm, hbm)
+        in_specs += [vmem, hbm, hbm, vmem, vmem, vmem]
+        extra = [slab, *fill]
+        scratch = [
+            v((2, count, tile), bf16), v((2, count, tile), bf16),
+            v((tile, inner), f32), v((tile, inner), f32), v((inner, tile), f32),
+            dma((2, 2)), dma((3,)),
+        ]
     done = pl.pallas_call(
         functools.partial(scatter_all_kernel, reps, shards, slabbed),
         out_shape=out_shape,
-        in_specs=[hbm] + [vmem] * slabbed,
-        out_specs=(vmem,) * len(out_shape),
-        scratch_shapes=line_scratch(n, (rows, width), p.dtype)
-        + [dma((PlaneScatter.sends(g, n) + 2 * n,)), dma((g.devices,)), dma((g.devices,)), dma((1,))]
-        + PlaneScatter.scratch(g, n, (rows, width), ((half, width), (half, width)), p.dtype),
+        in_specs=in_specs,
+        out_specs=out_specs,
+        scratch_shapes=scratch
+        + [dma((ScatterAll.sends(g),)), dma((g.devices,)), dma((g.devices,)), dma((1,))]
+        + ScatterAll.scratch(g, (rows, width), p.dtype),
         compiler_params=params(ident),
         name="scatter_all",
-    )(p.reshape(g.places, 2, n, rows, width), *([slab] if slabbed else []))
+    )(p.reshape(g.places, 2, n, rows, width), *extra)
     return done if slabbed else done[0]
 
 
-def scatter_wide(reps, shards, p, slab, ident, chunks):
+def scatter_wide(reps, shards, p, slab, fill, ident, chunks):
     if chunks == 1:
-        return scatter_all(reps, shards, p, slab, ident)
+        return scatter_all(reps, shards, p, slab, fill, ident)
     step = p.shape[2] // chunks
     parts = [
-        scatter_all(reps, shards, p[:, :, i * step : (i + 1) * step], slab if i == 0 else None, ident + i)
+        scatter_all(reps, shards, p[:, :, i * step : (i + 1) * step], slab if i == 0 else None, fill, ident + i)
         for i in range(chunks)
     ]
     if slab is None:
         return jnp.concatenate(parts, axis=1)
-    first, slabs = parts[0]
-    return jnp.concatenate([first] + parts[1:], axis=1), slabs
+    first, *others = parts[0]
+    return jnp.concatenate([first] + parts[1:], axis=1), *others
 
 
 def deliver_kernel(reps, shards, p_ref, w_ref, out_ref, ws_ref, line_own, rl, rr, sl, sr, sems, line_loads, wr, keep_sem, *rest):
@@ -704,7 +693,7 @@
         dst = ws_ref.at[g.z, g.r]
         keep = pltpu.make_async_copy(scatter.mine(turn), dst, keep_sem.at[0])
         pl.when(g.z == turn)(keep.start)
-        s.start(scatter.mine(turn), dst, wr.at[g.z], g.device(g.r, turn), g.z != turn)
+        s.start(scatter.mine(turn), dst, wr.at[g.z], g.device(g.r, turn), lambda: g.z != turn)
         pl.when(g.z == turn)(keep.wait)
 
     line(0)
@@ -1065,6 +1054,225 @@
         compiler_params=params(ident),
         name="attend_back",
     )(ga, qkv, wo, qg, kg, cosine, sine, bias, p.reshape(g.places, 2, n, rows, out_width))
+
+
+def slots_of(slab, capacity):
+    length = slab.shape[1]
+    member = slab >= 0.0
+    earlier = lax.broadcasted_iota(jnp.int32, (length, length), 0) < lax.broadcasted_iota(jnp.int32, (length, length), 1)
+    ones = jnp.where(member, 1.0, 0.0).astype(bf16)
+    slot = jnp.dot(ones, jnp.where(earlier, 1.0, 0.0).astype(bf16), preferred_element_type=f32)
+    slot = jnp.where(member, slot, -1.0)[0:1]
+    rows = lax.broadcasted_iota(jnp.int32, (capacity, length), 0).astype(f32)
+    return jnp.where(rows == slot, 1.0, 0.0), slab[0:1]
+
+
+def experts_kernel(reps, shards, capacity, held, *refs):
+    (
+        x_ref, slab_ref, cots_ref, wg_ref, wu_ref, wd_ref,
+        back_ref, sums_ref, grads_ref, rows_ref, cs_ref, gg_ref, gu_ref, act_ref, all_ref,
+        slabs, cot_buf, hid_buf, d_ref, x_buf, c_buf, gg_buf, gu_buf, act_buf, sum_buf, grad_buf,
+        sems, ps, pr, ls, cot_sem, hid_sem, out_sems, zr, *plane_sems,
+    ) = refs
+    g = Grid(reps, shards).here()
+    s = Sends(sems)
+    n, places = g.shards, g.places
+    length = x_ref.shape[0]
+    hidden = hid_buf if held else all_ref
+    s.samples = [x_ref, x_ref.at[pl.ds(0, length // 2)]]
+    gather = GatherAll(g, s, x_ref, hidden, zr, plane_sems)
+    order = gather.order
+    groups = 2 * n
+
+    def which(k):
+        return jnp.where(k % 2 == 0, g.core, 1 - g.core), pick(k // 2, order)
+
+    def cot_load(k, slot):
+        core, zp = which(k)
+        return pltpu.make_async_copy(cots_ref.at[:, core, zp], cot_buf.at[slot], cot_sem.at[slot])
+
+    def onehots(k):
+        core, zp = which(k)
+        return [slots_of(slabs[(q * 2 + core) * n + zp], capacity) for q in range(places)]
+
+    keep = pltpu.make_async_copy(x_ref, gather.own(), ls.at[0])
+    keep.start()
+    cot_load(0, 0).start()
+    greet_all(g)
+    push_rows(g, slab_ref, slabs, ps, pr)
+    me = g.r * n + g.z
+    keep_slab = pltpu.make_async_copy(slab_ref.at[me], slabs.at[me], ls.at[1])
+    keep_slab.start()
+    gather.line(0)
+    keep_slab.wait()
+    push_wait(g, slab_ref, slabs, ps, pr)
+    keep.wait()
+
+    def turns(k, steps):
+        for at, step in steps:
+            pl.when(k == at)(step)
+
+    def both(*fs):
+        def run():
+            for f, turn in fs:
+                f(turn)
+
+        return run
+
+    early = [(2, both((gather.first, 0))), (4, both((gather.line, 1), (gather.second, 0))), (6, both((gather.first, 1)))]
+
+    def outs(k):
+        return [
+            pltpu.make_async_copy(x_buf, rows_ref.at[k], out_sems.at[0]),
+            pltpu.make_async_copy(gg_buf, gg_ref.at[k], out_sems.at[1]),
+            pltpu.make_async_copy(gu_buf, gu_ref.at[k], out_sems.at[2]),
+            pltpu.make_async_copy(act_buf, act_ref.at[k], out_sems.at[3]),
+        ]
+
+    def blocks_out(k):
+        core, zp = which(k)
+        return [
+            pltpu.make_async_copy(sum_buf, sums_ref.at[:, core, zp], out_sems.at[4]),
+            pltpu.make_async_copy(grad_buf, grads_ref.at[:, core, zp], out_sems.at[5]),
+        ]
+
+    def c_out(k):
+        return pltpu.make_async_copy(c_buf, cs_ref.at[k], out_sems.at[6])
+
+    def backward_input(k, carry):
+        turns(k, early)
+        slot = k % 2
+        pl.when(k + 1 < groups)(lambda: cot_load(k + 1, 1 - slot).start())
+        cot_load(k, slot).wait()
+        pl.when(k > 0)(lambda: c_out(k).wait())
+        for q, (onehot, _) in enumerate(onehots(k)):
+            taken = jnp.dot(onehot.astype(bf16), cot_buf[slot, q], preferred_element_type=f32)
+            c_buf[q * capacity : (q + 1) * capacity, :] = taken.astype(bf16)
+        c_out(k).start()
+        d_ref[k] = dot_t(c_buf[...], wd_ref[...])
+        return carry
+
+    lax.fori_loop(0, groups, backward_input, 0)
+    c_out(0).wait()
+
+    late = []
+    for turn in range(n):
+        steps = []
+        if turn == 0:
+            steps += [(gather.line, 2)] if n > 2 else []
+        else:
+            if turn + 2 < n:
+                steps.append((gather.line, turn + 2))
+            if turn > 1:
+                steps.append((gather.first, turn))
+            steps.append((gather.second, turn))
+        if steps:
+            late.append((2 * turn, both(*steps)))
+        late.append((2 * turn + 1, both((lambda t: gather.plane.from_partner(order[t]), turn))))
+
+    def expert(k, carry):
+        turns(k, late)
+        core, zp = which(k)
+        if not held:
+            fetch = pltpu.make_async_copy(all_ref.at[pl.ds(0, places)], hid_buf, hid_sem.at[0])
+            for q in range(places):
+                pltpu.make_async_copy(all_ref.at[(q * 2 + core) * n + zp], hid_buf.at[q], hid_sem.at[0]).start()
+            fetch.wait()
+        hots = onehots(k)
+        pl.when(k > 0)(functools.partial(wait_for, outs, k))
+        for q, (onehot, _) in enumerate(hots):
+            block = hid_buf[(q * 2 + core) * n + zp] if held else hid_buf[q]
+            taken = jnp.dot(onehot.astype(bf16), block, preferred_element_type=f32)
+            x_buf[q * capacity : (q + 1) * capacity, :] = taken.astype(bf16)
+        weight = jnp.concatenate(
+            [jnp.sum(onehot * share, axis=1, keepdims=True) for onehot, share in hots], axis=0
+        )
+        gate = jnp.dot(x_buf[...], wg_ref[...], preferred_element_type=f32)
+        up = jnp.dot(x_buf[...], wu_ref[...], preferred_element_type=f32)
+        sigmoid = 1.0 / (1.0 + jnp.exp(-gate))
+        silu = gate * sigmoid
+        activated = silu * up
+        grad = d_ref[k]
+        row_mix = jnp.sum(activated * grad, axis=1, keepdims=True)
+        grad = grad * weight
+        act_buf[...] = (activated * weight).astype(bf16)
+        gg_buf[...] = (grad * up * sigmoid * (1.0 + gate * (1.0 - sigmoid))).astype(bf16)
+        gu_buf[...] = (grad * silu).astype(bf16)
+        for copy in outs(k):
+            copy.start()
+        for q, (onehot, _) in enumerate(hots):
+            back = jnp.sum(onehot * row_mix[q * capacity : (q + 1) * capacity], axis=0, keepdims=True)
+            back_ref[(q * 2 + core) * n + zp] = jnp.broadcast_to(back, slab_ref.shape[1:])
+        produced = jnp.dot(act_buf[...], wd_ref[...], preferred_element_type=f32).astype(bf16)
+        pl.when(k > 0)(functools.partial(wait_for, blocks_out, k))
+        for q, (onehot, _) in enumerate(hots):
+            part = produced[q * capacity : (q + 1) * capacity]
+            sum_buf[q] = t_dot(onehot.astype(bf16), part).astype(bf16)
+        grad_in = (dot_t(gg_buf[...], wg_ref[...]) + dot_t(gu_buf[...], wu_ref[...])).astype(bf16)
+        for q, (onehot, _) in enumerate(hots):
+            part = grad_in[q * capacity : (q + 1) * capacity]
+            grad_buf[q] = t_dot(onehot.astype(bf16), part).astype(bf16)
+        for copy in blocks_out(k):
+            copy.start()
+        return carry
+
+    lax.fori_loop(0, groups, expert, 0)
+    for copy in outs(0) + blocks_out(0):
+        copy.wait()
+    s.drain()
+
+
+def experts_all(reps, shards, capacity, x, slab, cots, wg, wu, wd, ident):
+    g = Grid(reps, shards)
+    dma, v = pltpu.SemaphoreType.DMA, pltpu.VMEM
+    n, places = shards, g.places
+    length, width = x.shape
+    inner = wg.shape[1]
+    rows = places * capacity
+    held = g.devices <= 32
+    blocks = jax.ShapeDtypeStruct((places, 2, n, length, width), bf16)
+    wide = jax.ShapeDtypeStruct((2 * n, rows, width), bf16)
+    narrow = jax.ShapeDtypeStruct((2 * n, rows, inner), bf16)
+    gathered = (g.devices, length, width)
+    return pl.pallas_call(
+        functools.partial(experts_kernel, reps, shards, capacity, held),
+        out_shape=(
+            jax.ShapeDtypeStruct(slab.shape, f32),
+            blocks,
+            blocks,
+            wide,
+            wide,
+            narrow,
+            narrow,
+            narrow,
+            jax.ShapeDtypeStruct((1, 16, 128) if held else gathered, bf16),
+        ),
+        in_specs=[vmem, vmem, hbm, vmem, vmem, vmem],
+        out_specs=(vmem,) + (hbm,) * 8,
+        scratch_shapes=[
+            v(slab.shape, f32),
+            v((2, places, length, width), bf16),
+            v(gathered if held else (places, length, width), bf16),
+            v((2 * n, rows, inner), f32),
+            v((rows, width), bf16),
+            v((rows, width), bf16),
+            v((rows, inner), bf16),
+            v((rows, inner), bf16),
+            v((rows, inner), bf16),
+            v((places, length, width), bf16),
+            v((places, length, width), bf16),
+            dma((GatherAll.sends(g),)),
+            dma((g.devices,)),
+            dma((g.devices,)),
+            dma((2,)),
+            dma((2,)),
+            dma((1,)),
+            dma((7,)),
+        ]
+        + GatherAll.scratch(g),
+        compiler_params=params(ident),
+        name="experts_all",
+    )(x, slab, cots.reshape(places, 2, n, length, width), wg, wu, wd)[:-1]
 
 
 def inverse_rms(values):
@@ -1181,48 +1389,16 @@
     mix = picked / picked_total
     slab = jnp.where(chosen, mix, -1.0).T.reshape(experts, 1, length)
     slab = jnp.broadcast_to(slab, (experts, 8, length))
-    hiddens, slabs = gather_all(reps, shards, hidden_two, slab, 4)
-
-    share = slabs[:, 0, :]
-    member = share >= 0.0
-    earlier = jnp.arange(length)[:, None] < jnp.arange(length)[None, :]
-    slot = matmul(member.astype(bf16), earlier.astype(bf16))
-    place = (jnp.arange(capacity, dtype=f32)[None, :, None] == slot[:, None, :]) & member[:, None, :]
-    row_weight = jnp.sum(jnp.where(place, share[:, None, :], 0.0), axis=2, keepdims=True)
-    onehot = place.astype(bf16)
-
-    def dispatch(blocks):
-        taken = jnp.einsum("bst,btd->bsd", onehot, blocks, preferred_element_type=f32)
-        return taken.astype(bf16).reshape(devices * capacity, width)
-
-    rows = dispatch(hiddens)
-    row_grads = dispatch(cotangents)
-    row_weight = row_weight.reshape(devices * capacity, 1)
-    gate = matmul(rows, w_gate[0])
-    up = matmul(rows, w_up[0])
-    sigmoid_gate = jax.nn.sigmoid(gate)
-    activated = (gate * sigmoid_gate * up).astype(bf16)
-    produced = matmul(activated, w_down[0]).astype(bf16).astype(f32)
-    row_grads = row_grads.astype(f32)
-    weighted = (row_weight * produced).astype(bf16)
-    row_mix = jnp.sum(row_grads * produced, axis=1).reshape(devices, capacity, 1)
-    back_mix = jnp.sum(jnp.where(place, row_mix, 0.0), axis=1).reshape(devices, 1, length)
-    back_mix = jnp.broadcast_to(back_mix, (devices, 8, length))
-    grad_pair = (row_weight * row_grads).astype(bf16)
-    grad_act = matmul(grad_pair, w_down[0], ((1,), (1,)))
-    grad_gate = (grad_act * up * sigmoid_gate * (1.0 + gate * (1.0 - sigmoid_gate))).astype(bf16)
-    grad_up = (grad_act * gate * sigmoid_gate).astype(bf16)
-    grad_in = matmul(grad_gate, w_gate[0], ((1,), (1,))) + matmul(grad_up, w_up[0], ((1,), (1,)))
-    grad_w_down = matmul(activated, grad_pair, ((0,), (0,)))
-    grad_w_gate = matmul(rows, grad_gate, ((0,), (0,)))
-    grad_w_up = matmul(rows, grad_up, ((0,), (0,)))
-
-    def combine(values):
-        values = values.reshape(devices, capacity, width)
-        return jnp.einsum("bst,bsd->btd", onehot, values, preferred_element_type=f32).astype(bf16)
-
-    grad_hidden, mixes = scatter_wide(reps, shards, combine(grad_in.astype(bf16)), back_mix, 8, chunks)
-    sums = combine(weighted)
+    back_mix, sums, grad_sums, rows, row_grads, grad_gate, grad_up, activated = experts_all(
+        reps, shards, capacity, hidden_two, slab, cotangents, w_gate[0], w_up[0], w_down[0], 4
+    )
+    sums = sums.reshape(devices, length, width)
+    grad_sums = grad_sums.reshape(devices, length, width)
+    rows, row_grads = rows.reshape(-1, width), row_grads.reshape(-1, width)
+    fill = (rows, row_grads) + tuple(a.reshape(rows.shape[0], -1) for a in (grad_gate, grad_up, activated))
+    grad_hidden, mixes, grad_w_gate, grad_w_up, grad_w_down = scatter_wide(
+        reps, shards, grad_sums, back_mix, fill, 8, chunks
+    )
 
     grad_out = cotangent.astype(f32)
     grad_mix = mixes[:, 0, :].T
@@ -1239,7 +1415,7 @@
         sums[:, :, :fused], 5,
     )
     if chunks > 1:
-        rest = scatter_wide(reps, shards, sums[:, :, fused:], None, 16, chunks - 1)
+        rest = scatter_wide(reps, shards, sums[:, :, fused:], None, None, 16, chunks - 1)
         moe = jnp.concatenate([moe, rest], axis=1)
     output = (resid + moe).astype(bf16)
     grad_attn = grad_attn.reshape(shards * length, width)

time: 829 us -> 718 us (0.87)
  matrix products: 176 us -> 20.2 us
  Pallas kernels: 554 us -> 606 us
  other arithmetic: 55.5 us -> 36.2 us
  local copies, waits for them, and re-layouts: 19.9 us -> 32 us
    dot_general x16 -> x6, matrix products: 129 us -> 20.2 us  [matmul(): return lax.dot_general(a, b, (dims, ((), ())), preferred_element_type=f32)]
    dot_general x4 -> x0, matrix products: 46.9 us -> none  [the longest x2 27.3 us: combine(): jnp.einsum('bst,bsd->btd', onehot, values, preferred_element_type=f32)]
    pallas_call x1, Pallas kernels: 96 us -> 122 us  [experts_all(): pl.pallas_call(functools.partial(experts_kernel, reps, shards, capacity,...]
    pallas_call x1, Pallas kernels: 86.1 us -> 111 us  [scatter_all(): pl.pallas_call(functools.partial(scatter_all_kernel, reps, shards, slabbe...]
    convert_element_type x2 -> x0, other arithmetic: 22.4 us -> none  [local(): grad_pair = (row_weight * row_grads).astype(bf16)]
    unnamed x65 -> x50, local copies, waits for them, and re-layouts: 2.61 us -> 16.4 us
  transfers between devices with their start and end apart: 1 -> 1, of which waited for: 0 -> 0; matrix products, arithmetic and copies ran while one was open for 8% -> 6% of each run, Pallas kernels for 13% -> 15%
where the time goes in v4:
time: 718 us; the launch traced here: 710 us
  Pallas kernels  606 us (84%)
  other arithmetic  36.2 us (5%)
  local copies, waits for them, and re-layouts  32 us (4%)
  matrix products  20.2 us (3%)
  between operations  14.8 us (2%)
    pallas_call x1, Pallas kernels, experts_all(): pl.pallas_call(functools.partial(experts_kernel, reps, shards, capacity,...  122 us
    pallas_call x1, Pallas kernels, scatter_all(): pl.pallas_call(functools.partial(scatter_all_kernel, reps, shards, slabbe...  111 us
    pallas_call x1, Pallas kernels, attend(): pl.pallas_call(functools.partial(attend_kernel, reps, shards, heads), out...  107 us
    pallas_call x1, Pallas kernels, deliver(): pl.pallas_call(functools.partial(deliver_kernel, reps, shards), out_shape...  105 us
    pallas_call x1, Pallas kernels, attend_back(): pl.pallas_call(functools.partial(attend_back_kernel, reps, shards, heads)...  101 us
    pallas_call x1, Pallas kernels, collect(): pl.pallas_call(functools.partial(collect_kernel, reps, shards, layout), o...  61.1 us
    dot_general x6, matrix products, matmul(): return lax.dot_general(a, b, (dims, ((), ())), preferred_element_type=f32)  20.2 us
    unnamed x50, local copies, waits for them, and re-layouts  16.4 us
  transfers between devices with their start and end apart: 1, of which 0 were waited for; matrix products, arithmetic and copies ran while one was open for 6% of the time, Pallas kernels for 15%

profile of v4, /device:TPU:17, one launch (start us, length us, event | category | flops | bytes accessed | tf_op | source)
XLA Modules:
  0.0 709.7 jit_solution(14479026439038620088)
XLA Ops:
  7.2 0.0 all-reduce.9.cloned.1.call-start
  7.3 0.7 convert_bitcast_fusion.3
  7.9 0.7 pad.29
  8.6 0.7 pad.30
  9.3 0.7 reshape.260
  9.9 0.7 reshape.261
  10.6 0.8 concatenate.22
  11.4 0.1 copy.72
  11.6 0.7 pad.32.small_ref
  12.2 61.1 %collect.1 = (bf16[4,128,2048]{2,1,0:T(8,128)(2,1)}, bf16[4,512,128]{2,1,0:T(8,128)(2,1)}, bf16[2048,1280]{1,0:T(8,128)(2,1)}) custom-call(bf16[128,2048]{1,0:T(8,128)(2,1)} %x_ref.1, bf16[512,128]{1,0:T(8,128)(2,1)} %pad.32.small_ref, bf16[512,4096]{1,0:T(8,128)(2,1)} %wq_ref.1, bf16[512,512]{1,0:T(8,128)(2,1)} %wk_ref.1, bf16[512,512]{1,0:T(8,128)(2,1)} %wv_ref.1), custom_call_target="tpu_custom_call" | custom-call | tf_op jit(solution)/shard_map/collect/pallas_call | solution.py:505
  73.4 1.1 convert_reduce_fusion.3
  74.5 1.9 convert_reduce_fusion
  76.4 1.0 convert_reduce_fusion.4
  77.4 0.2 fusion.9
  77.7 0.8 fusion.10.refs_8_.refs_7_
  78.5 0.6 copy.86
  79.1 0.6 reshape.281.refs_4_.refs_3_
  79.7 0.6 reshape.282.refs_5_.refs_4_
  80.3 1.0 fusion.12
  81.3 1.0 pad_maximum_fusion.1
  82.3 107.0 %attend.1 = (bf16[4,128,2048]{2,1,0:T(8,128)(2,1)}, f32[4,128,1280]{2,1,0:T(8,128)}, bf16[4,128,1024]{2,1,0:T(8,128)(2,1)}, f32[128,2048]{1,0:T(8,128)}, bf16[32,128,2048]{2,1,0:T(8,128)(2,1)}) custom-call(bf16[4,128,2048]{2,1,0:T(8,128)(2,1)} %get-tuple-element.42.refs_0_, bf16[2048,1280]{1,0:T(8,128)(2,1)} %get-tuple-element.43.refs_1_, ...), custom_call_target="tpu_custom_call" | custom-call | tf_op jit(solution)/shard_map/attend/pallas_call | solution.py:973
  189.3 1.7 multiply_reduce_fusion.3
  191.1 0.2 multiply_convert_fusion.refs_0_
  191.3 0.8 copy-done.4
  192.0 0.3 fusion.19
  192.5 0.7 broadcast_in_dim.71.refs_1_
  193.1 121.7 %experts_all.1 = (f32[32,8,128]{2,1,0:T(8,128)}, bf16[4,2,4,128,2048]{4,3,2,1,0:T(8,128)(2,1)}, bf16[4,2,4,128,2048]{4,3,2,1,0:T(8,128)(2,1)}, bf16[8,256,2048]{...) custom-call(bf16[128,2048]{1,0:T(8,128)(2,1)} %copy-done.4, ...), custom_call_target="tpu_custom_call" | custom-call | tf_op jit(solution)/shard_map/experts_all/pallas_call | solution.py:1237
  314.8 111.0 %scatter_all.1 = (f32[128,2048]{1,0:T(8,128)}, f32[32,8,128]{2,1,0:T(8,128)}, f32[2048,768]{1,0:T(8,128)}, f32[2048,768]{1,0:T(8,128)}, f32[768,2048]{1,0:T(8,128)}) custom-call(bf16[4,2,4,128,2048]{4,3,2,1,0:T(8,128)(2,1)} %get-tuple-element.47.refs_0_, f32[32,8,128]{2,1,0:T(8,128)} %get-tuple-element.48.refs_1_, bf16[2048,2048]{1,0:T(8,128)(2,1)} %bitcast.94, ...), custom_call_target="tpu_custom_call" | custom-call | tf_op jit(solution)/shard_map/scatter_all/pallas_call | solution.py:627
  425.9 1.0 slice.54
  426.9 1.8 multiply_reduce_fusion.1
  428.7 0.0 copy-start.1
  428.7 1.0 copy-done.1
  429.7 1.1 fusion.18.refs_0_
  430.8 100.7 %attend_back.1 = (bf16[4,128,2048]{2,1,0:T(8,128)(2,1)}, bf16[4,128,1280]{2,1,0:T(8,128)(2,1)}, f32[1,128]{1,0:T(1,128)}, f32[1,128]{1,0:T(1,128)}, f32[128,2048]{1,0:T(8,128)}) custom-call(bf16[128,2048]{1,0:T(8,128)(2,1)} %fusion.18.refs_0_, f32[4,128,1280]{2,1,0:T(8,128)} %get-tuple-element.56.refs_1_, bf16[1024,2048]{1,0:T(8,128)(2,1)} %refs_2_.3, ...), custom_call_target="tpu_custom_call" | custom-call | tf_op jit(solution)/shard_map/attend_back/pallas_call | solution.py:1041
  531.6 6.3 bitcast_convert_fusion.1
  537.9 0.0 all-reduce.9.cloned.1.call-update
  537.9 1.0 copy-done.5
  538.9 0.2 convolution_convert_fusion
  539.1 2.2 multiply_reduce_fusion
  541.4 7.4 %bitcast_convert_fusion = bf16[2048,1280]{1,0:T(8,128)(2,1)} fusion(bf16[4,128,2048]{2,1,0:T(8,128)(2,1)} %get-tuple-element.60, bf16[4,128,1280]{2,1,0:T(8,128)(2,1)} %get-tuple-element.59), kind=kOutput, calls=%fused_computation | convolution fusion | flops 2686976000 | bytes 8650752 | tf_op jit(solution)/shard_map/dot_general | solution.py:1304
  548.9 4.1 fusion.1
  553.0 0.1 reshape.275
  553.2 0.1 reshape.277
  553.3 0.1 concatenate.26
  553.4 0.3 copy.82
  553.7 0.1 pad.35.clone
  553.8 5.7 pad_maximum_fusion.w_ref
  559.5 104.9 %deliver.1 = (f32[128,2048]{1,0:T(8,128)}, bf16[4,8,64,1408]{3,2,1,0:T(8,128)(2,1)}) custom-call(bf16[4,128,2048]{2,1,0:T(8,128)(2,1)} %bitcast.117, bf16[4,4,2,64,1408]{4,3,2,1,0:T(8,128)(2,1)} %pad_maximum_fusion.w_ref), custom_call_target="tpu_custom_call" | custom-call | tf_op jit(solution)/shard_map/deliver/pallas_call | solution.py:737
  664.4 3.2 convert_bitcast_fusion
  667.6 4.2 copy.83
  671.9 1.4 convert_bitcast_fusion.1
  673.3 1.1 copy.93
  674.4 1.1 copy.94
  675.5 1.1 convert_reduce_fusion.2
  676.7 0.7 copy.79
  677.4 0.7 slice_reduce_fusion.2
  678.1 0.9 slice_reduce_fusion
  679.1 1.5 fusion.4
  680.6 3.2 fusion.7
  683.8 6.8 convert_element_type.171
  690.6 6.1 copy.99
  696.7 2.8 copy.100
  699.5 0.3 slice-done.1
  699.8 2.7 copy.101
  (62 shorter events, 0.4 us)
Async XLA Ops:
  7.2 676.6 %all-reduce.9.cloned.1.call-start = ((), (), s32[]{:S(2)}) async-start(), calls=%async_computation | async-start | bytes 8388608 | tf_op jit(solution)/shard_map/psum | solution.py:1424
  82.3 108.7 %copy-start.9 = (s32[128,8]{0,1:T(8,128)S(1)}, s32[128,8]{0,1:T(8,128)}, u32[]{:S(2)}) copy-start(s32[128,8]{0,1:T(8,128)} %param.18) | copy-start | bytes 12292
  189.3 2.7 copy-start
  191.2 0.8 copy-start.4
  425.9 3.8 copy-start.7
  428.7 1.0 copy-start.1
  537.9 1.0 copy-start.5
  539.1 9.7 %slice-start.4 = ((s8[5242880]{0:T(1024)(128)(4,1)}), s8[4194304]{0:T(1024)(128)(4,1)S(1)}, s32[]{:S(2)}) async-start(s8[5242880]{0:T(1024)(128)(4,1)} %bitcast.106), calls=%async_computation.5 | async-start | bytes 8388608
  541.4 7.4 %copy-start.6 = (bf16[4,128,2048]{2,1,0:T(8,128)(2,1)S(1)}, bf16[4,128,2048]{2,1,0:T(8,128)(2,1)}, u32[]{:S(2)}) copy-start(bf16[4,128,2048]{2,1,0:T(8,128)(2,1)} %get-tuple-element.42.refs_0_) | copy-start | bytes 6291460
  541.4 7.4 %slice-start.5 = ((s8[5242880]{0:T(1024)(128)(4,1)}), s8[1048576]{0:T(1024)(128)(4,1)S(1)}, s32[]{:S(2)}) async-start(s8[5242880]{0:T(1024)(128)(4,1)} %bitcast.106), calls=%async_computation.6 | async-start | bytes 2097152
  541.4 7.4 %copy-start.10 = (bf16[4,128,1280]{2,1,0:T(8,128)(2,1)S(1)}, bf16[4,128,1280]{2,1,0:T(8,128)(2,1)}, u32[]{:S(2)}) copy-start(bf16[4,128,1280]{2,1,0:T(8,128)(2,1)} %get-tuple-element.59) | copy-start | bytes 3932164
  548.8 4.2 copy-start.12
  548.8 4.3 copy-start.11
  671.9 7.2 %copy-start.3 = (bf16[128,2048]{1,0:T(8,128)(2,1)S(1)}, bf16[128,2048]{1,0:T(8,128)(2,1)}, u32[]{:S(2)}) copy-start(bf16[128,2048]{1,0:T(8,128)(2,1)} %x_ref.1) | copy-start | bytes 1572868
  673.3 7.3 %copy-start.2 = (f32[128,2048]{1,0:T(8,128)S(1)}, f32[128,2048]{1,0:T(8,128)}, u32[]{:S(2)}) copy-start(f32[128,2048]{1,0:T(8,128)} %copy-done.1) | copy-start | bytes 3145732
  673.3 7.3 %copy-start.8 = (bf16[128,2048]{1,0:T(8,128)(2,1)S(1)}, bf16[128,2048]{1,0:T(8,128)(2,1)}, u32[]{:S(2)}) copy-start(bf16[128,2048]{1,0:T(8,128)(2,1)} %refs_9_.1) | copy-start | bytes 1572868
  683.8 12.9 %slice-start.2 = ((s8[6291456]{0:T(1024)(128)(4,1)}), s8[4194304]{0:T(1024)(128)(4,1)S(1)}, s32[]{:S(2)}) async-start(s8[6291456]{0:T(1024)(128)(4,1)} %bitcast.99), calls=%async_computation.3 | async-start | bytes 8388608
  690.6 6.1 slice-start.3
  690.6 8.9 %slice-start = ((s8[6291456]{0:T(1024)(128)(4,1)}), s8[4194304]{0:T(1024)(128)(4,1)S(1)}, s32[]{:S(2)}) async-start(s8[6291456]{0:T(1024)(128)(4,1)} %bitcast.96), calls=%async_computation.1 | async-start | bytes 8388608
  696.6 3.1 slice-start.1
Sparse Core Ops, SparseCore 0:
  538.0 114.3 all-reduce.8

commit v5 on v4

--- a/solution.py
+++ b/solution.py
@@ -410,113 +410,6 @@
 
 def params(ident):
     return pltpu.CompilerParams(collective_id=ident, has_side_effects=True, vmem_limit_bytes=vmem_cap)
-
-
-def collect_kernel(reps, shards, layout, x_ref, small_ref, wq_ref, wk_ref, wv_ref, xs_ref, smalls_ref, w_ref, sems, xr, mr, wr, lr, hr, dr, cr, ls):
-    g = Grid(reps, shards).here()
-    s = Sends(sems)
-    n = g.shards
-    q_cols, kv_cols, kv_heads, head_dim = layout
-    deep = wq_ref.shape[0]
-    piece = deep // g.reps
-    cols = q_cols + 2 * kv_cols
-    first = cols // 2 // 128 * 128
-    spans = {0: pl.ds(0, first), 1: pl.ds(first, cols - first), None: pl.ds(0, cols)}
-    mine = pl.ds(pl.multiple_of(g.r * piece, piece), piece)
-
-    def view(u, hi, lo, core, part):
-        row = pl.multiple_of(u * deep + g.rep_of(hi, lo, core) * piece, piece)
-        return w_ref.at[pl.ds(row, piece), spans[part]]
-
-    def pieces(zp, u):
-        row = pl.ds(pl.multiple_of(u * deep + g.r * piece, piece), piece)
-        at_q = pl.ds(pl.multiple_of(zp * q_cols, 128), q_cols)
-        at_kv = pl.ds(pl.multiple_of(zp * kv_heads // n * head_dim, 128), kv_cols)
-        return (
-            (wq_ref.at[mine, at_q], w_ref.at[row, pl.ds(0, q_cols)]),
-            (wk_ref.at[mine, at_kv], w_ref.at[row, pl.ds(q_cols, kv_cols)]),
-            (wv_ref.at[mine, at_kv], w_ref.at[row, pl.ds(q_cols + kv_cols, kv_cols)]),
-        )
-
-    keeps = [
-        pltpu.make_async_copy(x_ref, xs_ref.at[g.z], ls.at[0]),
-        pltpu.make_async_copy(small_ref, smalls_ref.at[g.z], ls.at[1]),
-    ]
-    locals_ = [pltpu.make_async_copy(src, dst, ls.at[2 + i]) for i, (src, dst) in enumerate(pieces(g.z, g.z))]
-    for copy in locals_ + keeps:
-        copy.start()
-    barrier = pltpu.get_barrier_semaphore()
-    peers = [g.device(g.r, (g.z + step) % n) for step in range(1, n)]
-    peers += [g.device(g.rep_of(g.hi, g.other_lo(step), g.core), g.z) for step in range(1, g.los)]
-    peers += [g.device(g.rep_of(1 - g.hi, g.lo, g.core), g.z), g.device(g.rep_of(g.hi, g.lo, 1 - g.core), g.z)]
-    for peer in peers:
-        pl.semaphore_signal(barrier, inc=1, device_id=peer, device_id_type=pl.DeviceIdType.MESH)
-    pl.semaphore_wait(barrier, len(peers))
-
-    plane = PlaneGather(g, s, view, lr, hr, dr, cr)
-    for step in range(1, n):
-        zp = (g.z + step) % n
-        for i, (src, dst) in enumerate(pieces(zp, g.z)):
-            s.start(src, dst, wr.at[step, i], g.device(g.r, zp))
-    order = g.nearest()
-
-    def line(turn):
-        zp = order[turn]
-        if turn:
-            s.arrived(smalls_ref.at[zp], mr.at[zp], g.device(g.r, zp))
-        pass_along(g, s, zp, smalls_ref.at[zp] if turn else small_ref, smalls_ref.at[zp], mr)
-        if turn:
-            s.arrived(xs_ref.at[zp], xr.at[zp], g.device(g.r, zp))
-        pass_along(g, s, zp, xs_ref.at[zp] if turn else x_ref, xs_ref.at[zp], xr)
-
-    line(0)
-    for copy in locals_:
-        copy.wait()
-    plane.own(g.z)
-
-    def unit(step):
-        return (g.z + n - step) % n
-
-    for step in range(1, n):
-        u = unit(step)
-        for i, (_, dst) in enumerate(pieces(g.z, u)):
-            s.arrived(dst, wr.at[step, i], g.device(g.r, u))
-        plane.own(u)
-    line(1)
-    for step in range(n):
-        plane.first(unit(step))
-        if step:
-            plane.second(unit(step - 1))
-        if 2 + step < n:
-            line(2 + step)
-    plane.second(unit(n - 1))
-    for step in range(n):
-        plane.from_partner(unit(step))
-    for copy in keeps:
-        copy.wait()
-    s.drain()
-
-
-def collect(reps, shards, x, small, wq, wk, wv, layout, ident):
-    g = Grid(reps, shards)
-    dma = pltpu.SemaphoreType.DMA
-    n = shards
-    cols = layout[0] + 2 * layout[1]
-    return pl.pallas_call(
-        functools.partial(collect_kernel, reps, shards, layout),
-        out_shape=(
-            jax.ShapeDtypeStruct((n,) + x.shape, x.dtype),
-            jax.ShapeDtypeStruct((n,) + small.shape, small.dtype),
-            jax.ShapeDtypeStruct((n * wq.shape[0], cols), wq.dtype),
-        ),
-        in_specs=[vmem, vmem, hbm, hbm, hbm],
-        out_specs=(vmem, vmem, vmem),
-        scratch_shapes=[dma((PlaneGather.sends(g, n) + 7 * n,)), dma((n,)), dma((n,)), dma((n, 3))]
-        + PlaneGather.scratch(g, n)
-        + [dma((5,))],
-        compiler_params=params(ident),
-        name="collect",
-    )(x, small, wq, wk, wv)
 
 
 def scatter_all_kernel(reps, shards, slabbed, *refs):
@@ -931,65 +824,6 @@
             send_line(self.g, self.s, self.order[t], self.plane.mine(t), self.out_ref, *self.lines, last=t == n - 1)
 
 
-def attend_kernel(reps, shards, heads, *refs):
-    (
-        x_ref, w_ref, wo_ref, gain_ref, qg_ref, kg_ref, cos_ref, sin_ref, bias_ref, cot_ref,
-        hid_ref, qkv_ref, att_ref, out_ref, cots_ref,
-        own, rl, rr, sl, sr, sems, keep_sem, *gather_sems,
-    ) = refs
-    g = Grid(reps, shards).here()
-    s = Sends(sems)
-    n = g.shards
-    gather = GatherAll(g, s, cot_ref, cots_ref, gather_sems[0], gather_sems[1:])
-    keep = pltpu.make_async_copy(cot_ref, gather.own(), keep_sem.at[0])
-    keep.start()
-    greet_all(g)
-    gather.line(0)
-    order = g.nearest()[::-1]
-    for turn in range(n):
-        zp = order[turn]
-        attend_block(
-            zp, heads, x_ref, w_ref, wo_ref, gain_ref, qg_ref, kg_ref, cos_ref, sin_ref, bias_ref,
-            hid_ref, qkv_ref, att_ref, own.at[turn],
-        )
-        send_line(g, s, zp, own.at[turn], out_ref, rl, rr, sl, sr, last=turn == n - 1)
-        if turn + 1 < n:
-            gather.line(turn + 1)
-            gather.first(turn)
-        if turn > 0:
-            gather.second(turn - 1)
-    gather.first(n - 1)
-    gather.second(n - 1)
-    gather.finish()
-    keep.wait()
-    s.drain()
-
-
-def attend(reps, shards, heads, x, w, wo, gain, qg, kg, cosine, sine, bias, cot, ident):
-    g = Grid(reps, shards)
-    dma, v = pltpu.SemaphoreType.DMA, pltpu.VMEM
-    n, rows, width = x.shape
-    cols = w.shape[1]
-    return pl.pallas_call(
-        functools.partial(attend_kernel, reps, shards, heads),
-        out_shape=(
-            jax.ShapeDtypeStruct(x.shape, bf16),
-            jax.ShapeDtypeStruct((n, rows, cols), f32),
-            jax.ShapeDtypeStruct((n, rows, wo.shape[0]), bf16),
-            jax.ShapeDtypeStruct((rows, width), f32),
-            jax.ShapeDtypeStruct((g.devices, rows, width), bf16),
-        ),
-        in_specs=[vmem] * 10,
-        out_specs=(vmem, vmem, vmem, vmem, hbm),
-        scratch_shapes=[v((n, rows, width), bf16)]
-        + line_scratch(n, (rows, width), bf16)
-        + [dma((GatherAll.sends(g) + 2 * n,)), dma((1,))]
-        + GatherAll.scratch(g),
-        compiler_params=params(ident),
-        name="attend",
-    )(x, w, wo, gain, qg, kg, cosine, sine, bias, cot)
-
-
 def attend_back_kernel(reps, shards, heads, *refs):
     (
         ga_ref, qkv_ref, wo_ref, qg_ref, kg_ref, cos_ref, sin_ref, bias_ref, p_ref,
@@ -1056,6 +890,223 @@
     )(ga, qkv, wo, qg, kg, cosine, sine, bias, p.reshape(g.places, 2, n, rows, out_width))
 
 
+def tables_of(segment_column, segment_row, frequency):
+    length = segment_row.shape[1]
+    rows = lax.broadcasted_iota(jnp.int32, (length, length), 0).astype(f32)
+    columns = lax.broadcasted_iota(jnp.int32, (length, length), 1).astype(f32)
+    same = segment_column == segment_row
+    first = jnp.min(jnp.where(same, columns, float(length)), axis=1, keepdims=True)
+    width = frequency.shape[1]
+    place = lax.broadcasted_iota(jnp.int32, (length, width), 0).astype(f32)
+    angle = (place - first) * frequency
+    second_half = lax.broadcasted_iota(jnp.int32, (length, width), 1) >= width // 2
+    sine = jnp.sin(angle)
+    bias = jnp.where(same & (columns <= rows), 0.0, masked_score)
+    return jnp.cos(angle), jnp.where(second_half, sine, -sine), bias
+
+
+def front_kernel(reps, shards, heads, layout, *refs):
+    (
+        x_ref, cot_ref, small_ref, freq_ref, wq_ref, wk_ref, wv_ref, wo_in,
+        smalls_ref, gains_ref, qk_ref, cos_ref, sin_ref, bias_ref, out_ref,
+        xs_out, w_out, hid_out, qkv_out, att_out, cots_ref,
+        xs_ref, w_ref, wo_ref, hid_ref, qkv_ref, att_ref, own, rl, rr, sl, sr,
+        sems, xr, mr, wr, ls, out_sems, lr, hr, dr, cr, *gather_sems,
+    ) = refs
+    g = Grid(reps, shards).here()
+    s = Sends(sems)
+    n = g.shards
+    q_cols, kv_cols, kv_heads, experts = layout
+    head_dim = heads[2]
+    deep = wq_ref.shape[0]
+    piece = deep // g.reps
+    cols = q_cols + 2 * kv_cols
+    first = cols // 2 // 128 * 128
+    spans = {0: pl.ds(0, first), 1: pl.ds(first, cols - first), None: pl.ds(0, cols)}
+    mine = pl.ds(pl.multiple_of(g.r * piece, piece), piece)
+
+    def view(u, hi, lo, core, part):
+        row = pl.multiple_of(u * deep + g.rep_of(hi, lo, core) * piece, piece)
+        return w_ref.at[pl.ds(row, piece), spans[part]]
+
+    def pieces(zp, u):
+        row = pl.ds(pl.multiple_of(u * deep + g.r * piece, piece), piece)
+        at_q = pl.ds(pl.multiple_of(zp * q_cols, 128), q_cols)
+        at_kv = pl.ds(pl.multiple_of(zp * kv_heads // n * head_dim, 128), kv_cols)
+        return (
+            (wq_ref.at[mine, at_q], w_ref.at[row, pl.ds(0, q_cols)]),
+            (wk_ref.at[mine, at_kv], w_ref.at[row, pl.ds(q_cols, kv_cols)]),
+            (wv_ref.at[mine, at_kv], w_ref.at[row, pl.ds(q_cols + kv_cols, kv_cols)]),
+        )
+
+    plane = PlaneGather(g, s, view, lr, hr, dr, cr)
+    gather = GatherAll(g, s, cot_ref, cots_ref, gather_sems[0], gather_sems[1:])
+    locals_ = [pltpu.make_async_copy(src, dst, ls.at[i]) for i, (src, dst) in enumerate(pieces(g.z, g.z))]
+    keeps = [
+        pltpu.make_async_copy(x_ref, xs_ref.at[g.z], ls.at[3]),
+        pltpu.make_async_copy(small_ref, smalls_ref.at[g.z], ls.at[4]),
+        pltpu.make_async_copy(wo_in, wo_ref, ls.at[5]),
+        pltpu.make_async_copy(cot_ref, gather.own(), ls.at[6]),
+    ]
+    for copy in locals_ + keeps:
+        copy.start()
+    barrier = pltpu.get_barrier_semaphore()
+    peers = [g.device(g.r, (g.z + step) % n) for step in range(1, n)]
+    peers += [g.device(g.rep_of(g.hi, g.other_lo(step), g.core), g.z) for step in range(1, g.los)]
+    peers += [g.device(g.rep_of(1 - g.hi, g.lo, g.core), g.z), g.device(g.rep_of(g.hi, g.lo, 1 - g.core), g.z)]
+    for peer in peers:
+        pl.semaphore_signal(barrier, inc=1, device_id=peer, device_id_type=pl.DeviceIdType.MESH)
+    pl.semaphore_wait(barrier, len(peers))
+
+    order = g.nearest()
+
+    def unit(step):
+        return (g.z + n - step) % n
+
+    def line(turn):
+        zp = order[turn]
+        if turn:
+            s.arrived(smalls_ref.at[zp], mr.at[zp], g.device(g.r, zp))
+        pass_along(g, s, zp, smalls_ref.at[zp] if turn else small_ref, smalls_ref.at[zp], mr)
+        if turn:
+            s.arrived(xs_ref.at[zp], xr.at[zp], g.device(g.r, zp))
+        pass_along(g, s, zp, xs_ref.at[zp] if turn else x_ref, xs_ref.at[zp], xr)
+
+    for step in range(1, n):
+        zp = (g.z + step) % n
+        for i, (src, dst) in enumerate(pieces(zp, g.z)):
+            s.start(src, dst, wr.at[step, i], g.device(g.r, zp))
+    line(0)
+    for copy in locals_:
+        copy.wait()
+    plane.own(g.z)
+    for step in range(1, n):
+        u = unit(step)
+        for i, (_, dst) in enumerate(pieces(g.z, u)):
+            s.arrived(dst, wr.at[step, i], g.device(g.r, u))
+        plane.own(u)
+    gather.plane.own(g.z, lambda part: cot_ref.at[gather.spans[part]])
+    line(1)
+    for step in range(n):
+        plane.first(unit(step))
+        if step:
+            plane.second(unit(step - 1))
+        if 2 + step < n:
+            line(2 + step)
+        if step == max(0, n - 3):
+            pass_along(g, s, g.z, cot_ref, gather.own(), gather.zr)
+    plane.second(unit(n - 1))
+    for step in range(n):
+        plane.from_partner(unit(step))
+    for copy in keeps[:3]:
+        copy.wait()
+
+    outs = [pltpu.make_async_copy(w_ref, w_out, out_sems.at[0]), pltpu.make_async_copy(xs_ref, xs_out, out_sems.at[1])]
+    for copy in outs:
+        copy.start()
+    length = x_ref.shape[0]
+    for zp in range(n):
+        rows = smalls_ref[zp].astype(f32)
+        gains_ref[:, zp * deep : (zp + 1) * deep] = rows.T[experts : experts + 8]
+    for i in range(2):
+        qk_ref[i : i + 1] = sum(gains_ref[2 + i : 3 + i, zp * deep : zp * deep + head_dim] for zp in range(n))
+
+    def compute(turn):
+        zp = order[turn]
+        column = smalls_ref[zp, 0:length, experts + 4 : experts + 5].astype(f32)
+        row = gains_ref[4:5, pl.ds(pl.multiple_of(zp * deep, 128), length)]
+        cos_ref[zp], sin_ref[zp], bias_ref[zp] = tables_of(column, row, freq_ref[...])
+        attend_block(
+            zp, heads, xs_ref, w_ref, wo_ref, gains_ref.at[0:1], qk_ref.at[0:1], qk_ref.at[1:2],
+            cos_ref, sin_ref, bias_ref, hid_ref, qkv_ref, att_ref, own.at[turn],
+        )
+
+    def sums(turn):
+        send_line(g, s, order[turn], own.at[turn], out_ref, rl, rr, sl, sr, last=turn == 0)
+
+    compute(n - 1)
+    sums(n - 1)
+    gather.first(0)
+    gather.line(1)
+    for turn in range(n - 2, -1, -1):
+        compute(turn)
+        at = n - 1 - turn
+        if turn > 0:
+            sums(turn)
+            gather.second(at - 1)
+            gather.first(at)
+            if at + 1 < n:
+                gather.line(at + 1)
+    late = [
+        pltpu.make_async_copy(hid_ref, hid_out, out_sems.at[2]),
+        pltpu.make_async_copy(qkv_ref, qkv_out, out_sems.at[3]),
+        pltpu.make_async_copy(att_ref, att_out, out_sems.at[4]),
+    ]
+    for copy in late:
+        copy.start()
+    gather.second(n - 2)
+    gather.first(n - 1)
+    gather.second(n - 1)
+    sums(0)
+    gather.finish()
+    for copy in outs + late + keeps[3:]:
+        copy.wait()
+    s.drain()
+
+
+def front(reps, shards, heads, layout, x, cot, small, frequency, wq, wk, wv, wo, ident):
+    g = Grid(reps, shards)
+    dma, v = pltpu.SemaphoreType.DMA, pltpu.VMEM
+    n = shards
+    rows, width = x.shape
+    head_dim = heads[2]
+    cols = layout[0] + 2 * layout[1]
+    table = jax.ShapeDtypeStruct((n, rows, head_dim), f32)
+    lines = (n, rows, width)
+    return pl.pallas_call(
+        functools.partial(front_kernel, reps, shards, heads, layout),
+        out_shape=(
+            jax.ShapeDtypeStruct((n,) + small.shape, bf16),
+            jax.ShapeDtypeStruct((8, width), f32),
+            jax.ShapeDtypeStruct((8, head_dim), f32),
+            table,
+            table,
+            jax.ShapeDtypeStruct((n, rows, rows), f32),
+            jax.ShapeDtypeStruct((rows, width), f32),
+            jax.ShapeDtypeStruct(lines, bf16),
+            jax.ShapeDtypeStruct((width, cols), bf16),
+            jax.ShapeDtypeStruct(lines, bf16),
+            jax.ShapeDtypeStruct((n, rows, cols), f32),
+            jax.ShapeDtypeStruct((n, rows, wo.shape[0]), bf16),
+            jax.ShapeDtypeStruct((g.devices, rows, width), bf16),
+        ),
+        in_specs=[vmem] * 4 + [hbm] * 4,
+        out_specs=(vmem,) * 7 + (hbm,) * 6,
+        scratch_shapes=[
+            v(lines, bf16),
+            v((width, cols), bf16),
+            v(wo.shape, bf16),
+            v(lines, bf16),
+            v((n, rows, cols), f32),
+            v((n, rows, wo.shape[0]), bf16),
+            v(lines, bf16),
+        ]
+        + line_scratch(n, (rows, width), bf16)
+        + [
+            dma((PlaneGather.sends(g, n) + GatherAll.sends(g) + 9 * n,)),
+            dma((n,)),
+            dma((n,)),
+            dma((n, 3)),
+            dma((7,)),
+            dma((5,)),
+        ]
+        + PlaneGather.scratch(g, n)
+        + GatherAll.scratch(g),
+        compiler_params=params(ident),
+        name="front",
+    )(x, cot, small, frequency, wq, wk, wv, wo)
+
+
 def slots_of(slab, capacity):
     length = slab.shape[1]
     member = slab >= 0.0
@@ -1119,7 +1170,9 @@
 
         return run
 
-    early = [(2, both((gather.first, 0))), (4, both((gather.line, 1), (gather.second, 0))), (6, both((gather.first, 1)))]
+    early = [(2, both((gather.first, 0))), (3, both((gather.line, 1))), (5, both((gather.second, 0)))]
+    if n > 2:
+        early.append((7, both((gather.line, 2))))
 
     def outs(k):
         return [
@@ -1155,20 +1208,21 @@
     lax.fori_loop(0, groups, backward_input, 0)
     c_out(0).wait()
 
-    late = []
+    def partner(turn):
+        gather.plane.from_partner(order[turn])
+
+    late = [(0, both((gather.first, 1)))]
     for turn in range(n):
-        steps = []
-        if turn == 0:
-            steps += [(gather.line, 2)] if n > 2 else []
-        else:
-            if turn + 2 < n:
-                steps.append((gather.line, turn + 2))
-            if turn > 1:
-                steps.append((gather.first, turn))
-            steps.append((gather.second, turn))
-        if steps:
-            late.append((2 * turn, both(*steps)))
-        late.append((2 * turn + 1, both((lambda t: gather.plane.from_partner(order[t]), turn))))
+        if 0 < turn < n - 1:
+            late.append((2 * turn, both((gather.second, turn))))
+        steps = [(partner, turn)]
+        if turn + 3 < n:
+            steps.append((gather.line, turn + 3))
+        if turn + 2 < n:
+            steps.append((gather.first, turn + 2))
+        if turn == n - 2:
+            steps.append((gather.second, n - 1))
+        late.append((2 * turn + 1, both(*steps)))
 
     def expert(k, carry):
         turns(k, late)
@@ -1279,22 +1333,6 @@
     return lax.rsqrt(jnp.mean(values * values, axis=-1, keepdims=True) + epsilon)
 
 
-def rope_tables(segment_rows, width):
-    length = segment_rows.shape[1]
-    places = jnp.arange(length, dtype=jnp.int32)
-    same = segment_rows[:, :, None] == segment_rows[:, None, :]
-    first = jnp.min(jnp.where(same, places[None, None, :], length), axis=2)
-    offset = (places[None] - first).astype(f32)
-    half = width // 2
-    frequency = rope_base ** (-2.0 * jnp.arange(half, dtype=f32) / width)
-    angle = offset[..., None] * frequency[None, None, :]
-    cosine, sine = jnp.cos(angle), jnp.sin(angle)
-    cosine = jnp.concatenate([cosine, cosine], axis=-1)
-    sine = jnp.concatenate([-sine, sine], axis=-1)
-    allowed = same & (places[None, None, :] <= places[None, :, None])
-    return cosine, sine, allowed
-
-
 def norm_back(grad_scaled, unit, inverse, gain):
     gained = grad_scaled * gain
     return inverse * (gained - unit * jnp.mean(gained * unit, axis=-1, keepdims=True))
@@ -1345,36 +1383,38 @@
     def column(values, rows=deep):
         return jnp.pad(values.reshape(-1, 1), ((0, rows - values.size), (0, 0)))
 
+    spot = lax.broadcasted_iota(jnp.int32, (deep, 1), 0) // part == z
+
+    def spotted(values):
+        return jnp.where(spot, jnp.tile(column(values, part), (deep // part, 1)), 0)
+
     small = jnp.concatenate(
         [
             w_router,
             column(attn_gain),
             column(ffn_gain),
-            column(query_gain),
-            column(key_gain),
+            spotted(query_gain),
+            spotted(key_gain),
             column(segments[0].astype(bf16)),
         ],
         axis=1,
     )
-    small_cols = -(-small.shape[1] // 128) * 128
+    small_cols = -(-(experts + 8) // 128) * 128
     small = jnp.pad(small, ((0, 0), (0, small_cols - small.shape[1])))
-    layout = (q_cols, kv_cols, kv_heads, head_dim)
-    block_tokens, small_all, w_in = collect(
-        reps, shards, tokens, small, w_query, key_weight, value_weight, layout, 1
+    half = rope_base ** (-2.0 * jnp.arange(head_dim // 2, dtype=f32) / head_dim)
+    frequency = jnp.concatenate([half, half]).reshape(1, head_dim)
+    head_sizes = (my_heads, my_kv, head_dim)
+    layout = (q_cols, kv_cols, kv_heads, experts)
+    (
+        small_all, gains, qk_gains, cosine, sine, bias, mixed,
+        block_tokens, w_in, hidden_in, qkv, attn_out, cotangents,
+    ) = front(
+        reps, shards, head_sizes, layout, tokens, cotangent, small, frequency,
+        w_query, key_weight, value_weight, w_out, 1,
     )
     router_full = small_all[:, :, :experts].reshape(width, experts)
-    gain_one = small_all[:, :, experts].reshape(1, width).astype(f32)
-    gain_two = small_all[:, :, experts + 1].reshape(1, width).astype(f32)
-    qgain = small_all[:, :part, experts + 2].reshape(1, head_dim).astype(f32)
-    kgain = small_all[:, :part, experts + 3].reshape(1, head_dim).astype(f32)
-    segment_rows = small_all[:, :length, experts + 4].astype(jnp.int32)
-
-    head_sizes = (my_heads, my_kv, head_dim)
-    cosine, sine, allowed = rope_tables(segment_rows, head_dim)
-    bias = jnp.where(allowed, 0.0, masked_score)
-    hidden_in, qkv, attn_out, mixed, cotangents = attend(
-        reps, shards, head_sizes, block_tokens, w_in, w_out, gain_one, qgain, kgain, cosine, sine, bias, cotangent, 2
-    )
+    gain_one, gain_two = gains[0:1], gains[1:2]
+    qgain, kgain = qk_gains[0:1], qk_gains[1:2]
     own_tokens = tokens.astype(f32)
     resid = own_tokens + mixed
 

time: 718 us -> 685 us (0.954)
  Pallas kernels: 606 us -> 581 us
  other arithmetic: 36.2 us -> 25.8 us
    pallas_call x2 -> x1, Pallas kernels: 168 us -> 150 us  [front(): pl.pallas_call(functools.partial(front_kernel, reps, shards, heads, layou...]
    unnamed x50 -> x41, local copies, waits for them, and re-layouts: 16.4 us -> 15 us
where the time goes in v5:
time: 685 us; the launch traced here: 676 us
  Pallas kernels  581 us (85%)
  local copies, waits for them, and re-layouts  33 us (5%)
  other arithmetic  25.8 us (4%)
  matrix products  21.8 us (3%)
  between operations  14.8 us (2%)
    pallas_call x1, Pallas kernels, front(): pl.pallas_call(functools.partial(front_kernel, reps, shards, heads, layou...  150 us
    pallas_call x1, Pallas kernels, experts_all(): pl.pallas_call(functools.partial(experts_kernel, reps, shards, capacity,...  119 us
    pallas_call x1, Pallas kernels, scatter_all(): pl.pallas_call(functools.partial(scatter_all_kernel, reps, shards, slabbe...  106 us
    pallas_call x1, Pallas kernels, deliver(): pl.pallas_call(functools.partial(deliver_kernel, reps, shards), out_shape...  104 us
    pallas_call x1, Pallas kernels, attend_back(): pl.pallas_call(functools.partial(attend_back_kernel, reps, shards, heads)...  100 us
    dot_general x6, matrix products, matmul(): return lax.dot_general(a, b, (dims, ((), ())), preferred_element_type=f32)  21.8 us
    unnamed x41, local copies, waits for them, and re-layouts  15 us
  transfers between devices with their start and end apart: 1, of which 0 were waited for; matrix products, arithmetic and copies ran while one was open for 6% of the time, Pallas kernels for 15%

profile of v5, /device:TPU:17, one launch (start us, length us, event | category | flops | bytes accessed | tf_op | source)
XLA Modules:
  0.0 676.0 jit_solution(17074143540234694000)
XLA Ops:
  7.2 0.0 all-reduce.7.cloned.1.call-start
  7.2 0.7 convert_bitcast_fusion.3
  7.9 0.6 maximum_bitcast_fusion.refs_3_
  8.5 0.7 reshape.273
  9.2 0.7 reshape.274
  9.9 0.7 fusion.9
  10.6 0.7 tile.8
  11.2 0.1 tile.9
  11.3 0.7 tile.20
  12.0 0.1 tile.21
  12.1 0.8 concatenate.19
  12.9 0.1 copy.70
  13.0 0.7 pad.23.refs_2_
  13.7 150.5 %front.1 = (bf16[4,512,128]{2,1,0:T(8,128)(2,1)}, f32[8,2048]{1,0:T(8,128)}, f32[8,128]{1,0:T(8,128)}, f32[4,128,128]{2,1,0:T(8,128)}, f32[4,128,128]{2,1,0:T(8,...) custom-call(bf16[128,2048]{1,0:T(8,128)(2,1)} %refs_0_.1, ...), custom_call_target="tpu_custom_call" | custom-call | tf_op jit(solution)/shard_map/front/pallas_call | solution.py:1066
  164.2 0.0 copy-start.8
  164.2 0.0 copy-done.4
  164.2 1.6 multiply_reduce_fusion.3
  165.8 1.3 fusion.17
  167.1 0.9 fusion.16
  168.0 0.2 multiply_convert_fusion.refs_0_
  168.2 0.0 copy-start.2
  168.2 0.3 fusion.18
  168.6 0.7 broadcast_in_dim.45.refs_1_
  169.3 119.1 %experts_all.1 = (f32[32,8,128]{2,1,0:T(8,128)}, bf16[4,2,4,128,2048]{4,3,2,1,0:T(8,128)(2,1)}, bf16[4,2,4,128,2048]{4,3,2,1,0:T(8,128)(2,1)}, bf16[8,256,2048]{...) custom-call(bf16[128,2048]{1,0:T(8,128)(2,1)} %copy-done.2, ...), custom_call_target="tpu_custom_call" | custom-call | tf_op jit(solution)/shard_map/experts_all/pallas_call | solution.py:1291
  288.3 106.4 %scatter_all.1 = (f32[128,2048]{1,0:T(8,128)}, f32[32,8,128]{2,1,0:T(8,128)}, f32[2048,768]{1,0:T(8,128)}, f32[2048,768]{1,0:T(8,128)}, f32[768,2048]{1,0:T(8,128)}) custom-call(bf16[4,2,4,128,2048]{4,3,2,1,0:T(8,128)(2,1)} %get-tuple-element.51.refs_0_, f32[32,8,128]{2,1,0:T(8,128)} %get-tuple-element.52.refs_1_, bf16[2048,2048]{1,0:T(8,128)(2,1)} %bitcast.87, ...), custom_call_target="tpu_custom_call" | custom-call | tf_op jit(solution)/shard_map/scatter_all/pallas_call | solution.py:520
  394.7 0.0 copy-start.6
  394.7 1.0 slice.47
  395.8 1.9 multiply_reduce_fusion.1
  397.7 0.0 copy-start
  397.7 1.0 copy-done
  398.7 1.2 fusion.15.refs_0_
  399.8 100.2 %attend_back.1 = (bf16[4,128,2048]{2,1,0:T(8,128)(2,1)}, bf16[4,128,1280]{2,1,0:T(8,128)(2,1)}, f32[1,128]{1,0:T(1,128)}, f32[1,128]{1,0:T(1,128)}, f32[128,2048]{1,0:T(8,128)}) custom-call(bf16[128,2048]{1,0:T(8,128)(2,1)} %fusion.15.refs_0_, f32[4,128,1280]{2,1,0:T(8,128)} %get-tuple-element.60.refs_1_, bf16[1024,2048]{1,0:T(8,128)(2,1)} %refs_2_.1, ...), custom_call_target="tpu_custom_call" | custom-call | tf_op jit(solution)/shard_map/attend_back/pallas_call | solution.py:875
  500.0 6.3 bitcast_convert_fusion.1
  506.4 0.0 all-reduce.7.cloned.1.call-update
  506.4 1.0 copy-done.3
  507.4 0.2 convolution_convert_fusion
  507.6 2.1 multiply_reduce_fusion
  509.8 0.1 reshape.287
  509.9 0.1 reshape.289
  510.0 7.8 %fusion.1 = (bf16[2048]{0:T(1024)(128)(2,1)S(1)}, bf16[512,2048]{1,0:T(8,128)(2,1)}) fusion(f32[512]{0:T(512)S(1)} %rsqrt_bitcast_fusion, bf16[4,128,2048]{2,1,0:T(8,128)(2,1)} %get-tuple-element.70, bf16[512,1280]{1,0:T(8,128)(2,1)} %bitcast.125, bf16[2048,1280]{1,0:T(8,128)(2,1)} %get-tuple-element.68), kind=kOutput, calls=%fused_computation.6 | convolution fusion | flops 2689595392 | bytes 10754048 | tf_op jit(solution)/shard_map/dot_general | solution.py:1342
  517.8 0.1 concatenate.22
  517.9 0.3 copy.80
  518.2 0.1 pad.26.clone
  518.3 5.3 bitcast_convert_fusion
  523.5 3.1 pad_maximum_fusion.w_ref
  526.7 104.5 %deliver.1 = (f32[128,2048]{1,0:T(8,128)}, bf16[4,8,64,1408]{3,2,1,0:T(8,128)(2,1)}) custom-call(bf16[4,128,2048]{2,1,0:T(8,128)(2,1)} %bitcast.108, bf16[4,4,2,64,1408]{4,3,2,1,0:T(8,128)(2,1)} %pad_maximum_fusion.w_ref), custom_call_target="tpu_custom_call" | custom-call | tf_op jit(solution)/shard_map/deliver/pallas_call | solution.py:630
  631.2 2.3 convert_bitcast_fusion.1
  633.5 1.1 convert_reduce_fusion
  634.6 0.7 copy.77
  635.4 2.3 copy.88
  637.7 1.1 copy.89
  638.8 3.2 convert_bitcast_fusion
  642.0 0.0 copy-start.5
  642.0 0.0 copy-start.1
  642.1 4.3 copy.81
  646.3 0.7 slice_reduce_fusion.2
  647.0 0.9 slice_reduce_fusion
  648.0 0.3 fusion.4
  648.3 1.7 fusion.7
  650.0 6.8 %convert_element_type.116 = f32[1024,2048]{1,0:T(8,128)} convert(bf16[1024,2048]{1,0:T(8,128)(2,1)} %all-reduce.7.cloned.1.call-done) | non-fusion elementwise | flops 2097152 | bytes 12582912 | tf_op jit(solution)/shard_map/convert_element_type | solution.py:1464
  656.8 6.1 copy.94
  662.9 2.8 copy.95
  665.7 0.3 slice-done.1
  666.0 2.7 copy.96
  (46 shorter events, 0.3 us)
Async XLA Ops:
  7.2 642.8 %all-reduce.7.cloned.1.call-start = ((), (), s32[]{:S(2)}) async-start(), calls=%async_computation | async-start | bytes 8388608 | tf_op jit(solution)/shard_map/psum | solution.py:1464
  13.7 150.5 %copy-start.4 = (bf16[128,2048]{1,0:T(8,128)(2,1)S(1)}, bf16[128,2048]{1,0:T(8,128)(2,1)}, u32[]{:S(2)}) copy-start(bf16[128,2048]{1,0:T(8,128)(2,1)} %refs_0_.1) | copy-start | bytes 1572868
  164.2 4.0 copy-start.8
  168.2 1.1 copy-start.2
  394.7 4.0 copy-start.6
  397.7 1.0 copy-start
  506.4 1.0 copy-start.3
  506.4 3.4 copy-start.11
  506.4 3.5 copy-start.10
  642.0 6.0 copy-start.5
  642.0 6.0 copy-start.7
  642.0 6.3 copy-start.1
  642.1 6.3 copy-start.9
  650.0 12.9 %slice-start.2 = ((s8[6291456]{0:T(1024)(128)(4,1)}), s8[4194304]{0:T(1024)(128)(4,1)S(1)}, s32[]{:S(2)}) async-start(s8[6291456]{0:T(1024)(128)(4,1)} %bitcast.92), calls=%async_computation.3 | async-start | bytes 8388608
  656.8 6.1 slice-start.3
  656.8 8.9 %slice-start = ((s8[6291456]{0:T(1024)(128)(4,1)}), s8[4194304]{0:T(1024)(128)(4,1)S(1)}, s32[]{:S(2)}) async-start(s8[6291456]{0:T(1024)(128)(4,1)} %bitcast.89), calls=%async_computation.1 | async-start | bytes 8388608
  662.9 3.1 slice-start.1
Sparse Core Ops, SparseCore 0:
  506.5 113.8 all-reduce.6

commit v6 on v5

--- a/solution.py
+++ b/solution.py
@@ -298,11 +298,13 @@
     def mine(self, turn):
         return self.owned.at[turn, self.g.hi * self.g.los + self.g.lo]
 
-    def a(self, turn):
+    def a(self, turn, waited=False):
         g, s = self.g, self.s
         far = 1 - g.hi
-        self.loads[turn].wait()
-        s.arrived(self.ra.at[turn], self.sa.at[turn], self.partner())
+        if self.loads[turn] is not None:
+            self.loads[turn].wait()
+        if not waited:
+            s.arrived(self.ra.at[turn], self.sa.at[turn], self.partner())
 
         def one(q, carry):
             line = self.owned.at[turn, q]
@@ -545,27 +547,40 @@
     return jnp.concatenate([first] + parts[1:], axis=1), *others
 
 
-def deliver_kernel(reps, shards, p_ref, w_ref, out_ref, ws_ref, line_own, rl, rr, sl, sr, sems, line_loads, wr, keep_sem, *rest):
+def deliver_kernel(reps, shards, split, *refs):
+    (
+        gqkv_ref, small_ref, qsum_ref, ksum_ref, wo_sum_ref, w_in, hid_in, xs_in,
+        out_ref, q_out, rest_out, wo_out,
+        w_ref, hid_ref, xs_ref, both, acc, ws_ref, wo_all, line_own, rl, rr, sl, sr,
+        sems, wr, small_sem, keep_sem, ls, *rest,
+    ) = refs
+    q_cols, experts, part = split
     g = Grid(reps, shards).here()
     s = Sends(sems)
-    n = g.shards
-    gather_refs, scatter_refs = rest[:4], rest[4:]
-    cols = w_ref.shape[-1]
-    first = cols // 2 // 128 * 128
-    spans = {0: pl.ds(0, first), 1: pl.ds(first, cols - first), None: pl.ds(0, cols)}
+    n, places = g.shards, g.places
+    gather_refs, wo_refs, scatter_refs = rest[:4], rest[4:8], rest[8:]
+    length = out_ref.shape[0]
+    total, cols = ws_ref.shape[-1], gqkv_ref.shape[1]
+    piece = ws_ref.shape[2]
+    deep = hid_ref.shape[1] // n
+    first = total // 2 // 128 * 128
+    spans = {0: pl.ds(0, first), 1: pl.ds(first, total - first), None: pl.ds(0, total)}
+    owned = wo_sum_ref.shape[0]
+    halves = {0: pl.ds(0, owned // 2), 1: pl.ds(owned // 2, owned // 2), None: pl.ds(0, owned)}
     order = g.nearest()[::-1]
-    scatter = PlaneScatter(
-        g, s, lambda turn, core: w_ref.at[turn, :, core], lambda part: (slice(None), spans[part]), *scatter_refs
+    scatter = PlaneScatter(g, s, None, lambda p: (slice(None), spans[p]), both.at[g.core], *scatter_refs)
+    scatter.loads = [None] * n
+    gather = PlaneGather(
+        g, s, lambda u, hi, lo, core, p: ws_ref.at[u, g.rep_of(hi, lo, core), :, spans[p]], *gather_refs
     )
-    gather = PlaneGather(
-        g, s, lambda u, hi, lo, core, part: ws_ref.at[u, g.rep_of(hi, lo, core), :, spans[part]], *gather_refs
-    )
-    scatter.load(n)
-    loads = []
-    for turn in range(n):
-        load = pltpu.make_async_copy(p_ref.at[order[turn]], line_own.at[turn], line_loads.at[turn])
-        load.start()
-        loads.append(load)
+    out_weight = PlaneGather(g, s, lambda u, hi, lo, core, p: wo_all.at[g.rep_of(hi, lo, core), halves[p]], *wo_refs)
+    loads = [
+        pltpu.make_async_copy(hid_in, hid_ref, ls.at[0]),
+        pltpu.make_async_copy(w_in, w_ref, ls.at[1]),
+        pltpu.make_async_copy(xs_in, xs_ref, ls.at[2]),
+    ]
+    for copy in loads:
+        copy.start()
     barrier = pltpu.get_barrier_semaphore()
     peers = [g.device(g.r, (g.z + step) % n) for step in range(1, n)]
     peers += [g.device(g.rep_of(g.hi, g.other_lo(step), g.core), g.z) for step in range(1, g.los)]
@@ -573,13 +588,54 @@
     for peer in peers:
         pl.semaphore_signal(barrier, inc=1, device_id=peer, device_id_type=pl.DeviceIdType.MESH)
     pl.semaphore_wait(barrier, len(peers))
-
+    out_weight.own(0, lambda p: wo_sum_ref.at[halves[p]])
+
+    ra = scatter.ra
+    loads[0].wait()
+    for zp in range(n):
+        grad = t_dot(hid_ref[:, zp * deep : (zp + 1) * deep], gqkv_ref[...]).astype(bf16)
+        for place in range(places):
+            for core in range(2):
+                row = (place * 2 + core) * piece
+                both[core, zp, place, :, 0:cols] = grad[row : row + piece]
+        src = both.at[1 - g.core, zp, :, :, pl.ds(0, cols)]
+        s.start(src, ra.at[zp, :, :, pl.ds(0, cols)], scatter.sa.at[zp], scatter.partner())
+
+    loads[1].wait()
+    loads[2].wait()
+    lane = lax.broadcasted_iota(jnp.int32, (length, total - cols), 1)
+    marked = jnp.where(lane == experts, 1.0, 0.0).astype(bf16)
+
+    def line(turn):
+        send_line(g, s, order[turn], line_own.at[turn], out_ref, rl, rr, sl, sr, last=turn == n - 1)
+
+    acc[...] = small_ref[...]
     for turn in range(n):
-        scatter.to_partner(turn)
-
-    def line(turn):
-        loads[turn].wait()
-        send_line(g, s, order[turn], line_own.at[turn], out_ref, rl, rr, sl, sr, last=turn == n - 1)
+        at = pl.ds(pl.multiple_of(order[turn] * length, length), length)
+        share = dot_t(gqkv_ref[at, :], w_ref[...])
+        line_own[turn] = share.astype(bf16)
+        _, unit = unit_of(xs_ref[at, :].astype(f32))
+        acc[...] += t_dot((share * unit).astype(bf16), marked)
+        if turn == 0:
+            line(0)
+    for i, ref in ((2, qsum_ref), (3, ksum_ref)):
+        width = ref.shape[1]
+        columns = jnp.broadcast_to(ref[...], (total - cols, width)).T
+        mask = lax.broadcasted_iota(jnp.int32, (part, total - cols), 1) == experts + i
+        for zp in range(n):
+            acc[zp * deep : zp * deep + part] += jnp.where(mask, columns[zp * part : (zp + 1) * part], 0.0)
+    for zp in range(n):
+        for place in range(places):
+            for core in range(2):
+                row = zp * deep + (place * 2 + core) * piece
+                both[core, zp, place, :, cols:total] = acc[row : row + piece].astype(bf16)
+    tail = pl.ds(cols, total - cols)
+    s.start(both.at[1 - g.core, :, :, :, tail], ra.at[:, :, :, tail], small_sem.at[0], scatter.partner())
+
+    def from_partner(turn):
+        if turn == 0:
+            s.arrived(ra.at[:, :, :, tail], small_sem.at[0], scatter.partner())
+        s.arrived(ra.at[turn, :, :, pl.ds(0, cols)], scatter.sa.at[turn], scatter.partner())
 
     def owner(turn):
         scatter.c(turn)
@@ -589,62 +645,103 @@
         s.start(scatter.mine(turn), dst, wr.at[g.z], g.device(g.r, turn), lambda: g.z != turn)
         pl.when(g.z == turn)(keep.wait)
 
-    line(0)
     for turn in range(n + 2):
         if turn < n:
-            scatter.a(turn)
+            from_partner(turn)
+            scatter.a(turn, waited=True)
+        if turn == 0:
+            out_weight.first(0)
+        if turn == 1:
+            out_weight.second(0)
         if 0 <= turn - 1 < n:
             scatter.b(turn - 1)
         if 1 <= turn < n - 1:
             line(turn)
         if 0 <= turn - 2 < n:
             owner(turn - 2)
+    out_weight.from_partner(0)
+    keep = pltpu.make_async_copy(wo_sum_ref, wo_all.at[g.r], keep_sem.at[0])
+    keep.start()
+    keep.wait()
+    saves = [pltpu.make_async_copy(wo_all, wo_out, ls.at[3])]
+    saves[0].start()
     gather.own(g.z)
 
-    def unit(step):
+    def unit_at(step):
         return (g.z + n - step) % n
 
     for step in range(1, n):
-        u = unit(step)
+        u = unit_at(step)
         s.arrived(ws_ref.at[u, g.r], wr.at[u], g.device(g.r, u))
         gather.own(u)
-        gather.first(unit(step - 1))
+        gather.first(unit_at(step - 1))
         if step > 1:
-            gather.second(unit(step - 2))
-    gather.first(unit(n - 1))
-    gather.second(unit(n - 2))
-    gather.second(unit(n - 1))
+            gather.second(unit_at(step - 2))
+    gather.first(unit_at(n - 1))
+    gather.second(unit_at(n - 2))
+    gather.second(unit_at(n - 1))
     line(n - 1)
     for step in range(n):
-        gather.from_partner(unit(step))
+        u = unit_at(step)
+        gather.from_partner(u)
+        q_span = pl.ds(pl.multiple_of(u * q_cols, 128), q_cols)
+        saves += [
+            pltpu.make_async_copy(ws_ref.at[u, :, :, pl.ds(0, q_cols)], q_out.at[:, :, q_span], ls.at[4 + 2 * step]),
+            pltpu.make_async_copy(
+                ws_ref.at[u, :, :, pl.ds(q_cols, total - q_cols)], rest_out.at[u], ls.at[5 + 2 * step]
+            ),
+        ]
+        saves[-1].start()
+        saves[-2].start()
+    for copy in saves:
+        copy.wait()
     s.drain()
 
 
-def deliver(reps, shards, p, w, ident):
+def deliver(reps, shards, q_cols, experts, part, gqkv, small, qsum, ksum, wo_sum, w, hid, xs, ident):
     g = Grid(reps, shards)
     n = shards
-    dma = pltpu.SemaphoreType.DMA
-    _, rows, width = p.shape
-    _, _, piece, cols = w.shape
-    first = cols // 2 // 128 * 128
+    dma, v = pltpu.SemaphoreType.DMA, pltpu.VMEM
+    width = hid.shape[1]
+    rows = hid.shape[0] // n
+    cols = gqkv.shape[1]
+    total = cols + small.shape[1]
+    piece = width // n // reps
+    first = total // 2 // 128 * 128
     return pl.pallas_call(
-        functools.partial(deliver_kernel, reps, shards),
-        out_shape=(jax.ShapeDtypeStruct((rows, width), f32), jax.ShapeDtypeStruct(w.shape, w.dtype)),
-        in_specs=[hbm, hbm],
-        out_specs=(vmem, vmem),
-        scratch_shapes=[pltpu.VMEM(p.shape, p.dtype)]
-        + line_scratch(n, (rows, width), p.dtype)
+        functools.partial(deliver_kernel, reps, shards, (q_cols, experts, part)),
+        out_shape=(
+            jax.ShapeDtypeStruct((rows, width), f32),
+            jax.ShapeDtypeStruct((reps, piece, n * q_cols), bf16),
+            jax.ShapeDtypeStruct((n, reps, piece, total - q_cols), bf16),
+            jax.ShapeDtypeStruct((reps,) + wo_sum.shape, bf16),
+        ),
+        in_specs=[vmem] * 5 + [hbm] * 3,
+        out_specs=(vmem, hbm, hbm, hbm),
+        scratch_shapes=[
+            v(w.shape, bf16),
+            v(hid.shape, bf16),
+            v(xs.shape, bf16),
+            v((2, n, g.places, piece, total), bf16),
+            v(small.shape, f32),
+            v((n, reps, piece, total), bf16),
+            v((reps,) + wo_sum.shape, bf16),
+            v((n, rows, width), bf16),
+        ]
+        + line_scratch(n, (rows, width), bf16)
         + [
-            dma((PlaneGather.sends(g, n) + PlaneScatter.sends(g, n) + 3 * n,)),
-            dma((n,)),
+            dma((PlaneGather.sends(g, n) + PlaneGather.sends(g, 1) + PlaneScatter.sends(g, n) + 4 * n + 1,)),
             dma((n,)),
             dma((1,)),
+            dma((1,)),
+            dma((4 + 2 * n,)),
         ]
         + PlaneGather.scratch(g, n)
-        + PlaneScatter.scratch(g, n, (piece, cols), ((piece, first), (piece, cols - first)), w.dtype),
+        + PlaneGather.scratch(g, 1)
+        + PlaneScatter.scratch(g, n, (piece, total), ((piece, first), (piece, total - first)), bf16)[1:],
         compiler_params=params(ident),
         name="deliver",
-    )(p, w.reshape(n, g.places, 2, piece, cols))
+    )(gqkv, small, qsum, ksum, wo_sum, w, hid, xs)
 
 
 def turned(x, cosine, sine):
@@ -826,17 +923,29 @@
 
 def attend_back_kernel(reps, shards, heads, *refs):
     (
-        ga_ref, qkv_ref, wo_ref, qg_ref, kg_ref, cos_ref, sin_ref, bias_ref, p_ref,
-        gas_ref, gqkv_ref, qsum_ref, ksum_ref, out_ref,
-        gm, zr, sems, keep_sem, *scatter_refs,
+        ga_ref, qg_ref, kg_ref, cos_ref, sin_ref, bias_ref, qkv_in, wo_in, att_in, p_ref,
+        gqkv_ref, qsum_ref, ksum_ref, out_ref, wo_sum_ref,
+        gas_ref, qkv_ref, wo_ref, att_ref, both, gm, zr, sems, ls, *scatter_refs,
     ) = refs
     g = Grid(reps, shards).here()
     s = Sends(sems)
-    n = g.shards
-    scatter = ScatterAll(g, s, p_ref, out_ref, *scatter_refs)
+    n, rows = g.shards, ga_ref.shape[0]
+    half = both.shape[3] // 2
+    count = len(scatter_refs) - 11
+    scatter = ScatterAll(g, s, p_ref, out_ref, *scatter_refs[:count])
+    own = both.at[g.core]
+    owner = PlaneScatter(
+        g, s, lambda turn, core: both.at[core, turn], lambda part: (pl.ds(part * half, half),), own, *scatter_refs[count:]
+    )
     scatter.load()
-    keep = pltpu.make_async_copy(ga_ref, gas_ref.at[g.z], keep_sem.at[0])
-    keep.start()
+    loads = [
+        pltpu.make_async_copy(wo_in, wo_ref, ls.at[0]),
+        pltpu.make_async_copy(qkv_in, qkv_ref, ls.at[1]),
+        pltpu.make_async_copy(att_in, att_ref, ls.at[2]),
+    ]
+    keep = pltpu.make_async_copy(ga_ref, gas_ref.at[g.z], ls.at[3])
+    for copy in loads + [keep]:
+        copy.start()
     qsum_ref[...] = jnp.zeros(qsum_ref.shape, f32)
     ksum_ref[...] = jnp.zeros(ksum_ref.shape, f32)
     greet_all(g)
@@ -849,45 +958,78 @@
             s.arrived(dst, zr.at[zp], g.device(g.r, zp))
         pass_along(g, s, zp, dst if turn else ga_ref, dst, zr)
 
+    def out_weight():
+        width = ga_ref.shape[1]
+        block = att_ref.shape[2] // g.reps
+        grads = gas_ref[...].reshape(n * rows, width)
+        for place in range(g.places):
+            for core in range(2):
+                at = (place * 2 + core) * block
+                mixed = att_ref[:, :, at : at + block].reshape(n * rows, block)
+                both[core, 0, place] = t_dot(mixed, grads).astype(bf16)
+
     line(0)
     scatter.to_partner()
-    keep.wait()
+    for copy in loads + [keep]:
+        copy.wait()
     for turn in range(n):
         scatter.step(turn)
         if turn + 1 < n:
             line(turn + 1)
+        else:
+            out_weight()
+            owner.to_partner(0)
         attend_back_block(
             order[turn], heads, gas_ref, qkv_ref, wo_ref, qg_ref, kg_ref, cos_ref, sin_ref, bias_ref,
             gm, gqkv_ref, qsum_ref, ksum_ref,
         )
+    owner.loads = [None]
     scatter.step(n)
+    owner.a(0)
     scatter.step(n + 1)
+    owner.b(0)
+    owner.c(0)
+    wo_sum_ref[...] = own[0, g.hi * g.los + g.lo]
     s.drain()
 
 
-def attend_back(reps, shards, heads, ga, qkv, wo, qg, kg, cosine, sine, bias, p, ident):
+def attend_back(reps, shards, heads, ga, qkv, wo, att, qg, kg, cosine, sine, bias, p, ident):
     g = Grid(reps, shards)
     dma, v = pltpu.SemaphoreType.DMA, pltpu.VMEM
     n = shards
     rows, width = ga.shape
     out_width = p.shape[2]
+    owned = wo.shape[0] // reps
     row = jax.ShapeDtypeStruct(qg.shape, f32)
+    block = (owned, width)
+    half = (owned // 2, width)
     return pl.pallas_call(
         functools.partial(attend_back_kernel, reps, shards, heads),
         out_shape=(
-            jax.ShapeDtypeStruct((n, rows, width), bf16),
             jax.ShapeDtypeStruct(qkv.shape, bf16),
             row,
             row,
             jax.ShapeDtypeStruct((rows, out_width), f32),
+            jax.ShapeDtypeStruct(block, bf16),
         ),
-        in_specs=[vmem] * 8 + [hbm],
+        in_specs=[vmem] * 6 + [hbm] * 4,
         out_specs=(vmem,) * 5,
-        scratch_shapes=[v((rows, wo.shape[0]), bf16), dma((n,)), dma((ScatterAll.sends(g) + 2 * n,)), dma((1,))]
-        + ScatterAll.scratch(g, (rows, out_width), p.dtype),
+        scratch_shapes=[
+            v((n, rows, width), bf16),
+            v(qkv.shape, f32),
+            v(wo.shape, bf16),
+            v(att.shape, bf16),
+            v((2, 1, g.places) + block, bf16),
+            v((rows, wo.shape[0]), bf16),
+            dma((n,)),
+            dma((ScatterAll.sends(g) + PlaneScatter.sends(g, 1) + 2 * n,)),
+            dma((4,)),
+        ]
+        + ScatterAll.scratch(g, (rows, out_width), p.dtype)
+        + PlaneScatter.scratch(g, 1, block, (half, half), bf16)[1:],
         compiler_params=params(ident),
         name="attend_back",
-    )(ga, qkv, wo, qg, kg, cosine, sine, bias, p.reshape(g.places, 2, n, rows, out_width))
+    )(ga, qg, kg, cosine, sine, bias, qkv, wo, att, p.reshape(g.places, 2, n, rows, out_width))
 
 
 def tables_of(segment_column, segment_row, frequency):
@@ -991,9 +1133,9 @@
         plane.first(unit(step))
         if step:
             plane.second(unit(step - 1))
-        if 2 + step < n:
+        if 2 + step < n - 1:
             line(2 + step)
-        if step == max(0, n - 3):
+        if step == max(0, n - 4):
             pass_along(g, s, g.z, cot_ref, gather.own(), gather.zr)
     plane.second(unit(n - 1))
     for step in range(n):
@@ -1001,20 +1143,19 @@
     for copy in keeps[:3]:
         copy.wait()
 
-    outs = [pltpu.make_async_copy(w_ref, w_out, out_sems.at[0]), pltpu.make_async_copy(xs_ref, xs_out, out_sems.at[1])]
-    for copy in outs:
-        copy.start()
     length = x_ref.shape[0]
+    smalls_late = order[n - 1]
+    s.arrived(smalls_ref.at[smalls_late], mr.at[smalls_late], g.device(g.r, smalls_late))
+    pass_along(g, s, smalls_late, smalls_ref.at[smalls_late], smalls_ref.at[smalls_late], mr)
     for zp in range(n):
-        rows = smalls_ref[zp].astype(f32)
-        gains_ref[:, zp * deep : (zp + 1) * deep] = rows.T[experts : experts + 8]
+        gains_ref[:, zp * deep : (zp + 1) * deep] = smalls_ref[zp].astype(f32)[experts : experts + 8]
     for i in range(2):
         qk_ref[i : i + 1] = sum(gains_ref[2 + i : 3 + i, zp * deep : zp * deep + head_dim] for zp in range(n))
 
     def compute(turn):
         zp = order[turn]
-        column = smalls_ref[zp, 0:length, experts + 4 : experts + 5].astype(f32)
         row = gains_ref[4:5, pl.ds(pl.multiple_of(zp * deep, 128), length)]
+        column = jnp.broadcast_to(row, (length, length)).T
         cos_ref[zp], sin_ref[zp], bias_ref[zp] = tables_of(column, row, freq_ref[...])
         attend_block(
             zp, heads, xs_ref, w_ref, wo_ref, gains_ref.at[0:1], qk_ref.at[0:1], qk_ref.at[1:2],
@@ -1024,12 +1165,23 @@
     def sums(turn):
         send_line(g, s, order[turn], own.at[turn], out_ref, rl, rr, sl, sr, last=turn == 0)
 
+    farthest = order[n - 1]
+    between = lambda: (g.z > 0) & (g.z + 1 < n)
+    at_end = lambda: (g.z == 0) | (g.z + 1 == n)
+    s.arrived(xs_ref.at[farthest], xr.at[farthest], g.device(g.r, farthest), between)
+    pass_along(g, s, farthest, xs_ref.at[farthest], xs_ref.at[farthest], xr)
+    compute(0)
+    s.arrived(xs_ref.at[farthest], xr.at[farthest], g.device(g.r, farthest), at_end)
+    outs = [pltpu.make_async_copy(w_ref, w_out, out_sems.at[0]), pltpu.make_async_copy(xs_ref, xs_out, out_sems.at[1])]
+    for copy in outs:
+        copy.start()
     compute(n - 1)
     sums(n - 1)
     gather.first(0)
     gather.line(1)
     for turn in range(n - 2, -1, -1):
-        compute(turn)
+        if turn > 0:
+            compute(turn)
         at = n - 1 - turn
         if turn > 0:
             sums(turn)
@@ -1380,27 +1532,27 @@
     chunks = max(1, devices // 32)
     part = head_dim // shards
 
-    def column(values, rows=deep):
-        return jnp.pad(values.reshape(-1, 1), ((0, rows - values.size), (0, 0)))
-
-    spot = lax.broadcasted_iota(jnp.int32, (deep, 1), 0) // part == z
+    spot = lax.broadcasted_iota(jnp.int32, (1, deep), 1) // part == z
+
+    def row_of(values):
+        return jnp.pad(values.reshape(1, -1), ((0, 0), (0, deep - values.size)))
 
     def spotted(values):
-        return jnp.where(spot, jnp.tile(column(values, part), (deep // part, 1)), 0)
+        return jnp.where(spot, jnp.tile(values.reshape(1, part), (1, deep // part)), 0)
 
     small = jnp.concatenate(
         [
-            w_router,
-            column(attn_gain),
-            column(ffn_gain),
+            w_router.T,
+            row_of(attn_gain),
+            row_of(ffn_gain),
             spotted(query_gain),
             spotted(key_gain),
-            column(segments[0].astype(bf16)),
+            row_of(segments[0].astype(bf16)),
         ],
-        axis=1,
+        axis=0,
     )
+    small = jnp.pad(small, ((0, -(-(experts + 8) // 16) * 16 - small.shape[0]), (0, 0)))
     small_cols = -(-(experts + 8) // 128) * 128
-    small = jnp.pad(small, ((0, 0), (0, small_cols - small.shape[1])))
     half = rope_base ** (-2.0 * jnp.arange(head_dim // 2, dtype=f32) / head_dim)
     frequency = jnp.concatenate([half, half]).reshape(1, head_dim)
     head_sizes = (my_heads, my_kv, head_dim)
@@ -1412,7 +1564,7 @@
         reps, shards, head_sizes, layout, tokens, cotangent, small, frequency,
         w_query, key_weight, value_weight, w_out, 1,
     )
-    router_full = small_all[:, :, :experts].reshape(width, experts)
+    router = small_all[:, :experts].transpose(1, 0, 2).reshape(experts, width)
     gain_one, gain_two = gains[0:1], gains[1:2]
     qgain, kgain = qk_gains[0:1], qk_gains[1:2]
     own_tokens = tokens.astype(f32)
@@ -1421,7 +1573,7 @@
     inverse_two = inverse_rms(resid)
     normed_two = resid * inverse_two
     hidden_two = (normed_two * gain_two).astype(bf16)
-    logits = matmul(hidden_two, router_full)
+    logits = matmul(hidden_two, router, ((1,), (1,)))
     gate_probs = jax.nn.softmax(logits, axis=-1)
     chosen = jnp.any(routes[:, :, None] == jnp.arange(experts, dtype=jnp.int32)[None, None, :], axis=1)
     picked = jnp.where(chosen, gate_probs, 0.0)
@@ -1444,67 +1596,48 @@
     grad_mix = mixes[:, 0, :].T
     grad_picked = jnp.where(chosen, grad_mix - jnp.sum(grad_mix * mix, axis=-1, keepdims=True), 0.0) / picked_total
     grad_logits = (gate_probs * (grad_picked - jnp.sum(grad_picked * picked, axis=-1, keepdims=True))).astype(bf16)
-    grad_hidden = grad_hidden + matmul(grad_logits, router_full, ((1,), (1,)))
+    grad_hidden = grad_hidden + matmul(grad_logits, router)
     grad_ffn_gain = jnp.sum(grad_hidden * normed_two, axis=0)
     grad_resid = grad_out + norm_back(grad_hidden, normed_two, inverse_two, gain_two)
     grad_w_router = matmul(hidden_two, grad_logits, ((0,), (0,)))
 
     fused = width // chunks
-    grad_attn, grad_qkv, grad_query_gain, grad_key_gain, moe = attend_back(
-        reps, shards, head_sizes, grad_resid.astype(bf16), qkv, w_out, qgain, kgain, cosine, sine, bias,
+    grad_qkv, grad_query_gain, grad_key_gain, moe, out_grad = attend_back(
+        reps, shards, head_sizes, grad_resid.astype(bf16), qkv, w_out, attn_out, qgain, kgain, cosine, sine, bias,
         sums[:, :, :fused], 5,
     )
     if chunks > 1:
         rest = scatter_wide(reps, shards, sums[:, :, fused:], None, None, 16, chunks - 1)
         moe = jnp.concatenate([moe, rest], axis=1)
     output = (resid + moe).astype(bf16)
-    grad_attn = grad_attn.reshape(shards * length, width)
-    grad_qkv = grad_qkv.reshape(shards * length, cols)
-    grad_w_out = matmul(attn_out.reshape(shards * length, q_cols), grad_attn, ((0,), (0,)))
-    owned_out = lax.psum(grad_w_out.astype(bf16), "rep").astype(f32)
-    hidden_in = hidden_in.reshape(shards * length, width)
-    _, normed_one = unit_of(block_tokens.reshape(shards * length, width).astype(f32))
-    grad_part = matmul(grad_qkv, w_in, ((1,), (1,)))
-    grad_attn_gain = jnp.sum(grad_part * normed_one, axis=0)
-    grad_w_in = matmul(hidden_in, grad_qkv, ((0,), (0,)))
-
-    def spread(values):
-        return jnp.pad(values.reshape(shards, part), ((0, 0), (0, deep - part))).reshape(width, 1)
 
     small_grads = jnp.concatenate(
-        [
-            grad_w_router,
-            grad_attn_gain.reshape(width, 1),
-            grad_ffn_gain.reshape(width, 1),
-            spread(grad_query_gain),
-            spread(grad_key_gain),
-        ],
-        axis=1,
+        [grad_w_router, jnp.zeros((width, 1), f32), grad_ffn_gain.reshape(width, 1)], axis=1
     )
     small_grads = jnp.pad(small_grads, ((0, 0), (0, small_cols - small_grads.shape[1])))
-    sent = jnp.concatenate([grad_w_in, small_grads], axis=1).astype(bf16)
-    sent = sent.reshape(shards, reps, piece, cols + small_cols)
-    grad_part = grad_part.astype(bf16).reshape(shards, length, width)
-    grad_hidden_in, sent = deliver(reps, shards, grad_part, sent, 6)
-    sent = sent.reshape(shards, deep, cols + small_cols)
-    own_inverse = inverse_rms(own_tokens)
-    own_normed = own_tokens * own_inverse
+    grad_hidden_in, sent_q, sent, sent_out = deliver(
+        reps, shards, q_cols, experts, part, grad_qkv.reshape(shards * length, cols), small_grads,
+        grad_query_gain, grad_key_gain, out_grad, w_in, hidden_in.reshape(shards * length, width),
+        block_tokens.reshape(shards * length, width), 6,
+    )
+    own_inverse, own_normed = unit_of(own_tokens)
     grad_tokens = grad_resid + norm_back(grad_hidden_in, own_normed, own_inverse, gain_one)
+    sent = sent.reshape(shards, deep, 2 * kv_cols + small_cols)
 
     def joined(values):
         if shared_by > 1:
             values = values.astype(f32).reshape(-1, shared_by, deep, values.shape[-1]).sum(axis=1)
         return values.transpose(1, 0, 2).reshape(deep, -1).astype(f32)
 
-    owned_small = jnp.sum(sent[:, :, cols:].astype(f32), axis=0)
+    owned_small = jnp.sum(sent[:, :, 2 * kv_cols :].astype(f32), axis=0)
     return (
         output,
         grad_tokens,
         owned_small[:, experts],
-        sent[:, :, :q_cols].transpose(1, 0, 2).reshape(deep, -1).astype(f32),
-        joined(sent[:, :, q_cols : q_cols + kv_cols]),
-        joined(sent[:, :, q_cols + kv_cols : cols]),
-        owned_out,
+        sent_q.reshape(deep, -1).astype(f32),
+        joined(sent[:, :, :kv_cols]),
+        joined(sent[:, :, kv_cols : 2 * kv_cols]),
+        sent_out.reshape(w_out.shape).astype(f32),
         owned_small[:part, experts + 2],
         owned_small[:part, experts + 3],
         owned_small[:, experts + 1],

time: 685 us -> 643 us (0.939)
  matrix products: 21.8 us -> 2.27 us
  between operations: 14.8 us -> 1.31 us
    dot_general x6 -> x3, matrix products: 21.8 us -> 2.27 us  [matmul(): return lax.dot_general(a, b, (dims, ((), ())), preferred_element_type=f32)]
    pallas_call x1, Pallas kernels: 104 us -> 114 us  [deliver(): pl.pallas_call(functools.partial(deliver_kernel, reps, shards, (q_cols, e...]
    unnamed x41 -> x33, local copies, waits for them, and re-layouts: 15 us -> 13.3 us
  transfers between devices with their start and end apart: 1 -> 0, of which waited for: 0 -> 0; matrix products, arithmetic and copies ran while one was open for 6% -> 0% of each run, Pallas kernels for 15% -> 0%
where the time goes in v6:
time: 643 us; the launch traced here: 635 us
  Pallas kernels  582 us (91%)
  local copies, waits for them, and re-layouts  26.8 us (4%)
  other arithmetic  23 us (4%)
    pallas_call x1, Pallas kernels, front(): pl.pallas_call(functools.partial(front_kernel, reps, shards, heads, layou...  145 us
    pallas_call x1, Pallas kernels, deliver(): pl.pallas_call(functools.partial(deliver_kernel, reps, shards, (q_cols, e...  114 us
    pallas_call x1, Pallas kernels, experts_all(): pl.pallas_call(functools.partial(experts_kernel, reps, shards, capacity,...  113 us
    pallas_call x1, Pallas kernels, scatter_all(): pl.pallas_call(functools.partial(scatter_all_kernel, reps, shards, slabbe...  106 us
    pallas_call x1, Pallas kernels, attend_back(): pl.pallas_call(functools.partial(attend_back_kernel, reps, shards, heads)...  103 us
    unnamed x33, local copies, waits for them, and re-layouts  13.3 us

profile of v6, /device:TPU:17, one launch (start us, length us, event | category | flops | bytes accessed | tf_op | source)
XLA Modules:
  0.0 635.3 jit_solution(1580937089798743221)
XLA Ops:
  0.6 0.7 convert_element_type.65
  1.3 0.1 pad.16.clone
  1.4 0.6 maximum_bitcast_fusion.refs_3_
  2.0 0.7 reshape.216
  2.7 0.7 reshape.217
  3.4 0.7 fusion.7
  4.1 0.7 tile.16
  4.7 0.1 tile.17
  4.8 0.7 tile.18
  5.5 0.1 tile.19
  5.6 0.8 concatenate.9
  6.4 0.6 pad.13.refs_2_
  7.0 145.2 %front.1 = (bf16[4,48,512]{2,1,0:T(8,128)(2,1)}, f32[8,2048]{1,0:T(8,128)}, f32[8,128]{1,0:T(8,128)}, f32[4,128,128]{2,1,0:T(8,128)}, f32[4,128,128]{2,1,0:T(8,1...) custom-call(bf16[128,2048]{1,0:T(8,128)(2,1)} %refs_0_.1, ...), custom_call_target="tpu_custom_call" | custom-call | tf_op jit(solution)/shard_map/front/pallas_call | solution.py:1218
  152.2 0.0 copy-done.3
  152.2 1.5 multiply_reduce_fusion.2
  153.8 1.3 fusion.15
  155.0 0.9 fusion.14
  156.0 0.9 slice_bitcast_fusion
  156.9 0.2 multiply_convert_fusion.refs_0_
  157.1 0.0 copy-start.1
  157.1 0.3 fusion.16
  157.5 0.7 broadcast_in_dim.47.refs_1_
  158.1 0.0 copy-done.1
  158.1 112.7 %experts_all.1 = (f32[32,8,128]{2,1,0:T(8,128)}, bf16[4,2,4,128,2048]{4,3,2,1,0:T(8,128)(2,1)}, bf16[4,2,4,128,2048]{4,3,2,1,0:T(8,128)(2,1)}, bf16[8,256,2048]{...) custom-call(bf16[128,2048]{1,0:T(8,128)(2,1)} %copy-done.1, ...), custom_call_target="tpu_custom_call" | custom-call | tf_op jit(solution)/shard_map/experts_all/pallas_call | solution.py:1443
  270.9 0.0 copy-start.2
  270.9 106.4 %scatter_all.1 = (f32[128,2048]{1,0:T(8,128)}, f32[32,8,128]{2,1,0:T(8,128)}, f32[2048,768]{1,0:T(8,128)}, f32[2048,768]{1,0:T(8,128)}, f32[768,2048]{1,0:T(8,128)}) custom-call(bf16[4,2,4,128,2048]{4,3,2,1,0:T(8,128)(2,1)} %get-tuple-element.53.refs_0_, f32[32,8,128]{2,1,0:T(8,128)} %get-tuple-element.54.refs_1_, bf16[2048,2048]{1,0:T(8,128)(2,1)} %bitcast.62, ...), custom_call_target="tpu_custom_call" | custom-call | tf_op jit(solution)/shard_map/scatter_all/pallas_call | solution.py:522
  377.3 0.0 copy-start.5
  377.3 1.0 slice.44
  378.3 0.0 copy-done.2
  378.4 0.2 fusion.17
  378.6 1.8 multiply_reduce_fusion
  380.3 0.0 copy-start
  380.3 0.1 pad_maximum_fusion
  380.4 0.9 copy-done
  381.3 0.0 copy-done.5
  381.3 1.1 fusion.13.refs_0_
  382.5 103.4 %attend_back.1 = (bf16[4,128,1280]{2,1,0:T(8,128)(2,1)}, f32[1,128]{1,0:T(1,128)}, f32[1,128]{1,0:T(1,128)}, f32[128,2048]{1,0:T(8,128)}, bf16[128,2048]{1,0:T(8,128)(2,1)}) custom-call(bf16[128,2048]{1,0:T(8,128)(2,1)} %fusion.13.refs_0_, f32[1,128]{1,0:T(1,128)} %get-tuple-element.142.refs_1_, f32[1,128]{1,0:T(1,128)} %get-tuple-element.141.refs_2_, ...), custom_call_target="tpu_custom_call" | custom-call | tf_op jit(solution)/shard_map/attend_back/pallas_call | solution.py:1006
  485.8 0.4 copy.53
  486.2 1.0 pad.14.refs_1_
  487.2 114.2 %deliver.1 = (f32[128,2048]{1,0:T(8,128)}, bf16[8,64,4096]{2,1,0:T(8,128)(2,1)}, bf16[4,8,64,384]{3,2,1,0:T(8,128)(2,1)}, bf16[8,128,2048]{2,1,0:T(8,128)(2,1)}) custom-call(bf16[512,1280]{1,0:T(8,128)(2,1)} %bitcast.84, f32[2048,128]{1,0:T(8,128)} %pad.14.refs_1_, f32[1,128]{1,0:T(1,128)} %get-tuple-element.71.refs_2_, f32[1,128]{1,0:T(1,128)} %get-tuple-element.72.refs_3_, ...), custom_call_target="tpu_custom_call" | custom-call | tf_op jit(solution)/shard_map/deliver/pallas_call | solution.py:711
  601.4 0.0 copy-done.4
  601.4 1.5 fusion.2
  603.0 3.6 fusion.5
  606.6 1.1 convert_reduce_fusion
  607.8 0.7 slice_reduce_fusion.2
  608.5 0.9 slice_reduce_fusion
  609.4 0.7 copy.56
  610.1 1.5 convert_bitcast_fusion
  611.6 1.1 copy.62
  612.7 1.1 copy.63
  613.9 0.0 copy-done.7
  613.9 5.5 bitcast_convert_fusion.1
  619.3 0.0 copy-done.6
  619.3 4.7 bitcast_convert_fusion
  624.1 0.0 slice-done.4
  624.1 0.0 slice-done.5
  624.1 0.0 slice-start
  624.1 3.2 copy.67
  627.3 0.0 slice-done.2
  627.3 0.0 slice-done.3
  627.3 3.2 copy.68
  630.5 0.9 slice-done
  631.4 0.8 slice-done.1
  632.1 2.7 copy.69
  (25 shorter events, 0.2 us)
Async XLA Ops:
  7.0 145.2 %copy-start.3 = (bf16[128,2048]{1,0:T(8,128)(2,1)S(1)}, bf16[128,2048]{1,0:T(8,128)(2,1)}, u32[]{:S(2)}) copy-start(bf16[128,2048]{1,0:T(8,128)(2,1)} %refs_0_.1) | copy-start | bytes 1572868
  157.1 1.1 copy-start.1
  270.9 107.5 %copy-start.2 = (bf16[128,2048]{1,0:T(8,128)(2,1)S(1)}, bf16[128,2048]{1,0:T(8,128)(2,1)}, u32[]{:S(2)}) copy-start(bf16[128,2048]{1,0:T(8,128)(2,1)} %copy-done.1) | copy-start | bytes 1572868
  377.3 4.0 copy-start.5
  380.3 1.0 copy-start
  487.2 114.2 %copy-start.4 = (bf16[128,2048]{1,0:T(8,128)(2,1)S(1)}, bf16[128,2048]{1,0:T(8,128)(2,1)}, u32[]{:S(2)}) copy-start(bf16[128,2048]{1,0:T(8,128)(2,1)} %refs_0_.1) | copy-start | bytes 1572868
  610.1 3.7 copy-start.7
  613.9 5.5 copy-start.6
  613.9 10.2 %slice-start.4 = ((s8[6291456]{0:T(1024)(128)(4,1)}), s8[4194304]{0:T(1024)(128)(4,1)S(1)}, s32[]{:S(2)}) async-start(s8[6291456]{0:T(1024)(128)(4,1)} %bitcast.70), calls=%async_computation.4 | async-start | bytes 8388608
  619.3 4.8 slice-start.5
  619.3 8.0 %slice-start.2 = ((s8[6291456]{0:T(1024)(128)(4,1)}), s8[4194304]{0:T(1024)(128)(4,1)S(1)}, s32[]{:S(2)}) async-start(s8[6291456]{0:T(1024)(128)(4,1)} %bitcast.67), calls=%async_computation.2 | async-start | bytes 8388608
  624.1 3.2 slice-start.3
  624.1 7.3 %slice-start = ((s8[6291456]{0:T(1024)(128)(4,1)}), s8[4194304]{0:T(1024)(128)(4,1)S(1)}, s32[]{:S(2)}) async-start(s8[6291456]{0:T(1024)(128)(4,1)} %bitcast.64), calls=%async_computation | async-start | bytes 8388608
  627.3 4.8 slice-start.1

commit v7 on v6

--- a/solution.py
+++ b/solution.py
@@ -12,6 +12,40 @@
 epsilon = 1e-06
 rope_base = 1000000.0
 masked_score = -1e30
+tuned_front = {
+    4: [
+        ("w", 0), ("m", 0), ("w", 1), ("x", 0), ("cz", 0), ("pf", 1), ("co", 0), ("m", 1), ("w", 2), ("pf", 0),
+        ("xe", 1), ("w", 3), ("m", 2), ("xm", 2), ("ps", 0), ("xm", 1), ("pf", 3), ("gf", 0), ("pf", 2), ("ps", 1),
+        ("m", 3), ("glm", 1), ("glm", 2), ("ps", 2), ("gle", 1), ("xm", 3), ("ps", 3), ("pp", 3), ("g", 0),
+        ("glm", 3), ("gle", 2), ("pp", 2), ("xe", 3), ("pp", 0), ("pp", 1), ("c", 3), ("gf", 1), ("r", 3), ("c", 1),
+        ("xe", 2), ("gf", 2), ("c", 2), ("r", 2), ("o", 0), ("gs", 1), ("gle", 3), ("r", 1), ("gf", 3), ("gs", 2),
+        ("c", 0), ("gs", 0), ("gs", 3), ("o", 1), ("r", 0),
+    ]
+}
+tuned_back = {
+    4: [
+        ("a", 0), ("l", 1), ("a", 1), ("l", 2), ("a", 2), ("k", 0), ("b", 0), ("l", 3), ("a", 3), ("w", 0), ("b", 1),
+        ("k", 2), ("c", 0), ("b", 2), ("wa", 0), ("s", 0), ("k", 1), ("k", 3), ("c", 1), ("s", 1), ("c", 2), ("s", 2),
+        ("b", 3), ("wb", 0), ("c", 3), ("s", 3), ("wc", 0),
+    ]
+}
+tuned_deliver = {
+    4: [
+        ("wi", 0), ("pt", 0), ("pt", 3), ("l", 0), ("pt", 2), ("of", 0), ("pt", 1), ("sm", 0), ("wi", 1), ("a", 0),
+        ("wi", 2), ("a", 1), ("l", 1), ("os", 0), ("b", 0), ("a", 2), ("wi", 3), ("o", 0), ("a", 3), ("op", 0),
+        ("b", 1), ("b", 2), ("b", 3), ("o", 1), ("o", 3), ("o", 2), ("u", 0), ("l", 2), ("u", 3), ("f", 0), ("f", 3),
+        ("u", 2), ("f", 2), ("u", 1), ("s", 3), ("l", 3), ("s", 0), ("s", 2), ("f", 1), ("s", 1), ("p", 0), ("p", 2),
+        ("p", 1), ("p", 3),
+    ]
+}
+tuned_experts = {
+    4: [
+        (5, "s", 0), (13, "p", 2), (10, "s", 1), (9, "f", 2), (12, "s", 2), (14, "s", 3), (11, "p", 1), (11, "e", 3),
+        (15, "p", 3), (0, "f", 0), (9, "l", 3), (0, "l", 1), (7, "f", 1), (2, "e", 1), (5, "e", 2), (5, "p", 0),
+        (1, "l", 2), (13, "f", 3),
+    ]
+}
+tuned_sum = {(4, 8): [0, 2, 3, 5, 6, 7, 7, 6, 8, 8, 8, 8, 8, 8, 8, 8]}
 
 
 class Grid:
@@ -39,6 +73,12 @@
     def other_lo(self, step):
         return (self.lo + step) % self.los
 
+    def inside(self):
+        return (self.z > 0) & (self.z + 1 < self.shards)
+
+    def outside(self):
+        return (self.z == 0) | (self.z + 1 == self.shards)
+
     def nearest(self):
         n = self.shards
         rows = [sorted(range(n), key=lambda p: (abs(p - z), p)) for z in range(n)]
@@ -54,7 +94,18 @@
 
 class Sends:
     def __init__(self, sems):
-        self.sems, self.used, self.open, self.samples = sems, 0, [], []
+        self.sems, self.used, self.open, self.samples, self.guard = sems, 0, [], [], None
+
+    def under(self, guard, task):
+        self.guard = guard
+        task()
+        self.guard = None
+
+    def all_of(self, when):
+        guard = self.guard
+        if guard is None or when is None:
+            return guard or when
+        return lambda: guard() & when()
 
     def copy(self, src, dst, sem, recv, device):
         return pltpu.make_async_remote_copy(
@@ -72,6 +123,7 @@
         for other in self.samples:
             if other.shape == src.shape:
                 sample = other
+        when = self.all_of(when)
         self.open.append((self.used, sample, when))
         self.used += 1
         if when is None:
@@ -81,6 +133,7 @@
 
     def arrived(self, dst, recv, device, when=None):
         copy = self.copy(dst, dst, 0, recv, device)
+        when = self.all_of(when)
         if when is None:
             copy.wait_recv()
         else:
@@ -404,6 +457,40 @@
 def wait_for(copies, k):
     for copy in copies(k):
         copy.wait()
+
+
+def run_all(steps):
+    for step in steps:
+        step()
+
+
+def in_order(tasks, default, tuned, n):
+    order = tuned.get(n, default)
+    assert sorted(order) == sorted(tasks), "task list"
+    for key in order:
+        tasks[key]()
+
+
+def staged(n):
+    steps = []
+    for turn in range(n + 2):
+        if turn < n:
+            steps.append(("a", turn))
+        if 0 <= turn - 1 < n:
+            steps.append(("b", turn - 1))
+        if 0 <= turn - 2 < n:
+            steps += [("c", turn - 2), ("s", turn - 2)]
+    return steps
+
+
+def sum_steps(n, tiles):
+    tuned = tuned_sum.get((n, tiles))
+    if tuned is None:
+        tuned = [min(tiles, (turn + {"a": 0, "b": 1, "c": 2, "s": 2}[name]) * tiles // n) for name, turn in staged(n)]
+    timed = {at: [] for at in range(tiles + 1)}
+    for at, step in zip(tuned, staged(n)):
+        timed[at].append(step)
+    return timed
 
 
 hbm = pl.BlockSpec(memory_space=pl.ANY)
@@ -434,8 +521,8 @@
     if not slabbed:
         greet_all(g)
         scatter.to_partner()
-        for turn in range(n + 2):
-            scatter.step(turn)
+        for name, turn in staged(n):
+            scatter.stage(name, turn)
         s.drain()
         return
 
@@ -466,13 +553,16 @@
     keep_slab = pltpu.make_async_copy(slab_ref.at[me], slabs_ref.at[me], slab_sem.at[0])
     keep_slab.start()
 
+    timed = sum_steps(n, tiles)
+
     def next_tiles(j):
         for copy in tile_in(j + 1, (j + 1) % 2):
             copy.start()
 
     def weight_grads(j, carry):
-        for turn in range(n):
-            pl.when(j == turn * tiles // n)(functools.partial(scatter.step, turn))
+        for at, steps in timed.items():
+            if at < tiles:
+                pl.when(j == at)(functools.partial(run_all, [functools.partial(scatter.stage, *step) for step in steps]))
         pl.when(j + 1 < tiles)(functools.partial(next_tiles, j))
         slot = j % 2
         for copy in tile_in(j, slot):
@@ -486,8 +576,8 @@
         return carry
 
     lax.fori_loop(0, tiles, weight_grads, 0)
-    scatter.step(n)
-    scatter.step(n + 1)
+    for step in timed[tiles]:
+        scatter.stage(*step)
     wait_for(tile_out, 0)
     keep_slab.wait()
     push_wait(g, slab_ref, slabs_ref, ps, pr)
@@ -591,8 +681,11 @@
     out_weight.own(0, lambda p: wo_sum_ref.at[halves[p]])
 
     ra = scatter.ra
-    loads[0].wait()
-    for zp in range(n):
+    tail = pl.ds(cols, total - cols)
+
+    def projection(zp):
+        if zp == 0:
+            loads[0].wait()
         grad = t_dot(hid_ref[:, zp * deep : (zp + 1) * deep], gqkv_ref[...]).astype(bf16)
         for place in range(places):
             for core in range(2):
@@ -601,41 +694,41 @@
         src = both.at[1 - g.core, zp, :, :, pl.ds(0, cols)]
         s.start(src, ra.at[zp, :, :, pl.ds(0, cols)], scatter.sa.at[zp], scatter.partner())
 
-    loads[1].wait()
-    loads[2].wait()
-    lane = lax.broadcasted_iota(jnp.int32, (length, total - cols), 1)
-    marked = jnp.where(lane == experts, 1.0, 0.0).astype(bf16)
+    def share(turn):
+        if turn == 0:
+            loads[1].wait()
+            loads[2].wait()
+            acc[...] = small_ref[...]
+        lane = lax.broadcasted_iota(jnp.int32, (length, total - cols), 1)
+        marked = jnp.where(lane == experts, 1.0, 0.0).astype(bf16)
+        at = pl.ds(pl.multiple_of(order[turn] * length, length), length)
+        grad = dot_t(gqkv_ref[at, :], w_ref[...])
+        line_own[turn] = grad.astype(bf16)
+        _, unit = unit_of(xs_ref[at, :].astype(f32))
+        acc[...] += t_dot((grad * unit).astype(bf16), marked)
+
+    def small_grads():
+        for i, ref in ((2, qsum_ref), (3, ksum_ref)):
+            width = ref.shape[1]
+            columns = jnp.broadcast_to(ref[...], (total - cols, width)).T
+            mask = lax.broadcasted_iota(jnp.int32, (part, total - cols), 1) == experts + i
+            for zp in range(n):
+                acc[zp * deep : zp * deep + part] += jnp.where(mask, columns[zp * part : (zp + 1) * part], 0.0)
+        for zp in range(n):
+            for place in range(places):
+                for core in range(2):
+                    row = zp * deep + (place * 2 + core) * piece
+                    both[core, zp, place, :, cols:total] = acc[row : row + piece].astype(bf16)
+        s.start(both.at[1 - g.core, :, :, :, tail], ra.at[:, :, :, tail], small_sem.at[0], scatter.partner())
 
     def line(turn):
         send_line(g, s, order[turn], line_own.at[turn], out_ref, rl, rr, sl, sr, last=turn == n - 1)
-
-    acc[...] = small_ref[...]
-    for turn in range(n):
-        at = pl.ds(pl.multiple_of(order[turn] * length, length), length)
-        share = dot_t(gqkv_ref[at, :], w_ref[...])
-        line_own[turn] = share.astype(bf16)
-        _, unit = unit_of(xs_ref[at, :].astype(f32))
-        acc[...] += t_dot((share * unit).astype(bf16), marked)
-        if turn == 0:
-            line(0)
-    for i, ref in ((2, qsum_ref), (3, ksum_ref)):
-        width = ref.shape[1]
-        columns = jnp.broadcast_to(ref[...], (total - cols, width)).T
-        mask = lax.broadcasted_iota(jnp.int32, (part, total - cols), 1) == experts + i
-        for zp in range(n):
-            acc[zp * deep : zp * deep + part] += jnp.where(mask, columns[zp * part : (zp + 1) * part], 0.0)
-    for zp in range(n):
-        for place in range(places):
-            for core in range(2):
-                row = zp * deep + (place * 2 + core) * piece
-                both[core, zp, place, :, cols:total] = acc[row : row + piece].astype(bf16)
-    tail = pl.ds(cols, total - cols)
-    s.start(both.at[1 - g.core, :, :, :, tail], ra.at[:, :, :, tail], small_sem.at[0], scatter.partner())
 
     def from_partner(turn):
         if turn == 0:
             s.arrived(ra.at[:, :, :, tail], small_sem.at[0], scatter.partner())
         s.arrived(ra.at[turn, :, :, pl.ds(0, cols)], scatter.sa.at[turn], scatter.partner())
+        scatter.a(turn, waited=True)
 
     def owner(turn):
         scatter.c(turn)
@@ -645,54 +738,73 @@
         s.start(scatter.mine(turn), dst, wr.at[g.z], g.device(g.r, turn), lambda: g.z != turn)
         pl.when(g.z == turn)(keep.wait)
 
-    for turn in range(n + 2):
-        if turn < n:
-            from_partner(turn)
-            scatter.a(turn, waited=True)
-        if turn == 0:
-            out_weight.first(0)
-        if turn == 1:
-            out_weight.second(0)
-        if 0 <= turn - 1 < n:
-            scatter.b(turn - 1)
-        if 1 <= turn < n - 1:
-            line(turn)
-        if 0 <= turn - 2 < n:
-            owner(turn - 2)
-    out_weight.from_partner(0)
-    keep = pltpu.make_async_copy(wo_sum_ref, wo_all.at[g.r], keep_sem.at[0])
-    keep.start()
-    keep.wait()
     saves = [pltpu.make_async_copy(wo_all, wo_out, ls.at[3])]
-    saves[0].start()
-    gather.own(g.z)
+
+    def weight_done():
+        out_weight.from_partner(0)
+        keep = pltpu.make_async_copy(wo_sum_ref, wo_all.at[g.r], keep_sem.at[0])
+        keep.start()
+        keep.wait()
+        saves[0].start()
 
     def unit_at(step):
         return (g.z + n - step) % n
 
-    for step in range(1, n):
+    def hand_out(step):
         u = unit_at(step)
-        s.arrived(ws_ref.at[u, g.r], wr.at[u], g.device(g.r, u))
+        if step:
+            s.arrived(ws_ref.at[u, g.r], wr.at[u], g.device(g.r, u))
         gather.own(u)
-        gather.first(unit_at(step - 1))
-        if step > 1:
-            gather.second(unit_at(step - 2))
-    gather.first(unit_at(n - 1))
-    gather.second(unit_at(n - 2))
-    gather.second(unit_at(n - 1))
-    line(n - 1)
-    for step in range(n):
+
+    def save(step):
         u = unit_at(step)
         gather.from_partner(u)
         q_span = pl.ds(pl.multiple_of(u * q_cols, 128), q_cols)
-        saves += [
+        rest_span = pl.ds(q_cols, total - q_cols)
+        pair = [
             pltpu.make_async_copy(ws_ref.at[u, :, :, pl.ds(0, q_cols)], q_out.at[:, :, q_span], ls.at[4 + 2 * step]),
-            pltpu.make_async_copy(
-                ws_ref.at[u, :, :, pl.ds(q_cols, total - q_cols)], rest_out.at[u], ls.at[5 + 2 * step]
-            ),
+            pltpu.make_async_copy(ws_ref.at[u, :, :, rest_span], rest_out.at[u], ls.at[5 + 2 * step]),
         ]
-        saves[-1].start()
-        saves[-2].start()
+        for copy in pair:
+            copy.start()
+        saves.extend(pair)
+
+    tasks = {
+        ("sm", 0): small_grads,
+        ("of", 0): functools.partial(out_weight.first, 0),
+        ("os", 0): functools.partial(out_weight.second, 0),
+        ("op", 0): weight_done,
+    }
+    for k in range(n):
+        tasks["wi", k] = functools.partial(projection, k)
+        tasks["pt", k] = functools.partial(share, k)
+        tasks["l", k] = functools.partial(line, k)
+        tasks["a", k] = functools.partial(from_partner, k)
+        tasks["b", k] = functools.partial(scatter.b, k)
+        tasks["o", k] = functools.partial(owner, k)
+        tasks["u", k] = functools.partial(hand_out, k)
+        tasks["f", k] = functools.partial(gather.first, unit_at(k))
+        tasks["s", k] = functools.partial(gather.second, unit_at(k))
+        tasks["p", k] = functools.partial(save, k)
+    default = [("wi", k) for k in range(n)] + [("pt", 0), ("l", 0)] + [("pt", k) for k in range(1, n)] + [("sm", 0)]
+    for turn in range(n + 2):
+        if turn < n:
+            default.append(("a", turn))
+        if turn < 2:
+            default.append((("of", "os")[turn], 0))
+        if 0 <= turn - 1 < n:
+            default.append(("b", turn - 1))
+        if 1 <= turn < n - 1:
+            default.append(("l", turn))
+        if 0 <= turn - 2 < n:
+            default.append(("o", turn - 2))
+    default += [("op", 0), ("u", 0)]
+    for k in range(1, n):
+        default += [("u", k), ("f", k - 1)]
+        if k > 1:
+            default.append(("s", k - 2))
+    default += [("f", n - 1), ("s", n - 2), ("s", n - 1), ("l", n - 1)] + [("p", k) for k in range(n)]
+    in_order(tasks, default, tuned_deliver, n)
     for copy in saves:
         copy.wait()
     s.drain()
@@ -909,16 +1021,13 @@
         for turn in range(self.g.shards):
             self.plane.to_partner(turn)
 
-    def step(self, turn):
-        n = self.g.shards
-        if turn < n:
-            self.plane.a(turn)
-        if 0 <= turn - 1 < n:
-            self.plane.b(turn - 1)
-        if 0 <= turn - 2 < n:
-            t = turn - 2
-            self.plane.c(t)
-            send_line(self.g, self.s, self.order[t], self.plane.mine(t), self.out_ref, *self.lines, last=t == n - 1)
+    def stage(self, name, turn):
+        if name == "s":
+            last = turn == self.g.shards - 1
+            line = self.plane.mine(turn)
+            send_line(self.g, self.s, self.order[turn], line, self.out_ref, *self.lines, last=last)
+        else:
+            getattr(self.plane, name)(turn)
 
 
 def attend_back_kernel(reps, shards, heads, *refs):
@@ -972,23 +1081,41 @@
     scatter.to_partner()
     for copy in loads + [keep]:
         copy.wait()
-    for turn in range(n):
-        scatter.step(turn)
-        if turn + 1 < n:
-            line(turn + 1)
-        else:
-            out_weight()
-            owner.to_partner(0)
+    owner.loads = [None]
+
+    def block(turn):
         attend_back_block(
             order[turn], heads, gas_ref, qkv_ref, wo_ref, qg_ref, kg_ref, cos_ref, sin_ref, bias_ref,
             gm, gqkv_ref, qsum_ref, ksum_ref,
         )
-    owner.loads = [None]
-    scatter.step(n)
-    owner.a(0)
-    scatter.step(n + 1)
-    owner.b(0)
-    owner.c(0)
+
+    def weigh():
+        out_weight()
+        owner.to_partner(0)
+
+    tasks = {("w", 0): weigh}
+    for name in "abc":
+        tasks["w" + name, 0] = functools.partial(getattr(owner, name), 0)
+    for turn in range(n):
+        if turn:
+            tasks["l", turn] = functools.partial(line, turn)
+        tasks["k", turn] = functools.partial(block, turn)
+        for name in "abcs":
+            tasks[name, turn] = functools.partial(scatter.stage, name, turn)
+    default = []
+    for turn in range(n + 2):
+        default += [step for step in staged(n) if step[1] + {"a": 0, "b": 1, "c": 2, "s": 2}[step[0]] == turn]
+        if turn + 1 < n:
+            default.append(("l", turn + 1))
+        elif turn + 1 == n:
+            default.append(("w", 0))
+        if turn < n:
+            default.append(("k", turn))
+        elif turn == n:
+            default.append(("wa", 0))
+        else:
+            default += [("wb", 0), ("wc", 0)]
+    in_order(tasks, default, tuned_back, n)
     wo_sum_ref[...] = own[0, g.hi * g.los + g.lo]
     s.drain()
 
@@ -1105,52 +1232,43 @@
     def unit(step):
         return (g.z + n - step) % n
 
-    def line(turn):
+    def small_line(turn):
         zp = order[turn]
         if turn:
             s.arrived(smalls_ref.at[zp], mr.at[zp], g.device(g.r, zp))
         pass_along(g, s, zp, smalls_ref.at[zp] if turn else small_ref, smalls_ref.at[zp], mr)
+
+    def token_line(turn):
+        zp = order[turn]
+        here = xs_ref.at[zp]
         if turn:
-            s.arrived(xs_ref.at[zp], xr.at[zp], g.device(g.r, zp))
-        pass_along(g, s, zp, xs_ref.at[zp] if turn else x_ref, xs_ref.at[zp], xr)
+            s.arrived(here, xr.at[zp], g.device(g.r, zp))
+        pass_along(g, s, zp, here if turn else x_ref, here, xr)
 
     for step in range(1, n):
         zp = (g.z + step) % n
         for i, (src, dst) in enumerate(pieces(zp, g.z)):
             s.start(src, dst, wr.at[step, i], g.device(g.r, zp))
-    line(0)
-    for copy in locals_:
-        copy.wait()
-    plane.own(g.z)
-    for step in range(1, n):
+    def own_pieces():
+        for copy in locals_:
+            copy.wait()
+        plane.own(g.z)
+
+    def other_pieces(step):
         u = unit(step)
         for i, (_, dst) in enumerate(pieces(g.z, u)):
             s.arrived(dst, wr.at[step, i], g.device(g.r, u))
         plane.own(u)
-    gather.plane.own(g.z, lambda part: cot_ref.at[gather.spans[part]])
-    line(1)
-    for step in range(n):
-        plane.first(unit(step))
-        if step:
-            plane.second(unit(step - 1))
-        if 2 + step < n - 1:
-            line(2 + step)
-        if step == max(0, n - 4):
-            pass_along(g, s, g.z, cot_ref, gather.own(), gather.zr)
-    plane.second(unit(n - 1))
-    for step in range(n):
-        plane.from_partner(unit(step))
-    for copy in keeps[:3]:
-        copy.wait()
 
     length = x_ref.shape[0]
-    smalls_late = order[n - 1]
-    s.arrived(smalls_ref.at[smalls_late], mr.at[smalls_late], g.device(g.r, smalls_late))
-    pass_along(g, s, smalls_late, smalls_ref.at[smalls_late], smalls_ref.at[smalls_late], mr)
-    for zp in range(n):
-        gains_ref[:, zp * deep : (zp + 1) * deep] = smalls_ref[zp].astype(f32)[experts : experts + 8]
-    for i in range(2):
-        qk_ref[i : i + 1] = sum(gains_ref[2 + i : 3 + i, zp * deep : zp * deep + head_dim] for zp in range(n))
+
+    def gains():
+        for copy in keeps[:3]:
+            copy.wait()
+        for zp in range(n):
+            gains_ref[:, zp * deep : (zp + 1) * deep] = smalls_ref[zp].astype(f32)[experts : experts + 8]
+        for i in range(2):
+            qk_ref[i : i + 1] = sum(gains_ref[2 + i : 3 + i, zp * deep : zp * deep + head_dim] for zp in range(n))
 
     def compute(turn):
         zp = order[turn]
@@ -1165,43 +1283,55 @@
     def sums(turn):
         send_line(g, s, order[turn], own.at[turn], out_ref, rl, rr, sl, sr, last=turn == 0)
 
-    farthest = order[n - 1]
-    between = lambda: (g.z > 0) & (g.z + 1 < n)
-    at_end = lambda: (g.z == 0) | (g.z + 1 == n)
-    s.arrived(xs_ref.at[farthest], xr.at[farthest], g.device(g.r, farthest), between)
-    pass_along(g, s, farthest, xs_ref.at[farthest], xs_ref.at[farthest], xr)
-    compute(0)
-    s.arrived(xs_ref.at[farthest], xr.at[farthest], g.device(g.r, farthest), at_end)
-    outs = [pltpu.make_async_copy(w_ref, w_out, out_sems.at[0]), pltpu.make_async_copy(xs_ref, xs_out, out_sems.at[1])]
-    for copy in outs:
-        copy.start()
-    compute(n - 1)
-    sums(n - 1)
-    gather.first(0)
-    gather.line(1)
-    for turn in range(n - 2, -1, -1):
-        if turn > 0:
-            compute(turn)
-        at = n - 1 - turn
-        if turn > 0:
-            sums(turn)
-            gather.second(at - 1)
-            gather.first(at)
-            if at + 1 < n:
-                gather.line(at + 1)
-    late = [
+    outs = [
+        pltpu.make_async_copy(w_ref, w_out, out_sems.at[0]),
+        pltpu.make_async_copy(xs_ref, xs_out, out_sems.at[1]),
         pltpu.make_async_copy(hid_ref, hid_out, out_sems.at[2]),
         pltpu.make_async_copy(qkv_ref, qkv_out, out_sems.at[3]),
         pltpu.make_async_copy(att_ref, att_out, out_sems.at[4]),
     ]
-    for copy in late:
-        copy.start()
-    gather.second(n - 2)
-    gather.first(n - 1)
-    gather.second(n - 1)
-    sums(0)
+    tasks = {
+        ("w", 0): own_pieces,
+        ("g", 0): gains,
+        ("co", 0): functools.partial(gather.plane.own, g.z, lambda part: cot_ref.at[gather.spans[part]]),
+        ("cz", 0): functools.partial(pass_along, g, s, g.z, cot_ref, gather.own(), gather.zr),
+        ("o", 0): functools.partial(run_all, [copy.start for copy in outs[:2]]),
+        ("o", 1): functools.partial(run_all, [copy.start for copy in outs[2:]]),
+    }
+    for k in range(n):
+        tasks["m", k] = functools.partial(small_line, k)
+        tasks["c", k] = functools.partial(compute, k)
+        tasks["r", k] = functools.partial(sums, k)
+        tasks["pf", k] = functools.partial(plane.first, unit(k))
+        tasks["ps", k] = functools.partial(plane.second, unit(k))
+        tasks["pp", k] = functools.partial(plane.from_partner, unit(k))
+        tasks["gf", k] = functools.partial(gather.first, k)
+        tasks["gs", k] = functools.partial(gather.second, k)
+        if k:
+            tasks["w", k] = functools.partial(other_pieces, k)
+            for name, guard in (("m", g.inside), ("e", g.outside)):
+                tasks["x" + name, k] = functools.partial(s.under, guard, functools.partial(token_line, k))
+                tasks["gl" + name, k] = functools.partial(s.under, guard, functools.partial(gather.line, k))
+    tasks["x", 0] = functools.partial(token_line, 0)
+    default = [("m", 0), ("x", 0)] + [("w", k) for k in range(n)] + [("co", 0), ("m", 1), ("xm", 1), ("xe", 1)]
+    for k in range(n):
+        default.append(("pf", k))
+        if k:
+            default.append(("ps", k - 1))
+        if 2 + k < n - 1:
+            default += [("m", 2 + k), ("xm", 2 + k), ("xe", 2 + k)]
+        if k == max(0, n - 4):
+            default.append(("cz", 0))
+    default += [("ps", n - 1)] + [("pp", k) for k in range(n)]
+    default += [("m", n - 1), ("g", 0), ("xm", n - 1), ("c", 0), ("xe", n - 1), ("o", 0), ("c", n - 1), ("r", n - 1)]
+    default += [("gf", 0), ("glm", 1), ("gle", 1)]
+    for k in range(n - 2, 0, -1):
+        at = n - 1 - k
+        default += [("c", k), ("r", k), ("gs", at - 1), ("gf", at), ("glm", at + 1), ("gle", at + 1)]
+    default += [("o", 1), ("gs", n - 2), ("gf", n - 1), ("gs", n - 1), ("r", 0)]
+    in_order(tasks, default, tuned_front, n)
     gather.finish()
-    for copy in outs + late + keeps[3:]:
+    for copy in outs + keeps[3:]:
         copy.wait()
     s.drain()
 
@@ -1245,7 +1375,7 @@
         ]
         + line_scratch(n, (rows, width), bf16)
         + [
-            dma((PlaneGather.sends(g, n) + GatherAll.sends(g) + 9 * n,)),
+            dma((PlaneGather.sends(g, n) + 2 * GatherAll.sends(g) + 11 * n,)),
             dma((n,)),
             dma((n,)),
             dma((n, 3)),
@@ -1268,6 +1398,24 @@
     slot = jnp.where(member, slot, -1.0)[0:1]
     rows = lax.broadcasted_iota(jnp.int32, (capacity, length), 0).astype(f32)
     return jnp.where(rows == slot, 1.0, 0.0), slab[0:1]
+
+
+def expert_steps(n):
+    base = 2 * n
+    steps = [(2, "f", 0), (3, "l", 1), (3, "e", 1), (5, "s", 0)]
+    steps += [(7, "l", 2), (7, "e", 2)] * (n > 2) + [(base, "f", 1)]
+    for turn in range(n):
+        if 0 < turn < n - 1:
+            steps.append((base + 2 * turn, "s", turn))
+        at = base + 2 * turn + 1
+        steps.append((at, "p", turn))
+        if turn + 3 < n:
+            steps += [(at, "l", turn + 3), (at, "e", turn + 3)]
+        if turn + 2 < n:
+            steps.append((at, "f", turn + 2))
+        if turn == n - 2:
+            steps.append((at, "s", n - 1))
+    return steps
 
 
 def experts_kernel(reps, shards, capacity, held, *refs):
@@ -1315,16 +1463,23 @@
         for at, step in steps:
             pl.when(k == at)(step)
 
-    def both(*fs):
-        def run():
-            for f, turn in fs:
-                f(turn)
-
-        return run
-
-    early = [(2, both((gather.first, 0))), (3, both((gather.line, 1))), (5, both((gather.second, 0)))]
-    if n > 2:
-        early.append((7, both((gather.line, 2))))
+    def split(guard, turn):
+        s.under(guard, functools.partial(gather.line, turn))
+
+    named = {
+        "l": functools.partial(split, g.inside),
+        "e": functools.partial(split, g.outside),
+        "f": gather.first,
+        "s": gather.second,
+        "p": lambda turn: gather.plane.from_partner(order[turn]),
+    }
+    early, late = [], []
+    for at, name, turn in tuned_experts.get(n) or expert_steps(n):
+        step = functools.partial(named[name], turn)
+        if at < groups:
+            early.append((at, step))
+        else:
+            late.append((at - groups, step))
 
     def outs(k):
         return [
@@ -1359,22 +1514,6 @@
 
     lax.fori_loop(0, groups, backward_input, 0)
     c_out(0).wait()
-
-    def partner(turn):
-        gather.plane.from_partner(order[turn])
-
-    late = [(0, both((gather.first, 1)))]
-    for turn in range(n):
-        if 0 < turn < n - 1:
-            late.append((2 * turn, both((gather.second, turn))))
-        steps = [(partner, turn)]
-        if turn + 3 < n:
-            steps.append((gather.line, turn + 3))
-        if turn + 2 < n:
-            steps.append((gather.first, turn + 2))
-        if turn == n - 2:
-            steps.append((gather.second, n - 1))
-        late.append((2 * turn + 1, both(*steps)))
 
     def expert(k, carry):
         turns(k, late)
@@ -1467,7 +1606,7 @@
             v((rows, inner), bf16),
             v((places, length, width), bf16),
             v((places, length, width), bf16),
-            dma((GatherAll.sends(g),)),
+            dma((2 * GatherAll.sends(g),)),
             dma((g.devices,)),
             dma((g.devices,)),
             dma((2,)),

time: 643 us -> 573 us (0.89)
  Pallas kernels: 582 us -> 511 us
    pallas_call x1, Pallas kernels: 114 us -> 89.4 us  [deliver(): pl.pallas_call(functools.partial(deliver_kernel, reps, shards, (q_cols, e...]
    pallas_call x1, Pallas kernels: 145 us -> 121 us  [front(): pl.pallas_call(functools.partial(front_kernel, reps, shards, heads, layou...]
    pallas_call x1, Pallas kernels: 113 us -> 103 us  [experts_all(): pl.pallas_call(functools.partial(experts_kernel, reps, shards, capacity,...]
    pallas_call x1, Pallas kernels: 106 us -> 98.5 us  [scatter_all(): pl.pallas_call(functools.partial(scatter_all_kernel, reps, shards, slabbe...]
where the time goes in v7:
time: 573 us; the launch traced here: 565 us
  Pallas kernels  511 us (89%)
  local copies, waits for them, and re-layouts  26.8 us (5%)
  other arithmetic  23 us (4%)
    pallas_call x1, Pallas kernels, front(): pl.pallas_call(functools.partial(front_kernel, reps, shards, heads, layou...  121 us
    pallas_call x1, Pallas kernels, experts_all(): pl.pallas_call(functools.partial(experts_kernel, reps, shards, capacity,...  103 us
    pallas_call x1, Pallas kernels, attend_back(): pl.pallas_call(functools.partial(attend_back_kernel, reps, shards, heads)...  99.5 us
    pallas_call x1, Pallas kernels, scatter_all(): pl.pallas_call(functools.partial(scatter_all_kernel, reps, shards, slabbe...  98.5 us
    pallas_call x1, Pallas kernels, deliver(): pl.pallas_call(functools.partial(deliver_kernel, reps, shards, (q_cols, e...  89.4 us
    unnamed x33, local copies, waits for them, and re-layouts  13.3 us

profile of v7, /device:TPU:17, one launch (start us, length us, event | category | flops | bytes accessed | tf_op | source)
XLA Modules:
  0.0 564.6 jit_solution(5736652903810385256)
XLA Ops:
  0.6 0.7 convert_element_type.65
  1.3 0.1 pad.16.clone
  1.4 0.6 maximum_bitcast_fusion.refs_3_
  2.0 0.7 reshape.216
  2.7 0.7 reshape.217
  3.4 0.7 fusion.7
  4.1 0.7 tile.16
  4.7 0.1 tile.17
  4.8 0.7 tile.18
  5.5 0.1 tile.19
  5.6 0.8 concatenate.9
  6.4 0.6 pad.13.refs_2_
  7.0 121.1 %front.1 = (bf16[4,48,512]{2,1,0:T(8,128)(2,1)}, f32[8,2048]{1,0:T(8,128)}, f32[8,128]{1,0:T(8,128)}, f32[4,128,128]{2,1,0:T(8,128)}, f32[4,128,128]{2,1,0:T(8,1...) custom-call(bf16[128,2048]{1,0:T(8,128)(2,1)} %refs_0_.1, ...), custom_call_target="tpu_custom_call" | custom-call | tf_op jit(solution)/shard_map/front/pallas_call | solution.py:1348
  128.1 0.0 copy-done.3
  128.1 1.5 multiply_reduce_fusion.2
  129.6 1.3 fusion.15
  130.9 0.9 fusion.14
  131.8 0.9 slice_bitcast_fusion
  132.8 0.2 multiply_convert_fusion.refs_0_
  132.9 0.0 copy-start.1
  133.0 0.3 fusion.16
  133.3 0.7 broadcast_in_dim.47.refs_1_
  134.0 0.0 copy-done.1
  134.0 102.7 %experts_all.1 = (f32[32,8,128]{2,1,0:T(8,128)}, bf16[4,2,4,128,2048]{4,3,2,1,0:T(8,128)(2,1)}, bf16[4,2,4,128,2048]{4,3,2,1,0:T(8,128)(2,1)}, bf16[8,256,2048]{...) custom-call(bf16[128,2048]{1,0:T(8,128)(2,1)} %copy-done.1, ...), custom_call_target="tpu_custom_call" | custom-call | tf_op jit(solution)/shard_map/experts_all/pallas_call | solution.py:1582
  236.8 0.0 copy-start.2
  236.8 98.5 %scatter_all.1 = (f32[128,2048]{1,0:T(8,128)}, f32[32,8,128]{2,1,0:T(8,128)}, f32[2048,768]{1,0:T(8,128)}, f32[2048,768]{1,0:T(8,128)}, f32[768,2048]{1,0:T(8,128)}) custom-call(bf16[4,2,4,128,2048]{4,3,2,1,0:T(8,128)(2,1)} %get-tuple-element.53.refs_0_, f32[32,8,128]{2,1,0:T(8,128)} %get-tuple-element.54.refs_1_, bf16[2048,2048]{1,0:T(8,128)(2,1)} %bitcast.62, ...), custom_call_target="tpu_custom_call" | custom-call | tf_op jit(solution)/shard_map/scatter_all/pallas_call | solution.py:612
  335.2 0.0 copy-start.5
  335.3 1.0 slice.44
  336.3 0.0 copy-done.2
  336.3 0.2 fusion.17
  336.5 1.8 multiply_reduce_fusion
  338.3 0.0 copy-start
  338.3 0.1 pad_maximum_fusion
  338.4 0.9 copy-done
  339.3 0.0 copy-done.5
  339.3 1.1 fusion.13.refs_0_
  340.4 99.5 %attend_back.1 = (bf16[4,128,1280]{2,1,0:T(8,128)(2,1)}, f32[1,128]{1,0:T(1,128)}, f32[1,128]{1,0:T(1,128)}, f32[128,2048]{1,0:T(8,128)}, bf16[128,2048]{1,0:T(8,128)(2,1)}) custom-call(bf16[128,2048]{1,0:T(8,128)(2,1)} %fusion.13.refs_0_, f32[1,128]{1,0:T(1,128)} %get-tuple-element.142.refs_1_, f32[1,128]{1,0:T(1,128)} %get-tuple-element.141.refs_2_, ...), custom_call_target="tpu_custom_call" | custom-call | tf_op jit(solution)/shard_map/attend_back/pallas_call | solution.py:1133
  439.9 0.4 copy.53
  440.3 1.0 pad.14.refs_1_
  441.3 89.4 %deliver.1 = (f32[128,2048]{1,0:T(8,128)}, bf16[8,64,4096]{2,1,0:T(8,128)(2,1)}, bf16[4,8,64,384]{3,2,1,0:T(8,128)(2,1)}, bf16[8,128,2048]{2,1,0:T(8,128)(2,1)}) custom-call(bf16[512,1280]{1,0:T(8,128)(2,1)} %bitcast.84, f32[2048,128]{1,0:T(8,128)} %pad.14.refs_1_, f32[1,128]{1,0:T(1,128)} %get-tuple-element.71.refs_2_, f32[1,128]{1,0:T(1,128)} %get-tuple-element.72.refs_3_, ...), custom_call_target="tpu_custom_call" | custom-call | tf_op jit(solution)/shard_map/deliver/pallas_call | solution.py:823
  530.8 0.0 copy-done.4
  530.8 1.5 fusion.2
  532.3 3.6 fusion.5
  536.0 1.1 convert_reduce_fusion
  537.1 0.7 slice_reduce_fusion.2
  537.8 0.9 slice_reduce_fusion
  538.7 0.7 copy.56
  539.5 1.5 convert_bitcast_fusion
  541.0 1.1 copy.62
  542.1 1.1 copy.63
  543.2 0.0 copy-done.7
  543.2 5.5 bitcast_convert_fusion.1
  548.7 0.0 copy-done.6
  548.7 4.7 bitcast_convert_fusion
  553.4 0.0 slice-done.4
  553.4 0.0 slice-done.5
  553.4 0.0 slice-start
  553.4 3.2 copy.67
  556.6 0.0 slice-done.2
  556.6 0.0 slice-done.3
  556.6 3.2 copy.68
  559.8 0.9 slice-done
  560.7 0.8 slice-done.1
  561.5 2.7 copy.69
  (25 shorter events, 0.2 us)
Async XLA Ops:
  7.0 121.1 %copy-start.3 = (bf16[128,2048]{1,0:T(8,128)(2,1)S(1)}, bf16[128,2048]{1,0:T(8,128)(2,1)}, u32[]{:S(2)}) copy-start(bf16[128,2048]{1,0:T(8,128)(2,1)} %refs_0_.1) | copy-start | bytes 1572868
  132.9 1.1 copy-start.1
  236.8 99.5 %copy-start.2 = (bf16[128,2048]{1,0:T(8,128)(2,1)S(1)}, bf16[128,2048]{1,0:T(8,128)(2,1)}, u32[]{:S(2)}) copy-start(bf16[128,2048]{1,0:T(8,128)(2,1)} %copy-done.1) | copy-start | bytes 1572868
  335.2 4.0 copy-start.5
  338.3 1.0 copy-start
  441.3 89.4 %copy-start.4 = (bf16[128,2048]{1,0:T(8,128)(2,1)S(1)}, bf16[128,2048]{1,0:T(8,128)(2,1)}, u32[]{:S(2)}) copy-start(bf16[128,2048]{1,0:T(8,128)(2,1)} %refs_0_.1) | copy-start | bytes 1572868
  539.5 3.7 copy-start.7
  543.2 5.5 copy-start.6
  543.2 10.2 %slice-start.4 = ((s8[6291456]{0:T(1024)(128)(4,1)}), s8[4194304]{0:T(1024)(128)(4,1)S(1)}, s32[]{:S(2)}) async-start(s8[6291456]{0:T(1024)(128)(4,1)} %bitcast.70), calls=%async_computation.4 | async-start | bytes 8388608
  548.7 4.8 slice-start.5
  548.7 8.0 %slice-start.2 = ((s8[6291456]{0:T(1024)(128)(4,1)}), s8[4194304]{0:T(1024)(128)(4,1)S(1)}, s32[]{:S(2)}) async-start(s8[6291456]{0:T(1024)(128)(4,1)} %bitcast.67), calls=%async_computation.2 | async-start | bytes 8388608
  553.4 3.2 slice-start.3
  553.4 7.3 %slice-start = ((s8[6291456]{0:T(1024)(128)(4,1)}), s8[4194304]{0:T(1024)(128)(4,1)S(1)}, s32[]{:S(2)}) async-start(s8[6291456]{0:T(1024)(128)(4,1)} %bitcast.64), calls=%async_computation | async-start | bytes 8388608
  556.6 4.8 slice-start.1

commit v8 on v7

--- a/solution.py
+++ b/solution.py
@@ -14,38 +14,38 @@
 masked_score = -1e30
 tuned_front = {
     4: [
-        ("w", 0), ("m", 0), ("w", 1), ("x", 0), ("cz", 0), ("pf", 1), ("co", 0), ("m", 1), ("w", 2), ("pf", 0),
-        ("xe", 1), ("w", 3), ("m", 2), ("xm", 2), ("ps", 0), ("xm", 1), ("pf", 3), ("gf", 0), ("pf", 2), ("ps", 1),
-        ("m", 3), ("glm", 1), ("glm", 2), ("ps", 2), ("gle", 1), ("xm", 3), ("ps", 3), ("pp", 3), ("g", 0),
-        ("glm", 3), ("gle", 2), ("pp", 2), ("xe", 3), ("pp", 0), ("pp", 1), ("c", 3), ("gf", 1), ("r", 3), ("c", 1),
-        ("xe", 2), ("gf", 2), ("c", 2), ("r", 2), ("o", 0), ("gs", 1), ("gle", 3), ("r", 1), ("gf", 3), ("gs", 2),
-        ("c", 0), ("gs", 0), ("gs", 3), ("o", 1), ("r", 0),
+        ("w", 1), ("w", 0), ("x", 0), ("pf", 0), ("w", 3), ("m", 0), ("pf", 3), ("xm", 1), ("co", 0), ("xe", 1),
+        ("xm", 2), ("m", 2), ("ps", 3), ("pf", 1), ("ps", 0), ("m", 1), ("cz", 0), ("pp", 3), ("gf", 0), ("w", 2),
+        ("ps", 1), ("m", 3), ("xm", 3), ("pp", 1), ("g", 0), ("pf", 2), ("glm", 1), ("glm", 2), ("ps", 2), ("pp", 2),
+        ("pp", 0), ("gle", 1), ("xe", 3), ("c", 3), ("xe", 2), ("glm", 3), ("r", 3), ("gf", 1), ("c", 1), ("gle", 2),
+        ("c", 2), ("gs", 1), ("r", 2), ("gs", 0), ("gf", 2), ("gle", 3), ("o", 0), ("r", 1), ("c", 0), ("gf", 3),
+        ("gs", 2), ("o", 1), ("gs", 3), ("r", 0),
     ]
 }
 tuned_back = {
     4: [
-        ("a", 0), ("l", 1), ("a", 1), ("l", 2), ("a", 2), ("k", 0), ("b", 0), ("l", 3), ("a", 3), ("w", 0), ("b", 1),
-        ("k", 2), ("c", 0), ("b", 2), ("wa", 0), ("s", 0), ("k", 1), ("k", 3), ("c", 1), ("s", 1), ("c", 2), ("s", 2),
+        ("a", 0), ("k", 0), ("a", 1), ("a", 2), ("l", 2), ("l", 1), ("b", 0), ("k", 2), ("l", 3), ("w", 0), ("b", 2),
+        ("b", 1), ("c", 0), ("a", 3), ("s", 0), ("wa", 0), ("k", 3), ("c", 1), ("k", 1), ("s", 1), ("c", 2), ("s", 2),
         ("b", 3), ("wb", 0), ("c", 3), ("s", 3), ("wc", 0),
     ]
 }
 tuned_deliver = {
     4: [
-        ("wi", 0), ("pt", 0), ("pt", 3), ("l", 0), ("pt", 2), ("of", 0), ("pt", 1), ("sm", 0), ("wi", 1), ("a", 0),
-        ("wi", 2), ("a", 1), ("l", 1), ("os", 0), ("b", 0), ("a", 2), ("wi", 3), ("o", 0), ("a", 3), ("op", 0),
-        ("b", 1), ("b", 2), ("b", 3), ("o", 1), ("o", 3), ("o", 2), ("u", 0), ("l", 2), ("u", 3), ("f", 0), ("f", 3),
-        ("u", 2), ("f", 2), ("u", 1), ("s", 3), ("l", 3), ("s", 0), ("s", 2), ("f", 1), ("s", 1), ("p", 0), ("p", 2),
-        ("p", 1), ("p", 3),
+        ("wi", 0), ("pt", 0), ("pt", 3), ("pt", 1), ("pt", 2), ("sm", 0), ("l", 0), ("a", 0), ("wi", 1), ("wi", 3),
+        ("a", 3), ("wi", 2), ("b", 0), ("a", 2), ("l", 1), ("o", 0), ("a", 1), ("b", 3), ("b", 2), ("b", 1), ("o", 3),
+        ("of", 0), ("o", 1), ("o", 2), ("u", 0), ("os", 0), ("u", 3), ("l", 2), ("f", 3), ("u", 2), ("f", 2),
+        ("f", 0), ("u", 1), ("s", 2), ("s", 3), ("p", 3), ("s", 0), ("p", 0), ("p", 2), ("op", 0), ("f", 1), ("s", 1),
+        ("l", 3), ("p", 1),
     ]
 }
 tuned_experts = {
     4: [
-        (5, "s", 0), (13, "p", 2), (10, "s", 1), (9, "f", 2), (12, "s", 2), (14, "s", 3), (11, "p", 1), (11, "e", 3),
-        (15, "p", 3), (0, "f", 0), (9, "l", 3), (0, "l", 1), (7, "f", 1), (2, "e", 1), (5, "e", 2), (5, "p", 0),
-        (1, "l", 2), (13, "f", 3),
+        (1, "l", 1), (11, "e", 3), (14, "s", 3), (12, "s", 2), (13, "f", 3), (9, "f", 2), (15, "p", 3), (1, "e", 1),
+        (10, "s", 1), (6, "e", 2), (0, "f", 0), (11, "p", 1), (7, "p", 0), (13, "p", 2), (7, "f", 1), (1, "l", 2),
+        (5, "s", 0), (9, "l", 3),
     ]
 }
-tuned_sum = {(4, 8): [0, 2, 3, 5, 6, 7, 7, 6, 8, 8, 8, 8, 8, 8, 8, 8]}
+tuned_sum = {(4, 8): [0, 0, 3, 3, 4, 5, 5, 5, 7, 8, 8, 8, 8, 8, 8, 8]}
 
 
 class Grid:
@@ -505,7 +505,7 @@
     if slabbed:
         (
             p_ref, slab_ref, x_ref, c_ref, gg_ref, gu_ref, act_ref, out_ref, slabs_ref, wg_ref, wu_ref, wd_ref,
-            xt, ct, og, ou, od, tile_sems, out_sems, *rest,
+            gg_buf, gu_buf, act_buf, xt, ct, og, ou, od, tile_sems, out_sems, in_sems, *rest,
         ) = refs
     else:
         p_ref, out_ref, *rest = refs
@@ -544,7 +544,11 @@
             pltpu.make_async_copy(od, wd_ref.at[:, span], out_sems.at[2]),
         ]
 
-    for copy in tile_in(0, 0):
+    inner = [
+        pltpu.make_async_copy(src, dst, in_sems.at[i])
+        for i, (src, dst) in enumerate(((gg_ref, gg_buf), (gu_ref, gu_buf), (act_ref, act_buf)))
+    ]
+    for copy in tile_in(0, 0) + inner:
         copy.start()
     greet_all(g)
     scatter.to_partner()
@@ -567,10 +571,11 @@
         slot = j % 2
         for copy in tile_in(j, slot):
             copy.wait()
+        pl.when(j == 0)(functools.partial(run_all, [copy.wait for copy in inner]))
         pl.when(j > 0)(functools.partial(wait_for, tile_out, j))
-        og[...] = t_dot(xt[slot], gg_ref[...])
-        ou[...] = t_dot(xt[slot], gu_ref[...])
-        od[...] = t_dot(act_ref[...], ct[slot])
+        og[...] = t_dot(xt[slot], gg_buf[...])
+        ou[...] = t_dot(xt[slot], gu_buf[...])
+        od[...] = t_dot(act_buf[...], ct[slot])
         for copy in tile_out(j):
             copy.start()
         return carry
@@ -602,12 +607,12 @@
             jax.ShapeDtypeStruct(slab.shape, slab.dtype), narrow, narrow, jax.ShapeDtypeStruct((inner, wide), f32)
         )
         out_specs += (vmem, hbm, hbm, hbm)
-        in_specs += [vmem, hbm, hbm, vmem, vmem, vmem]
+        in_specs += [vmem] + [hbm] * 5
         extra = [slab, *fill]
-        scratch = [
+        scratch = [v((count, inner), bf16)] * 3 + [
             v((2, count, tile), bf16), v((2, count, tile), bf16),
             v((tile, inner), f32), v((tile, inner), f32), v((inner, tile), f32),
-            dma((2, 2)), dma((3,)),
+            dma((2, 2)), dma((3,)), dma((3,)),
         ]
     done = pl.pallas_call(
         functools.partial(scatter_all_kernel, reps, shards, slabbed),
@@ -888,6 +893,17 @@
     return inverse * (gained - unit * mean_last(gained * unit))
 
 
+def loop_heads(first, last, head, carry):
+    width = 4 if (last - first) % 4 == 0 else 1
+
+    def some(i, carry):
+        for j in range(width):
+            carry = head(first + i * width + j, carry)
+        return carry
+
+    return lax.fori_loop(0, (last - first) // width, some, carry)
+
+
 def attend_block(b, heads, x_ref, w_ref, wo_ref, gain_ref, qg_ref, kg_ref, cos_ref, sin_ref, bias_ref, hid_ref, qkv_ref, att_ref, line):
     my_heads, my_kv, head_dim = heads
     x = x_ref[b].astype(f32)
@@ -902,13 +918,17 @@
         _, k_unit = unit_of(qkv_ref[b, :, at_k : at_k + head_dim])
         k_rot = turned(k_unit * kg_ref[...], cosine, sine).astype(bf16)
         values = qkv_ref[b, :, at_v : at_v + head_dim].astype(bf16)
-        for h in range(n * group, (n + 1) * group):
-            span = slice(h * head_dim, (h + 1) * head_dim)
+
+        def head(h, carry):
+            span = pl.ds(pl.multiple_of(h * head_dim, head_dim), head_dim)
             _, q_unit = unit_of(qkv_ref[b, :, span])
             q_rot = turned(q_unit * qg_ref[...], cosine, sine).astype(bf16)
             probs = softmax_rows(q_rot, k_rot, bias, head_dim)
             mixed = jnp.dot(probs.astype(bf16), values, preferred_element_type=f32)
             att_ref[b, :, span] = mixed.astype(bf16)
+            return carry
+
+        loop_heads(n * group, (n + 1) * group, head, 0)
     line[...] = jnp.dot(att_ref[b], wo_ref[...], preferred_element_type=f32).astype(bf16)
 
 
@@ -924,10 +944,11 @@
         k_inverse, k_unit = unit_of(qkv_ref[b, :, at_k : at_k + head_dim])
         k_rot = turned(k_unit * kg, cosine, sine).astype(bf16)
         values = qkv_ref[b, :, at_v : at_v + head_dim].astype(bf16)
-        grad_k = jnp.zeros(k_unit.shape, f32)
-        grad_v = jnp.zeros(k_unit.shape, f32)
-        for h in range(n * group, (n + 1) * group):
-            span = slice(h * head_dim, (h + 1) * head_dim)
+        nothing = jnp.zeros(k_unit.shape, f32)
+
+        def head(h, carry):
+            grad_k, grad_v = carry
+            span = pl.ds(pl.multiple_of(h * head_dim, head_dim), head_dim)
             q_inverse, q_unit = unit_of(qkv_ref[b, :, span])
             q_rot = turned(q_unit * qg, cosine, sine).astype(bf16)
             probs = softmax_rows(q_rot, k_rot, bias, head_dim)
@@ -941,6 +962,9 @@
             grad_q = turned(grad_q, cosine, -sine)
             qsum_ref[...] += jnp.sum(grad_q * q_unit, axis=0, keepdims=True)
             gqkv_ref[b, :, span] = back_unit(grad_q, q_unit, q_inverse, qg).astype(bf16)
+            return grad_k, grad_v
+
+        grad_k, grad_v = loop_heads(n * group, (n + 1) * group, head, (nothing, nothing))
         grad_k = turned(grad_k, cosine, -sine)
         ksum_ref[...] += jnp.sum(grad_k * k_unit, axis=0, keepdims=True)
         gqkv_ref[b, :, at_k : at_k + head_dim] = back_unit(grad_k, k_unit, k_inverse, kg).astype(bf16)
@@ -1071,11 +1095,17 @@
         width = ga_ref.shape[1]
         block = att_ref.shape[2] // g.reps
         grads = gas_ref[...].reshape(n * rows, width)
-        for place in range(g.places):
-            for core in range(2):
-                at = (place * 2 + core) * block
-                mixed = att_ref[:, :, at : at + block].reshape(n * rows, block)
-                both[core, 0, place] = t_dot(mixed, grads).astype(bf16)
+        def one(i, carry):
+            at = pl.ds(pl.multiple_of(i * block, 128), block) if block % 128 == 0 else slice(i * block, (i + 1) * block)
+            mixed = att_ref[:, :, at].reshape(n * rows, block)
+            both[i % 2, 0, i // 2] = t_dot(mixed, grads).astype(bf16)
+            return carry
+
+        if block % 128 == 0:
+            lax.fori_loop(0, g.reps, one, 0)
+        else:
+            for i in range(g.reps):
+                one(i, 0)
 
     line(0)
     scatter.to_partner()
@@ -1420,9 +1450,10 @@
 
 def experts_kernel(reps, shards, capacity, held, *refs):
     (
-        x_ref, slab_ref, cots_ref, wg_ref, wu_ref, wd_ref,
+        x_ref, slab_ref, cots_ref, wg_in, wu_in, wd_in,
         back_ref, sums_ref, grads_ref, rows_ref, cs_ref, gg_ref, gu_ref, act_ref, all_ref,
         slabs, cot_buf, hid_buf, d_ref, x_buf, c_buf, gg_buf, gu_buf, act_buf, sum_buf, grad_buf,
+        wg_ref, wu_ref, wd_ref,
         sems, ps, pr, ls, cot_sem, hid_sem, out_sems, zr, *plane_sems,
     ) = refs
     g = Grid(reps, shards).here()
@@ -1447,7 +1478,12 @@
         return [slots_of(slabs[(q * 2 + core) * n + zp], capacity) for q in range(places)]
 
     keep = pltpu.make_async_copy(x_ref, gather.own(), ls.at[0])
-    keep.start()
+    weights = [
+        pltpu.make_async_copy(src, dst, ls.at[2 + i])
+        for i, (src, dst) in enumerate(((wd_in, wd_ref), (wg_in, wg_ref), (wu_in, wu_ref)))
+    ]
+    for copy in [keep] + weights:
+        copy.start()
     cot_load(0, 0).start()
     greet_all(g)
     push_rows(g, slab_ref, slabs, ps, pr)
@@ -1458,6 +1494,8 @@
     keep_slab.wait()
     push_wait(g, slab_ref, slabs, ps, pr)
     keep.wait()
+    for copy in weights:
+        copy.wait()
 
     def turns(k, steps):
         for at, step in steps:
@@ -1592,7 +1630,7 @@
             narrow,
             jax.ShapeDtypeStruct((1, 16, 128) if held else gathered, bf16),
         ),
-        in_specs=[vmem, vmem, hbm, vmem, vmem, vmem],
+        in_specs=[vmem, vmem, hbm, hbm, hbm, hbm],
         out_specs=(vmem,) + (hbm,) * 8,
         scratch_shapes=[
             v(slab.shape, f32),
@@ -1606,10 +1644,13 @@
             v((rows, inner), bf16),
             v((places, length, width), bf16),
             v((places, length, width), bf16),
+            v(wg.shape, bf16),
+            v(wu.shape, bf16),
+            v(wd.shape, bf16),
             dma((2 * GatherAll.sends(g),)),
             dma((g.devices,)),
             dma((g.devices,)),
-            dma((2,)),
+            dma((5,)),
             dma((2,)),
             dma((1,)),
             dma((7,)),

time: 573 us -> 563 us (0.983)
    pallas_call x1, Pallas kernels: 121 us -> 134 us  [front(): pl.pallas_call(functools.partial(front_kernel, reps, shards, heads, layou...]
    pallas_call x1, Pallas kernels: 98.5 us -> 89.9 us  [scatter_all(): pl.pallas_call(functools.partial(scatter_all_kernel, reps, shards, slabbe...]
    pallas_call x1, Pallas kernels: 103 us -> 95.4 us  [experts_all(): pl.pallas_call(functools.partial(experts_kernel, reps, shards, capacity,...]
where the time goes in v8:
time: 563 us; the launch traced here: 559 us
  Pallas kernels  506 us (90%)
  local copies, waits for them, and re-layouts  26.8 us (5%)
  other arithmetic  23 us (4%)
    pallas_call x1, Pallas kernels, front(): pl.pallas_call(functools.partial(front_kernel, reps, shards, heads, layou...  134 us
    pallas_call x1, Pallas kernels, attend_back(): pl.pallas_call(functools.partial(attend_back_kernel, reps, shards, heads)...  96.3 us
    pallas_call x1, Pallas kernels, experts_all(): pl.pallas_call(functools.partial(experts_kernel, reps, shards, capacity,...  95.4 us
    pallas_call x1, Pallas kernels, deliver(): pl.pallas_call(functools.partial(deliver_kernel, reps, shards, (q_cols, e...  90.4 us
    pallas_call x1, Pallas kernels, scatter_all(): pl.pallas_call(functools.partial(scatter_all_kernel, reps, shards, slabbe...  89.9 us
    unnamed x33, local copies, waits for them, and re-layouts  13.3 us

profile of v8, /device:TPU:17, one launch (start us, length us, event | category | flops | bytes accessed | tf_op | source)
XLA Modules:
  0.0 558.8 jit_solution(16644736521445423353)
XLA Ops:
  0.6 0.7 convert_element_type.65
  1.3 0.1 pad.16.clone
  1.4 0.6 maximum_bitcast_fusion.refs_3_
  2.0 0.7 reshape.216
  2.7 0.7 reshape.217
  3.4 0.7 fusion.7
  4.1 0.7 tile.16
  4.7 0.1 tile.17
  4.8 0.7 tile.18
  5.5 0.1 tile.19
  5.6 0.8 concatenate.9
  6.4 0.6 pad.13.refs_2_
  7.0 133.5 %front.1 = (bf16[4,48,512]{2,1,0:T(8,128)(2,1)}, f32[8,2048]{1,0:T(8,128)}, f32[8,128]{1,0:T(8,128)}, f32[4,128,128]{2,1,0:T(8,128)}, f32[4,128,128]{2,1,0:T(8,1...) custom-call(bf16[128,2048]{1,0:T(8,128)(2,1)} %refs_0_.1, ...), custom_call_target="tpu_custom_call" | custom-call | tf_op jit(solution)/shard_map/front/pallas_call | solution.py:1378
  140.5 0.0 copy-done.3
  140.5 1.5 multiply_reduce_fusion.2
  142.1 1.3 fusion.15
  143.3 0.9 fusion.14
  144.3 0.9 slice_bitcast_fusion
  145.2 0.2 multiply_convert_fusion.refs_0_
  145.4 0.0 copy-start.1
  145.4 0.3 fusion.16
  145.8 0.7 broadcast_in_dim.47.refs_1_
  146.4 0.0 copy-done.1
  146.4 95.4 %experts_all.1 = (f32[32,8,128]{2,1,0:T(8,128)}, bf16[4,2,4,128,2048]{4,3,2,1,0:T(8,128)(2,1)}, bf16[4,2,4,128,2048]{4,3,2,1,0:T(8,128)(2,1)}, bf16[8,256,2048]{...) custom-call(bf16[128,2048]{1,0:T(8,128)(2,1)} %copy-done.1, ...), custom_call_target="tpu_custom_call" | custom-call | tf_op jit(solution)/shard_map/experts_all/pallas_call | solution.py:1620
  241.9 0.0 copy-start.2
  241.9 89.9 %scatter_all.1 = (f32[128,2048]{1,0:T(8,128)}, f32[32,8,128]{2,1,0:T(8,128)}, f32[2048,768]{1,0:T(8,128)}, f32[2048,768]{1,0:T(8,128)}, f32[768,2048]{1,0:T(8,128)}) custom-call(bf16[4,2,4,128,2048]{4,3,2,1,0:T(8,128)(2,1)} %get-tuple-element.53.refs_0_, f32[32,8,128]{2,1,0:T(8,128)} %get-tuple-element.54.refs_1_, bf16[2048,2048]{1,0:T(8,128)(2,1)} %bitcast.62, ...), custom_call_target="tpu_custom_call" | custom-call | tf_op jit(solution)/shard_map/scatter_all/pallas_call | solution.py:617
  331.8 0.0 copy-start.5
  331.9 1.0 slice.44
  332.9 0.0 copy-done.2
  332.9 0.2 fusion.17
  333.1 1.8 multiply_reduce_fusion
  334.9 0.0 copy-start
  334.9 0.1 pad_maximum_fusion
  335.0 0.9 copy-done
  335.9 0.0 copy-done.5
  335.9 1.1 fusion.13.refs_0_
  337.0 96.3 %attend_back.1 = (bf16[4,128,1280]{2,1,0:T(8,128)(2,1)}, f32[1,128]{1,0:T(1,128)}, f32[1,128]{1,0:T(1,128)}, f32[128,2048]{1,0:T(8,128)}, bf16[128,2048]{1,0:T(8,128)(2,1)}) custom-call(bf16[128,2048]{1,0:T(8,128)(2,1)} %fusion.13.refs_0_, f32[1,128]{1,0:T(1,128)} %get-tuple-element.142.refs_1_, f32[1,128]{1,0:T(1,128)} %get-tuple-element.141.refs_2_, ...), custom_call_target="tpu_custom_call" | custom-call | tf_op jit(solution)/shard_map/attend_back/pallas_call | solution.py:1163
  433.4 0.4 copy.53
  433.7 1.0 pad.14.refs_1_
  434.8 90.4 %deliver.1 = (f32[128,2048]{1,0:T(8,128)}, bf16[8,64,4096]{2,1,0:T(8,128)(2,1)}, bf16[4,8,64,384]{3,2,1,0:T(8,128)(2,1)}, bf16[8,128,2048]{2,1,0:T(8,128)(2,1)}) custom-call(bf16[512,1280]{1,0:T(8,128)(2,1)} %bitcast.84, f32[2048,128]{1,0:T(8,128)} %pad.14.refs_1_, f32[1,128]{1,0:T(1,128)} %get-tuple-element.71.refs_2_, f32[1,128]{1,0:T(1,128)} %get-tuple-element.72.refs_3_, ...), custom_call_target="tpu_custom_call" | custom-call | tf_op jit(solution)/shard_map/deliver/pallas_call | solution.py:828
  525.1 0.0 copy-done.4
  525.1 1.5 fusion.2
  526.7 3.6 fusion.5
  530.3 1.1 convert_reduce_fusion
  531.5 0.7 slice_reduce_fusion.2
  532.1 0.9 slice_reduce_fusion
  533.1 0.7 copy.56
  533.8 1.5 convert_bitcast_fusion
  535.3 1.1 copy.62
  536.4 1.1 copy.63
  537.6 0.0 copy-done.7
  537.6 5.5 bitcast_convert_fusion.1
  543.0 0.0 copy-done.6
  543.0 4.7 bitcast_convert_fusion
  547.8 0.0 slice-done.4
  547.8 0.0 slice-done.5
  547.8 0.0 slice-start
  547.8 3.2 copy.67
  551.0 0.0 slice-done.2
  551.0 0.0 slice-done.3
  551.0 3.2 copy.68
  554.2 0.9 slice-done
  555.1 0.8 slice-done.1
  555.8 2.7 copy.69
  (25 shorter events, 0.2 us)
Async XLA Ops:
  7.0 133.5 %copy-start.3 = (bf16[128,2048]{1,0:T(8,128)(2,1)S(1)}, bf16[128,2048]{1,0:T(8,128)(2,1)}, u32[]{:S(2)}) copy-start(bf16[128,2048]{1,0:T(8,128)(2,1)} %refs_0_.1) | copy-start | bytes 1572868
  145.4 1.1 copy-start.1
  241.9 91.0 %copy-start.2 = (bf16[128,2048]{1,0:T(8,128)(2,1)S(1)}, bf16[128,2048]{1,0:T(8,128)(2,1)}, u32[]{:S(2)}) copy-start(bf16[128,2048]{1,0:T(8,128)(2,1)} %copy-done.1) | copy-start | bytes 1572868
  331.8 4.0 copy-start.5
  334.9 1.0 copy-start
  434.8 90.4 %copy-start.4 = (bf16[128,2048]{1,0:T(8,128)(2,1)S(1)}, bf16[128,2048]{1,0:T(8,128)(2,1)}, u32[]{:S(2)}) copy-start(bf16[128,2048]{1,0:T(8,128)(2,1)} %refs_0_.1) | copy-start | bytes 1572868
  533.8 3.7 copy-start.7
  537.6 5.5 copy-start.6
  537.6 10.2 %slice-start.4 = ((s8[6291456]{0:T(1024)(128)(4,1)}), s8[4194304]{0:T(1024)(128)(4,1)S(1)}, s32[]{:S(2)}) async-start(s8[6291456]{0:T(1024)(128)(4,1)} %bitcast.70), calls=%async_computation.4 | async-start | bytes 8388608
  543.0 4.8 slice-start.5
  543.0 8.0 %slice-start.2 = ((s8[6291456]{0:T(1024)(128)(4,1)}), s8[4194304]{0:T(1024)(128)(4,1)S(1)}, s32[]{:S(2)}) async-start(s8[6291456]{0:T(1024)(128)(4,1)} %bitcast.67), calls=%async_computation.2 | async-start | bytes 8388608
  547.8 3.2 slice-start.3
  547.8 7.3 %slice-start = ((s8[6291456]{0:T(1024)(128)(4,1)}), s8[4194304]{0:T(1024)(128)(4,1)S(1)}, s32[]{:S(2)}) async-start(s8[6291456]{0:T(1024)(128)(4,1)} %bitcast.64), calls=%async_computation | async-start | bytes 8388608
  551.0 4.8 slice-start.1
